TPU v7x, 128 devices: a whole 4x4x4 slice. The times are simulated.
128 devices in a mesh: batch: 4 (over y_hi, core), tm: 8 (over x, y_lo), space: 4 (over z).
Axes of the slice: x: 4, y: 4 (y_hi: 2, y_lo: 2; y = y_hi * 2 + y_lo), z: 4, core: 2. Of those that a mesh axis runs over, the one named last changes fastest.
Arguments:
- clip_tokens: bfloat16 [4, 16, 32, 32, 1024], P('batch', None, 'space', 'tm'), may hold values from -6 to 6
- frame_order: int32 [4, 16], P('batch'), may hold values from 0 to 15, each once within a row
- row_reach: int32 [4, 16], P('batch', 'tm'), may hold values from 1 to 4
- spatial_gain: float32 [1024], replicated, may hold values from 0.1 to 1.9
- spatial_heads: bfloat16 [1024, 3072], replicated, may hold values from -2 to 2
- spatial_merge: bfloat16 [1024, 1024], replicated, may hold values from -0.1875 to 0.1875
- temporal_gain: float32 [1024], replicated, may hold values from 0.1 to 1.9
- temporal_heads: bfloat16 [1024, 3072], replicated, may hold values from -2 to 2
- temporal_merge: bfloat16 [1024, 1024], replicated, may hold values from -0.1875 to 0.1875
- cotangent: bfloat16 [4, 16, 32, 32, 1024], P('batch', 'tm', 'space'), may hold values from -0.059814453 to 0.059814453
Outputs:
- output: bfloat16 [4, 16, 32, 32, 1024], P('batch', 'tm', 'space')
- weight_grad: float32 [1024, 1024], P(('tm', 'space'))
Inputs may be any that keep to these rules, and one draw needn't show every extreme that they name: Each row of frame_order names every number from 0 to 15 once.
All inputs are finite; a program needn't handle non-finite values.
Results may differ from a plain program's by a relative error of at most 0.025.
Values may be sent and summed in bfloat16 or wider, within the bound.
No kernel may reach another device: no remote copies, remote signals or barrier semaphores. Data moves between devices by JAX's collectives and lax.ppermute only.
A program may use at most 128 MiB of HBM per device.

v0:
```python
import jax
import jax.numpy as jnp
from jax import lax
from jax.sharding import PartitionSpec as P

HALO = 4
D = 1024
HEADS = 16
HEAD_DIM = 64


floor_term = 0.5


def extended(value, sides, width):
    for axis, dim in sides:
        devices, length = (lax.axis_size(axis), value.shape[dim])
        up = [(i, (i + 1) % devices) for i in range(devices - 1)]
        down = [(j, i) for i, j in up]
        last = lax.slice_in_dim(value, length - width, length, axis=dim)
        initial = lax.slice_in_dim(value, 0, width, axis=dim)
        before = lax.ppermute(last, axis, up)
        after = lax.ppermute(initial, axis, down)
        value = jnp.concatenate([before, value, after], axis=dim)
    return value


def in_blocks(value, dim, devices):
    before, after = (value.shape[:dim], value.shape[dim + 1 :])
    return jnp.moveaxis(value.reshape(*before, devices, -1, *after), dim, 0)


def summed_on_arrival(value, axis, dim):
    parts = in_blocks(value, dim, lax.axis_size(axis))
    arrived = lax.all_to_all(parts, axis, split_axis=0, concat_axis=0, tiled=True)
    return arrived.astype(jnp.float32).sum(axis=0)


def gathered_total(value, axis):
    return lax.all_gather(value, axis).astype(jnp.float32).sum(0)


def normalize(values, gain_vector):
    widened = values.astype(jnp.float32)
    scaled = widened * lax.rsqrt(jnp.mean(widened * widened, axis=-1, keepdims=True) + floor_term)
    return (scaled * gain_vector).astype(jnp.bfloat16)


def softmax_rounded(scores, allowed):
    masked = jnp.where(allowed, scores, -1e30)
    top_score = jnp.max(masked, axis=-1, keepdims=True)
    exponent = jnp.exp(masked - top_score)
    return (exponent / jnp.sum(exponent, axis=-1, keepdims=True)).astype(jnp.bfloat16)


def temporal_attend(queries, keys_all, values_all, query_order, key_order):
    clip_count, query_frames, positions, _ = queries.shape
    key_frames = keys_all.shape[1]
    query_heads = queries.reshape(clip_count, query_frames, positions, HEADS, HEAD_DIM)
    key_heads = keys_all.reshape(clip_count, key_frames, positions, HEADS, HEAD_DIM)
    value_heads = values_all.reshape(clip_count, key_frames, positions, HEADS, HEAD_DIM)
    scores = jnp.einsum(
        "cfthd,cgthd->cthfg", query_heads, key_heads, preferred_element_type=jnp.float32
    ) * HEAD_DIM ** (-0.5)
    allowed = key_order[:, None, :] <= query_order[:, :, None]
    weights = softmax_rounded(scores, allowed[:, None, None])
    context = jnp.einsum(
        "cthfg,cgthd->cfthd", weights, value_heads, preferred_element_type=jnp.float32
    )
    return context.reshape(clip_count, query_frames, positions, D).astype(jnp.bfloat16)


def per_device(
    clip_tokens,
    frame_order,
    row_reach,
    spatial_gain,
    spatial_heads,
    spatial_merge,
    temporal_gain,
    temporal_heads,
    temporal_merge,
    cotangent,
):
    frames_here = lax.all_to_all(clip_tokens, "tm", split_axis=1, concat_axis=3, tiled=True)
    clip_count, frame_count, row_count, col_count, _ = frames_here.shape
    tokens = row_count * col_count
    normed = normalize(frames_here, spatial_gain)
    projected = jnp.dot(normed, spatial_heads, preferred_element_type=jnp.float32).astype(
        jnp.bfloat16
    )
    widened = extended(normed, (("space", 2),), HALO)
    key_weight = spatial_heads[:, D:]
    upper_rows = jnp.dot(
        widened[:, :, :HALO], key_weight, preferred_element_type=jnp.float32
    ).astype(jnp.bfloat16)
    lower_rows = jnp.dot(
        widened[:, :, HALO + row_count :], key_weight, preferred_element_type=jnp.float32
    ).astype(jnp.bfloat16)
    key_value = jnp.concatenate([upper_rows, projected[..., D:], lower_rows], axis=2)
    extent = (row_count + 2 * HALO) * col_count
    first_row = lax.axis_index("space") * row_count
    all_rows = row_count * lax.axis_size("space")
    query_rows = first_row + jnp.arange(tokens, dtype=jnp.int32) // col_count
    key_rows = first_row - HALO + jnp.arange(extent, dtype=jnp.int32) // col_count
    inside = (key_rows >= 0) & (key_rows < all_rows)
    distance = jnp.abs(key_rows[None, :] - query_rows[:, None])

    def spatial_item(inputs):
        queries, key_pairs, reach_now = inputs
        query_heads = queries.reshape(tokens, HEADS, HEAD_DIM)
        key_heads = key_pairs[:, :D].reshape(extent, HEADS, HEAD_DIM)
        value_heads = key_pairs[:, D:].reshape(extent, HEADS, HEAD_DIM)
        scores = jnp.einsum(
            "qhd,khd->hqk", query_heads, key_heads, preferred_element_type=jnp.float32
        ) * HEAD_DIM ** (-0.5)
        allowed = inside[None, :] & (distance <= reach_now)
        weights = softmax_rounded(scores, allowed[None])
        context = jnp.einsum(
            "hqk,khd->qhd", weights, value_heads, preferred_element_type=jnp.float32
        )
        return context.reshape(tokens, D).astype(jnp.bfloat16)

    item_count = clip_count * frame_count
    spatial_context = lax.map(
        spatial_item,
        (
            projected[..., :D].reshape(item_count, tokens, D),
            key_value.reshape(item_count, extent, 2 * D),
            row_reach.reshape(item_count),
        ),
    )
    flat_input = frames_here.reshape(clip_count, frame_count, tokens, D)
    spatial_context = spatial_context.reshape(clip_count, frame_count, tokens, D)
    middle = (
        flat_input.astype(jnp.float32)
        + jnp.dot(spatial_context, spatial_merge, preferred_element_type=jnp.float32)
    ).astype(jnp.bfloat16)
    normed_two = normalize(middle, temporal_gain)
    projected_two = jnp.dot(normed_two, temporal_heads, preferred_element_type=jnp.float32).astype(
        jnp.bfloat16
    )
    regrouped = lax.all_to_all(projected_two, "tm", split_axis=2, concat_axis=1, tiled=True)
    context_all = temporal_attend(
        regrouped[..., :D],
        regrouped[..., D : 2 * D],
        regrouped[..., 2 * D :],
        frame_order,
        frame_order,
    )
    temporal_context = lax.all_to_all(context_all, "tm", split_axis=1, concat_axis=2, tiled=True)
    output = (
        middle.astype(jnp.float32)
        + jnp.dot(temporal_context, temporal_merge, preferred_element_type=jnp.float32)
    ).astype(jnp.bfloat16)
    flat_context = temporal_context.reshape(-1, D)
    flat_cotangent = cotangent.reshape(-1, D)
    own_rows = summed_on_arrival(
        lax.dot_general(
            flat_context,
            flat_cotangent,
            (((0,), (0,)), ((), ())),
            preferred_element_type=jnp.float32,
        ).astype(jnp.bfloat16),
        ("tm", "space"),
        0,
    )
    weight_grad = gathered_total(own_rows.astype(jnp.bfloat16), "batch").astype(jnp.float32)
    return (output.reshape(clip_count, frame_count, row_count, col_count, D), weight_grad)


def solution(mesh):
    in_specs = (
        P("batch", None, "space", "tm", None),
        P("batch", None),
        P("batch", "tm"),
        P(),
        P(),
        P(),
        P(),
        P(),
        P(),
        P("batch", "tm", "space", None, None),
    )
    out_specs = (P("batch", "tm", "space", None, None), P(("tm", "space"), None))
    return jax.shard_map(
        per_device, mesh=mesh, in_specs=in_specs, out_specs=out_specs, check_vma=False
    )
```

profile of v0, /device:TPU:1, one launch (start us, length us, event | category | flops | bytes accessed | tf_op | source)
XLA Modules:
  0.0 272.9 jit_solution(8427147431864572981)
XLA Ops:
  0.6 6.0 %all-to-all-start = ((bf16[1,16,8,4,1024]{4,3,2,0,1:T(4,128)(2,1)}), bf16[1,16,8,4,1024]{4,3,2,0,1:T(4,128)(2,1)S(1)}, u32[]{:S(2)}, u32[]{:S(2)}) async-start(bf16[1,16,8,4,1024]{4,3,2,0,1:T(4,128)(2,1)} %bitcast.156), calls=%async_computation | async-start | bytes 2097152 | tf_op jit(solution)/shard_map/all_to_all | solution.py:85
  6.7 15.3 %all-to-all-done = bf16[1,16,8,4,1024]{4,3,2,0,1:T(4,128)(2,1)S(1)} async-done(((bf16[1,16,8,4,1024]{4,3,2,0,1:T(4,128)(2,1)}), bf16[1,16,8,4,1024]{4,3,2,0,1:T(4,128)(2,1)S(1)}, u32[]{:S(2)}, u32[]{:S(2)}) %all-to-all-start) | async-done | bytes 1048608 | tf_op jit(solution)/shard_map/all_to_all | solution.py:85
  21.9 2.0 copy_bitcast_fusion
  23.9 3.0 %reshape.333 = f32[2,8,32,1024]{3,2,1,0:T(8,128)} reshape(f32[1,2,8,8,4,1024]{5,4,3,2,1,0:T(4,128)} %copy_bitcast_fusion) | data formatting | bytes 4194304 | tf_op jit(solution)/shard_map/convert_element_type | solution.py:44
  26.9 3.0 %reshape.330 = f32[1,2,8,32,1024]{4,3,2,1,0:T(8,128)} reshape(f32[1,2,8,8,4,1024]{5,4,3,2,1,0:T(4,128)} %copy_bitcast_fusion) | data formatting | bytes 4194304 | tf_op jit(solution)/shard_map/convert_element_type | solution.py:44
  30.8 2.0 multiply_convert_fusion.1
  32.9 1.3 collective-permute-start.1
  34.2 5.0 %collective-permute-start = (bf16[1,2,4,32,1024]{4,3,2,1,0:T(8,128)(2,1)S(1)}, bf16[1,2,4,32,1024]{4,3,2,1,0:T(8,128)(2,1)}, u32[]{:S(2)}, u32[]{:S(2)}) collective-permute-start(bf16[1,2,4,32,1024]{4,3,2,1,0:T(8,128)(2,1)S(1)} %get-tuple-element.133), channel_id=1, source_target_pairs={{0,1},{1,2},{2,3},{4,5},{5,6},{6,7},{8,9},{9,10},{10,11},{12,13},{... | collective-permute-start | bytes 1572872 | tf_op jit(solution)/shard_map/ppermute | solution.py:22
  39.1 6.5 %fusion.35 = bf16[1,2,8,32,3072]{4,3,2,1,0:T(8,128)(2,1)S(1)} fusion(bf16[1024,3072]{1,0:T(8,128)(2,1)} %param.16, f32[2,8,32,1024]{3,2,1,0:T(8,128)S(1)} %copy-done.7, f32[1024]{0:T(1024)S(1)} %copy-done.8, f32[2,8,32]{2,1,0:T(8,128)S(1)} %copy.95), kind=kOutput, calls=%fused_computation.45 | convolution fusion | flops 3224371200 | bytes 11540480 | tf_op jit(solution)/shard_map/dot_general | solution.py:89
  45.7 1.6 copy-done.3
  47.3 1.1 slice.45
  48.4 2.9 %reshape.329 = f32[2,256,1024]{2,1,0:T(8,128)} reshape(f32[1,2,8,8,4,1024]{5,4,3,2,1,0:T(4,128)} %copy_bitcast_fusion) | data formatting | bytes 4194304 | tf_op jit(solution)/shard_map/convert_element_type | solution.py:136
  51.4 3.6 %fusion.50 = bf16[1,2,4,32,2048]{4,3,2,1,0:T(8,128)(2,1)S(1)} fusion(bf16[1024,3072]{1,0:T(8,128)(2,1)} %param.16, bf16[1,2,4,32,1024]{4,3,2,1,0:T(8,128)(2,1)} %collective-permute-done.1), kind=kOutput, calls=%fused_computation.55 | convolution fusion | flops 1074266112 | bytes 5767168 | tf_op jit(solution)/shard_map/dot_general | solution.py:97
  55.0 3.7 %fusion.53 = bf16[1,2,4,32,2048]{4,3,2,1,0:T(8,128)(2,1)S(1)} fusion(bf16[1024,3072]{1,0:T(8,128)(2,1)} %param.16, bf16[1,2,4,32,1024]{4,3,2,1,0:T(8,128)(2,1)} %collective-permute-done), kind=kOutput, calls=%fused_computation.56 | convolution fusion | flops 1074266112 | bytes 5767168 | tf_op jit(solution)/shard_map/dot_general | solution.py:94
  58.8 2.2 pad_maximum_fusion
  61.0 52.2 %while.11 = (s32[]{:T(128)}, bf16[2,256,1024]{1,2,0:T(8,128)(2,1)}, bf16[2,512,2048]{2,1,0:T(8,128)(2,1)}, s32[2]{0:T(128)S(1)}, bf16[2,256,1024]{2,1,0:T(8,128)...) while((s32[]{:T(128)}, bf16[2,256,1024]{1,2,0:T(8,128)(2,1)}, ...), condition=%wide.region_4.5_spmd.clone, body=%wide.region_1.4_spmd.clone.sunk | while | flops 550246912 | bytes 44339888 | solution.py:125
  62.6 3.2 %constant_dynamic-slice_fusion.4 = bf16[1,512,2048]{2,1,0:T(8,128)(2,1)} fusion(bf16[2,512,2048]{2,1,0:T(8,128)(2,1)} %get-tuple-element.216, s32[]{:T(128)} %get-tuple-element.205), kind=kLoop, calls=%fused_computation.26.clone.1 | loop fusion | bytes 4194308 | tf_op jit(solution)/shard_map/while/body/jit(dynamic_index_in_dim)/dynamic_slice | solution.py:125
  65.8 3.9 %copy.132 = bf16[1,512,2048]{1,2,0:T(8,128)(2,1)} copy(bf16[1,512,2048]{2,1,0:T(8,128)(2,1)} %constant_dynamic-slice_fusion.4) | data formatting | bytes 4194304 | tf_op jit(solution)/shard_map/while/body/jit(dynamic_index_in_dim)/dynamic_slice | solution.py:125
  69.7 3.1 %fusion.119 = (bf16[512,1024]{0,1:T(8,128)(2,1)}, bf16[512,1024]{0,1:T(8,128)(2,1)}) fusion(bf16[512,2048]{0,1:T(8,128)(2,1)} %bitcast.141), kind=kLoop, calls=%fused_computation.108.clone.1 | loop fusion | bytes 4194304 | tf_op jit(solution)/shard_map/while/body/eval_jaxpr/slice | solution.py:112
  73.8 7.6 %fusion.121 = (f32[16,256]{1,0:T(8,128)S(1)}, f32[16,256,512]{2,1,0:T(8,128)}) fusion(pred[256,512]{1,0:T(8,128)(4,1)S(1)} %fusion.120, bf16[256,16,64]{0,2,1:T(8,128)(2,1)} %bitcast.145, bf16[512,16,64]{0,2,1:T(8,128)(2,1)} %bitcast.144), kind=kOutput, calls=%fused_computation.109.clone.1 | convolution fusion | flops 276824576 | bytes 10108928 | tf_op jit(solution)/shard_map/while/body/eval_jaxpr/sub | solution.py:52
  81.4 4.9 %fusion.122 = bf16[16,64,256]{2,1,0:T(8,128)(2,1)S(1)} fusion(bf16[512,16,64]{0,2,1:T(8,128)(2,1)S(1)} %bitcast.143, f32[16,256,512]{2,1,0:T(8,128)} %get-tuple-element.194, f32[16,256]{1,0:T(8,128)S(1)} %get-tuple-element.195), kind=kOutput, calls=%fused_computation.11.clone.1 | convolution fusion | flops 272891904 | bytes 9977856 | tf_op jit(solution)/shard_map/while/body/eval_jaxpr/hqk,khd->qhd/dot_general | solution.py:119
  88.7 3.2 %constant_dynamic-slice_fusion.4 = bf16[1,512,2048]{2,1,0:T(8,128)(2,1)} fusion(bf16[2,512,2048]{2,1,0:T(8,128)(2,1)} %get-tuple-element.216, s32[]{:T(128)} %get-tuple-element.205), kind=kLoop, calls=%fused_computation.26.clone.1 | loop fusion | bytes 4194308 | tf_op jit(solution)/shard_map/while/body/jit(dynamic_index_in_dim)/dynamic_slice | solution.py:125
  91.9 3.9 %copy.132 = bf16[1,512,2048]{1,2,0:T(8,128)(2,1)} copy(bf16[1,512,2048]{2,1,0:T(8,128)(2,1)} %constant_dynamic-slice_fusion.4) | data formatting | bytes 4194304 | tf_op jit(solution)/shard_map/while/body/jit(dynamic_index_in_dim)/dynamic_slice | solution.py:125
  95.8 3.1 %fusion.119 = (bf16[512,1024]{0,1:T(8,128)(2,1)}, bf16[512,1024]{0,1:T(8,128)(2,1)}) fusion(bf16[512,2048]{0,1:T(8,128)(2,1)} %bitcast.141), kind=kLoop, calls=%fused_computation.108.clone.1 | loop fusion | bytes 4194304 | tf_op jit(solution)/shard_map/while/body/eval_jaxpr/slice | solution.py:112
  99.9 7.6 %fusion.121 = (f32[16,256]{1,0:T(8,128)S(1)}, f32[16,256,512]{2,1,0:T(8,128)}) fusion(pred[256,512]{1,0:T(8,128)(4,1)S(1)} %fusion.120, bf16[256,16,64]{0,2,1:T(8,128)(2,1)} %bitcast.145, bf16[512,16,64]{0,2,1:T(8,128)(2,1)} %bitcast.144), kind=kOutput, calls=%fused_computation.109.clone.1 | convolution fusion | flops 276824576 | bytes 10108928 | tf_op jit(solution)/shard_map/while/body/eval_jaxpr/sub | solution.py:52
  107.6 4.9 %fusion.122 = bf16[16,64,256]{2,1,0:T(8,128)(2,1)S(1)} fusion(bf16[512,16,64]{0,2,1:T(8,128)(2,1)S(1)} %bitcast.143, f32[16,256,512]{2,1,0:T(8,128)} %get-tuple-element.194, f32[16,256]{1,0:T(8,128)S(1)} %get-tuple-element.195), kind=kOutput, calls=%fused_computation.11.clone.1 | convolution fusion | flops 272891904 | bytes 9977856 | tf_op jit(solution)/shard_map/while/body/eval_jaxpr/hqk,khd->qhd/dot_general | solution.py:119
  113.3 3.3 %fusion.56 = (f32[2,256]{1,0:T(2,128)S(1)}, bf16[2,256,1024]{2,1,0:T(8,128)(2,1)S(1)}) fusion(f32[2,256,1024]{2,1,0:T(8,128)} %reshape.329, bf16[2,256,1024]{1,2,0:T(8,128)(2,1)} %get-tuple-element.39, bf16[1024,1024]{1,0:T(8,128)(2,1)S(1)} %copy-done), kind=kOutput, calls=%fused_computation.57 | convolution fusion | flops 1076362752 | bytes 6293504 | tf_op jit(solution)/shard_map/dot_general | solution.py:137
  117.5 6.6 %fusion.38 = bf16[1,2,256,3072]{3,2,1,0:T(8,128)(2,1)S(1)} fusion(bf16[1024,3072]{1,0:T(8,128)(2,1)} %param.19, bf16[2,256,1024]{2,1,0:T(8,128)(2,1)S(1)} %get-tuple-element.136, f32[1024]{0:T(1024)S(1)} %copy-done.10, f32[2,256]{1,0:T(2,128)S(1)} %add_rsqrt_fusion.1), kind=kOutput, calls=%fused_computation.46 | convolution fusion | flops 3224895488 | bytes 10491904 | tf_op jit(solution)/shard_map/dot_general | solution.py:140
  124.1 4.9 %copy.100 = bf16[1,2,256,3072]{3,1,0,2:T(2,128)(2,1)} copy(bf16[1,2,256,3072]{3,2,1,0:T(8,128)(2,1)S(1)} %fusion.38) | data formatting | bytes 6291456 | tf_op jit(solution)/shard_map/convert_element_type | solution.py:140
  129.0 4.6 %all-to-all-start.1 = ((bf16[1,2,256,3072]{3,1,0,2:T(2,128)(2,1)}), bf16[1,2,256,3072]{3,1,0,2:T(2,128)(2,1)}, u32[]{:S(2)}, u32[]{:S(2)}) async-start(bf16[1,2,256,3072]{3,1,0,2:T(2,128)(2,1)} %copy.100), calls=%async_computation.1 | async-start | bytes 6291456 | tf_op jit(solution)/shard_map/all_to_all | solution.py:143
  133.7 44.3 %all-to-all-done.1 = bf16[1,2,256,3072]{3,1,0,2:T(2,128)(2,1)} async-done(((bf16[1,2,256,3072]{3,1,0,2:T(2,128)(2,1)}), bf16[1,2,256,3072]{3,1,0,2:T(2,128)(2,1)}, u32[]{:S(2)}, u32[]{:S(2)}) %all-to-all-start.1) | async-done | bytes 3145760 | tf_op jit(solution)/shard_map/all_to_all | solution.py:143
  178.0 2.7 copy.101
  181.0 1.7 fusion.98
  182.7 4.0 %reshape.322 = bf16[16,32,16,64]{3,2,1,0:T(8,128)(2,1)} reshape(bf16[1,16,32,1024]{3,2,1,0:T(8,128)(2,1)} %get-tuple-element.132) | data formatting | bytes 2097152 | tf_op jit(solution)/shard_map/reshape.38
  186.7 4.0 %reshape.323 = bf16[16,32,16,64]{3,2,1,0:T(8,128)(2,1)} reshape(bf16[1,16,32,1024]{3,2,1,0:T(8,128)(2,1)} %get-tuple-element.131) | data formatting | bytes 2097152 | tf_op jit(solution)/shard_map/reshape.39
  190.7 2.3 reshape.321
  193.1 4.7 %fusion.66 = f32[32,16,16,16]{2,3,1,0:T(8,128)S(1)} fusion(bf16[16,32,16,64]{3,2,1,0:T(8,128)(2,1)} %reshape.323, bf16[16,32,16,64]{3,2,1,0:T(8,128)(2,1)} %reshape.322), kind=kOutput, calls=%fused_computation.68 | convolution fusion | flops 16777216 | bytes 2621440 | tf_op jit(solution)/shard_map/cfthd,cgthd->cthfg/dot_general | solution.py:62
  197.8 2.0 fusion.100
  199.8 1.7 convert_bitcast_fusion
  201.5 1.9 copy.107
  203.4 3.2 %convert_element_type.175 = bf16[1,16,32,1024]{3,2,1,0:T(8,128)(2,1)S(1)} reshape(bf16[1,16,32,16,64]{4,3,2,1,0:T(8,128)(2,1)} %copy.107) | data formatting | bytes 2097152 | tf_op jit(solution)/shard_map/convert_element_type | solution.py:70
  206.7 15.3 %all_to_all.47 = bf16[1,16,32,1024]{3,2,0,1:T(8,128)(2,1)S(1)} all-to-all(bf16[1,16,32,1024]{3,2,0,1:T(8,128)(2,1)S(1)} %bitcast.151), channel_id=1, replica_groups=mesh['batch'=4,'tm'=8,'space'=4] {'tm'}, dimensions={1} | all-to-all | bytes 2097152 | tf_op jit(solution)/shard_map/all_to_all | solution.py:151
  221.9 4.2 %bitcast_convert_fusion = bf16[1024,1024]{1,0:T(8,128)(2,1)} fusion(bf16[1,2,8,32,1024]{4,3,2,1,0:T(8,128)(2,1)} %param.21, bf16[1,8,2,32,1024]{4,3,2,1,0:T(8,128)(2,1)S(1)} %bitcast.152), kind=kOutput, calls=%fused_computation.37 | convolution fusion | flops 1074790400 | bytes 4194304 | tf_op jit(solution)/shard_map/dot_general | solution.py:159
  226.2 7.3 %all-to-all-start.3 = ((bf16[32,32,1024]{2,1,0:T(8,128)(2,1)}), bf16[32,32,1024]{2,1,0:T(8,128)(2,1)}, u32[]{:S(2)}, u32[]{:S(2)}) async-start(bf16[32,32,1024]{2,1,0:T(8,128)(2,1)} %bitcast.154), calls=%async_computation.3 | async-start | bytes 4194304 | tf_op jit(solution)/shard_map/all_to_all | solution.py:35
  233.6 4.1 %fusion.59 = bf16[2,256,1024]{2,1,0:T(8,128)(2,1)} fusion(bf16[2,256,1024]{2,1,0:T(8,128)(2,1)} %copy-done.12, bf16[2,256,1024]{2,1,0:T(8,128)(2,1)S(1)} %bitcast.157, bf16[1024,1024]{1,0:T(8,128)(2,1)} %param.20), kind=kOutput, calls=%fused_computation.60 | convolution fusion | flops 1075314688 | bytes 5242880 | tf_op jit(solution)/shard_map/dot_general | solution.py:154
  237.7 19.5 %all-to-all-done.3 = bf16[32,32,1024]{2,1,0:T(8,128)(2,1)} async-done(((bf16[32,32,1024]{2,1,0:T(8,128)(2,1)}), bf16[32,32,1024]{2,1,0:T(8,128)(2,1)}, u32[]{:S(2)}, u32[]{:S(2)}) %all-to-all-start.3) | async-done | bytes 2097184 | tf_op jit(solution)/shard_map/all_to_all | solution.py:35
  257.2 2.0 reduce_sum.63
  259.2 13.1 %all-gather = bf16[128,1024]{1,0:T(8,128)(2,1)S(1)} all-gather(bf16[32,1024]{1,0:T(8,128)(2,1)S(1)} %reduce_sum.63), channel_id=2, replica_groups=mesh['batch'=4,'tm'=8,'space'=4] {'batch'}, dimensions={0}, use_global_device_ids=true | all-gather | bytes 327680 | tf_op jit(solution)/shard_map/all_gather | solution.py:40
  (60 shorter events, 10.1 us)
Async XLA Ops:
  0.6 112.6 %copy-start = (bf16[1024,1024]{1,0:T(8,128)(2,1)S(1)}, bf16[1024,1024]{1,0:T(8,128)(2,1)}, u32[]{:S(2)}) copy-start(bf16[1024,1024]{1,0:T(8,128)(2,1)} %param.17) | copy-start | bytes 6291460
  0.6 21.3 %all-to-all-start = ((bf16[1,16,8,4,1024]{4,3,2,0,1:T(4,128)(2,1)}), bf16[1,16,8,4,1024]{4,3,2,0,1:T(4,128)(2,1)S(1)}, u32[]{:S(2)}, u32[]{:S(2)}) async-start(bf16[1,16,8,4,1024]{4,3,2,0,1:T(4,128)(2,1)} %bitcast.156), calls=%async_computation | async-start | bytes 2097152 | tf_op jit(solution)/shard_map/all_to_all | solution.py:85
  26.9 3.9 %copy-start.8 = (f32[1024]{0:T(1024)S(1)}, f32[1024]{0:T(1024)}, u32[]{:S(2)}) copy-start(f32[1024]{0:T(1024)} %param.15) | copy-start | bytes 12292
  30.8 8.4 %copy-start.7 = (f32[2,8,32,1024]{3,2,1,0:T(8,128)S(1)}, f32[2,8,32,1024]{3,2,1,0:T(8,128)}, u32[]{:S(2)}) copy-start(f32[2,8,32,1024]{3,2,1,0:T(8,128)} %reshape.333) | copy-start | bytes 6291460
  32.9 18.5 %collective-permute-start.1 = (bf16[1,2,4,32,1024]{4,3,2,1,0:T(8,128)(2,1)S(1)}, bf16[1,2,4,32,1024]{4,3,2,1,0:T(8,128)(2,1)}, u32[]{:S(2)}, u32[]{:S(2)}) collective-permute-start(bf16[1,2,4,32,1024]{4,3,2,1,0:T(8,128)(2,1)S(1)} %get-tuple-element.134), channel_id=1, source_target_pairs={{1,0},{2,1},{3,2},{5,4},{6,5},{7,6},{9,8},{10,9},{11,10},{13,12},{... | collective-permute-start | bytes 1572872 | tf_op jit(solution)/shard_map/ppermute | solution.py:23
  34.2 20.8 %collective-permute-start = (bf16[1,2,4,32,1024]{4,3,2,1,0:T(8,128)(2,1)S(1)}, bf16[1,2,4,32,1024]{4,3,2,1,0:T(8,128)(2,1)}, u32[]{:S(2)}, u32[]{:S(2)}) collective-permute-start(bf16[1,2,4,32,1024]{4,3,2,1,0:T(8,128)(2,1)S(1)} %get-tuple-element.133), channel_id=1, source_target_pairs={{0,1},{1,2},{2,3},{4,5},{5,6},{6,7},{8,9},{9,10},{10,11},{12,13},{... | collective-permute-start | bytes 1572872 | tf_op jit(solution)/shard_map/ppermute | solution.py:22
  45.7 1.7 copy-start.3
  55.0 3.8 %slice-start = ((bf16[1,2,8,32,3072]{4,3,2,1,0:T(8,128)(2,1)}), bf16[1,2,8,32,2048]{4,3,2,1,0:T(8,128)(2,1)S(1)}, s32[]{:S(2)}) async-start(bf16[1,2,8,32,3072]{4,3,2,1,0:T(8,128)(2,1)} %copy-done.3), calls=%async_computation.4 | async-start | bytes 4194304 | tf_op jit(solution)/shard_map/slice | solution.py:100
  58.8 2.2 copy-start.11
  69.7 3.1 %copy-start.2 = (bf16[2,256,1024]{2,1,0:T(8,128)(2,1)S(1)}, bf16[2,256,1024]{2,1,0:T(8,128)(2,1)}, u32[]{:S(2)}) copy-start(bf16[2,256,1024]{2,1,0:T(8,128)(2,1)} %get-tuple-element.218) | copy-start | bytes 3145732 | tf_op jit(solution)/shard_map/while
  73.8 7.6 %copy-start.1 = (bf16[512,1024]{0,1:T(8,128)(2,1)S(1)}, bf16[512,1024]{0,1:T(8,128)(2,1)}, u32[]{:S(2)}) copy-start(bf16[512,1024]{0,1:T(8,128)(2,1)} %get-tuple-element.192) | copy-start | bytes 3145732 | tf_op jit(solution)/shard_map/while
  95.8 3.1 %copy-start.2 = (bf16[2,256,1024]{2,1,0:T(8,128)(2,1)S(1)}, bf16[2,256,1024]{2,1,0:T(8,128)(2,1)}, u32[]{:S(2)}) copy-start(bf16[2,256,1024]{2,1,0:T(8,128)(2,1)} %get-tuple-element.218) | copy-start | bytes 3145732 | tf_op jit(solution)/shard_map/while
  99.9 7.6 %copy-start.1 = (bf16[512,1024]{0,1:T(8,128)(2,1)S(1)}, bf16[512,1024]{0,1:T(8,128)(2,1)}, u32[]{:S(2)}) copy-start(bf16[512,1024]{0,1:T(8,128)(2,1)} %get-tuple-element.192) | copy-start | bytes 3145732 | tf_op jit(solution)/shard_map/while
  113.3 4.3 %copy-start.10 = (f32[1024]{0:T(1024)S(1)}, f32[1024]{0:T(1024)}, u32[]{:S(2)}) copy-start(f32[1024]{0:T(1024)} %param.18) | copy-start | bytes 12292
  116.5 1.0 copy-start.12
  129.0 4.6 %copy-start.9 = (s32[1,16]{1,0:T(1,128)S(1)}, s32[1,16]{1,0:T(1,128)}, u32[]{:S(2)}) copy-start(s32[1,16]{1,0:T(1,128)} %param.13) | copy-start | bytes 196
  129.0 49.0 %all-to-all-start.1 = ((bf16[1,2,256,3072]{3,1,0,2:T(2,128)(2,1)}), bf16[1,2,256,3072]{3,1,0,2:T(2,128)(2,1)}, u32[]{:S(2)}, u32[]{:S(2)}) async-start(bf16[1,2,256,3072]{3,1,0,2:T(2,128)(2,1)} %copy.100), calls=%async_computation.1 | async-start | bytes 6291456 | tf_op jit(solution)/shard_map/all_to_all | solution.py:143
  197.8 2.0 copy-start.6
  221.9 4.2 %copy-start.4 = (bf16[1,16,32,1024]{3,2,0,1:T(8,128)(2,1)}, bf16[1,16,32,1024]{3,2,0,1:T(8,128)(2,1)S(1)}, u32[]{:S(2)}) copy-start(bf16[1,16,32,1024]{3,2,0,1:T(8,128)(2,1)S(1)} %all_to_all.47) | copy-start | bytes 3145732
  226.2 7.3 %copy-start.5 = (bf16[1,16,32,1024]{3,2,0,1:T(8,128)(2,1)S(1)}, bf16[1,16,32,1024]{3,2,0,1:T(8,128)(2,1)}, u32[]{:S(2)}) copy-start(bf16[1,16,32,1024]{3,2,0,1:T(8,128)(2,1)} %copy-done.4) | copy-start | bytes 3145732
  226.2 31.1 %all-to-all-start.3 = ((bf16[32,32,1024]{2,1,0:T(8,128)(2,1)}), bf16[32,32,1024]{2,1,0:T(8,128)(2,1)}, u32[]{:S(2)}, u32[]{:S(2)}) async-start(bf16[32,32,1024]{2,1,0:T(8,128)(2,1)} %bitcast.154), calls=%async_computation.3 | async-start | bytes 4194304 | tf_op jit(solution)/shard_map/all_to_all | solution.py:35
where the time goes:
time: 274 us; the launch traced here: 273 us
  waiting for transfers between devices  79.1 us (29%)
  local copies, waits for them, and re-layouts  63.6 us (23%)
  matrix products  63.5 us (23%)
  blocking collectives  28.3 us (10%)
  starting transfers between devices  24.2 us (9%)
  other arithmetic  13.3 us (5%)
    all_to_all x1, waiting for transfers between devices, per_device(): lax.all_to_all(projected_two, 'tm', split_axis=2, concat_axis=1, tiled=True)  44.3 us
    all_to_all x1, waiting for transfers between devices, summed_on_arrival(): lax.all_to_all(parts, axis, split_axis=0, concat_axis=0, tiled=True)  19.5 us
    dynamic_slice x10, local copies, waits for them, and re-layouts, per_device(): lax.map(spatial_item, (projected[..., :D].reshape(item_count, tokens, D),...  17.6 us
    sub x2, matrix products, softmax_rounded(): exponent = jnp.exp(masked - top_score)  15.3 us
    all_to_all x1, waiting for transfers between devices, per_device(): lax.all_to_all(clip_tokens, 'tm', split_axis=1, concat_axis=3, tiled=True)  15.3 us
    all_to_all x1, blocking collectives, per_device(): lax.all_to_all(context_all, 'tm', split_axis=1, concat_axis=2, tiled=True)  15.3 us
    all_gather x1, blocking collectives, gathered_total(): return lax.all_gather(value, axis).astype(jnp.float32).sum(0)  13.1 us
    another operation x3, local copies, waits for them, and re-layouts  10.4 us
  transfers between devices with their start and end apart: 5, of which 3 were waited for; matrix products, arithmetic and copies ran while one was open for 7% of the time, Pallas kernels for 0%

commit v1 on v0

v1 whole, which is shorter than its diff:
```python
import jax
import jax.numpy as jnp
from jax import lax
from jax.experimental import pallas as pl
from jax.experimental.pallas import tpu as pltpu
from jax.sharding import PartitionSpec as P

HALO = 4
D = 1024
HEADS = 16
HEAD_DIM = 64
PAIRS = HEADS // 2
WIDE = 2 * HEAD_DIM
FLOOR = 0.5
SCALE = HEAD_DIM ** (-0.5) * 1.4426950408889634
BF = jnp.bfloat16
F32 = jnp.float32
MASKED = -1e30


def normalized(x, gain):
    return x * lax.rsqrt(jnp.mean(x * x, axis=-1, keepdims=True) + FLOOR) * gain


def norm_kernel(x_ref, gain_ref, tok_ref, normed_ref):
    sources, _, rows, cols, _ = x_ref.shape
    gain = gain_ref[...]
    for r in range(rows):
        for s in range(sources):
            x = x_ref[s, 0, r]
            y = normalized(x.astype(F32), gain).astype(BF)
            tok_ref[0, r, s * cols:(s + 1) * cols, :] = x
            normed_ref[0, r, s * cols:(s + 1) * cols, :] = y


def norm_reorder(arrived, gain):
    sources, frames, rows, cols, _ = arrived.shape
    half = rows // 2
    wide = sources * cols
    out = pl.BlockSpec((1, half, wide, D), lambda f, h: (f, h, 0, 0))
    shape = jax.ShapeDtypeStruct((frames, rows, wide, D), BF)
    return pl.pallas_call(
        norm_kernel,
        grid=(frames, 2),
        in_specs=[
            pl.BlockSpec((sources, 1, half, cols, D), lambda f, h: (0, f, h, 0, 0)),
            pl.BlockSpec((1, D), lambda f, h: (0, 0)),
        ],
        out_specs=[out, out],
        out_shape=[shape, shape],
        name="norm_reorder",
    )(arrived, gain.reshape(1, D))


def pair_attention(q, k, v, bias):
    n = q.shape[0]
    lane = lax.broadcasted_iota(jnp.int32, (n, WIDE), 1)
    low = lane < HEAD_DIM
    zero = jnp.zeros_like(q)
    both = jnp.concatenate([jnp.where(low, q, zero), jnp.where(low, zero, q)], axis=0)
    scores = lax.dot_general(both, k, (((1,), (1,)), ((), ())), preferred_element_type=F32)
    scores = scores * SCALE + jnp.concatenate([bias, bias], axis=0)
    top = jnp.max(scores, axis=-1, keepdims=True)
    p = jnp.exp2(scores - top).astype(BF)
    widened = jnp.concatenate([v, jnp.ones_like(v)], axis=1)
    o = jnp.dot(p, widened, preferred_element_type=F32)
    o = o[:, :WIDE] / o[:, WIDE:]
    return jnp.where(low, o[:n], o[n:]).astype(BF)


def spatial_kernel(info_ref, qkv_ref, up_ref, down_ref, tok_ref, wk_ref, wv_ref, wm_ref, mid_ref,
                   k_ref, v_ref, ctx_ref, bias_ref, *, rows, all_rows):
    f = pl.program_id(0)
    reach = info_ref[f]
    first_row = info_ref[pl.num_programs(0)] * rows
    tokens = qkv_ref.shape[1]
    cols = tokens // rows
    edge = HALO * cols
    extent = tokens + 2 * edge
    halo = jnp.concatenate([up_ref[0], down_ref[0]], axis=0)
    for w_ref, buf, at in ((wk_ref, k_ref, D), (wv_ref, v_ref, 2 * D)):
        side = jnp.dot(halo, w_ref[...], preferred_element_type=F32).astype(BF)
        buf[0:edge] = side[:edge]
        buf[edge:edge + tokens] = qkv_ref[0, :, at:at + D]
        buf[edge + tokens:] = side[edge:]
    qrow = lax.broadcasted_iota(jnp.int32, (tokens, extent), 0) // cols
    krow = lax.broadcasted_iota(jnp.int32, (tokens, extent), 1) // cols - HALO
    allowed = (jnp.abs(krow - qrow) <= reach) & (krow + first_row >= 0) & (krow + first_row < all_rows)
    bias_ref[...] = jnp.where(allowed, 0.0, MASKED)
    for pair in range(PAIRS):
        at = slice(pair * WIDE, (pair + 1) * WIDE)
        half = tokens // 2
        for side in range(2):
            keys = slice(side * edge, side * edge + half + 2 * edge)
            own = slice(side * half, (side + 1) * half)
            ctx_ref[own, at] = pair_attention(qkv_ref[0, own, at], k_ref[keys, at], v_ref[keys, at], bias_ref[own, keys])
    mid = tok_ref[0].astype(F32) + jnp.dot(ctx_ref[...], wm_ref[...], preferred_element_type=F32)
    mid_ref[:, 0] = mid.astype(BF).reshape(rows, cols, D)


def spatial_phase(info, qkv, up, down, tok, heads, merge, rows, all_rows):
    import functools
    frames, tokens, _ = qkv.shape
    cols = tokens // rows
    edge = HALO * cols
    extent = tokens + 2 * edge
    per_frame = lambda n, d: pl.BlockSpec((1, n, d), lambda f, info: (f, 0, 0))
    column = lambda c: pl.BlockSpec((D, D), lambda f, info: (0, c))
    return pl.pallas_call(
        functools.partial(spatial_kernel, rows=rows, all_rows=all_rows),
        grid_spec=pltpu.PrefetchScalarGridSpec(
            num_scalar_prefetch=1,
            grid=(frames,),
            in_specs=[per_frame(tokens, 3 * D), per_frame(edge, D), per_frame(edge, D), per_frame(tokens, D),
                      column(1), column(2), column(0)],
            out_specs=pl.BlockSpec((rows, 1, cols, D), lambda f, info: (0, f, 0, 0)),
            scratch_shapes=[pltpu.VMEM((extent, D), BF), pltpu.VMEM((extent, D), BF),
                            pltpu.VMEM((tokens, D), BF), pltpu.VMEM((tokens, extent), F32)],
        ),
        out_shape=jax.ShapeDtypeStruct((rows, frames, cols, D), BF),
        compiler_params=pltpu.CompilerParams(vmem_limit_bytes=56 * 2**20),
        name="spatial_phase",
    )(info, qkv, up, down, tok, heads, heads, merge)


GROUP = 8


def temporal_kernel(core_ref, mid_ref, order_q_ref, order_k_ref, gain_ref, cot_ref, heads_ref, merge_ref,
                    out_ref, send_ref, keep_ref,
                    w_ref, wm_ref, normed_ref, q_ref, k_ref, v_ref, ctx_ref, cotb_ref, sems):
    frames, cols, _ = mid_ref.shape
    groups = cols // GROUP
    n = frames * GROUP
    copies = [pltpu.make_async_copy(heads_ref.at[:, i * D:(i + 1) * D], w_ref.at[i], sems.at[i]) for i in range(3)]
    copies.append(pltpu.make_async_copy(merge_ref, wm_ref, sems.at[3]))
    for c in copies:
        c.start()
    gain = gain_ref[...]
    for g in range(groups):
        x = mid_ref[:, g * GROUP:(g + 1) * GROUP, :].astype(F32).reshape(n, D)
        normed_ref[g * n:(g + 1) * n] = normalized(x, gain).astype(BF)
        cotb_ref[g * n:(g + 1) * n] = cot_ref[:, g * GROUP:(g + 1) * GROUP, :].astype(F32).reshape(n, D).astype(BF)
    for i, buf in enumerate((q_ref, k_ref, v_ref)):
        copies[i].wait()
        buf[...] = jnp.dot(normed_ref[...], w_ref[i], preferred_element_type=F32).astype(BF)
    place_q = lax.broadcasted_iota(jnp.int32, (n, n), 0) % GROUP
    place_k = lax.broadcasted_iota(jnp.int32, (n, n), 1) % GROUP
    allowed = (place_q == place_k) & (order_k_ref[...] <= order_q_ref[...])
    bias = jnp.where(allowed, 0.0, MASKED)
    for g in range(groups):
        own = slice(g * n, (g + 1) * n)
        for pair in range(PAIRS):
            at = slice(pair * WIDE, (pair + 1) * WIDE)
            ctx_ref[own, at] = pair_attention(q_ref[own, at], k_ref[own, at], v_ref[own, at], bias)
    core = core_ref[0]
    half = D // 2
    for ref, which in ((send_ref, 1 - core), (keep_ref, core)):
        cot = cotb_ref[:, pl.ds(pl.multiple_of(which * half, half), half)]
        grad = lax.dot_general(ctx_ref[...], cot, (((0,), (0,)), ((), ())), preferred_element_type=F32).astype(BF)
        spaces, times, block, _ = ref.shape
        for t in range(times):
            for s in range(spaces):
                row = (t * spaces + s) * block
                ref[s, t] = grad[row:row + block]
    copies[3].wait()
    for g in range(groups):
        y = jnp.dot(ctx_ref[g * n:(g + 1) * n], wm_ref[...], preferred_element_type=F32)
        x = mid_ref[:, g * GROUP:(g + 1) * GROUP, :].astype(F32) + y.reshape(frames, GROUP, D)
        out_ref[:, g * GROUP:(g + 1) * GROUP, :] = x.astype(BF)


def temporal_phase(core, mid, order, gain, cot, heads, merge, spaces, times):
    frames, cols, _ = mid.shape
    n = frames * GROUP
    tokens = frames * cols
    spread = jnp.repeat(order, GROUP)
    block = D // (spaces * times)
    part = jax.ShapeDtypeStruct((spaces, times, block, D // 2), BF)
    vmem = pl.BlockSpec(memory_space=pltpu.VMEM)
    hbm = pl.BlockSpec(memory_space=pl.ANY)
    return pl.pallas_call(
        temporal_kernel,
        in_specs=[pl.BlockSpec(memory_space=pltpu.SMEM), vmem, vmem, vmem, vmem, vmem, hbm, hbm],
        out_specs=[vmem, vmem, vmem],
        out_shape=[jax.ShapeDtypeStruct((frames, cols, D), BF), part, part],
        scratch_shapes=[pltpu.VMEM((3, D, D), BF), pltpu.VMEM((D, D), BF)]
        + [pltpu.VMEM((tokens, D), BF)] * 6
        + [pltpu.SemaphoreType.DMA((4,))],
        compiler_params=pltpu.CompilerParams(vmem_limit_bytes=56 * 2**20),
        name="temporal_phase",
    )(core, mid, spread.reshape(n, 1), spread.reshape(1, n), gain.reshape(1, D), cot, heads, merge)


def per_device(
    clip_tokens,
    frame_order,
    row_reach,
    spatial_gain,
    spatial_heads,
    spatial_merge,
    temporal_gain,
    temporal_heads,
    temporal_merge,
    cotangent,
):
    tm, space = lax.axis_size("tm"), lax.axis_size("space")
    _, frame_count, rows, cols, _ = clip_tokens.shape
    frames = frame_count // tm
    wide = tm * cols
    tokens = rows * wide
    exchange = lambda v, axis: lax.all_to_all(v, axis, split_axis=0, concat_axis=0, tiled=True)

    arrived = exchange(clip_tokens.reshape(tm, frames, rows, cols, D), "tm")
    cot = exchange(cotangent.reshape(frames, rows, wide, D).swapaxes(0, 1), "tm")
    tok, normed = norm_reorder(arrived, spatial_gain)
    up = [(i, i + 1) for i in range(space - 1)]
    down = [(j, i) for i, j in up]
    above = lax.ppermute(normed[:, rows - HALO:], "space", up)
    below = lax.ppermute(normed[:, :HALO], "space", down)
    qkv = jnp.dot(normed.reshape(frames * tokens, D), spatial_heads, preferred_element_type=F32).astype(BF)
    here = lax.axis_index("space").astype(jnp.int32)
    info = jnp.concatenate([row_reach.reshape(frames), here.reshape(1)])
    middle = spatial_phase(
        info,
        qkv.reshape(frames, tokens, 3 * D),
        above.reshape(frames, HALO * wide, D),
        below.reshape(frames, HALO * wide, D),
        tok.reshape(frames, tokens, D),
        spatial_heads,
        spatial_merge,
        rows,
        rows * space,
    )
    mid = exchange(middle, "tm").reshape(frame_count, wide, D)
    core = (lax.axis_index("batch") % 2).astype(jnp.int32).reshape(1)
    out, send, keep = temporal_phase(
        core, mid, frame_order.reshape(frame_count), temporal_gain, cot.reshape(frame_count, wide, D),
        temporal_heads, temporal_merge, space, tm,
    )
    batch = lax.axis_size("batch")
    got = lax.ppermute(send, "batch", [(i, i ^ 1) for i in range(batch)])
    output = exchange(out.reshape(tm, frames, wide, D), "tm").swapaxes(0, 1)
    chip = (keep.astype(F32) + got.astype(F32)).astype(BF)
    over_space = exchange(chip, "space").astype(F32).sum(0).astype(BF)
    over_tm = exchange(over_space, "tm").astype(F32).sum(0).astype(BF)
    block = over_tm.shape[0]
    parts = lax.all_gather(over_tm, "batch").astype(F32).reshape(batch // 2, 2, block, D // 2).sum(0)
    weight_grad = parts.swapaxes(0, 1).reshape(block, D)
    return (output.reshape(1, frames, rows, wide, D), weight_grad)


def solution(mesh):
    in_specs = (
        P("batch", None, "space", "tm", None),
        P("batch", None),
        P("batch", "tm"),
        P(),
        P(),
        P(),
        P(),
        P(),
        P(),
        P("batch", "tm", "space", None, None),
    )
    out_specs = (P("batch", "tm", "space", None, None), P(("tm", "space"), None))
    return jax.shard_map(
        per_device, mesh=mesh, in_specs=in_specs, out_specs=out_specs, check_vma=False
    )
```

time: 274 us -> 164 us (0.60)
  matrix products: 63.5 us -> 8.18 us
  local copies, waits for them, and re-layouts: 63.6 us -> 8.51 us
  Pallas kernels: 0 us -> 35.3 us
  waiting for transfers between devices: 79.1 us -> 48.7 us
  other arithmetic: 13.3 us -> 3.17 us
  starting transfers between devices: 24.2 us -> 30.2 us
    dot_general x11 -> x1, matrix products: 48.2 us -> 8.18 us  [per_device(): jnp.dot(normed.reshape(frames * tokens, D), spatial_heads, preferred_elem...]
    all_to_all x3 -> x5, waiting for transfers between devices: 79.1 us -> 41.9 us  [per_device(): lax.all_to_all(v, axis, split_axis=0, concat_axis=0, tiled=True)]
    pallas_call x0 -> x3, Pallas kernels: none -> 35.3 us  [the longest x1 16.3 us: spatial_phase(): pl.pallas_call(functools.partial(spatial_kernel, rows=rows, all_rows=all_...]
    convert_element_type x6 -> x0, local copies, waits for them, and re-layouts: 19 us -> none  [the longest x2 5.97 us: normalize(): widened = values.astype(jnp.float32)]
    dynamic_slice x10 -> x0, local copies, waits for them, and re-layouts: 17.6 us -> none  [per_device(): lax.map(spatial_item, (projected[..., :D].reshape(item_count, tokens, D),...]
    sub x2 -> x0, matrix products: 15.3 us -> none  [softmax_rounded(): exponent = jnp.exp(masked - top_score)]
    another operation x3 -> x2, local copies, waits for them, and re-layouts: 10.4 us -> 1.32 us  [the longest x1 0.72 us: temporal_phase(): spread.reshape(n, 1)]
    slice x7 -> x1, local copies, waits for them, and re-layouts: 9.03 us -> 1.29 us  [per_device(): below = lax.ppermute(normed[:, :HALO], 'space', down)]
  transfers between devices with their start and end apart: 5 -> 8, of which waited for: 3 -> 7; matrix products, arithmetic and copies ran while one was open for 7% -> 10% of each run, Pallas kernels for 0% -> 12%
where the time goes in v1:
time: 164 us; the launch traced here: 163 us
  waiting for transfers between devices  48.7 us (30%)
  Pallas kernels  35.3 us (22%)
  starting transfers between devices  30.2 us (18%)
  blocking collectives  28 us (17%)
  local copies, waits for them, and re-layouts  8.51 us (5%)
  matrix products  8.18 us (5%)
  other arithmetic  3.17 us (2%)
    all_to_all x5, waiting for transfers between devices, per_device(): lax.all_to_all(v, axis, split_axis=0, concat_axis=0, tiled=True)  41.9 us
    all_to_all x5, starting transfers between devices, per_device(): lax.all_to_all(v, axis, split_axis=0, concat_axis=0, tiled=True)  21.4 us
    all_to_all x1, blocking collectives, per_device(): lax.all_to_all(v, axis, split_axis=0, concat_axis=0, tiled=True)  18.3 us
    pallas_call x1, Pallas kernels, spatial_phase(): pl.pallas_call(functools.partial(spatial_kernel, rows=rows, all_rows=all_...  16.3 us
    pallas_call x1, Pallas kernels, temporal_phase(): pl.pallas_call(temporal_kernel, in_specs=[pl.BlockSpec(memory_space=pltpu...  15.2 us
    all_gather x1, blocking collectives, per_device(): lax.all_gather(over_tm, 'batch').astype(F32)  9.76 us
    dot_general x1, matrix products, per_device(): jnp.dot(normed.reshape(frames * tokens, D), spatial_heads, preferred_elem...  8.18 us
    unnamed x16, local copies, waits for them, and re-layouts  5.16 us
  transfers between devices with their start and end apart: 8, of which 7 were waited for; matrix products, arithmetic and copies ran while one was open for 10% of the time, Pallas kernels for 12%

profile of v1, /device:TPU:1, one launch (start us, length us, event | category | flops | bytes accessed | tf_op | source)
XLA Modules:
  0.0 162.9 jit_solution(12811293623503444084)
XLA Ops:
  0.6 0.0 copy-start.6
  0.6 5.9 %all-to-all-start = ((bf16[8,2,8,4,1024]{4,3,2,1,0:T(4,128)(2,1)}), bf16[8,2,8,4,1024]{4,3,2,1,0:T(4,128)(2,1)S(1)}, u32[]{:S(2)}, u32[]{:S(2)}) async-start(bf16[8,2,8,4,1024]{4,3,2,1,0:T(4,128)(2,1)} %bitcast.35), calls=%async_computation | async-start | bytes 2097152 | tf_op jit(solution)/shard_map/all_to_all | solution.py:212
  6.5 2.3 %copy.30 = bf16[1,2,8,32,1024]{4,3,1,2,0:T(8,128)(2,1)} copy(bf16[1,2,8,32,1024]{4,3,2,1,0:T(8,128)(2,1)} %param.19) | data formatting | bytes 2097152 | tf_op args[9]
  8.8 0.0 copy-done.6
  8.8 0.6 pad_add_fusion.info_ref
  9.4 12.4 %all-to-all-done.x_ref = bf16[8,2,8,4,1024]{4,3,2,1,0:T(4,128)(2,1)S(1)} async-done(((bf16[8,2,8,4,1024]{4,3,2,1,0:T(4,128)(2,1)}), bf16[8,2,8,4,1024]{4,3,2,1,0:T(4,128)(2,1)S(1)}, u32[]{:S(2)}, u32[]{:S(2)}) %all-to-all-start) | async-done | bytes 1048608 | tf_op jit(solution)/shard_map/all_to_all | solution.py:212
  21.8 0.0 copy-start.2
  21.8 3.6 %all-to-all-start.2 = ((bf16[8,2,32,1024]{3,2,1,0:T(8,128)(2,1)}), bf16[8,2,32,1024]{3,2,1,0:T(8,128)(2,1)S(1)}, u32[]{:S(2)}, u32[]{:S(2)}) async-start(bf16[8,2,32,1024]{3,2,1,0:T(8,128)(2,1)} %bitcast.29), calls=%async_computation.2 | async-start | bytes 2097152 | tf_op jit(solution)/shard_map/all_to_all | solution.py:212
  25.4 0.0 copy-done.2
  25.4 3.9 %norm_reorder.1 = (bf16[2,8,32,1024]{3,2,1,0:T(8,128)(2,1)}, bf16[2,8,32,1024]{3,2,1,0:T(8,128)(2,1)}) custom-call(bf16[8,2,8,4,1024]{4,3,2,1,0:T(4,128)(2,1)} %copy-done.2, f32[1,1024]{1,0:T(1,128)} %bitcast.43), custom_call_target="tpu_custom_call" | custom-call | tf_op jit(solution)/shard_map/norm_reorder/pallas_call | solution.py:42
  29.3 1.3 fusion
  30.5 3.6 %collective-permute-start = (bf16[2,4,32,1024]{3,2,1,0:T(8,128)(2,1)S(1)}, bf16[2,4,32,1024]{3,2,1,0:T(8,128)(2,1)S(1)}, u32[]{:S(2)}, u32[]{:S(2)}) collective-permute-start(bf16[2,4,32,1024]{3,2,1,0:T(8,128)(2,1)S(1)} %get-tuple-element.19), channel_id=1, source_target_pairs={{0,1},{1,2},{2,3},{4,5},{5,6},{6,7},{8,9},{9,10},{10,11},{12,13},{... | collective-permute-start | bytes 1572872 | tf_op jit(solution)/shard_map/ppermute | solution.py:219
  34.1 1.3 collective-permute-start.1
  35.4 8.2 %convolution_convert_fusion = bf16[512,3072]{1,0:T(8,128)(2,1)} fusion(bf16[512,1024]{1,0:T(8,128)(2,1)} %bitcast.36, bf16[1024,3072]{1,0:T(8,128)(2,1)} %wv_ref.1), kind=kOutput, calls=%fused_computation | convolution fusion | flops 3222798336 | bytes 10485760 | tf_op jit(solution)/shard_map/dot_general | solution.py:221
  43.6 0.2 collective-permute-done
  43.8 0.0 copy-start.3
  43.8 4.2 %collective-permute-done.1 = bf16[2,4,32,1024]{3,2,1,0:T(8,128)(2,1)S(1)} collective-permute-done((bf16[2,4,32,1024]{3,2,1,0:T(8,128)(2,1)S(1)}, bf16[2,4,32,1024]{3,2,1,0:T(8,128)(2,1)S(1)}, u32[]{:S(2)}, u32[]{:S(2)}) %collective-permute-start.1) | collective-permute-done | bytes 524320 | tf_op jit(solution)/shard_map/ppermute | solution.py:220
  48.0 0.0 copy-start.4
  48.0 0.0 copy-done.3
  48.0 0.8 copy-done.4
  48.8 0.0 copy-start.5
  48.8 16.3 %spatial_phase.1 = bf16[8,2,32,1024]{3,2,1,0:T(8,128)(2,1)} custom-call(s32[3]{0:T(128)} %pad_add_fusion.info_ref, bf16[2,256,3072]{2,1,0:T(8,128)(2,1)} %bitcast.33, bf16[2,128,1024]{2,1,0:T(8,128)(2,1)} %bitcast.37, bf16[2,128,1024]{2,1,0:T(8,128)(2,1)} %bitcast.38, bf16[2,256,1024]{2,1,0:T(8,128)(2,1)} %bitcast.34, bf16[1024,3072]{1,0:T(8,128)(2,1)} %wv_ref.1, ...), custom_call_target="tpu_custom_call" | custom-call | tf_op jit(solution)/shard_map/spatial_phase/pallas_call | solution.py:109
  65.1 0.0 all-to-all-done.2
  65.1 0.0 copy-start
  65.1 4.8 %all-to-all-start.1 = ((bf16[8,2,32,1024]{3,2,1,0:T(8,128)(2,1)}), bf16[8,2,32,1024]{3,2,1,0:T(8,128)(2,1)S(1)}, u32[]{:S(2)}, u32[]{:S(2)}) async-start(bf16[8,2,32,1024]{3,2,1,0:T(8,128)(2,1)} %spatial_phase.1), calls=%async_computation.1 | async-start | bytes 2097152 | tf_op jit(solution)/shard_map/all_to_all | solution.py:212
  69.9 0.0 copy-done.5
  69.9 0.1 broadcast_in_dim.3
  69.9 0.7 reshape_reshape.8.order_q_ref
  70.7 0.6 reshape_reshape.7.order_k_ref
  71.3 11.4 %all-to-all-done.1 = bf16[8,2,32,1024]{3,2,1,0:T(8,128)(2,1)S(1)} async-done(((bf16[8,2,32,1024]{3,2,1,0:T(8,128)(2,1)}), bf16[8,2,32,1024]{3,2,1,0:T(8,128)(2,1)S(1)}, u32[]{:S(2)}, u32[]{:S(2)}) %all-to-all-start.1) | async-done | bytes 1048608 | tf_op jit(solution)/shard_map/all_to_all | solution.py:212
  82.6 0.0 copy-start.1
  82.6 0.0 copy-done
  82.6 1.0 copy-done.1
  83.6 15.2 %temporal_phase.1 = (bf16[16,32,1024]{2,1,0:T(8,128)(2,1)}, bf16[4,8,32,512]{3,2,1,0:T(8,128)(2,1)}, bf16[4,8,32,512]{3,2,1,0:T(8,128)(2,1)}) custom-call(s32[1]{0:T(128)} %bitcast.core_ref, bf16[16,32,1024]{2,1,0:T(8,128)(2,1)} %bitcast.31, s32[128,1]{1,0:T(8,128)} %reshape_reshape.8.order_q_ref, s32[1,128]{1,0:T(1,128)} %reshape_reshape.7.order_k_ref, ...), custom_call_target="tpu_custom_call" | custom-call | tf_op jit(solution)/shard_map/temporal_phase/pallas_call | solution.py:182
  98.8 4.0 %collective-permute-start.2 = (bf16[4,8,32,512]{3,2,1,0:T(8,128)(2,1)}, bf16[4,8,32,512]{3,2,1,0:T(8,128)(2,1)S(1)}, u32[]{:S(2)}, u32[]{:S(2)}) collective-permute-start(bf16[4,8,32,512]{3,2,1,0:T(8,128)(2,1)} %get-tuple-element.11), channel_id=1, source_target_pairs={{0,32},{32,0},{64,96},{96,64},{1,33},{33,1},{65,97},{97,65},{2,34}... | collective-permute-start | bytes 3145736 | tf_op jit(solution)/shard_map/ppermute | solution.py:242
  102.7 2.5 %collective-permute-done.2 = bf16[4,8,32,512]{3,2,1,0:T(8,128)(2,1)S(1)} collective-permute-done((bf16[4,8,32,512]{3,2,1,0:T(8,128)(2,1)}, bf16[4,8,32,512]{3,2,1,0:T(8,128)(2,1)S(1)}, u32[]{:S(2)}, u32[]{:S(2)}) %collective-permute-start.2) | collective-permute-done | bytes 1048608 | tf_op jit(solution)/shard_map/ppermute | solution.py:242
  105.2 1.6 add_convert_fusion
  106.8 18.3 %all_to_all.30 = bf16[4,8,32,512]{3,2,1,0:T(8,128)(2,1)S(1)} all-to-all(bf16[4,8,32,512]{3,2,1,0:T(8,128)(2,1)S(1)} %add_convert_fusion), channel_id=1, replica_groups=mesh['batch'=4,'tm'=8,'space'=4] {'space'}, dimensions={0} | all-to-all | bytes 2097152 | tf_op jit(solution)/shard_map/all_to_all | solution.py:212
  125.1 3.6 %all-to-all-start.3 = ((bf16[8,2,32,1024]{3,2,1,0:T(8,128)(2,1)}), bf16[8,2,32,1024]{3,2,1,0:T(8,128)(2,1)S(1)}, u32[]{:S(2)}, u32[]{:S(2)}) async-start(bf16[8,2,32,1024]{3,2,1,0:T(8,128)(2,1)} %bitcast.16), calls=%async_computation.3 | async-start | bytes 2097152 | tf_op jit(solution)/shard_map/all_to_all | solution.py:212
  128.7 0.9 reduce_sum.33
  129.6 13.3 %all-to-all-done.3 = bf16[8,2,32,1024]{3,2,1,0:T(8,128)(2,1)S(1)} async-done(((bf16[8,2,32,1024]{3,2,1,0:T(8,128)(2,1)}), bf16[8,2,32,1024]{3,2,1,0:T(8,128)(2,1)S(1)}, u32[]{:S(2)}, u32[]{:S(2)}) %all-to-all-start.3) | async-done | bytes 1048608 | tf_op jit(solution)/shard_map/all_to_all | solution.py:212
  143.0 3.6 %all-to-all-start.5 = ((bf16[8,32,512]{2,1,0:T(8,128)(2,1)}), bf16[8,32,512]{2,1,0:T(8,128)(2,1)S(1)}, u32[]{:S(2)}, u32[]{:S(2)}) async-start(bf16[8,32,512]{2,1,0:T(8,128)(2,1)} %reduce_sum.33), calls=%async_computation.5 | async-start | bytes 524288 | tf_op jit(solution)/shard_map/all_to_all | solution.py:212
  146.6 1.1 copy.27
  147.7 4.8 %all-to-all-done.5 = bf16[8,32,512]{2,1,0:T(8,128)(2,1)S(1)} async-done(((bf16[8,32,512]{2,1,0:T(8,128)(2,1)}), bf16[8,32,512]{2,1,0:T(8,128)(2,1)S(1)}, u32[]{:S(2)}, u32[]{:S(2)}) %all-to-all-start.5) | async-done | bytes 262176 | tf_op jit(solution)/shard_map/all_to_all | solution.py:212
  152.5 9.8 %all-gather = bf16[128,512]{1,0:T(8,128)(2,1)S(1)} all-gather(bf16[32,512]{1,0:T(8,128)(2,1)S(1)} %reduce_sum.34), channel_id=2, replica_groups=mesh['batch'=4,'tm'=8,'space'=4] {'batch'}, dimensions={0}, use_global_device_ids=true | all-gather | bytes 163840 | tf_op jit(solution)/shard_map/all_gather | solution.py:248
  162.2 0.7 copy.28
  (2 shorter events, 0.1 us)
Async XLA Ops:
  0.6 8.2 %copy-start.6 = (s32[1,2]{1,0:T(1,128)S(1)}, s32[1,2]{1,0:T(1,128)}, u32[]{:S(2)}) copy-start(s32[1,2]{1,0:T(1,128)} %param.12) | copy-start | bytes 28
  0.6 21.2 %all-to-all-start = ((bf16[8,2,8,4,1024]{4,3,2,1,0:T(4,128)(2,1)}), bf16[8,2,8,4,1024]{4,3,2,1,0:T(4,128)(2,1)S(1)}, u32[]{:S(2)}, u32[]{:S(2)}) async-start(bf16[8,2,8,4,1024]{4,3,2,1,0:T(4,128)(2,1)} %bitcast.35), calls=%async_computation | async-start | bytes 2097152 | tf_op jit(solution)/shard_map/all_to_all | solution.py:212
  21.8 3.6 %copy-start.2 = (bf16[8,2,8,4,1024]{4,3,2,1,0:T(4,128)(2,1)}, bf16[8,2,8,4,1024]{4,3,2,1,0:T(4,128)(2,1)S(1)}, u32[]{:S(2)}) copy-start(bf16[8,2,8,4,1024]{4,3,2,1,0:T(4,128)(2,1)S(1)} %all-to-all-done.x_ref) | copy-start | bytes 3145732
  21.8 43.3 %all-to-all-start.2 = ((bf16[8,2,32,1024]{3,2,1,0:T(8,128)(2,1)}), bf16[8,2,32,1024]{3,2,1,0:T(8,128)(2,1)S(1)}, u32[]{:S(2)}, u32[]{:S(2)}) async-start(bf16[8,2,32,1024]{3,2,1,0:T(8,128)(2,1)} %bitcast.29), calls=%async_computation.2 | async-start | bytes 2097152 | tf_op jit(solution)/shard_map/all_to_all | solution.py:212
  30.5 13.2 %collective-permute-start = (bf16[2,4,32,1024]{3,2,1,0:T(8,128)(2,1)S(1)}, bf16[2,4,32,1024]{3,2,1,0:T(8,128)(2,1)S(1)}, u32[]{:S(2)}, u32[]{:S(2)}) collective-permute-start(bf16[2,4,32,1024]{3,2,1,0:T(8,128)(2,1)S(1)} %get-tuple-element.19), channel_id=1, source_target_pairs={{0,1},{1,2},{2,3},{4,5},{5,6},{6,7},{8,9},{9,10},{10,11},{12,13},{... | collective-permute-start | bytes 1572872 | tf_op jit(solution)/shard_map/ppermute | solution.py:219
  34.1 13.8 %collective-permute-start.1 = (bf16[2,4,32,1024]{3,2,1,0:T(8,128)(2,1)S(1)}, bf16[2,4,32,1024]{3,2,1,0:T(8,128)(2,1)S(1)}, u32[]{:S(2)}, u32[]{:S(2)}) collective-permute-start(bf16[2,4,32,1024]{3,2,1,0:T(8,128)(2,1)S(1)} %get-tuple-element.18), channel_id=1, source_target_pairs={{1,0},{2,1},{3,2},{5,4},{6,5},{7,6},{9,8},{10,9},{11,10},{13,12},{... | collective-permute-start | bytes 1572872 | tf_op jit(solution)/shard_map/ppermute | solution.py:220
  43.8 4.2 %copy-start.3 = (bf16[2,4,32,1024]{3,2,1,0:T(8,128)(2,1)}, bf16[2,4,32,1024]{3,2,1,0:T(8,128)(2,1)S(1)}, u32[]{:S(2)}) copy-start(bf16[2,4,32,1024]{3,2,1,0:T(8,128)(2,1)S(1)} %collective-permute-done) | copy-start | bytes 1572868
  48.0 0.8 copy-start.4
  48.8 21.1 %copy-start.5 = (s32[1,16]{1,0:T(1,128)S(1)}, s32[1,16]{1,0:T(1,128)}, u32[]{:S(2)}) copy-start(s32[1,16]{1,0:T(1,128)} %param.11) | copy-start | bytes 196
  65.1 17.6 %copy-start = (bf16[8,2,32,1024]{3,2,1,0:T(8,128)(2,1)}, bf16[8,2,32,1024]{3,2,1,0:T(8,128)(2,1)S(1)}, u32[]{:S(2)}) copy-start(bf16[8,2,32,1024]{3,2,1,0:T(8,128)(2,1)S(1)} %all-to-all-done.2) | copy-start | bytes 3145732
  65.1 17.5 %all-to-all-start.1 = ((bf16[8,2,32,1024]{3,2,1,0:T(8,128)(2,1)}), bf16[8,2,32,1024]{3,2,1,0:T(8,128)(2,1)S(1)}, u32[]{:S(2)}, u32[]{:S(2)}) async-start(bf16[8,2,32,1024]{3,2,1,0:T(8,128)(2,1)} %spatial_phase.1), calls=%async_computation.1 | async-start | bytes 2097152 | tf_op jit(solution)/shard_map/all_to_all | solution.py:212
  82.6 1.0 copy-start.1
  98.8 6.5 %collective-permute-start.2 = (bf16[4,8,32,512]{3,2,1,0:T(8,128)(2,1)}, bf16[4,8,32,512]{3,2,1,0:T(8,128)(2,1)S(1)}, u32[]{:S(2)}, u32[]{:S(2)}) collective-permute-start(bf16[4,8,32,512]{3,2,1,0:T(8,128)(2,1)} %get-tuple-element.11), channel_id=1, source_target_pairs={{0,32},{32,0},{64,96},{96,64},{1,33},{33,1},{65,97},{97,65},{2,34}... | collective-permute-start | bytes 3145736 | tf_op jit(solution)/shard_map/ppermute | solution.py:242
  125.1 17.9 %all-to-all-start.3 = ((bf16[8,2,32,1024]{3,2,1,0:T(8,128)(2,1)}), bf16[8,2,32,1024]{3,2,1,0:T(8,128)(2,1)S(1)}, u32[]{:S(2)}, u32[]{:S(2)}) async-start(bf16[8,2,32,1024]{3,2,1,0:T(8,128)(2,1)} %bitcast.16), calls=%async_computation.3 | async-start | bytes 2097152 | tf_op jit(solution)/shard_map/all_to_all | solution.py:212
  143.0 9.5 %all-to-all-start.5 = ((bf16[8,32,512]{2,1,0:T(8,128)(2,1)}), bf16[8,32,512]{2,1,0:T(8,128)(2,1)S(1)}, u32[]{:S(2)}, u32[]{:S(2)}) async-start(bf16[8,32,512]{2,1,0:T(8,128)(2,1)} %reduce_sum.33), calls=%async_computation.5 | async-start | bytes 524288 | tf_op jit(solution)/shard_map/all_to_all | solution.py:212

commit v2 on v1

v2 whole, which is shorter than its diff:
```python
import functools

import jax
import jax.numpy as jnp
from jax import lax
from jax.experimental import pallas as pl
from jax.experimental.pallas import tpu as pltpu
from jax.sharding import PartitionSpec as P


HALO = 4
D = 1024
HEADS = 16
HEAD_DIM = 64
PAIRS = HEADS // 2
WIDE = 2 * HEAD_DIM
FLOOR = 0.5
SCALE = HEAD_DIM ** (-0.5) * 1.4426950408889634
BF = jnp.bfloat16
F32 = jnp.float32
MASKED = -1e30


def normalized(x, gain):
    return x * lax.rsqrt(jnp.mean(x * x, axis=-1, keepdims=True) + FLOOR) * gain


def in_vmem(x):
    return pltpu.with_memory_space_constraint(x, pltpu.VMEM)


def in_hbm(x):
    return pltpu.with_memory_space_constraint(x, pltpu.HBM)


VMEM = pl.BlockSpec(memory_space=pltpu.VMEM)
SMEM = pl.BlockSpec(memory_space=pltpu.SMEM)
HBM = pl.BlockSpec(memory_space=pltpu.HBM)


def norm_kernel(x_ref, gain_ref, tok_out, *refs):
    part_refs, (tok_ref, sems) = refs[:-2], refs[-2:]
    sources, frames, rows, cols, _ = x_ref.shape
    half = rows // 2
    gain = gain_ref[...]
    for f in range(frames):
        for h in range(2):
            part_ref = part_refs[2 * f + h]

            def one_row(r, carry):
                for s in range(sources):
                    x = x_ref[s, f, h * half + r]
                    y = normalized(x.astype(F32), gain).astype(BF)
                    tok_ref[f, h * half + r, s * cols:(s + 1) * cols, :] = x
                    part_ref[r, s * cols:(s + 1) * cols, :] = y
                return carry

            lax.fori_loop(0, half, one_row, 0)
        pltpu.make_async_copy(tok_ref.at[f], tok_out.at[f], sems.at[f]).start()
    for f in range(frames):
        pltpu.make_async_copy(tok_ref.at[f], tok_out.at[f], sems.at[f]).wait()


def norm_reorder(arrived, gain):
    sources, frames, rows, cols, _ = arrived.shape
    wide = sources * cols
    return pl.pallas_call(
        norm_kernel,
        in_specs=[VMEM, VMEM],
        out_specs=[HBM] + [VMEM] * (2 * frames),
        scratch_shapes=[pltpu.VMEM((frames, rows, wide, D), BF), pltpu.SemaphoreType.DMA((frames,))],
        out_shape=[pltpu.HBM((frames, rows, wide, D), BF)] + [pltpu.VMEM((rows // 2, wide, D), BF)] * (2 * frames),
        compiler_params=pltpu.CompilerParams(vmem_limit_bytes=8 * 2**20),
        name="norm_reorder",
    )(in_vmem(arrived), gain.reshape(1, D))


def column_copies(w_ref, buf, sems, columns):
    return [pltpu.make_async_copy(w_ref.at[:, c * D:(c + 1) * D], buf.at[i], sems.at[i]) for i, c in enumerate(columns)]


def qkv_kernel(*refs):
    parts, (w_ref, out_ref, x_ref, buf, y_ref, sems) = refs[:-6], refs[-6:]
    copies = column_copies(w_ref, buf, sems, range(3))
    for c in copies:
        c.start()
    n = parts[0].shape[0]
    for i, p in enumerate(parts):
        x_ref[i * n:(i + 1) * n] = p[...]
    for i, c in enumerate(copies):
        c.wait()
        y_ref[i] = jnp.dot(x_ref[...], buf[i], preferred_element_type=F32).astype(BF)
        pltpu.make_async_copy(y_ref.at[i], out_ref.at[i], sems.at[3 + i]).start()
    for i in range(3):
        pltpu.make_async_copy(y_ref.at[i], out_ref.at[i], sems.at[3 + i]).wait()


def qkv_own(parts, heads):
    n = parts[0].shape[0]
    tokens = n * len(parts)
    return pl.pallas_call(
        qkv_kernel,
        in_specs=[VMEM] * len(parts) + [HBM],
        out_specs=HBM,
        out_shape=pltpu.HBM((3, tokens, D), BF),
        scratch_shapes=[pltpu.VMEM((tokens, D), BF), pltpu.VMEM((3, D, D), BF), pltpu.VMEM((3, tokens, D), BF),
                        pltpu.SemaphoreType.DMA((6,))],
        compiler_params=pltpu.CompilerParams(vmem_limit_bytes=24 * 2**20),
        name="qkv_own",
    )(*[in_vmem(p) for p in parts], in_hbm(heads))


def pair_attention(q, k, v, bias):
    n = q.shape[0]
    lane = lax.broadcasted_iota(jnp.int32, (n, WIDE), 1)
    low = lane < HEAD_DIM
    zero = jnp.zeros_like(q)
    both = jnp.concatenate([jnp.where(low, q, zero), jnp.where(low, zero, q)], axis=0)
    scores = lax.dot_general(both, k, (((1,), (1,)), ((), ())), preferred_element_type=F32)
    scores = scores * SCALE + jnp.concatenate([bias, bias], axis=0)
    top = jnp.max(scores, axis=-1, keepdims=True)
    p = jnp.exp2(scores - top).astype(BF)
    widened = jnp.concatenate([v, jnp.ones_like(v)], axis=1)
    o = jnp.dot(p, widened, preferred_element_type=F32)
    o = o[:, :WIDE] / o[:, WIDE:]
    return jnp.where(low, o[:n], o[n:]).astype(BF)


def spatial_kernel(*refs, frame, rows, all_rows):
    info_ref, up_ref, down_ref, qkv_ref, tok_ref, w_ref, wm_ref = refs[:7]
    mid_out, q_buf, tok_buf, mid_buf, wkv_buf, wm_buf, k_ref, v_ref, ctx_ref, bias_ref, sems = refs[-11:]
    tokens = ctx_ref.shape[0]
    copies = column_copies(w_ref, wkv_buf, sems, (1, 2))
    cols = tokens // rows
    edge = HALO * cols
    mine = pl.ds(frame * tokens, tokens)
    for i, buf in enumerate((q_buf, k_ref.at[edge:edge + tokens], v_ref.at[edge:edge + tokens])):
        copies.append(pltpu.make_async_copy(qkv_ref.at[i, mine], buf, sems.at[5 + i]))
    copies.append(pltpu.make_async_copy(wm_ref, wm_buf, sems.at[3]))
    copies.append(pltpu.make_async_copy(tok_ref.at[frame], tok_buf, sems.at[4]))
    for c in copies:
        c.start()
    reach = info_ref[frame]
    first_row = info_ref[info_ref.shape[0] - 1] * rows
    extent = tokens + 2 * edge
    qrow = lax.broadcasted_iota(jnp.int32, (tokens, extent), 0) // cols
    krow = lax.broadcasted_iota(jnp.int32, (tokens, extent), 1) // cols - HALO
    allowed = (jnp.abs(krow - qrow) <= reach) & (krow + first_row >= 0) & (krow + first_row < all_rows)
    bias_ref[...] = jnp.where(allowed, 0.0, MASKED)
    halo = jnp.concatenate([up_ref[...], down_ref[...]], axis=0)
    for i, buf in enumerate((k_ref, v_ref)):
        copies[i].wait()
        side = jnp.dot(halo, wkv_buf[i], preferred_element_type=F32).astype(BF)
        buf[0:edge] = side[:edge]
        buf[edge + tokens:] = side[edge:]
    for c in copies[2:5]:
        c.wait()
    half = tokens // 2
    for pair in range(PAIRS):
        at = slice(pair * WIDE, (pair + 1) * WIDE)
        for side in range(2):
            keys = slice(side * edge, side * edge + half + 2 * edge)
            own = slice(side * half, (side + 1) * half)
            ctx_ref[own, at] = pair_attention(q_buf[own, at], k_ref[keys, at], v_ref[keys, at], bias_ref[own, keys])
    copies[5].wait()
    copies[6].wait()
    mid = tok_buf[...].reshape(tokens, D).astype(F32) + jnp.dot(ctx_ref[...], wm_buf[...], preferred_element_type=F32)
    mid_buf[...] = mid.astype(BF).reshape(rows, cols, D)
    out = pltpu.make_async_copy(mid_buf, mid_out.at[:, frame], sems.at[8])
    out.start()
    out.wait()


def spatial_phase(info, qkv, halos, tok, heads, merge, all_rows):
    frames, rows, cols, _ = tok.shape
    tokens = rows * cols
    extent = tokens + 2 * HALO * cols
    mid = None
    for f in range(frames):
        up, down = halos[f]
        operands = [info, in_vmem(up), in_vmem(down)] + [in_hbm(v) for v in (qkv, tok, heads, merge)]
        specs = [SMEM, VMEM, VMEM, HBM, HBM, HBM, HBM]
        if mid is not None:
            operands.append(in_hbm(mid))
            specs.append(HBM)
        mid = pl.pallas_call(
            functools.partial(spatial_kernel, frame=f, rows=rows, all_rows=all_rows),
            in_specs=specs,
            out_specs=HBM,
            out_shape=pltpu.HBM((rows, frames, cols, D), BF),
            scratch_shapes=[pltpu.VMEM((tokens, D), BF), pltpu.VMEM((rows, cols, D), BF), pltpu.VMEM((rows, cols, D), BF),
                            pltpu.VMEM((2, D, D), BF), pltpu.VMEM((D, D), BF),
                            pltpu.VMEM((extent, D), BF), pltpu.VMEM((extent, D), BF),
                            pltpu.VMEM((tokens, D), BF), pltpu.VMEM((tokens, extent), F32),
                            pltpu.SemaphoreType.DMA((9,))],
            input_output_aliases={} if f == 0 else {len(operands) - 1: 0},
            compiler_params=pltpu.CompilerParams(vmem_limit_bytes=32 * 2**20),
            name="spatial_phase",
        )(*operands)
    return mid


GROUP = 8


def temporal_kernel(core_ref, mid_ref, order_q_ref, order_k_ref, gain_ref, cot_ref, w_ref, wm_ref,
                    out_hbm, send_ref, keep_hbm,
                    out_ref, keep_ref, wqkv_buf, wm_buf, cot_buf, normed_ref, q_ref, k_ref, v_ref, ctx_ref, cotb_ref, sems):
    frames, cols, _ = mid_ref.shape
    groups = cols // GROUP
    n = frames * GROUP
    copies = column_copies(w_ref, wqkv_buf, sems, range(3))
    copies.append(pltpu.make_async_copy(cot_ref, cot_buf, sems.at[3]))
    copies.append(pltpu.make_async_copy(wm_ref, wm_buf, sems.at[4]))
    for c in copies:
        c.start()
    gain = gain_ref[...]
    for g in range(groups):
        x = mid_ref[:, g * GROUP:(g + 1) * GROUP, :].astype(F32).reshape(n, D)
        normed_ref[g * n:(g + 1) * n] = normalized(x, gain).astype(BF)
    for i, buf in enumerate((q_ref, k_ref, v_ref)):
        copies[i].wait()
        buf[...] = jnp.dot(normed_ref[...], wqkv_buf[i], preferred_element_type=F32).astype(BF)
    copies[3].wait()
    for g in range(groups):
        cotb_ref[g * n:(g + 1) * n] = cot_buf[:, g * GROUP:(g + 1) * GROUP, :].astype(F32).reshape(n, D).astype(BF)
    place_q = lax.broadcasted_iota(jnp.int32, (n, n), 0) % GROUP
    place_k = lax.broadcasted_iota(jnp.int32, (n, n), 1) % GROUP
    allowed = (place_q == place_k) & (order_k_ref[...] <= order_q_ref[...])
    bias = jnp.where(allowed, 0.0, MASKED)
    for g in range(groups):
        own = slice(g * n, (g + 1) * n)
        for pair in range(PAIRS):
            at = slice(pair * WIDE, (pair + 1) * WIDE)
            ctx_ref[own, at] = pair_attention(q_ref[own, at], k_ref[own, at], v_ref[own, at], bias)
    core = core_ref[0]
    here = core_ref[1]
    half = D // 2
    for ref, which in ((send_ref, 1 - core), (keep_ref, core)):
        cot = cotb_ref[:, pl.ds(pl.multiple_of(which * half, half), half)]
        grad = lax.dot_general(ctx_ref[...], cot, (((0,), (0,)), ((), ())), preferred_element_type=F32).astype(BF)
        spaces, times, block, _ = ref.shape
        for s in range(spaces):
            slot = lax.rem(s + spaces - here, spaces)
            for t in range(times):
                row = (t * spaces + s) * block
                ref[slot, t] = grad[row:row + block]
    kept = pltpu.make_async_copy(keep_ref, keep_hbm, sems.at[5])
    kept.start()
    copies[4].wait()
    y = jnp.dot(ctx_ref[...], wm_buf[...], preferred_element_type=F32)
    for g in range(groups):
        x = mid_ref[:, g * GROUP:(g + 1) * GROUP, :].astype(F32) + y[g * n:(g + 1) * n].reshape(frames, GROUP, D)
        out_ref[:, g * GROUP:(g + 1) * GROUP, :] = x.astype(BF)
    done = pltpu.make_async_copy(out_ref, out_hbm, sems.at[6])
    done.start()
    done.wait()
    kept.wait()


def temporal_phase(core, mid, order, gain, cot, heads, merge, spaces, times):
    frames, cols, _ = mid.shape
    n = frames * GROUP
    tokens = frames * cols
    spread = jnp.repeat(order, GROUP)
    block = D // (spaces * times)
    part = (spaces, times, block, D // 2)
    return pl.pallas_call(
        temporal_kernel,
        in_specs=[SMEM] + [VMEM] * 4 + [HBM] * 3,
        out_specs=[HBM, VMEM, HBM],
        out_shape=[pltpu.HBM((frames, cols, D), BF), pltpu.VMEM(part, BF), pltpu.HBM(part, BF)],
        scratch_shapes=[pltpu.VMEM((frames, cols, D), BF), pltpu.VMEM(part, BF), pltpu.VMEM((3, D, D), BF), pltpu.VMEM((D, D), BF), pltpu.VMEM((frames, cols, D), BF)]
        + [pltpu.VMEM((tokens, D), BF)] * 6
        + [pltpu.SemaphoreType.DMA((7,))],
        compiler_params=pltpu.CompilerParams(vmem_limit_bytes=40 * 2**20),
        name="temporal_phase",
    )(core, in_vmem(mid), spread.reshape(n, 1), spread.reshape(1, n), gain.reshape(1, D),
      in_hbm(cot), in_hbm(heads), in_hbm(merge))


def per_device(
    clip_tokens,
    frame_order,
    row_reach,
    spatial_gain,
    spatial_heads,
    spatial_merge,
    temporal_gain,
    temporal_heads,
    temporal_merge,
    cotangent,
):
    tm, space = lax.axis_size("tm"), lax.axis_size("space")
    _, frame_count, rows, cols, _ = clip_tokens.shape
    frames = frame_count // tm
    wide = tm * cols
    exchange = lambda v, axis: lax.all_to_all(v, axis, split_axis=0, concat_axis=0, tiled=True)

    arrived = exchange(clip_tokens.reshape(tm, frames, rows, cols, D), "tm")
    cot = cotangent.reshape(frames, rows, wide, D).swapaxes(0, 1)
    tok, *parts = norm_reorder(arrived, spatial_gain)
    up = [(i, i + 1) for i in range(space - 1)]
    down = [(j, i) for i, j in up]
    edge = HALO * wide
    halos = []
    for f in range(frames):
        above = lax.ppermute(parts[2 * f + 1], "space", up)
        below = lax.ppermute(parts[2 * f], "space", down)
        halos.append((above.reshape(edge, D), below.reshape(edge, D)))
    qkv = qkv_own([p.reshape(edge, D) for p in parts], spatial_heads)
    cot, qkv = lax.optimization_barrier((cot, qkv))
    cot = exchange(cot, "tm")
    here = lax.axis_index("space").astype(jnp.int32)
    info = jnp.concatenate([row_reach.reshape(frames), here.reshape(1)])
    middle = spatial_phase(info, qkv, halos, tok, spatial_heads, spatial_merge, rows * space)
    mid = exchange(middle, "tm").reshape(frame_count, wide, D)
    core = jnp.stack([lax.axis_index("batch") & 1, here]).astype(jnp.int32)
    out, send, keep = temporal_phase(
        core, mid, frame_order.reshape(frame_count), temporal_gain, cot.reshape(frame_count, wide, D),
        temporal_heads, temporal_merge, space, tm,
    )
    batch = lax.axis_size("batch")
    got = lax.ppermute(send, "batch", [(i, i ^ 1) for i in range(batch)])
    output = exchange(out.reshape(tm, frames, wide, D), "tm").swapaxes(0, 1)
    chip = [keep[k].astype(F32) + got[k].astype(F32) for k in range(space)]
    total = chip[0]
    moved = [lax.ppermute(chip[k].astype(BF), "space", [(i, (i + k) % space) for i in range(space)])
             for k in range(1, space)]
    for part in moved:
        total = total + part.astype(F32)
    over_space = total.astype(BF)
    over_tm = exchange(over_space, "tm")
    over_tm = over_tm.astype(F32).sum(0).astype(BF)
    block = over_tm.shape[0]
    parts = lax.all_gather(over_tm, "batch").astype(F32).reshape(batch // 2, 2, block, D // 2).sum(0)
    weight_grad = parts.swapaxes(0, 1).reshape(block, D)
    return (output.reshape(1, frames, rows, wide, D), weight_grad)


def solution(mesh):
    in_specs = (
        P("batch", None, "space", "tm", None),
        P("batch", None),
        P("batch", "tm"),
        P(),
        P(),
        P(),
        P(),
        P(),
        P(),
        P("batch", "tm", "space", None, None),
    )
    out_specs = (P("batch", "tm", "space", None, None), P(("tm", "space"), None))

    return jax.shard_map(per_device, mesh=mesh, in_specs=in_specs, out_specs=out_specs, check_vma=False)
```

time: 164 us -> 147 us (0.90)
  blocking collectives: 28 us -> 9.1 us
  starting transfers between devices: 30.2 us -> 41.4 us
  matrix products: 8.18 us -> 0 us
  Pallas kernels: 35.3 us -> 41.7 us
  local copies, waits for them, and re-layouts: 8.51 us -> 4.31 us
  waiting for transfers between devices: 48.7 us -> 45.2 us
    all_to_all x1 -> x0, blocking collectives: 18.3 us -> none  [per_device(): lax.all_to_all(v, axis, split_axis=0, concat_axis=0, tiled=True)]
    all_to_all x5, waiting for transfers between devices: 41.9 us -> 29.9 us  [per_device(): lax.all_to_all(v, axis, split_axis=0, concat_axis=0, tiled=True)]
    ppermute x2 -> x7, waiting for transfers between devices: 4.36 us -> 15.3 us  [the longest x3 14.1 us: per_device(): lax.ppermute(chip[k].astype(BF), 'space', [(i, (i + k) % space) for i in...]
    ppermute x2 -> x7, starting transfers between devices: 4.87 us -> 14.4 us  [the longest x2 7.73 us: per_device(): above = lax.ppermute(parts[2 * f + 1], 'space', up)]
    dot_general x1 -> x0, matrix products: 8.18 us -> none  [per_device(): jnp.dot(normed.reshape(frames * tokens, D), spatial_heads, preferred_elem...]
    pallas_call x3 -> x5, Pallas kernels: 35.3 us -> 41.7 us  [the longest x2 18.3 us: spatial_phase(): pl.pallas_call(functools.partial(spatial_kernel, frame=f, rows=rows, all_...]
    ppermute x1, waiting for transfers between devices: 2.5 us -> 0.01 us  [per_device(): got = lax.ppermute(send, 'batch', [(i, i ^ 1) for i in range(batch)])]
    unnamed x16 -> x12, local copies, waits for them, and re-layouts: 5.16 us -> 3.41 us
  transfers between devices with their start and end apart: 8 -> 13, of which waited for: 7 -> 6; matrix products, arithmetic and copies ran while one was open for 10% -> 5% of each run, Pallas kernels for 12% -> 13%
where the time goes in v2:
time: 147 us; the launch traced here: 146 us
  waiting for transfers between devices  45.2 us (31%)
  Pallas kernels  41.7 us (28%)
  starting transfers between devices  41.4 us (28%)
  blocking collectives  9.1 us (6%)
  local copies, waits for them, and re-layouts  4.31 us (3%)
  other arithmetic  3.39 us (2%)
    all_to_all x5, waiting for transfers between devices, per_device(): lax.all_to_all(v, axis, split_axis=0, concat_axis=0, tiled=True)  29.9 us
    all_to_all x5, starting transfers between devices, per_device(): lax.all_to_all(v, axis, split_axis=0, concat_axis=0, tiled=True)  22.8 us
    pallas_call x2, Pallas kernels, spatial_phase(): pl.pallas_call(functools.partial(spatial_kernel, frame=f, rows=rows, all_...  18.3 us
    pallas_call x1, Pallas kernels, temporal_phase(): pl.pallas_call(temporal_kernel, in_specs=[SMEM] + [VMEM] * 4 + [HBM] * 3,...  14.3 us
    ppermute x3, waiting for transfers between devices, per_device(): lax.ppermute(chip[k].astype(BF), 'space', [(i, (i + k) % space) for i in...  14.1 us
    all_gather x1, blocking collectives, per_device(): lax.all_gather(over_tm, 'batch').astype(F32)  9.1 us
    ppermute x2, starting transfers between devices, per_device(): above = lax.ppermute(parts[2 * f + 1], 'space', up)  7.73 us
    pallas_call x1, Pallas kernels, qkv_own(): pl.pallas_call(qkv_kernel, in_specs=[VMEM] * len(parts) + [HBM], out_spec...  6.39 us
  transfers between devices with their start and end apart: 13, of which 6 were waited for; matrix products, arithmetic and copies ran while one was open for 5% of the time, Pallas kernels for 13%

profile of v2, /device:TPU:1, one launch (start us, length us, event | category | flops | bytes accessed | tf_op | source)
XLA Modules:
  0.0 145.9 jit_solution(951982488243398808)
XLA Ops:
  0.6 5.9 %all-to-all-start = ((bf16[8,2,8,4,1024]{4,3,2,1,0:T(4,128)(2,1)}), bf16[8,2,8,4,1024]{4,3,2,1,0:T(4,128)(2,1)S(1)}, u32[]{:S(2)}, u32[]{:S(2)}) async-start(bf16[8,2,8,4,1024]{4,3,2,1,0:T(4,128)(2,1)} %bitcast.58), calls=%async_computation | async-start | bytes 2097152 | tf_op jit(solution)/shard_map/all_to_all | solution.py:298
  6.5 2.3 %copy.31 = bf16[1,2,8,32,1024]{4,3,1,2,0:T(8,128)(2,1)} copy(bf16[1,2,8,32,1024]{4,3,2,1,0:T(8,128)(2,1)} %param.19) | data formatting | bytes 2097152 | tf_op args[9]
  8.8 13.0 %all-to-all-done.x_ref = bf16[8,2,8,4,1024]{4,3,2,1,0:T(4,128)(2,1)S(1)} async-done(((bf16[8,2,8,4,1024]{4,3,2,1,0:T(4,128)(2,1)}), bf16[8,2,8,4,1024]{4,3,2,1,0:T(4,128)(2,1)S(1)}, u32[]{:S(2)}, u32[]{:S(2)}) %all-to-all-start) | async-done | bytes 1048608 | tf_op jit(solution)/shard_map/all_to_all | solution.py:298
  21.8 0.0 copy-done.1
  21.8 2.8 %norm_reorder.1 = (bf16[2,8,32,1024]{3,2,1,0:T(8,128)(2,1)}, bf16[4,32,1024]{2,1,0:T(8,128)(2,1)S(1)}, bf16[4,32,1024]{2,1,0:T(8,128)(2,1)S(1)}, bf16[4,32,1024]...) custom-call(bf16[8,2,8,4,1024]{4,3,2,1,0:T(4,128)(2,1)S(1)} %all-to-all-done.x_ref, f32[1,1024]{1,0:T(1,128)S(1)} %bitcast.55), custom_call_target="tpu_custom_call" | custom-call | tf_op jit(solution)/shard_map/norm_reorder/pallas_call | solution.py:67
  24.6 0.0 copy-start.4
  24.6 6.4 %qkv_own.1.refs_3_ = bf16[3,512,1024]{2,1,0:T(8,128)(2,1)} custom-call(bf16[128,1024]{1,0:T(8,128)(2,1)S(1)} %bitcast.50, bf16[128,1024]{1,0:T(8,128)(2,1)S(1)} %bitcast.51, bf16[128,1024]{1,0:T(8,128)(2,1)S(1)} %bitcast.48, bf16[128,1024]{1,0:T(8,128)(2,1)S(1)} %bitcast.49, bf16[1024,3072]{1,0:T(8,128)(2,1)} %refs_5_.3), custom_call_target="tpu_custom_call" | custom-call | tf_op jit(solution)/shard_map/qkv_own/pallas_call | solution.py:101
  31.0 3.6 %all-to-all-start.2 = ((bf16[8,2,32,1024]{3,2,1,0:T(8,128)(2,1)}), bf16[8,2,32,1024]{3,2,1,0:T(8,128)(2,1)S(1)}, u32[]{:S(2)}, u32[]{:S(2)}) async-start(bf16[8,2,32,1024]{3,2,1,0:T(8,128)(2,1)} %bitcast.44), calls=%async_computation.2 | async-start | bytes 2097152 | tf_op jit(solution)/shard_map/all_to_all | solution.py:298
  34.6 3.6 %collective-permute-start.2 = (bf16[4,32,1024]{2,1,0:T(8,128)(2,1)S(1)}, bf16[4,32,1024]{2,1,0:T(8,128)(2,1)S(1)}, u32[]{:S(2)}, u32[]{:S(2)}) collective-permute-start(bf16[4,32,1024]{2,1,0:T(8,128)(2,1)S(1)} %get-tuple-element.15), channel_id=1, source_target_pairs={{0,1},{1,2},{2,3},{4,5},{5,6},{6,7},{8,9},{9,10},{10,11},{12,13},{... | collective-permute-start | bytes 786440 | tf_op jit(solution)/shard_map/ppermute | solution.py:308
  38.1 1.3 collective-permute-start.3
  39.4 4.2 %collective-permute-start = (bf16[4,32,1024]{2,1,0:T(8,128)(2,1)S(1)}, bf16[4,32,1024]{2,1,0:T(8,128)(2,1)S(1)}, u32[]{:S(2)}, u32[]{:S(2)}) collective-permute-start(bf16[4,32,1024]{2,1,0:T(8,128)(2,1)S(1)} %get-tuple-element.12), channel_id=1, source_target_pairs={{0,1},{1,2},{2,3},{4,5},{5,6},{6,7},{8,9},{9,10},{10,11},{12,13},{... | collective-permute-start | bytes 786440 | tf_op jit(solution)/shard_map/ppermute | solution.py:308
  43.6 1.5 %collective-permute-start.1 = (bf16[4,32,1024]{2,1,0:T(8,128)(2,1)S(1)}, bf16[4,32,1024]{2,1,0:T(8,128)(2,1)S(1)}, u32[]{:S(2)}, u32[]{:S(2)}) collective-permute-start(bf16[4,32,1024]{2,1,0:T(8,128)(2,1)S(1)} %get-tuple-element.13), channel_id=1, source_target_pairs={{1,0},{2,1},{3,2},{5,4},{6,5},{7,6},{9,8},{10,9},{11,10},{13,12},{... | collective-permute-start | bytes 786440 | tf_op jit(solution)/shard_map/ppermute | solution.py:309
  45.1 0.1 pad_add_fusion.1.refs_0_
  45.2 0.0 collective-permute-done.2
  45.2 1.2 collective-permute-done.3
  46.4 9.1 %spatial_phase.2.refs_7_ = bf16[8,2,32,1024]{3,2,1,0:T(8,128)(2,1)} custom-call(s32[3]{0:T(128)S(1)} %pad_add_fusion.1.refs_0_, bf16[128,1024]{1,0:T(8,128)(2,1)S(1)} %bitcast.52, bf16[128,1024]{1,0:T(8,128)(2,1)S(1)} %bitcast.53, bf16[3,512,1024]{2,1,0:T(8,128)(2,1)} %qkv_own.1.refs_3_, bf16[2,8,32,1024]{3,2,1,0:T(8,128)(2,1)} %get-tuple-element.17.refs_4_, ...), custom_call_target="tpu_custom_call" | custom-call | tf_op jit(solution)/shard_map/spatial_phase/pallas_call | solution.py:186
  55.5 0.0 collective-permute-done
  55.5 0.0 collective-permute-done.1
  55.5 0.0 copy-start.3
  55.5 0.0 copy-start
  55.5 9.2 %spatial_phase.3 = bf16[8,2,32,1024]{3,2,1,0:T(8,128)(2,1)} custom-call(s32[3]{0:T(128)S(1)} %pad_add_fusion.1.refs_0_, bf16[128,1024]{1,0:T(8,128)(2,1)S(1)} %bitcast.46, bf16[128,1024]{1,0:T(8,128)(2,1)S(1)} %bitcast.47, bf16[3,512,1024]{2,1,0:T(8,128)(2,1)} %qkv_own.1.refs_3_, ...), custom_call_target="tpu_custom_call", output_to_operand_aliasing={{}: (7, {})} | custom-call | tf_op jit(solution)/shard_map/spatial_phase/pallas_call | solution.py:186
  64.7 0.0 all-to-all-done.2
  64.7 0.0 copy-start.2
  64.7 4.8 %all-to-all-start.1 = ((bf16[8,2,32,1024]{3,2,1,0:T(8,128)(2,1)}), bf16[8,2,32,1024]{3,2,1,0:T(8,128)(2,1)S(1)}, u32[]{:S(2)}, u32[]{:S(2)}) async-start(bf16[8,2,32,1024]{3,2,1,0:T(8,128)(2,1)} %spatial_phase.3), calls=%async_computation.1 | async-start | bytes 2097152 | tf_op jit(solution)/shard_map/all_to_all | solution.py:298
  69.5 0.1 broadcast_in_dim.3
  69.6 0.1 reshape_reshape.8.order_q_ref
  69.7 0.1 reshape_reshape.7.order_k_ref
  69.7 0.1 pad_add_fusion.core_ref
  69.8 12.1 %all-to-all-done.1 = bf16[8,2,32,1024]{3,2,1,0:T(8,128)(2,1)S(1)} async-done(((bf16[8,2,32,1024]{3,2,1,0:T(8,128)(2,1)}), bf16[8,2,32,1024]{3,2,1,0:T(8,128)(2,1)S(1)}, u32[]{:S(2)}, u32[]{:S(2)}) %all-to-all-start.1) | async-done | bytes 1048608 | tf_op jit(solution)/shard_map/all_to_all | solution.py:298
  82.0 0.0 copy-done
  82.0 14.3 %temporal_phase.1 = (bf16[16,32,1024]{2,1,0:T(8,128)(2,1)}, bf16[4,8,32,512]{3,2,1,0:T(8,128)(2,1)S(1)}, bf16[4,8,32,512]{3,2,1,0:T(8,128)(2,1)}) custom-call(s32[2]{0:T(128)S(1)} %pad_add_fusion.core_ref, bf16[16,32,1024]{2,1,0:T(8,128)(2,1)S(1)} %bitcast.45, s32[128,1]{1,0:T(8,128)S(1)} %reshape_reshape.8.order_q_ref, ...), custom_call_target="tpu_custom_call" | custom-call | tf_op jit(solution)/shard_map/temporal_phase/pallas_call | solution.py:268
  96.3 4.2 %collective-permute-start.4 = (bf16[4,8,32,512]{3,2,1,0:T(8,128)(2,1)S(1)}, bf16[4,8,32,512]{3,2,1,0:T(8,128)(2,1)S(1)}, u32[]{:S(2)}, u32[]{:S(2)}) collective-permute-start(bf16[4,8,32,512]{3,2,1,0:T(8,128)(2,1)S(1)} %get-tuple-element.21), channel_id=1, source_target_pairs={{0,32},{32,0},{64,96},{96,64},{1,33},{33,1},{65,97},{97,65},{2,34}... | collective-permute-start | bytes 3145736 | tf_op jit(solution)/shard_map/ppermute | solution.py:324
  100.4 3.6 %all-to-all-start.3 = ((bf16[8,2,32,1024]{3,2,1,0:T(8,128)(2,1)}), bf16[8,2,32,1024]{3,2,1,0:T(8,128)(2,1)S(1)}, u32[]{:S(2)}, u32[]{:S(2)}) async-start(bf16[8,2,32,1024]{3,2,1,0:T(8,128)(2,1)} %bitcast.59), calls=%async_computation.3 | async-start | bytes 2097152 | tf_op jit(solution)/shard_map/all_to_all | solution.py:298
  104.0 0.0 collective-permute-done.4
  104.0 1.4 fusion.3
  105.4 3.3 %collective-permute-start.7 = (bf16[8,32,512]{2,1,0:T(8,128)(2,1)S(1)}, bf16[8,32,512]{2,1,0:T(8,128)(2,1)S(1)}, u32[]{:S(2)}, u32[]{:S(2)}) collective-permute-start(bf16[8,32,512]{2,1,0:T(8,128)(2,1)S(1)} %get-tuple-element.29), channel_id=1, source_target_pairs={{0,3},{1,0},{2,1},{3,2},{4,7},{5,4},{6,5},{7,6},{8,11},{9,8},{10,9... | collective-permute-start | bytes 786440 | tf_op jit(solution)/shard_map/ppermute | solution.py:328
  108.6 0.0 collective-permute-start.6
  108.6 0.7 collective-permute-start.5
  109.3 10.6 %collective-permute-done.7 = bf16[8,32,512]{2,1,0:T(8,128)(2,1)S(1)} collective-permute-done((bf16[8,32,512]{2,1,0:T(8,128)(2,1)S(1)}, bf16[8,32,512]{2,1,0:T(8,128)(2,1)S(1)}, u32[]{:S(2)}, u32[]{:S(2)}) %collective-permute-start.7) | collective-permute-done | bytes 262176 | tf_op jit(solution)/shard_map/ppermute | solution.py:328
  119.9 0.0 collective-permute-done.6
  119.9 3.5 %collective-permute-done.5 = bf16[8,32,512]{2,1,0:T(8,128)(2,1)S(1)} collective-permute-done((bf16[8,32,512]{2,1,0:T(8,128)(2,1)S(1)}, bf16[8,32,512]{2,1,0:T(8,128)(2,1)S(1)}, u32[]{:S(2)}, u32[]{:S(2)}) %collective-permute-start.5) | collective-permute-done | bytes 262176 | tf_op jit(solution)/shard_map/ppermute | solution.py:328
  123.4 1.8 %fusion.2 = bf16[8,32,512]{2,1,0:T(8,128)(2,1)} fusion(bf16[8,32,512]{2,1,0:T(8,128)(2,1)S(1)} %collective-permute-done.7, bf16[8,32,512]{2,1,0:T(8,128)(2,1)S(1)} %collective-permute-done.6, bf16[8,32,512]{2,1,0:T(8,128)(2,1)S(1)} %collective-permute-done.5, bf16[4,8,32,512]{3,2,1,0:T(8,128)(2,1)S(1)} %collective-permute-done.4, ...), kind=kLoop, calls=%fused_computation.4 | loop fusion | flops 1310720 | bytes 1572864 | tf_op jit(solution)/shard_map/convert_element_type | solution.py:332
  125.2 0.0 all-to-all-done.3
  125.2 5.1 %all-to-all-start.4 = ((bf16[8,32,512]{2,1,0:T(8,128)(2,1)}), bf16[8,32,512]{2,1,0:T(8,128)(2,1)S(1)}, u32[]{:S(2)}, u32[]{:S(2)}) async-start(bf16[8,32,512]{2,1,0:T(8,128)(2,1)} %fusion.2), calls=%async_computation.4 | async-start | bytes 524288 | tf_op jit(solution)/shard_map/all_to_all | solution.py:298
  130.3 1.1 copy.28
  131.4 4.8 %all-to-all-done.4 = bf16[8,32,512]{2,1,0:T(8,128)(2,1)S(1)} async-done(((bf16[8,32,512]{2,1,0:T(8,128)(2,1)}), bf16[8,32,512]{2,1,0:T(8,128)(2,1)S(1)}, u32[]{:S(2)}, u32[]{:S(2)}) %all-to-all-start.4) | async-done | bytes 262176 | tf_op jit(solution)/shard_map/all_to_all | solution.py:298
  136.2 9.1 %all-gather = bf16[128,512]{1,0:T(8,128)(2,1)S(1)} all-gather(bf16[32,512]{1,0:T(8,128)(2,1)S(1)} %reduce_sum.21), channel_id=2, replica_groups=mesh['batch'=4,'tm'=8,'space'=4] {'batch'}, dimensions={0}, use_global_device_ids=true | all-gather | bytes 163840 | tf_op jit(solution)/shard_map/all_gather | solution.py:336
  145.3 0.7 copy.29
  (6 shorter events, 0.1 us)
Async XLA Ops:
  0.6 21.2 %copy-start.1 = (f32[1024]{0:T(1024)S(1)}, f32[1024]{0:T(1024)}, u32[]{:S(2)}) copy-start(f32[1024]{0:T(1024)} %param.13) | copy-start | bytes 12292
  0.6 21.2 %all-to-all-start = ((bf16[8,2,8,4,1024]{4,3,2,1,0:T(4,128)(2,1)}), bf16[8,2,8,4,1024]{4,3,2,1,0:T(4,128)(2,1)S(1)}, u32[]{:S(2)}, u32[]{:S(2)}) async-start(bf16[8,2,8,4,1024]{4,3,2,1,0:T(4,128)(2,1)} %bitcast.58), calls=%async_computation | async-start | bytes 2097152 | tf_op jit(solution)/shard_map/all_to_all | solution.py:298
  24.6 20.5 %copy-start.4 = (s32[1,2]{1,0:T(1,128)S(1)}, s32[1,2]{1,0:T(1,128)}, u32[]{:S(2)}) copy-start(s32[1,2]{1,0:T(1,128)} %param.12) | copy-start | bytes 28
  31.0 33.7 %all-to-all-start.2 = ((bf16[8,2,32,1024]{3,2,1,0:T(8,128)(2,1)}), bf16[8,2,32,1024]{3,2,1,0:T(8,128)(2,1)S(1)}, u32[]{:S(2)}, u32[]{:S(2)}) async-start(bf16[8,2,32,1024]{3,2,1,0:T(8,128)(2,1)} %bitcast.44), calls=%async_computation.2 | async-start | bytes 2097152 | tf_op jit(solution)/shard_map/all_to_all | solution.py:298
  34.6 10.6 %collective-permute-start.2 = (bf16[4,32,1024]{2,1,0:T(8,128)(2,1)S(1)}, bf16[4,32,1024]{2,1,0:T(8,128)(2,1)S(1)}, u32[]{:S(2)}, u32[]{:S(2)}) collective-permute-start(bf16[4,32,1024]{2,1,0:T(8,128)(2,1)S(1)} %get-tuple-element.15), channel_id=1, source_target_pairs={{0,1},{1,2},{2,3},{4,5},{5,6},{6,7},{8,9},{9,10},{10,11},{12,13},{... | collective-permute-start | bytes 786440 | tf_op jit(solution)/shard_map/ppermute | solution.py:308
  38.1 8.3 %collective-permute-start.3 = (bf16[4,32,1024]{2,1,0:T(8,128)(2,1)S(1)}, bf16[4,32,1024]{2,1,0:T(8,128)(2,1)S(1)}, u32[]{:S(2)}, u32[]{:S(2)}) collective-permute-start(bf16[4,32,1024]{2,1,0:T(8,128)(2,1)S(1)} %get-tuple-element.14), channel_id=1, source_target_pairs={{1,0},{2,1},{3,2},{5,4},{6,5},{7,6},{9,8},{10,9},{11,10},{13,12},{... | collective-permute-start | bytes 786440 | tf_op jit(solution)/shard_map/ppermute | solution.py:309
  39.4 16.1 %collective-permute-start = (bf16[4,32,1024]{2,1,0:T(8,128)(2,1)S(1)}, bf16[4,32,1024]{2,1,0:T(8,128)(2,1)S(1)}, u32[]{:S(2)}, u32[]{:S(2)}) collective-permute-start(bf16[4,32,1024]{2,1,0:T(8,128)(2,1)S(1)} %get-tuple-element.12), channel_id=1, source_target_pairs={{0,1},{1,2},{2,3},{4,5},{5,6},{6,7},{8,9},{9,10},{10,11},{12,13},{... | collective-permute-start | bytes 786440 | tf_op jit(solution)/shard_map/ppermute | solution.py:308
  43.6 11.9 %collective-permute-start.1 = (bf16[4,32,1024]{2,1,0:T(8,128)(2,1)S(1)}, bf16[4,32,1024]{2,1,0:T(8,128)(2,1)S(1)}, u32[]{:S(2)}, u32[]{:S(2)}) collective-permute-start(bf16[4,32,1024]{2,1,0:T(8,128)(2,1)S(1)} %get-tuple-element.13), channel_id=1, source_target_pairs={{1,0},{2,1},{3,2},{5,4},{6,5},{7,6},{9,8},{10,9},{11,10},{13,12},{... | collective-permute-start | bytes 786440 | tf_op jit(solution)/shard_map/ppermute | solution.py:309
  55.5 14.0 %copy-start.3 = (s32[1,16]{1,0:T(1,128)S(1)}, s32[1,16]{1,0:T(1,128)}, u32[]{:S(2)}) copy-start(s32[1,16]{1,0:T(1,128)} %param.11) | copy-start | bytes 196
  55.5 26.4 %copy-start = (f32[1024]{0:T(1024)S(1)}, f32[1024]{0:T(1024)}, u32[]{:S(2)}) copy-start(f32[1024]{0:T(1024)} %param.16) | copy-start | bytes 12292
  64.7 17.2 %copy-start.2 = (bf16[8,2,32,1024]{3,2,1,0:T(8,128)(2,1)}, bf16[8,2,32,1024]{3,2,1,0:T(8,128)(2,1)S(1)}, u32[]{:S(2)}) copy-start(bf16[8,2,32,1024]{3,2,1,0:T(8,128)(2,1)S(1)} %all-to-all-done.2) | copy-start | bytes 3145732
  64.7 17.2 %all-to-all-start.1 = ((bf16[8,2,32,1024]{3,2,1,0:T(8,128)(2,1)}), bf16[8,2,32,1024]{3,2,1,0:T(8,128)(2,1)S(1)}, u32[]{:S(2)}, u32[]{:S(2)}) async-start(bf16[8,2,32,1024]{3,2,1,0:T(8,128)(2,1)} %spatial_phase.3), calls=%async_computation.1 | async-start | bytes 2097152 | tf_op jit(solution)/shard_map/all_to_all | solution.py:298
  96.3 7.7 %collective-permute-start.4 = (bf16[4,8,32,512]{3,2,1,0:T(8,128)(2,1)S(1)}, bf16[4,8,32,512]{3,2,1,0:T(8,128)(2,1)S(1)}, u32[]{:S(2)}, u32[]{:S(2)}) collective-permute-start(bf16[4,8,32,512]{3,2,1,0:T(8,128)(2,1)S(1)} %get-tuple-element.21), channel_id=1, source_target_pairs={{0,32},{32,0},{64,96},{96,64},{1,33},{33,1},{65,97},{97,65},{2,34}... | collective-permute-start | bytes 3145736 | tf_op jit(solution)/shard_map/ppermute | solution.py:324
  100.4 24.8 %all-to-all-start.3 = ((bf16[8,2,32,1024]{3,2,1,0:T(8,128)(2,1)}), bf16[8,2,32,1024]{3,2,1,0:T(8,128)(2,1)S(1)}, u32[]{:S(2)}, u32[]{:S(2)}) async-start(bf16[8,2,32,1024]{3,2,1,0:T(8,128)(2,1)} %bitcast.59), calls=%async_computation.3 | async-start | bytes 2097152 | tf_op jit(solution)/shard_map/all_to_all | solution.py:298
  105.4 14.5 %collective-permute-start.7 = (bf16[8,32,512]{2,1,0:T(8,128)(2,1)S(1)}, bf16[8,32,512]{2,1,0:T(8,128)(2,1)S(1)}, u32[]{:S(2)}, u32[]{:S(2)}) collective-permute-start(bf16[8,32,512]{2,1,0:T(8,128)(2,1)S(1)} %get-tuple-element.29), channel_id=1, source_target_pairs={{0,3},{1,0},{2,1},{3,2},{4,7},{5,4},{6,5},{7,6},{8,11},{9,8},{10,9... | collective-permute-start | bytes 786440 | tf_op jit(solution)/shard_map/ppermute | solution.py:328
  108.6 11.3 %collective-permute-start.6 = (bf16[8,32,512]{2,1,0:T(8,128)(2,1)S(1)}, bf16[8,32,512]{2,1,0:T(8,128)(2,1)S(1)}, u32[]{:S(2)}, u32[]{:S(2)}) collective-permute-start(bf16[8,32,512]{2,1,0:T(8,128)(2,1)S(1)} %get-tuple-element.30), channel_id=1, source_target_pairs={{0,2},{1,3},{2,0},{3,1},{4,6},{5,7},{6,4},{7,5},{8,10},{9,11},{10,... | collective-permute-start | bytes 786440 | tf_op jit(solution)/shard_map/ppermute | solution.py:328
  108.6 14.8 %collective-permute-start.5 = (bf16[8,32,512]{2,1,0:T(8,128)(2,1)S(1)}, bf16[8,32,512]{2,1,0:T(8,128)(2,1)S(1)}, u32[]{:S(2)}, u32[]{:S(2)}) collective-permute-start(bf16[8,32,512]{2,1,0:T(8,128)(2,1)S(1)} %get-tuple-element.28), channel_id=1, source_target_pairs={{0,1},{1,2},{2,3},{3,0},{4,5},{5,6},{6,7},{7,4},{8,9},{9,10},{10,1... | collective-permute-start | bytes 786440 | tf_op jit(solution)/shard_map/ppermute | solution.py:328
  125.2 10.9 %all-to-all-start.4 = ((bf16[8,32,512]{2,1,0:T(8,128)(2,1)}), bf16[8,32,512]{2,1,0:T(8,128)(2,1)S(1)}, u32[]{:S(2)}, u32[]{:S(2)}) async-start(bf16[8,32,512]{2,1,0:T(8,128)(2,1)} %fusion.2), calls=%async_computation.4 | async-start | bytes 524288 | tf_op jit(solution)/shard_map/all_to_all | solution.py:298

commit v3 on v2

--- a/solution.py
+++ b/solution.py
@@ -38,21 +38,19 @@
 HBM = pl.BlockSpec(memory_space=pltpu.HBM)
 
 
-def norm_kernel(x_ref, gain_ref, tok_out, *refs):
-    part_refs, (tok_ref, sems) = refs[:-2], refs[-2:]
+def norm_kernel(x_ref, gain_ref, tok_out, low_ref, high_ref, tok_ref, sems):
     sources, frames, rows, cols, _ = x_ref.shape
     half = rows // 2
     gain = gain_ref[...]
     for f in range(frames):
-        for h in range(2):
-            part_ref = part_refs[2 * f + h]
+        for h, part_ref in enumerate((low_ref, high_ref)):
 
             def one_row(r, carry):
                 for s in range(sources):
                     x = x_ref[s, f, h * half + r]
                     y = normalized(x.astype(F32), gain).astype(BF)
                     tok_ref[f, h * half + r, s * cols:(s + 1) * cols, :] = x
-                    part_ref[r, s * cols:(s + 1) * cols, :] = y
+                    part_ref[f, r, s * cols:(s + 1) * cols, :] = y
                 return carry
 
             lax.fori_loop(0, half, one_row, 0)
@@ -67,9 +65,9 @@
     return pl.pallas_call(
         norm_kernel,
         in_specs=[VMEM, VMEM],
-        out_specs=[HBM] + [VMEM] * (2 * frames),
+        out_specs=[HBM, VMEM, VMEM],
         scratch_shapes=[pltpu.VMEM((frames, rows, wide, D), BF), pltpu.SemaphoreType.DMA((frames,))],
-        out_shape=[pltpu.HBM((frames, rows, wide, D), BF)] + [pltpu.VMEM((rows // 2, wide, D), BF)] * (2 * frames),
+        out_shape=[pltpu.HBM((frames, rows, wide, D), BF)] + [pltpu.VMEM((frames, rows // 2, wide, D), BF)] * 2,
         compiler_params=pltpu.CompilerParams(vmem_limit_bytes=8 * 2**20),
         name="norm_reorder",
     )(in_vmem(arrived), gain.reshape(1, D))
@@ -79,14 +77,15 @@
     return [pltpu.make_async_copy(w_ref.at[:, c * D:(c + 1) * D], buf.at[i], sems.at[i]) for i, c in enumerate(columns)]
 
 
-def qkv_kernel(*refs):
-    parts, (w_ref, out_ref, x_ref, buf, y_ref, sems) = refs[:-6], refs[-6:]
+def qkv_kernel(low_ref, high_ref, w_ref, out_ref, x_ref, buf, y_ref, sems):
     copies = column_copies(w_ref, buf, sems, range(3))
     for c in copies:
         c.start()
-    n = parts[0].shape[0]
-    for i, p in enumerate(parts):
-        x_ref[i * n:(i + 1) * n] = p[...]
+    frames, edge, _ = low_ref.shape
+    for f in range(frames):
+        for h, part in enumerate((low_ref, high_ref)):
+            at = (2 * f + h) * edge
+            x_ref[at:at + edge] = part[f]
     for i, c in enumerate(copies):
         c.wait()
         y_ref[i] = jnp.dot(x_ref[...], buf[i], preferred_element_type=F32).astype(BF)
@@ -95,109 +94,124 @@
         pltpu.make_async_copy(y_ref.at[i], out_ref.at[i], sems.at[3 + i]).wait()
 
 
-def qkv_own(parts, heads):
-    n = parts[0].shape[0]
-    tokens = n * len(parts)
+def qkv_own(low, high, heads):
+    frames, edge, _ = low.shape
+    tokens = 2 * frames * edge
     return pl.pallas_call(
         qkv_kernel,
-        in_specs=[VMEM] * len(parts) + [HBM],
+        in_specs=[VMEM, VMEM, HBM],
         out_specs=HBM,
         out_shape=pltpu.HBM((3, tokens, D), BF),
         scratch_shapes=[pltpu.VMEM((tokens, D), BF), pltpu.VMEM((3, D, D), BF), pltpu.VMEM((3, tokens, D), BF),
                         pltpu.SemaphoreType.DMA((6,))],
         compiler_params=pltpu.CompilerParams(vmem_limit_bytes=24 * 2**20),
         name="qkv_own",
-    )(*[in_vmem(p) for p in parts], in_hbm(heads))
-
-
-def pair_attention(q, k, v, bias):
-    n = q.shape[0]
-    lane = lax.broadcasted_iota(jnp.int32, (n, WIDE), 1)
-    low = lane < HEAD_DIM
-    zero = jnp.zeros_like(q)
-    both = jnp.concatenate([jnp.where(low, q, zero), jnp.where(low, zero, q)], axis=0)
-    scores = lax.dot_general(both, k, (((1,), (1,)), ((), ())), preferred_element_type=F32)
-    scores = scores * SCALE + jnp.concatenate([bias, bias], axis=0)
-    top = jnp.max(scores, axis=-1, keepdims=True)
-    p = jnp.exp2(scores - top).astype(BF)
-    widened = jnp.concatenate([v, jnp.ones_like(v)], axis=1)
-    o = jnp.dot(p, widened, preferred_element_type=F32)
-    o = o[:, :WIDE] / o[:, WIDE:]
-    return jnp.where(low, o[:n], o[n:]).astype(BF)
-
-
-def spatial_kernel(*refs, frame, rows, all_rows):
-    info_ref, up_ref, down_ref, qkv_ref, tok_ref, w_ref, wm_ref = refs[:7]
-    mid_out, q_buf, tok_buf, mid_buf, wkv_buf, wm_buf, k_ref, v_ref, ctx_ref, bias_ref, sems = refs[-11:]
-    tokens = ctx_ref.shape[0]
-    copies = column_copies(w_ref, wkv_buf, sems, (1, 2))
+    )(in_vmem(low), in_vmem(high), in_hbm(heads))
+
+
+def staged_attention(items):
+    n = items[0][0]().shape[0]
+    low = lax.broadcasted_iota(jnp.int32, (n, WIDE), 1) < HEAD_DIM
+    scores, weights = [], []
+    for q, k, v, bias, ref, at in items:
+        q = q()
+        zero = jnp.zeros_like(q)
+        both = jnp.concatenate([jnp.where(low, q, zero), jnp.where(low, zero, q)], axis=0)
+        scores.append(lax.dot_general(both, k(), (((1,), (1,)), ((), ())), preferred_element_type=F32))
+    for s, (q, k, v, bias, ref, at) in zip(scores, items):
+        b = bias()
+        s = s * SCALE + jnp.concatenate([b, b], axis=0)
+        weights.append(jnp.exp2(s - jnp.max(s, axis=-1, keepdims=True)).astype(BF))
+    for p, (q, k, v, bias, ref, at) in zip(weights, items):
+        v = v()
+        o = jnp.dot(p, jnp.concatenate([v, jnp.ones_like(v)], axis=1), preferred_element_type=F32)
+        o = o[:, :WIDE] / o[:, WIDE:]
+        ref[at] = jnp.where(low, o[:n], o[n:]).astype(BF)
+
+
+def reader(ref, *at):
+    return lambda: ref[at]
+
+
+SPATIAL_STAGE = 4
+TEMPORAL_STAGE = 8
+
+
+def spatial_kernel(info_ref, up_ref, down_ref, qkv_ref, tok_ref, w_ref, wm_ref, mid_out,
+                   q_ref, tok_buf, mid_buf, wkv_buf, wm_buf, k_ref, v_ref, ctx_ref, bias_ref, sems, *, rows, all_rows):
+    frames, extent, _ = k_ref.shape
+    tokens = ctx_ref.shape[0] // frames
     cols = tokens // rows
     edge = HALO * cols
-    mine = pl.ds(frame * tokens, tokens)
-    for i, buf in enumerate((q_buf, k_ref.at[edge:edge + tokens], v_ref.at[edge:edge + tokens])):
-        copies.append(pltpu.make_async_copy(qkv_ref.at[i, mine], buf, sems.at[5 + i]))
-    copies.append(pltpu.make_async_copy(wm_ref, wm_buf, sems.at[3]))
-    copies.append(pltpu.make_async_copy(tok_ref.at[frame], tok_buf, sems.at[4]))
-    for c in copies:
+    weights = column_copies(w_ref, wkv_buf, sems, (1, 2))
+    own = [pltpu.make_async_copy(qkv_ref.at[0], q_ref, sems.at[2])]
+    for f in range(frames):
+        mine = pl.ds(f * tokens, tokens)
+        for i, buf in ((1, k_ref), (2, v_ref)):
+            own.append(pltpu.make_async_copy(qkv_ref.at[i, mine], buf.at[f, edge:edge + tokens], sems.at[2 + 2 * f + i]))
+    last = [pltpu.make_async_copy(wm_ref, wm_buf, sems.at[7]), pltpu.make_async_copy(tok_ref, tok_buf, sems.at[8])]
+    for c in weights + own + last:
         c.start()
-    reach = info_ref[frame]
-    first_row = info_ref[info_ref.shape[0] - 1] * rows
-    extent = tokens + 2 * edge
+    first_row = info_ref[frames] * rows
     qrow = lax.broadcasted_iota(jnp.int32, (tokens, extent), 0) // cols
     krow = lax.broadcasted_iota(jnp.int32, (tokens, extent), 1) // cols - HALO
-    allowed = (jnp.abs(krow - qrow) <= reach) & (krow + first_row >= 0) & (krow + first_row < all_rows)
-    bias_ref[...] = jnp.where(allowed, 0.0, MASKED)
-    halo = jnp.concatenate([up_ref[...], down_ref[...]], axis=0)
-    for i, buf in enumerate((k_ref, v_ref)):
-        copies[i].wait()
-        side = jnp.dot(halo, wkv_buf[i], preferred_element_type=F32).astype(BF)
-        buf[0:edge] = side[:edge]
-        buf[edge + tokens:] = side[edge:]
-    for c in copies[2:5]:
+    inside = (krow + first_row >= 0) & (krow + first_row < all_rows)
+    distance = jnp.where(inside, jnp.abs(krow - qrow), all_rows)
+    for f in range(frames):
+        bias_ref[f] = jnp.where(distance <= info_ref[f], 0.0, MASKED)
+    halo = jnp.concatenate([up_ref[...].reshape(frames * edge, D), down_ref[...].reshape(frames * edge, D)], axis=0)
+    for c, w, buf in zip(weights, range(2), (k_ref, v_ref)):
+        c.wait()
+        side = jnp.dot(halo, wkv_buf[w], preferred_element_type=F32).astype(BF)
+        for f in range(frames):
+            buf[f, 0:edge] = side[f * edge:(f + 1) * edge]
+            buf[f, edge + tokens:] = side[(frames + f) * edge:(frames + f + 1) * edge]
+    for c in own:
         c.wait()
     half = tokens // 2
-    for pair in range(PAIRS):
-        at = slice(pair * WIDE, (pair + 1) * WIDE)
-        for side in range(2):
-            keys = slice(side * edge, side * edge + half + 2 * edge)
-            own = slice(side * half, (side + 1) * half)
-            ctx_ref[own, at] = pair_attention(q_buf[own, at], k_ref[keys, at], v_ref[keys, at], bias_ref[own, keys])
-    copies[5].wait()
-    copies[6].wait()
-    mid = tok_buf[...].reshape(tokens, D).astype(F32) + jnp.dot(ctx_ref[...], wm_buf[...], preferred_element_type=F32)
-    mid_buf[...] = mid.astype(BF).reshape(rows, cols, D)
-    out = pltpu.make_async_copy(mid_buf, mid_out.at[:, frame], sems.at[8])
-    out.start()
-    out.wait()
-
-
-def spatial_phase(info, qkv, halos, tok, heads, merge, all_rows):
+    items = []
+    for f in range(frames):
+        for pair in range(PAIRS):
+            at = slice(pair * WIDE, (pair + 1) * WIDE)
+            for side in range(2):
+                keys = slice(side * edge, side * edge + half + 2 * edge)
+                rows_in = slice(side * half, (side + 1) * half)
+                mine = slice(f * tokens + side * half, f * tokens + (side + 1) * half)
+                items.append((reader(q_ref, mine, at), reader(k_ref, f, keys, at), reader(v_ref, f, keys, at),
+                              reader(bias_ref, f, rows_in, keys), ctx_ref, (mine, at)))
+    for i in range(0, len(items), SPATIAL_STAGE):
+        staged_attention(items[i:i + SPATIAL_STAGE])
+    for c in last:
+        c.wait()
+    sent = []
+    for f in range(frames):
+        mid = jnp.dot(ctx_ref[f * tokens:(f + 1) * tokens], wm_buf[...], preferred_element_type=F32)
+        mid = mid + tok_buf[f].reshape(tokens, D).astype(F32)
+        mid_buf[:, f] = mid.astype(BF).reshape(rows, cols, D)
+        sent.append(pltpu.make_async_copy(mid_buf.at[:, f], mid_out.at[:, f], sems.at[9 + f]))
+        sent[f].start()
+    for c in sent:
+        c.wait()
+
+
+def spatial_phase(info, up, down, qkv, tok, heads, merge, all_rows):
     frames, rows, cols, _ = tok.shape
     tokens = rows * cols
     extent = tokens + 2 * HALO * cols
-    mid = None
-    for f in range(frames):
-        up, down = halos[f]
-        operands = [info, in_vmem(up), in_vmem(down)] + [in_hbm(v) for v in (qkv, tok, heads, merge)]
-        specs = [SMEM, VMEM, VMEM, HBM, HBM, HBM, HBM]
-        if mid is not None:
-            operands.append(in_hbm(mid))
-            specs.append(HBM)
-        mid = pl.pallas_call(
-            functools.partial(spatial_kernel, frame=f, rows=rows, all_rows=all_rows),
-            in_specs=specs,
-            out_specs=HBM,
-            out_shape=pltpu.HBM((rows, frames, cols, D), BF),
-            scratch_shapes=[pltpu.VMEM((tokens, D), BF), pltpu.VMEM((rows, cols, D), BF), pltpu.VMEM((rows, cols, D), BF),
-                            pltpu.VMEM((2, D, D), BF), pltpu.VMEM((D, D), BF),
-                            pltpu.VMEM((extent, D), BF), pltpu.VMEM((extent, D), BF),
-                            pltpu.VMEM((tokens, D), BF), pltpu.VMEM((tokens, extent), F32),
-                            pltpu.SemaphoreType.DMA((9,))],
-            input_output_aliases={} if f == 0 else {len(operands) - 1: 0},
-            compiler_params=pltpu.CompilerParams(vmem_limit_bytes=32 * 2**20),
-            name="spatial_phase",
-        )(*operands)
-    return mid
+    return pl.pallas_call(
+        functools.partial(spatial_kernel, rows=rows, all_rows=all_rows),
+        in_specs=[SMEM, VMEM, VMEM, HBM, HBM, HBM, HBM],
+        out_specs=HBM,
+        out_shape=pltpu.HBM((rows, frames, cols, D), BF),
+        scratch_shapes=[pltpu.VMEM((frames * tokens, D), BF), pltpu.VMEM((frames, rows, cols, D), BF),
+                        pltpu.VMEM((rows, frames, cols, D), BF),
+                        pltpu.VMEM((2, D, D), BF), pltpu.VMEM((D, D), BF),
+                        pltpu.VMEM((frames, extent, D), BF), pltpu.VMEM((frames, extent, D), BF),
+                        pltpu.VMEM((frames * tokens, D), BF), pltpu.VMEM((frames, tokens, extent), F32),
+                        pltpu.SemaphoreType.DMA((9 + frames,))],
+        compiler_params=pltpu.CompilerParams(vmem_limit_bytes=40 * 2**20),
+        name="spatial_phase",
+    )(info, in_vmem(up), in_vmem(down), *[in_hbm(v) for v in (qkv, tok, heads, merge)])
 
 
 GROUP = 8
@@ -228,11 +242,15 @@
     place_k = lax.broadcasted_iota(jnp.int32, (n, n), 1) % GROUP
     allowed = (place_q == place_k) & (order_k_ref[...] <= order_q_ref[...])
     bias = jnp.where(allowed, 0.0, MASKED)
+    items = []
     for g in range(groups):
         own = slice(g * n, (g + 1) * n)
         for pair in range(PAIRS):
             at = slice(pair * WIDE, (pair + 1) * WIDE)
-            ctx_ref[own, at] = pair_attention(q_ref[own, at], k_ref[own, at], v_ref[own, at], bias)
+            items.append((reader(q_ref, own, at), reader(k_ref, own, at), reader(v_ref, own, at), lambda: bias,
+                          ctx_ref, (own, at)))
+    for i in range(0, len(items), TEMPORAL_STAGE):
+        staged_attention(items[i:i + TEMPORAL_STAGE])
     core = core_ref[0]
     here = core_ref[1]
     half = D // 2
@@ -299,21 +317,18 @@
 
     arrived = exchange(clip_tokens.reshape(tm, frames, rows, cols, D), "tm")
     cot = cotangent.reshape(frames, rows, wide, D).swapaxes(0, 1)
-    tok, *parts = norm_reorder(arrived, spatial_gain)
+    tok, low, high = norm_reorder(arrived, spatial_gain)
     up = [(i, i + 1) for i in range(space - 1)]
     down = [(j, i) for i, j in up]
     edge = HALO * wide
-    halos = []
-    for f in range(frames):
-        above = lax.ppermute(parts[2 * f + 1], "space", up)
-        below = lax.ppermute(parts[2 * f], "space", down)
-        halos.append((above.reshape(edge, D), below.reshape(edge, D)))
-    qkv = qkv_own([p.reshape(edge, D) for p in parts], spatial_heads)
+    above = lax.ppermute(high, "space", up)
+    below = lax.ppermute(low, "space", down)
+    qkv = qkv_own(low.reshape(frames, edge, D), high.reshape(frames, edge, D), spatial_heads)
     cot, qkv = lax.optimization_barrier((cot, qkv))
     cot = exchange(cot, "tm")
     here = lax.axis_index("space").astype(jnp.int32)
     info = jnp.concatenate([row_reach.reshape(frames), here.reshape(1)])
-    middle = spatial_phase(info, qkv, halos, tok, spatial_heads, spatial_merge, rows * space)
+    middle = spatial_phase(info, above, below, qkv, tok, spatial_heads, spatial_merge, rows * space)
     mid = exchange(middle, "tm").reshape(frame_count, wide, D)
     core = jnp.stack([lax.axis_index("batch") & 1, here]).astype(jnp.int32)
     out, send, keep = temporal_phase(

time: 147 us -> 141 us (0.959)
  waiting for transfers between devices: 45.2 us -> 55.4 us
  Pallas kernels: 41.7 us -> 32.4 us
  starting transfers between devices: 41.4 us -> 35.5 us
    ppermute x4 -> x2, waiting for transfers between devices: 1.2 us -> 12.4 us  [the longest x1 8.27 us: per_device(): above = lax.ppermute(high, 'space', up)]
    pallas_call x4 -> x3, Pallas kernels: 27.4 us -> 20.8 us  [the longest x1 11.6 us: spatial_phase(): pl.pallas_call(functools.partial(spatial_kernel, rows=rows, all_rows=all_...]
    ppermute x4 -> x2, starting transfers between devices: 10.5 us -> 4.87 us  [the longest x1 3.57 us: per_device(): above = lax.ppermute(high, 'space', up)]
    pallas_call x1, Pallas kernels: 14.3 us -> 11.7 us  [temporal_phase(): pl.pallas_call(temporal_kernel, in_specs=[SMEM] + [VMEM] * 4 + [HBM] * 3,...]
    ppermute x3, waiting for transfers between devices: 14.1 us -> 12.6 us  [per_device(): lax.ppermute(chip[k].astype(BF), 'space', [(i, (i + k) % space) for i in...]
  transfers between devices with their start and end apart: 13 -> 11, of which waited for: 6 -> 8; matrix products, arithmetic and copies ran while one was open for 5% -> 5% of each run, Pallas kernels for 13% -> 8%
where the time goes in v3:
time: 141 us
  waiting for transfers between devices  55.4 us (39%)
  starting transfers between devices  35.5 us (25%)
  Pallas kernels  32.4 us (23%)
  blocking collectives  8.87 us (6%)
  local copies, waits for them, and re-layouts  4.28 us (3%)
  other arithmetic  3.41 us (2%)
    all_to_all x5, waiting for transfers between devices, per_device(): lax.all_to_all(v, axis, split_axis=0, concat_axis=0, tiled=True)  30.3 us
    all_to_all x5, starting transfers between devices, per_device(): lax.all_to_all(v, axis, split_axis=0, concat_axis=0, tiled=True)  22.8 us
    ppermute x3, waiting for transfers between devices, per_device(): lax.ppermute(chip[k].astype(BF), 'space', [(i, (i + k) % space) for i in...  12.6 us
    pallas_call x1, Pallas kernels, temporal_phase(): pl.pallas_call(temporal_kernel, in_specs=[SMEM] + [VMEM] * 4 + [HBM] * 3,...  11.7 us
    pallas_call x1, Pallas kernels, spatial_phase(): pl.pallas_call(functools.partial(spatial_kernel, rows=rows, all_rows=all_...  11.6 us
    all_gather x1, blocking collectives, per_device(): lax.all_gather(over_tm, 'batch').astype(F32)  8.87 us
    ppermute x1, waiting for transfers between devices, per_device(): above = lax.ppermute(high, 'space', up)  8.27 us
    pallas_call x1, Pallas kernels, qkv_own(): pl.pallas_call(qkv_kernel, in_specs=[VMEM, VMEM, HBM], out_specs=HBM, out...  6.39 us
  transfers between devices with their start and end apart: 11, of which 8 were waited for; matrix products, arithmetic and copies ran while one was open for 5% of the time, Pallas kernels for 8%

profile of v3, /device:TPU:1, one launch (start us, length us, event | category | flops | bytes accessed | tf_op | source)
XLA Modules:
  0.0 140.7 jit_solution(13530882823250166123)
XLA Ops:
  0.6 0.0 copy-start.1
  0.6 5.9 %all-to-all-start = ((bf16[8,2,8,4,1024]{4,3,2,1,0:T(4,128)(2,1)}), bf16[8,2,8,4,1024]{4,3,2,1,0:T(4,128)(2,1)S(1)}, u32[]{:S(2)}, u32[]{:S(2)}) async-start(bf16[8,2,8,4,1024]{4,3,2,1,0:T(4,128)(2,1)} %bitcast.46), calls=%async_computation | async-start | bytes 2097152 | tf_op jit(solution)/shard_map/all_to_all | solution.py:316
  6.5 2.3 %copy.30 = bf16[1,2,8,32,1024]{4,3,1,2,0:T(8,128)(2,1)} copy(bf16[1,2,8,32,1024]{4,3,2,1,0:T(8,128)(2,1)} %param.19) | data formatting | bytes 2097152 | tf_op args[9]
  8.8 13.0 %all-to-all-done.x_ref = bf16[8,2,8,4,1024]{4,3,2,1,0:T(4,128)(2,1)S(1)} async-done(((bf16[8,2,8,4,1024]{4,3,2,1,0:T(4,128)(2,1)}), bf16[8,2,8,4,1024]{4,3,2,1,0:T(4,128)(2,1)S(1)}, u32[]{:S(2)}, u32[]{:S(2)}) %all-to-all-start) | async-done | bytes 1048608 | tf_op jit(solution)/shard_map/all_to_all | solution.py:316
  21.8 0.0 copy-done.1
  21.8 2.8 %norm_reorder.1 = (bf16[2,8,32,1024]{3,2,1,0:T(8,128)(2,1)}, bf16[2,4,32,1024]{3,2,1,0:T(8,128)(2,1)S(1)}, bf16[2,4,32,1024]{3,2,1,0:T(8,128)(2,1)S(1)}) custom-call(bf16[8,2,8,4,1024]{4,3,2,1,0:T(4,128)(2,1)S(1)} %all-to-all-done.x_ref, f32[1,1024]{1,0:T(1,128)S(1)} %bitcast.43), custom_call_target="tpu_custom_call" | custom-call | tf_op jit(solution)/shard_map/norm_reorder/pallas_call | solution.py:65
  24.6 0.0 copy-start.4
  24.6 6.4 %qkv_own.1.qkv_ref = bf16[3,512,1024]{2,1,0:T(8,128)(2,1)} custom-call(bf16[2,128,1024]{2,1,0:T(8,128)(2,1)S(1)} %bitcast.40, bf16[2,128,1024]{2,1,0:T(8,128)(2,1)S(1)} %bitcast.41, bf16[1024,3072]{1,0:T(8,128)(2,1)} %w_ref.4), custom_call_target="tpu_custom_call" | custom-call | tf_op jit(solution)/shard_map/qkv_own/pallas_call | solution.py:100
  31.0 3.6 %all-to-all-start.2 = ((bf16[8,2,32,1024]{3,2,1,0:T(8,128)(2,1)}), bf16[8,2,32,1024]{3,2,1,0:T(8,128)(2,1)S(1)}, u32[]{:S(2)}, u32[]{:S(2)}) async-start(bf16[8,2,32,1024]{3,2,1,0:T(8,128)(2,1)} %bitcast.38), calls=%async_computation.2 | async-start | bytes 2097152 | tf_op jit(solution)/shard_map/all_to_all | solution.py:316
  34.6 3.6 %collective-permute-start = (bf16[2,4,32,1024]{3,2,1,0:T(8,128)(2,1)S(1)}, bf16[2,4,32,1024]{3,2,1,0:T(8,128)(2,1)S(1)}, u32[]{:S(2)}, u32[]{:S(2)}) collective-permute-start(bf16[2,4,32,1024]{3,2,1,0:T(8,128)(2,1)S(1)} %get-tuple-element.10), channel_id=1, source_target_pairs={{0,1},{1,2},{2,3},{4,5},{5,6},{6,7},{8,9},{9,10},{10,11},{12,13},{... | collective-permute-start | bytes 1572872 | tf_op jit(solution)/shard_map/ppermute | solution.py:324
  38.1 1.3 collective-permute-start.1
  39.5 0.0 copy-done.4
  39.5 0.1 pad_add_fusion.1.info_ref
  39.5 8.3 %collective-permute-done.up_ref = bf16[2,4,32,1024]{3,2,1,0:T(8,128)(2,1)S(1)} collective-permute-done((bf16[2,4,32,1024]{3,2,1,0:T(8,128)(2,1)S(1)}, bf16[2,4,32,1024]{3,2,1,0:T(8,128)(2,1)S(1)}, u32[]{:S(2)}, u32[]{:S(2)}) %collective-permute-start) | collective-permute-done | bytes 524320 | tf_op jit(solution)/shard_map/ppermute | solution.py:324
  47.8 4.2 %collective-permute-done.1.down_ref = bf16[2,4,32,1024]{3,2,1,0:T(8,128)(2,1)S(1)} collective-permute-done((bf16[2,4,32,1024]{3,2,1,0:T(8,128)(2,1)S(1)}, bf16[2,4,32,1024]{3,2,1,0:T(8,128)(2,1)S(1)}, u32[]{:S(2)}, u32[]{:S(2)}) %collective-permute-start.1) | collective-permute-done | bytes 524320 | tf_op jit(solution)/shard_map/ppermute | solution.py:325
  52.0 0.0 copy-start.3
  52.0 0.0 copy-start
  52.0 11.6 %spatial_phase.1 = bf16[8,2,32,1024]{3,2,1,0:T(8,128)(2,1)} custom-call(s32[3]{0:T(128)S(1)} %pad_add_fusion.1.info_ref, bf16[2,4,32,1024]{3,2,1,0:T(8,128)(2,1)S(1)} %collective-permute-done.up_ref, bf16[2,4,32,1024]{3,2,1,0:T(8,128)(2,1)S(1)} %collective-permute-done.1.down_ref, bf16[3,512,1024]{2,1,0:T(8,128)(2,1)} %qkv_own.1.qkv_ref, ...), custom_call_target="tpu_custom_call" | custom-call | tf_op jit(solution)/shard_map/spatial_phase/pallas_call | solution.py:201
  63.6 0.0 all-to-all-done.2
  63.6 0.0 copy-start.2
  63.6 4.8 %all-to-all-start.1 = ((bf16[8,2,32,1024]{3,2,1,0:T(8,128)(2,1)}), bf16[8,2,32,1024]{3,2,1,0:T(8,128)(2,1)S(1)}, u32[]{:S(2)}, u32[]{:S(2)}) async-start(bf16[8,2,32,1024]{3,2,1,0:T(8,128)(2,1)} %spatial_phase.1), calls=%async_computation.1 | async-start | bytes 2097152 | tf_op jit(solution)/shard_map/all_to_all | solution.py:316
  68.4 0.0 copy-done.3
  68.4 0.1 broadcast_in_dim.3
  68.5 0.1 reshape_reshape.8.order_q_ref
  68.6 0.1 reshape_reshape.7.order_k_ref
  68.7 0.1 pad_add_fusion.core_ref
  68.7 12.4 %all-to-all-done.1 = bf16[8,2,32,1024]{3,2,1,0:T(8,128)(2,1)S(1)} async-done(((bf16[8,2,32,1024]{3,2,1,0:T(8,128)(2,1)}), bf16[8,2,32,1024]{3,2,1,0:T(8,128)(2,1)S(1)}, u32[]{:S(2)}, u32[]{:S(2)}) %all-to-all-start.1) | async-done | bytes 1048608 | tf_op jit(solution)/shard_map/all_to_all | solution.py:316
  81.2 0.0 copy-done.2
  81.2 0.0 copy-done
  81.2 11.7 %temporal_phase.1 = (bf16[16,32,1024]{2,1,0:T(8,128)(2,1)}, bf16[4,8,32,512]{3,2,1,0:T(8,128)(2,1)S(1)}, bf16[4,8,32,512]{3,2,1,0:T(8,128)(2,1)}) custom-call(s32[2]{0:T(128)S(1)} %pad_add_fusion.core_ref, bf16[16,32,1024]{2,1,0:T(8,128)(2,1)S(1)} %bitcast.39, s32[128,1]{1,0:T(8,128)S(1)} %reshape_reshape.8.order_q_ref, ...), custom_call_target="tpu_custom_call" | custom-call | tf_op jit(solution)/shard_map/temporal_phase/pallas_call | solution.py:286
  92.9 4.0 %collective-permute-start.2 = (bf16[4,8,32,512]{3,2,1,0:T(8,128)(2,1)S(1)}, bf16[4,8,32,512]{3,2,1,0:T(8,128)(2,1)S(1)}, u32[]{:S(2)}, u32[]{:S(2)}) collective-permute-start(bf16[4,8,32,512]{3,2,1,0:T(8,128)(2,1)S(1)} %get-tuple-element.17), channel_id=1, source_target_pairs={{0,32},{32,0},{64,96},{96,64},{1,33},{33,1},{65,97},{97,65},{2,34}... | collective-permute-start | bytes 3145736 | tf_op jit(solution)/shard_map/ppermute | solution.py:339
  96.8 3.6 %all-to-all-start.3 = ((bf16[8,2,32,1024]{3,2,1,0:T(8,128)(2,1)}), bf16[8,2,32,1024]{3,2,1,0:T(8,128)(2,1)S(1)}, u32[]{:S(2)}, u32[]{:S(2)}) async-start(bf16[8,2,32,1024]{3,2,1,0:T(8,128)(2,1)} %bitcast.47), calls=%async_computation.3 | async-start | bytes 2097152 | tf_op jit(solution)/shard_map/all_to_all | solution.py:316
  100.4 0.0 collective-permute-done.2
  100.4 1.4 fusion.3
  101.8 1.1 collective-permute-start.5
  102.9 2.0 %collective-permute-start.4 = (bf16[8,32,512]{2,1,0:T(8,128)(2,1)S(1)}, bf16[8,32,512]{2,1,0:T(8,128)(2,1)S(1)}, u32[]{:S(2)}, u32[]{:S(2)}) collective-permute-start(bf16[8,32,512]{2,1,0:T(8,128)(2,1)S(1)} %get-tuple-element.26), channel_id=1, source_target_pairs={{0,2},{1,3},{2,0},{3,1},{4,6},{5,7},{6,4},{7,5},{8,10},{9,11},{10,... | collective-permute-start | bytes 786440 | tf_op jit(solution)/shard_map/ppermute | solution.py:343
  104.9 0.7 collective-permute-start.3
  105.6 4.0 %collective-permute-done.5 = bf16[8,32,512]{2,1,0:T(8,128)(2,1)S(1)} collective-permute-done((bf16[8,32,512]{2,1,0:T(8,128)(2,1)S(1)}, bf16[8,32,512]{2,1,0:T(8,128)(2,1)S(1)}, u32[]{:S(2)}, u32[]{:S(2)}) %collective-permute-start.5) | collective-permute-done | bytes 262176 | tf_op jit(solution)/shard_map/ppermute | solution.py:343
  109.7 2.3 %collective-permute-done.4 = bf16[8,32,512]{2,1,0:T(8,128)(2,1)S(1)} collective-permute-done((bf16[8,32,512]{2,1,0:T(8,128)(2,1)S(1)}, bf16[8,32,512]{2,1,0:T(8,128)(2,1)S(1)}, u32[]{:S(2)}, u32[]{:S(2)}) %collective-permute-start.4) | collective-permute-done | bytes 262176 | tf_op jit(solution)/shard_map/ppermute | solution.py:343
  112.0 6.2 %collective-permute-done.3 = bf16[8,32,512]{2,1,0:T(8,128)(2,1)S(1)} collective-permute-done((bf16[8,32,512]{2,1,0:T(8,128)(2,1)S(1)}, bf16[8,32,512]{2,1,0:T(8,128)(2,1)S(1)}, u32[]{:S(2)}, u32[]{:S(2)}) %collective-permute-start.3) | collective-permute-done | bytes 262176 | tf_op jit(solution)/shard_map/ppermute | solution.py:343
  118.2 1.8 %fusion.2 = bf16[8,32,512]{2,1,0:T(8,128)(2,1)} fusion(bf16[8,32,512]{2,1,0:T(8,128)(2,1)S(1)} %collective-permute-done.5, bf16[8,32,512]{2,1,0:T(8,128)(2,1)S(1)} %collective-permute-done.4, bf16[8,32,512]{2,1,0:T(8,128)(2,1)S(1)} %collective-permute-done.3, bf16[4,8,32,512]{3,2,1,0:T(8,128)(2,1)S(1)} %collective-permute-done.2, ...), kind=kLoop, calls=%fused_computation.4 | loop fusion | flops 1310720 | bytes 1572864 | tf_op jit(solution)/shard_map/convert_element_type | solution.py:347
  120.1 0.0 all-to-all-done.3
  120.1 5.1 %all-to-all-start.4 = ((bf16[8,32,512]{2,1,0:T(8,128)(2,1)}), bf16[8,32,512]{2,1,0:T(8,128)(2,1)S(1)}, u32[]{:S(2)}, u32[]{:S(2)}) async-start(bf16[8,32,512]{2,1,0:T(8,128)(2,1)} %fusion.2), calls=%async_computation.4 | async-start | bytes 524288 | tf_op jit(solution)/shard_map/all_to_all | solution.py:316
  125.1 1.1 copy.27
  126.2 4.9 %all-to-all-done.4 = bf16[8,32,512]{2,1,0:T(8,128)(2,1)S(1)} async-done(((bf16[8,32,512]{2,1,0:T(8,128)(2,1)}), bf16[8,32,512]{2,1,0:T(8,128)(2,1)S(1)}, u32[]{:S(2)}, u32[]{:S(2)}) %all-to-all-start.4) | async-done | bytes 262176 | tf_op jit(solution)/shard_map/all_to_all | solution.py:316
  131.1 8.9 %all-gather = bf16[128,512]{1,0:T(8,128)(2,1)S(1)} all-gather(bf16[32,512]{1,0:T(8,128)(2,1)S(1)} %reduce_sum.21), channel_id=2, replica_groups=mesh['batch'=4,'tm'=8,'space'=4] {'batch'}, dimensions={0}, use_global_device_ids=true | all-gather | bytes 163840 | tf_op jit(solution)/shard_map/all_gather | solution.py:351
  140.0 0.7 copy.28
  (2 shorter events, 0.1 us)
Async XLA Ops:
  0.6 21.2 %copy-start.1 = (f32[1024]{0:T(1024)S(1)}, f32[1024]{0:T(1024)}, u32[]{:S(2)}) copy-start(f32[1024]{0:T(1024)} %param.13) | copy-start | bytes 12292
  0.6 21.2 %all-to-all-start = ((bf16[8,2,8,4,1024]{4,3,2,1,0:T(4,128)(2,1)}), bf16[8,2,8,4,1024]{4,3,2,1,0:T(4,128)(2,1)S(1)}, u32[]{:S(2)}, u32[]{:S(2)}) async-start(bf16[8,2,8,4,1024]{4,3,2,1,0:T(4,128)(2,1)} %bitcast.46), calls=%async_computation | async-start | bytes 2097152 | tf_op jit(solution)/shard_map/all_to_all | solution.py:316
  24.6 14.9 %copy-start.4 = (s32[1,2]{1,0:T(1,128)S(1)}, s32[1,2]{1,0:T(1,128)}, u32[]{:S(2)}) copy-start(s32[1,2]{1,0:T(1,128)} %param.12) | copy-start | bytes 28
  31.0 32.6 %all-to-all-start.2 = ((bf16[8,2,32,1024]{3,2,1,0:T(8,128)(2,1)}), bf16[8,2,32,1024]{3,2,1,0:T(8,128)(2,1)S(1)}, u32[]{:S(2)}, u32[]{:S(2)}) async-start(bf16[8,2,32,1024]{3,2,1,0:T(8,128)(2,1)} %bitcast.38), calls=%async_computation.2 | async-start | bytes 2097152 | tf_op jit(solution)/shard_map/all_to_all | solution.py:316
  34.6 13.2 %collective-permute-start = (bf16[2,4,32,1024]{3,2,1,0:T(8,128)(2,1)S(1)}, bf16[2,4,32,1024]{3,2,1,0:T(8,128)(2,1)S(1)}, u32[]{:S(2)}, u32[]{:S(2)}) collective-permute-start(bf16[2,4,32,1024]{3,2,1,0:T(8,128)(2,1)S(1)} %get-tuple-element.10), channel_id=1, source_target_pairs={{0,1},{1,2},{2,3},{4,5},{5,6},{6,7},{8,9},{9,10},{10,11},{12,13},{... | collective-permute-start | bytes 1572872 | tf_op jit(solution)/shard_map/ppermute | solution.py:324
  38.1 13.8 %collective-permute-start.1 = (bf16[2,4,32,1024]{3,2,1,0:T(8,128)(2,1)S(1)}, bf16[2,4,32,1024]{3,2,1,0:T(8,128)(2,1)S(1)}, u32[]{:S(2)}, u32[]{:S(2)}) collective-permute-start(bf16[2,4,32,1024]{3,2,1,0:T(8,128)(2,1)S(1)} %get-tuple-element.11), channel_id=1, source_target_pairs={{1,0},{2,1},{3,2},{5,4},{6,5},{7,6},{9,8},{10,9},{11,10},{13,12},{... | collective-permute-start | bytes 1572872 | tf_op jit(solution)/shard_map/ppermute | solution.py:325
  52.0 16.4 %copy-start.3 = (s32[1,16]{1,0:T(1,128)S(1)}, s32[1,16]{1,0:T(1,128)}, u32[]{:S(2)}) copy-start(s32[1,16]{1,0:T(1,128)} %param.11) | copy-start | bytes 196
  52.0 29.2 %copy-start = (f32[1024]{0:T(1024)S(1)}, f32[1024]{0:T(1024)}, u32[]{:S(2)}) copy-start(f32[1024]{0:T(1024)} %param.16) | copy-start | bytes 12292
  63.6 17.6 %copy-start.2 = (bf16[8,2,32,1024]{3,2,1,0:T(8,128)(2,1)}, bf16[8,2,32,1024]{3,2,1,0:T(8,128)(2,1)S(1)}, u32[]{:S(2)}) copy-start(bf16[8,2,32,1024]{3,2,1,0:T(8,128)(2,1)S(1)} %all-to-all-done.2) | copy-start | bytes 3145732
  63.6 17.6 %all-to-all-start.1 = ((bf16[8,2,32,1024]{3,2,1,0:T(8,128)(2,1)}), bf16[8,2,32,1024]{3,2,1,0:T(8,128)(2,1)S(1)}, u32[]{:S(2)}, u32[]{:S(2)}) async-start(bf16[8,2,32,1024]{3,2,1,0:T(8,128)(2,1)} %spatial_phase.1), calls=%async_computation.1 | async-start | bytes 2097152 | tf_op jit(solution)/shard_map/all_to_all | solution.py:316
  92.9 7.5 %collective-permute-start.2 = (bf16[4,8,32,512]{3,2,1,0:T(8,128)(2,1)S(1)}, bf16[4,8,32,512]{3,2,1,0:T(8,128)(2,1)S(1)}, u32[]{:S(2)}, u32[]{:S(2)}) collective-permute-start(bf16[4,8,32,512]{3,2,1,0:T(8,128)(2,1)S(1)} %get-tuple-element.17), channel_id=1, source_target_pairs={{0,32},{32,0},{64,96},{96,64},{1,33},{33,1},{65,97},{97,65},{2,34}... | collective-permute-start | bytes 3145736 | tf_op jit(solution)/shard_map/ppermute | solution.py:339
  96.8 23.2 %all-to-all-start.3 = ((bf16[8,2,32,1024]{3,2,1,0:T(8,128)(2,1)}), bf16[8,2,32,1024]{3,2,1,0:T(8,128)(2,1)S(1)}, u32[]{:S(2)}, u32[]{:S(2)}) async-start(bf16[8,2,32,1024]{3,2,1,0:T(8,128)(2,1)} %bitcast.47), calls=%async_computation.3 | async-start | bytes 2097152 | tf_op jit(solution)/shard_map/all_to_all | solution.py:316
  101.8 7.9 %collective-permute-start.5 = (bf16[8,32,512]{2,1,0:T(8,128)(2,1)S(1)}, bf16[8,32,512]{2,1,0:T(8,128)(2,1)S(1)}, u32[]{:S(2)}, u32[]{:S(2)}) collective-permute-start(bf16[8,32,512]{2,1,0:T(8,128)(2,1)S(1)} %get-tuple-element.25), channel_id=1, source_target_pairs={{0,3},{1,0},{2,1},{3,2},{4,7},{5,4},{6,5},{7,6},{8,11},{9,8},{10,9... | collective-permute-start | bytes 786440 | tf_op jit(solution)/shard_map/ppermute | solution.py:343
  102.9 9.1 %collective-permute-start.4 = (bf16[8,32,512]{2,1,0:T(8,128)(2,1)S(1)}, bf16[8,32,512]{2,1,0:T(8,128)(2,1)S(1)}, u32[]{:S(2)}, u32[]{:S(2)}) collective-permute-start(bf16[8,32,512]{2,1,0:T(8,128)(2,1)S(1)} %get-tuple-element.26), channel_id=1, source_target_pairs={{0,2},{1,3},{2,0},{3,1},{4,6},{5,7},{6,4},{7,5},{8,10},{9,11},{10,... | collective-permute-start | bytes 786440 | tf_op jit(solution)/shard_map/ppermute | solution.py:343
  104.9 13.3 %collective-permute-start.3 = (bf16[8,32,512]{2,1,0:T(8,128)(2,1)S(1)}, bf16[8,32,512]{2,1,0:T(8,128)(2,1)S(1)}, u32[]{:S(2)}, u32[]{:S(2)}) collective-permute-start(bf16[8,32,512]{2,1,0:T(8,128)(2,1)S(1)} %get-tuple-element.24), channel_id=1, source_target_pairs={{0,1},{1,2},{2,3},{3,0},{4,5},{5,6},{6,7},{7,4},{8,9},{9,10},{10,1... | collective-permute-start | bytes 786440 | tf_op jit(solution)/shard_map/ppermute | solution.py:343
  120.1 11.0 %all-to-all-start.4 = ((bf16[8,32,512]{2,1,0:T(8,128)(2,1)}), bf16[8,32,512]{2,1,0:T(8,128)(2,1)S(1)}, u32[]{:S(2)}, u32[]{:S(2)}) async-start(bf16[8,32,512]{2,1,0:T(8,128)(2,1)} %fusion.2), calls=%async_computation.4 | async-start | bytes 524288 | tf_op jit(solution)/shard_map/all_to_all | solution.py:316

commit v4 on v3

--- a/solution.py
+++ b/solution.py
@@ -339,12 +339,19 @@
     got = lax.ppermute(send, "batch", [(i, i ^ 1) for i in range(batch)])
     output = exchange(out.reshape(tm, frames, wide, D), "tm").swapaxes(0, 1)
     chip = [keep[k].astype(F32) + got[k].astype(F32) for k in range(space)]
-    total = chip[0]
-    moved = [lax.ppermute(chip[k].astype(BF), "space", [(i, (i + k) % space) for i in range(space)])
-             for k in range(1, space)]
-    for part in moved:
-        total = total + part.astype(F32)
-    over_space = total.astype(BF)
+    middle_blocks = tm // 2
+    ahead = [(i, (i + 1) % space) for i in range(space)]
+    back = [(j, i) for i, j in ahead]
+    far = [(keep[2, at].astype(F32) + got[2, at].astype(F32)).astype(BF)
+           for at in (slice(0, middle_blocks), slice(middle_blocks, tm))]
+    via_before = lax.ppermute(far[0], "space", ahead)
+    via_after = lax.ppermute(far[1], "space", back)
+    none = jnp.zeros_like(via_before)
+    to_next = chip[1] + jnp.concatenate([via_before, none]).astype(F32)
+    to_last = chip[3] + jnp.concatenate([none, via_after]).astype(F32)
+    from_before = lax.ppermute(to_next.astype(BF), "space", ahead)
+    from_after = lax.ppermute(to_last.astype(BF), "space", back)
+    over_space = (chip[0] + from_before.astype(F32) + from_after.astype(F32)).astype(BF)
     over_tm = exchange(over_space, "tm")
     over_tm = over_tm.astype(F32).sum(0).astype(BF)
     block = over_tm.shape[0]

time: 141 us -> 143 us (1.014)
  blocking collectives: 8.87 us -> 10.9 us
  waiting for transfers between devices: 55.4 us -> 53.5 us
    all_gather x1, blocking collectives: 8.87 us -> 10.9 us  [per_device(): lax.all_gather(over_tm, 'batch').astype(F32)]
    ppermute x3 -> x4, waiting for transfers between devices: 12.6 us -> 10.9 us  [the longest x1 4.4 us: per_device(): from_after = lax.ppermute(to_last.astype(BF), 'space', back)]
    ppermute x3 -> x4, starting transfers between devices: 3.87 us -> 5.21 us  [the longest x1 2.46 us: per_device(): from_after = lax.ppermute(to_last.astype(BF), 'space', back)]
    convert_element_type x2 -> x3, other arithmetic: 3.2 us -> 4.18 us  [the longest x1 1.79 us: per_device(): (chip[0] + from_before.astype(F32) + from_after.astype(F32)).astype(BF)]
    unnamed x12 -> x14, local copies, waits for them, and re-layouts: 3.38 us -> 3.39 us
  transfers between devices with their start and end apart: 11 -> 12, of which waited for: 8 -> 8; matrix products, arithmetic and copies ran while one was open for 5% -> 6% of each run, Pallas kernels for 8% -> 8%
where the time goes in v4:
time: 143 us
  waiting for transfers between devices  53.5 us (37%)
  starting transfers between devices  36.3 us (25%)
  Pallas kernels  32.4 us (23%)
  blocking collectives  10.9 us (8%)
  other arithmetic  4.38 us (3%)
  local copies, waits for them, and re-layouts  4.29 us (3%)
    all_to_all x5, waiting for transfers between devices, per_device(): lax.all_to_all(v, axis, split_axis=0, concat_axis=0, tiled=True)  30.2 us
    all_to_all x5, starting transfers between devices, per_device(): lax.all_to_all(v, axis, split_axis=0, concat_axis=0, tiled=True)  22.3 us
    pallas_call x1, Pallas kernels, temporal_phase(): pl.pallas_call(temporal_kernel, in_specs=[SMEM] + [VMEM] * 4 + [HBM] * 3,...  11.7 us
    pallas_call x1, Pallas kernels, spatial_phase(): pl.pallas_call(functools.partial(spatial_kernel, rows=rows, all_rows=all_...  11.6 us
    all_gather x1, blocking collectives, per_device(): lax.all_gather(over_tm, 'batch').astype(F32)  10.9 us
    ppermute x1, waiting for transfers between devices, per_device(): above = lax.ppermute(high, 'space', up)  8.27 us
    pallas_call x1, Pallas kernels, qkv_own(): pl.pallas_call(qkv_kernel, in_specs=[VMEM, VMEM, HBM], out_specs=HBM, out...  6.39 us
    ppermute x1, waiting for transfers between devices, per_device(): from_after = lax.ppermute(to_last.astype(BF), 'space', back)  4.4 us
  transfers between devices with their start and end apart: 12, of which 8 were waited for; matrix products, arithmetic and copies ran while one was open for 6% of the time, Pallas kernels for 8%

profile of v4, /device:TPU:1, one launch (start us, length us, event | category | flops | bytes accessed | tf_op | source)
XLA Modules:
  0.0 142.7 jit_solution(16106181797193144827)
XLA Ops:
  0.6 0.0 copy-start.1
  0.6 5.9 %all-to-all-start = ((bf16[8,2,8,4,1024]{4,3,2,1,0:T(4,128)(2,1)}), bf16[8,2,8,4,1024]{4,3,2,1,0:T(4,128)(2,1)S(1)}, u32[]{:S(2)}, u32[]{:S(2)}) async-start(bf16[8,2,8,4,1024]{4,3,2,1,0:T(4,128)(2,1)} %bitcast.50), calls=%async_computation | async-start | bytes 2097152 | tf_op jit(solution)/shard_map/all_to_all | solution.py:316
  6.5 2.3 %copy.30 = bf16[1,2,8,32,1024]{4,3,1,2,0:T(8,128)(2,1)} copy(bf16[1,2,8,32,1024]{4,3,2,1,0:T(8,128)(2,1)} %param.19) | data formatting | bytes 2097152 | tf_op args[9]
  8.8 13.0 %all-to-all-done.x_ref = bf16[8,2,8,4,1024]{4,3,2,1,0:T(4,128)(2,1)S(1)} async-done(((bf16[8,2,8,4,1024]{4,3,2,1,0:T(4,128)(2,1)}), bf16[8,2,8,4,1024]{4,3,2,1,0:T(4,128)(2,1)S(1)}, u32[]{:S(2)}, u32[]{:S(2)}) %all-to-all-start) | async-done | bytes 1048608 | tf_op jit(solution)/shard_map/all_to_all | solution.py:316
  21.8 0.0 copy-done.1
  21.8 2.8 %norm_reorder.1 = (bf16[2,8,32,1024]{3,2,1,0:T(8,128)(2,1)}, bf16[2,4,32,1024]{3,2,1,0:T(8,128)(2,1)S(1)}, bf16[2,4,32,1024]{3,2,1,0:T(8,128)(2,1)S(1)}) custom-call(bf16[8,2,8,4,1024]{4,3,2,1,0:T(4,128)(2,1)S(1)} %all-to-all-done.x_ref, f32[1,1024]{1,0:T(1,128)S(1)} %bitcast.47), custom_call_target="tpu_custom_call" | custom-call | tf_op jit(solution)/shard_map/norm_reorder/pallas_call | solution.py:65
  24.6 0.0 copy-start.5
  24.6 6.4 %qkv_own.1.qkv_ref = bf16[3,512,1024]{2,1,0:T(8,128)(2,1)} custom-call(bf16[2,128,1024]{2,1,0:T(8,128)(2,1)S(1)} %bitcast.44, bf16[2,128,1024]{2,1,0:T(8,128)(2,1)S(1)} %bitcast.45, bf16[1024,3072]{1,0:T(8,128)(2,1)} %w_ref.4), custom_call_target="tpu_custom_call" | custom-call | tf_op jit(solution)/shard_map/qkv_own/pallas_call | solution.py:100
  31.0 3.6 %all-to-all-start.2 = ((bf16[8,2,32,1024]{3,2,1,0:T(8,128)(2,1)}), bf16[8,2,32,1024]{3,2,1,0:T(8,128)(2,1)S(1)}, u32[]{:S(2)}, u32[]{:S(2)}) async-start(bf16[8,2,32,1024]{3,2,1,0:T(8,128)(2,1)} %bitcast.42), calls=%async_computation.2 | async-start | bytes 2097152 | tf_op jit(solution)/shard_map/all_to_all | solution.py:316
  34.6 3.6 %collective-permute-start = (bf16[2,4,32,1024]{3,2,1,0:T(8,128)(2,1)S(1)}, bf16[2,4,32,1024]{3,2,1,0:T(8,128)(2,1)S(1)}, u32[]{:S(2)}, u32[]{:S(2)}) collective-permute-start(bf16[2,4,32,1024]{3,2,1,0:T(8,128)(2,1)S(1)} %get-tuple-element.10), channel_id=1, source_target_pairs={{0,1},{1,2},{2,3},{4,5},{5,6},{6,7},{8,9},{9,10},{10,11},{12,13},{... | collective-permute-start | bytes 1572872 | tf_op jit(solution)/shard_map/ppermute | solution.py:324
  38.2 1.3 collective-permute-start.1
  39.5 0.0 copy-done.5
  39.5 0.1 pad_add_fusion.1.info_ref
  39.5 8.3 %collective-permute-done.up_ref = bf16[2,4,32,1024]{3,2,1,0:T(8,128)(2,1)S(1)} collective-permute-done((bf16[2,4,32,1024]{3,2,1,0:T(8,128)(2,1)S(1)}, bf16[2,4,32,1024]{3,2,1,0:T(8,128)(2,1)S(1)}, u32[]{:S(2)}, u32[]{:S(2)}) %collective-permute-start) | collective-permute-done | bytes 524320 | tf_op jit(solution)/shard_map/ppermute | solution.py:324
  47.8 4.2 %collective-permute-done.1.down_ref = bf16[2,4,32,1024]{3,2,1,0:T(8,128)(2,1)S(1)} collective-permute-done((bf16[2,4,32,1024]{3,2,1,0:T(8,128)(2,1)S(1)}, bf16[2,4,32,1024]{3,2,1,0:T(8,128)(2,1)S(1)}, u32[]{:S(2)}, u32[]{:S(2)}) %collective-permute-start.1) | collective-permute-done | bytes 524320 | tf_op jit(solution)/shard_map/ppermute | solution.py:325
  52.0 11.6 %spatial_phase.1 = bf16[8,2,32,1024]{3,2,1,0:T(8,128)(2,1)} custom-call(s32[3]{0:T(128)S(1)} %pad_add_fusion.1.info_ref, bf16[2,4,32,1024]{3,2,1,0:T(8,128)(2,1)S(1)} %collective-permute-done.up_ref, bf16[2,4,32,1024]{3,2,1,0:T(8,128)(2,1)S(1)} %collective-permute-done.1.down_ref, bf16[3,512,1024]{2,1,0:T(8,128)(2,1)} %qkv_own.1.qkv_ref, ...), custom_call_target="tpu_custom_call" | custom-call | tf_op jit(solution)/shard_map/spatial_phase/pallas_call | solution.py:201
  63.6 0.0 all-to-all-done.2
  63.6 0.0 copy-start.2
  63.6 4.8 %all-to-all-start.1 = ((bf16[8,2,32,1024]{3,2,1,0:T(8,128)(2,1)}), bf16[8,2,32,1024]{3,2,1,0:T(8,128)(2,1)S(1)}, u32[]{:S(2)}, u32[]{:S(2)}) async-start(bf16[8,2,32,1024]{3,2,1,0:T(8,128)(2,1)} %spatial_phase.1), calls=%async_computation.1 | async-start | bytes 2097152 | tf_op jit(solution)/shard_map/all_to_all | solution.py:316
  68.4 0.0 copy-done.4
  68.4 0.1 broadcast_in_dim.4
  68.5 0.1 reshape_reshape.8.order_q_ref
  68.6 0.1 reshape_reshape.7.order_k_ref
  68.7 0.1 pad_add_fusion.core_ref
  68.7 12.4 %all-to-all-done.1 = bf16[8,2,32,1024]{3,2,1,0:T(8,128)(2,1)S(1)} async-done(((bf16[8,2,32,1024]{3,2,1,0:T(8,128)(2,1)}), bf16[8,2,32,1024]{3,2,1,0:T(8,128)(2,1)S(1)}, u32[]{:S(2)}, u32[]{:S(2)}) %all-to-all-start.1) | async-done | bytes 1048608 | tf_op jit(solution)/shard_map/all_to_all | solution.py:316
  81.2 0.0 copy-done
  81.2 11.7 %temporal_phase.1 = (bf16[16,32,1024]{2,1,0:T(8,128)(2,1)}, bf16[4,8,32,512]{3,2,1,0:T(8,128)(2,1)S(1)}, bf16[4,8,32,512]{3,2,1,0:T(8,128)(2,1)}) custom-call(s32[2]{0:T(128)S(1)} %pad_add_fusion.core_ref, bf16[16,32,1024]{2,1,0:T(8,128)(2,1)S(1)} %bitcast.43, s32[128,1]{1,0:T(8,128)S(1)} %reshape_reshape.8.order_q_ref, ...), custom_call_target="tpu_custom_call" | custom-call | tf_op jit(solution)/shard_map/temporal_phase/pallas_call | solution.py:286
  92.9 4.0 %collective-permute-start.2 = (bf16[4,8,32,512]{3,2,1,0:T(8,128)(2,1)S(1)}, bf16[4,8,32,512]{3,2,1,0:T(8,128)(2,1)}, u32[]{:S(2)}, u32[]{:S(2)}) collective-permute-start(bf16[4,8,32,512]{3,2,1,0:T(8,128)(2,1)S(1)} %get-tuple-element.17), channel_id=1, source_target_pairs={{0,32},{32,0},{64,96},{96,64},{1,33},{33,1},{65,97},{97,65},{2,34}... | collective-permute-start | bytes 3145736 | tf_op jit(solution)/shard_map/ppermute | solution.py:339
  96.9 3.6 %all-to-all-start.3 = ((bf16[8,2,32,1024]{3,2,1,0:T(8,128)(2,1)}), bf16[8,2,32,1024]{3,2,1,0:T(8,128)(2,1)S(1)}, u32[]{:S(2)}, u32[]{:S(2)}) async-start(bf16[8,2,32,1024]{3,2,1,0:T(8,128)(2,1)} %bitcast.51), calls=%async_computation.3 | async-start | bytes 2097152 | tf_op jit(solution)/shard_map/all_to_all | solution.py:316
  100.4 0.0 collective-permute-done.2
  100.4 1.2 fusion.4
  101.6 1.3 collective-permute-start.3
  102.9 1.4 collective-permute-start.5
  104.3 3.4 %collective-permute-done.3 = bf16[4,32,512]{2,1,0:T(8,128)(2,1)S(1)} collective-permute-done((bf16[4,32,512]{2,1,0:T(8,128)(2,1)S(1)}, bf16[4,32,512]{2,1,0:T(8,128)(2,1)S(1)}, u32[]{:S(2)}, u32[]{:S(2)}) %collective-permute-start.3) | collective-permute-done | bytes 131104 | tf_op jit(solution)/shard_map/ppermute | solution.py:347
  107.8 0.0 collective-permute-done.5
  107.8 0.0 copy-done.3
  107.8 1.2 fusion.1
  109.0 2.5 %collective-permute-start.6 = (bf16[8,32,512]{2,1,0:T(8,128)(2,1)S(1)}, bf16[8,32,512]{2,1,0:T(8,128)(2,1)S(1)}, u32[]{:S(2)}, u32[]{:S(2)}) collective-permute-start(bf16[8,32,512]{2,1,0:T(8,128)(2,1)S(1)} %get-tuple-element.25), channel_id=1, source_target_pairs={{1,0},{2,1},{3,2},{0,3},{5,4},{6,5},{7,6},{4,7},{9,8},{10,9},{11,1... | collective-permute-start | bytes 786440 | tf_op jit(solution)/shard_map/ppermute | solution.py:353
  111.5 0.0 collective-permute-start.4
  111.5 4.4 %collective-permute-done.6 = bf16[8,32,512]{2,1,0:T(8,128)(2,1)S(1)} collective-permute-done((bf16[8,32,512]{2,1,0:T(8,128)(2,1)S(1)}, bf16[8,32,512]{2,1,0:T(8,128)(2,1)S(1)}, u32[]{:S(2)}, u32[]{:S(2)}) %collective-permute-start.6) | collective-permute-done | bytes 262176 | tf_op jit(solution)/shard_map/ppermute | solution.py:353
  115.9 3.1 %collective-permute-done.4 = bf16[8,32,512]{2,1,0:T(8,128)(2,1)S(1)} collective-permute-done((bf16[8,32,512]{2,1,0:T(8,128)(2,1)S(1)}, bf16[8,32,512]{2,1,0:T(8,128)(2,1)S(1)}, u32[]{:S(2)}, u32[]{:S(2)}) %collective-permute-start.4) | collective-permute-done | bytes 262176 | tf_op jit(solution)/shard_map/ppermute | solution.py:352
  119.0 1.8 %fusion.3 = bf16[8,32,512]{2,1,0:T(8,128)(2,1)} fusion(bf16[8,32,512]{2,1,0:T(8,128)(2,1)S(1)} %collective-permute-done.6, bf16[8,32,512]{2,1,0:T(8,128)(2,1)S(1)} %collective-permute-done.4, bf16[4,8,32,512]{3,2,1,0:T(8,128)(2,1)} %collective-permute-done.2, bf16[4,8,32,512]{3,2,1,0:T(8,128)(2,1)S(1)} %copy-done.3), kind=kLoop, calls=%fused_computation.7 | loop fusion | flops 1048576 | bytes 1310720 | tf_op jit(solution)/shard_map/convert_element_type | solution.py:354
  120.8 0.0 all-to-all-done.3
  120.8 4.5 %all-to-all-start.4 = ((bf16[8,32,512]{2,1,0:T(8,128)(2,1)}), bf16[8,32,512]{2,1,0:T(8,128)(2,1)S(1)}, u32[]{:S(2)}, u32[]{:S(2)}) async-start(bf16[8,32,512]{2,1,0:T(8,128)(2,1)} %fusion.3), calls=%async_computation.4 | async-start | bytes 524288 | tf_op jit(solution)/shard_map/all_to_all | solution.py:316
  125.3 1.1 copy.27
  126.3 4.7 %all-to-all-done.4 = bf16[8,32,512]{2,1,0:T(8,128)(2,1)S(1)} async-done(((bf16[8,32,512]{2,1,0:T(8,128)(2,1)}), bf16[8,32,512]{2,1,0:T(8,128)(2,1)S(1)}, u32[]{:S(2)}, u32[]{:S(2)}) %all-to-all-start.4) | async-done | bytes 262176 | tf_op jit(solution)/shard_map/all_to_all | solution.py:316
  131.1 10.9 %all-gather = bf16[128,512]{1,0:T(8,128)(2,1)S(1)} all-gather(bf16[32,512]{1,0:T(8,128)(2,1)S(1)} %reduce_sum.21), channel_id=2, replica_groups=mesh['batch'=4,'tm'=8,'space'=4] {'batch'}, dimensions={0}, use_global_device_ids=true | all-gather | bytes 163840 | tf_op jit(solution)/shard_map/all_gather | solution.py:358
  142.0 0.7 copy.28
  (6 shorter events, 0.1 us)
Async XLA Ops:
  0.6 21.2 %copy-start.1 = (f32[1024]{0:T(1024)S(1)}, f32[1024]{0:T(1024)}, u32[]{:S(2)}) copy-start(f32[1024]{0:T(1024)} %param.13) | copy-start | bytes 12292
  0.6 21.2 %all-to-all-start = ((bf16[8,2,8,4,1024]{4,3,2,1,0:T(4,128)(2,1)}), bf16[8,2,8,4,1024]{4,3,2,1,0:T(4,128)(2,1)S(1)}, u32[]{:S(2)}, u32[]{:S(2)}) async-start(bf16[8,2,8,4,1024]{4,3,2,1,0:T(4,128)(2,1)} %bitcast.50), calls=%async_computation | async-start | bytes 2097152 | tf_op jit(solution)/shard_map/all_to_all | solution.py:316
  24.6 14.9 %copy-start.5 = (s32[1,2]{1,0:T(1,128)S(1)}, s32[1,2]{1,0:T(1,128)}, u32[]{:S(2)}) copy-start(s32[1,2]{1,0:T(1,128)} %param.12) | copy-start | bytes 28
  31.0 32.6 %all-to-all-start.2 = ((bf16[8,2,32,1024]{3,2,1,0:T(8,128)(2,1)}), bf16[8,2,32,1024]{3,2,1,0:T(8,128)(2,1)S(1)}, u32[]{:S(2)}, u32[]{:S(2)}) async-start(bf16[8,2,32,1024]{3,2,1,0:T(8,128)(2,1)} %bitcast.42), calls=%async_computation.2 | async-start | bytes 2097152 | tf_op jit(solution)/shard_map/all_to_all | solution.py:316
  34.6 13.2 %collective-permute-start = (bf16[2,4,32,1024]{3,2,1,0:T(8,128)(2,1)S(1)}, bf16[2,4,32,1024]{3,2,1,0:T(8,128)(2,1)S(1)}, u32[]{:S(2)}, u32[]{:S(2)}) collective-permute-start(bf16[2,4,32,1024]{3,2,1,0:T(8,128)(2,1)S(1)} %get-tuple-element.10), channel_id=1, source_target_pairs={{0,1},{1,2},{2,3},{4,5},{5,6},{6,7},{8,9},{9,10},{10,11},{12,13},{... | collective-permute-start | bytes 1572872 | tf_op jit(solution)/shard_map/ppermute | solution.py:324
  38.2 13.8 %collective-permute-start.1 = (bf16[2,4,32,1024]{3,2,1,0:T(8,128)(2,1)S(1)}, bf16[2,4,32,1024]{3,2,1,0:T(8,128)(2,1)S(1)}, u32[]{:S(2)}, u32[]{:S(2)}) collective-permute-start(bf16[2,4,32,1024]{3,2,1,0:T(8,128)(2,1)S(1)} %get-tuple-element.11), channel_id=1, source_target_pairs={{1,0},{2,1},{3,2},{5,4},{6,5},{7,6},{9,8},{10,9},{11,10},{13,12},{... | collective-permute-start | bytes 1572872 | tf_op jit(solution)/shard_map/ppermute | solution.py:325
  52.0 16.4 %copy-start.4 = (s32[1,16]{1,0:T(1,128)S(1)}, s32[1,16]{1,0:T(1,128)}, u32[]{:S(2)}) copy-start(s32[1,16]{1,0:T(1,128)} %param.11) | copy-start | bytes 196
  52.0 29.2 %copy-start = (f32[1024]{0:T(1024)S(1)}, f32[1024]{0:T(1024)}, u32[]{:S(2)}) copy-start(f32[1024]{0:T(1024)} %param.16) | copy-start | bytes 12292
  63.6 17.6 %copy-start.2 = (bf16[8,2,32,1024]{3,2,1,0:T(8,128)(2,1)}, bf16[8,2,32,1024]{3,2,1,0:T(8,128)(2,1)S(1)}, u32[]{:S(2)}) copy-start(bf16[8,2,32,1024]{3,2,1,0:T(8,128)(2,1)S(1)} %all-to-all-done.2) | copy-start | bytes 3145732
  63.6 17.6 %all-to-all-start.1 = ((bf16[8,2,32,1024]{3,2,1,0:T(8,128)(2,1)}), bf16[8,2,32,1024]{3,2,1,0:T(8,128)(2,1)S(1)}, u32[]{:S(2)}, u32[]{:S(2)}) async-start(bf16[8,2,32,1024]{3,2,1,0:T(8,128)(2,1)} %spatial_phase.1), calls=%async_computation.1 | async-start | bytes 2097152 | tf_op jit(solution)/shard_map/all_to_all | solution.py:316
  92.9 14.9 %copy-start.3 = (bf16[4,8,32,512]{3,2,1,0:T(8,128)(2,1)S(1)}, bf16[4,8,32,512]{3,2,1,0:T(8,128)(2,1)}, u32[]{:S(2)}) copy-start(bf16[4,8,32,512]{3,2,1,0:T(8,128)(2,1)} %get-tuple-element.16) | copy-start | bytes 3145732
  92.9 7.6 %collective-permute-start.2 = (bf16[4,8,32,512]{3,2,1,0:T(8,128)(2,1)S(1)}, bf16[4,8,32,512]{3,2,1,0:T(8,128)(2,1)}, u32[]{:S(2)}, u32[]{:S(2)}) collective-permute-start(bf16[4,8,32,512]{3,2,1,0:T(8,128)(2,1)S(1)} %get-tuple-element.17), channel_id=1, source_target_pairs={{0,32},{32,0},{64,96},{96,64},{1,33},{33,1},{65,97},{97,65},{2,34}... | collective-permute-start | bytes 3145736 | tf_op jit(solution)/shard_map/ppermute | solution.py:339
  96.9 23.9 %all-to-all-start.3 = ((bf16[8,2,32,1024]{3,2,1,0:T(8,128)(2,1)}), bf16[8,2,32,1024]{3,2,1,0:T(8,128)(2,1)S(1)}, u32[]{:S(2)}, u32[]{:S(2)}) async-start(bf16[8,2,32,1024]{3,2,1,0:T(8,128)(2,1)} %bitcast.51), calls=%async_computation.3 | async-start | bytes 2097152 | tf_op jit(solution)/shard_map/all_to_all | solution.py:316
  101.6 6.2 %collective-permute-start.3 = (bf16[4,32,512]{2,1,0:T(8,128)(2,1)S(1)}, bf16[4,32,512]{2,1,0:T(8,128)(2,1)S(1)}, u32[]{:S(2)}, u32[]{:S(2)}) collective-permute-start(bf16[4,32,512]{2,1,0:T(8,128)(2,1)S(1)} %get-tuple-element.26), channel_id=1, source_target_pairs={{0,1},{1,2},{2,3},{3,0},{4,5},{5,6},{6,7},{7,4},{8,9},{9,10},{10,1... | collective-permute-start | bytes 393224 | tf_op jit(solution)/shard_map/ppermute | solution.py:347
  102.9 4.8 %collective-permute-start.5 = (bf16[4,32,512]{2,1,0:T(8,128)(2,1)S(1)}, bf16[4,32,512]{2,1,0:T(8,128)(2,1)S(1)}, u32[]{:S(2)}, u32[]{:S(2)}) collective-permute-start(bf16[4,32,512]{2,1,0:T(8,128)(2,1)S(1)} %get-tuple-element.27), channel_id=1, source_target_pairs={{1,0},{2,1},{3,2},{0,3},{5,4},{6,5},{7,6},{4,7},{9,8},{10,9},{11,1... | collective-permute-start | bytes 393224 | tf_op jit(solution)/shard_map/ppermute | solution.py:348
  109.0 6.9 %collective-permute-start.6 = (bf16[8,32,512]{2,1,0:T(8,128)(2,1)S(1)}, bf16[8,32,512]{2,1,0:T(8,128)(2,1)S(1)}, u32[]{:S(2)}, u32[]{:S(2)}) collective-permute-start(bf16[8,32,512]{2,1,0:T(8,128)(2,1)S(1)} %get-tuple-element.25), channel_id=1, source_target_pairs={{1,0},{2,1},{3,2},{0,3},{5,4},{6,5},{7,6},{4,7},{9,8},{10,9},{11,1... | collective-permute-start | bytes 786440 | tf_op jit(solution)/shard_map/ppermute | solution.py:353
  111.5 7.5 %collective-permute-start.4 = (bf16[8,32,512]{2,1,0:T(8,128)(2,1)S(1)}, bf16[8,32,512]{2,1,0:T(8,128)(2,1)S(1)}, u32[]{:S(2)}, u32[]{:S(2)}) collective-permute-start(bf16[8,32,512]{2,1,0:T(8,128)(2,1)S(1)} %get-tuple-element.24), channel_id=1, source_target_pairs={{0,1},{1,2},{2,3},{3,0},{4,5},{5,6},{6,7},{7,4},{8,9},{9,10},{10,1... | collective-permute-start | bytes 786440 | tf_op jit(solution)/shard_map/ppermute | solution.py:352
  120.8 10.3 %all-to-all-start.4 = ((bf16[8,32,512]{2,1,0:T(8,128)(2,1)}), bf16[8,32,512]{2,1,0:T(8,128)(2,1)S(1)}, u32[]{:S(2)}, u32[]{:S(2)}) async-start(bf16[8,32,512]{2,1,0:T(8,128)(2,1)} %fusion.3), calls=%async_computation.4 | async-start | bytes 524288 | tf_op jit(solution)/shard_map/all_to_all | solution.py:316

commit v5 on v3

--- a/solution.py
+++ b/solution.py
@@ -252,17 +252,11 @@
     for i in range(0, len(items), TEMPORAL_STAGE):
         staged_attention(items[i:i + TEMPORAL_STAGE])
     core = core_ref[0]
-    here = core_ref[1]
     half = D // 2
     for ref, which in ((send_ref, 1 - core), (keep_ref, core)):
         cot = cotb_ref[:, pl.ds(pl.multiple_of(which * half, half), half)]
         grad = lax.dot_general(ctx_ref[...], cot, (((0,), (0,)), ((), ())), preferred_element_type=F32).astype(BF)
-        spaces, times, block, _ = ref.shape
-        for s in range(spaces):
-            slot = lax.rem(s + spaces - here, spaces)
-            for t in range(times):
-                row = (t * spaces + s) * block
-                ref[slot, t] = grad[row:row + block]
+        ref[...] = grad.reshape(ref.shape)
     kept = pltpu.make_async_copy(keep_ref, keep_hbm, sems.at[5])
     kept.start()
     copies[4].wait()
@@ -282,7 +276,7 @@
     tokens = frames * cols
     spread = jnp.repeat(order, GROUP)
     block = D // (spaces * times)
-    part = (spaces, times, block, D // 2)
+    part = (D // block, block, D // 2)
     return pl.pallas_call(
         temporal_kernel,
         in_specs=[SMEM] + [VMEM] * 4 + [HBM] * 3,
@@ -330,25 +324,19 @@
     info = jnp.concatenate([row_reach.reshape(frames), here.reshape(1)])
     middle = spatial_phase(info, above, below, qkv, tok, spatial_heads, spatial_merge, rows * space)
     mid = exchange(middle, "tm").reshape(frame_count, wide, D)
-    core = jnp.stack([lax.axis_index("batch") & 1, here]).astype(jnp.int32)
+    core = (lax.axis_index("batch") & 1).astype(jnp.int32).reshape(1)
     out, send, keep = temporal_phase(
         core, mid, frame_order.reshape(frame_count), temporal_gain, cot.reshape(frame_count, wide, D),
         temporal_heads, temporal_merge, space, tm,
     )
     batch = lax.axis_size("batch")
     got = lax.ppermute(send, "batch", [(i, i ^ 1) for i in range(batch)])
+    chip = (keep.astype(F32) + got.astype(F32)).astype(BF)
+    pieces = exchange(chip, ("tm", "space"))
     output = exchange(out.reshape(tm, frames, wide, D), "tm").swapaxes(0, 1)
-    chip = [keep[k].astype(F32) + got[k].astype(F32) for k in range(space)]
-    total = chip[0]
-    moved = [lax.ppermute(chip[k].astype(BF), "space", [(i, (i + k) % space) for i in range(space)])
-             for k in range(1, space)]
-    for part in moved:
-        total = total + part.astype(F32)
-    over_space = total.astype(BF)
-    over_tm = exchange(over_space, "tm")
-    over_tm = over_tm.astype(F32).sum(0).astype(BF)
-    block = over_tm.shape[0]
-    parts = lax.all_gather(over_tm, "batch").astype(F32).reshape(batch // 2, 2, block, D // 2).sum(0)
+    own_sum = pieces.astype(F32).sum(0).astype(BF)
+    block = own_sum.shape[0]
+    parts = lax.all_gather(own_sum, "batch").astype(F32).reshape(batch // 2, 2, block, D // 2).sum(0)
     weight_grad = parts.swapaxes(0, 1).reshape(block, D)
     return (output.reshape(1, frames, rows, wide, D), weight_grad)
 

time: 141 us -> 148 us (1.050)
  waiting for transfers between devices: 55.4 us -> 66.4 us
  starting transfers between devices: 35.5 us -> 31.9 us
    all_to_all x5, waiting for transfers between devices: 30.3 us -> 54 us  [per_device(): lax.all_to_all(v, axis, split_axis=0, concat_axis=0, tiled=True)]
    ppermute x3 -> x0, waiting for transfers between devices: 12.6 us -> none  [per_device(): lax.ppermute(chip[k].astype(BF), 'space', [(i, (i + k) % space) for i in...]
    ppermute x3 -> x0, starting transfers between devices: 3.87 us -> none  [per_device(): lax.ppermute(chip[k].astype(BF), 'space', [(i, (i + k) % space) for i in...]
    unnamed x12 -> x16, local copies, waits for them, and re-layouts: 3.38 us -> 2.22 us
    convert_element_type x2 -> x1, other arithmetic: 3.2 us -> 2.59 us  [per_device(): chip = (keep.astype(F32) + got.astype(F32)).astype(BF)]
  transfers between devices with their start and end apart: 11 -> 8, of which waited for: 8 -> 6; matrix products, arithmetic and copies ran while one was open for 5% -> 3% of each run, Pallas kernels for 8% -> 8%
where the time goes in v5:
time: 148 us; the launch traced here: 147 us
  waiting for transfers between devices  66.4 us (45%)
  starting transfers between devices  31.9 us (22%)
  Pallas kernels  31.9 us (22%)
  blocking collectives  10.1 us (7%)
  local copies, waits for them, and re-layouts  3.12 us (2%)
  other arithmetic  2.84 us (2%)
    all_to_all x5, waiting for transfers between devices, per_device(): lax.all_to_all(v, axis, split_axis=0, concat_axis=0, tiled=True)  54 us
    all_to_all x5, starting transfers between devices, per_device(): lax.all_to_all(v, axis, split_axis=0, concat_axis=0, tiled=True)  23 us
    pallas_call x1, Pallas kernels, spatial_phase(): pl.pallas_call(functools.partial(spatial_kernel, rows=rows, all_rows=all_...  11.6 us
    pallas_call x1, Pallas kernels, temporal_phase(): pl.pallas_call(temporal_kernel, in_specs=[SMEM] + [VMEM] * 4 + [HBM] * 3,...  11.1 us
    all_gather x1, blocking collectives, per_device(): lax.all_gather(own_sum, 'batch').astype(F32)  10.1 us
    ppermute x1, waiting for transfers between devices, per_device(): above = lax.ppermute(high, 'space', up)  8.27 us
    pallas_call x1, Pallas kernels, qkv_own(): pl.pallas_call(qkv_kernel, in_specs=[VMEM, VMEM, HBM], out_specs=HBM, out...  6.38 us
    ppermute x1, waiting for transfers between devices, per_device(): below = lax.ppermute(low, 'space', down)  4.18 us
  transfers between devices with their start and end apart: 8, of which 6 were waited for; matrix products, arithmetic and copies ran while one was open for 3% of the time, Pallas kernels for 8%

profile of v5, /device:TPU:1, one launch (start us, length us, event | category | flops | bytes accessed | tf_op | source)
XLA Modules:
  0.0 147.0 jit_solution(3936073759365548154)
XLA Ops:
  0.6 0.0 copy-start.4
  0.6 0.0 copy-start.1
  0.6 6.0 %all-to-all-start = ((bf16[8,2,8,4,1024]{4,3,2,1,0:T(4,128)(2,1)}), bf16[8,2,8,4,1024]{4,3,2,1,0:T(4,128)(2,1)S(1)}, u32[]{:S(2)}, u32[]{:S(2)}) async-start(bf16[8,2,8,4,1024]{4,3,2,1,0:T(4,128)(2,1)} %bitcast.32), calls=%async_computation | async-start | bytes 2097152 | tf_op jit(solution)/shard_map/all_to_all | solution.py:310
  6.6 0.0 copy-done.4
  6.6 1.1 copy.30
  7.8 14.2 %all-to-all-done.x_ref = bf16[8,2,8,4,1024]{4,3,2,1,0:T(4,128)(2,1)S(1)} async-done(((bf16[8,2,8,4,1024]{4,3,2,1,0:T(4,128)(2,1)}), bf16[8,2,8,4,1024]{4,3,2,1,0:T(4,128)(2,1)S(1)}, u32[]{:S(2)}, u32[]{:S(2)}) %all-to-all-start) | async-done | bytes 1048608 | tf_op jit(solution)/shard_map/all_to_all | solution.py:310
  21.9 0.0 copy-done.1
  21.9 2.8 %norm_reorder.1 = (bf16[2,8,32,1024]{3,2,1,0:T(8,128)(2,1)}, bf16[2,4,32,1024]{3,2,1,0:T(8,128)(2,1)S(1)}, bf16[2,4,32,1024]{3,2,1,0:T(8,128)(2,1)S(1)}) custom-call(bf16[8,2,8,4,1024]{4,3,2,1,0:T(4,128)(2,1)S(1)} %all-to-all-done.x_ref, f32[1,1024]{1,0:T(1,128)S(1)} %bitcast.29), custom_call_target="tpu_custom_call" | custom-call | tf_op jit(solution)/shard_map/norm_reorder/pallas_call | solution.py:65
  24.7 6.4 %qkv_own.1.qkv_ref = bf16[3,512,1024]{2,1,0:T(8,128)(2,1)} custom-call(bf16[2,128,1024]{2,1,0:T(8,128)(2,1)S(1)} %bitcast.26, bf16[2,128,1024]{2,1,0:T(8,128)(2,1)S(1)} %bitcast.27, bf16[1024,3072]{1,0:T(8,128)(2,1)} %w_ref.4), custom_call_target="tpu_custom_call" | custom-call | tf_op jit(solution)/shard_map/qkv_own/pallas_call | solution.py:100
  31.1 0.0 copy-start.6
  31.1 3.6 %all-to-all-start.2 = ((bf16[8,2,32,1024]{3,2,1,0:T(8,128)(2,1)}), bf16[8,2,32,1024]{3,2,1,0:T(8,128)(2,1)S(1)}, u32[]{:S(2)}, u32[]{:S(2)}) async-start(bf16[8,2,32,1024]{3,2,1,0:T(8,128)(2,1)} %bitcast.24), calls=%async_computation.2 | async-start | bytes 2097152 | tf_op jit(solution)/shard_map/all_to_all | solution.py:310
  34.7 3.6 %collective-permute-start = (bf16[2,4,32,1024]{3,2,1,0:T(8,128)(2,1)S(1)}, bf16[2,4,32,1024]{3,2,1,0:T(8,128)(2,1)S(1)}, u32[]{:S(2)}, u32[]{:S(2)}) collective-permute-start(bf16[2,4,32,1024]{3,2,1,0:T(8,128)(2,1)S(1)} %get-tuple-element.10), channel_id=1, source_target_pairs={{0,1},{1,2},{2,3},{4,5},{5,6},{6,7},{8,9},{9,10},{10,11},{12,13},{... | collective-permute-start | bytes 1572872 | tf_op jit(solution)/shard_map/ppermute | solution.py:318
  38.3 1.3 collective-permute-start.1
  39.6 0.0 copy-done.6
  39.6 0.1 pad_add_fusion.info_ref
  39.7 8.3 %collective-permute-done.up_ref = bf16[2,4,32,1024]{3,2,1,0:T(8,128)(2,1)S(1)} collective-permute-done((bf16[2,4,32,1024]{3,2,1,0:T(8,128)(2,1)S(1)}, bf16[2,4,32,1024]{3,2,1,0:T(8,128)(2,1)S(1)}, u32[]{:S(2)}, u32[]{:S(2)}) %collective-permute-start) | collective-permute-done | bytes 524320 | tf_op jit(solution)/shard_map/ppermute | solution.py:318
  47.9 4.2 %collective-permute-done.1.down_ref = bf16[2,4,32,1024]{3,2,1,0:T(8,128)(2,1)S(1)} collective-permute-done((bf16[2,4,32,1024]{3,2,1,0:T(8,128)(2,1)S(1)}, bf16[2,4,32,1024]{3,2,1,0:T(8,128)(2,1)S(1)}, u32[]{:S(2)}, u32[]{:S(2)}) %collective-permute-start.1) | collective-permute-done | bytes 524320 | tf_op jit(solution)/shard_map/ppermute | solution.py:319
  52.1 11.6 %spatial_phase.1 = bf16[8,2,32,1024]{3,2,1,0:T(8,128)(2,1)} custom-call(s32[3]{0:T(128)S(1)} %pad_add_fusion.info_ref, bf16[2,4,32,1024]{3,2,1,0:T(8,128)(2,1)S(1)} %collective-permute-done.up_ref, bf16[2,4,32,1024]{3,2,1,0:T(8,128)(2,1)S(1)} %collective-permute-done.1.down_ref, bf16[3,512,1024]{2,1,0:T(8,128)(2,1)} %qkv_own.1.qkv_ref, ...), custom_call_target="tpu_custom_call" | custom-call | tf_op jit(solution)/shard_map/spatial_phase/pallas_call | solution.py:201
  63.7 0.0 copy-start.5
  63.7 0.0 copy-start
  63.8 0.0 all-to-all-done.2
  63.8 0.0 copy-start.2
  63.8 4.8 %all-to-all-start.1 = ((bf16[8,2,32,1024]{3,2,1,0:T(8,128)(2,1)}), bf16[8,2,32,1024]{3,2,1,0:T(8,128)(2,1)S(1)}, u32[]{:S(2)}, u32[]{:S(2)}) async-start(bf16[8,2,32,1024]{3,2,1,0:T(8,128)(2,1)} %spatial_phase.1), calls=%async_computation.1 | async-start | bytes 2097152 | tf_op jit(solution)/shard_map/all_to_all | solution.py:310
  68.6 0.0 copy-done.5
  68.6 0.1 broadcast_in_dim.3
  68.6 0.1 reshape_reshape.8.order_q_ref
  68.7 0.1 reshape_reshape.7.order_k_ref
  68.8 12.5 %all-to-all-done.1 = bf16[8,2,32,1024]{3,2,1,0:T(8,128)(2,1)S(1)} async-done(((bf16[8,2,32,1024]{3,2,1,0:T(8,128)(2,1)}), bf16[8,2,32,1024]{3,2,1,0:T(8,128)(2,1)S(1)}, u32[]{:S(2)}, u32[]{:S(2)}) %all-to-all-start.1) | async-done | bytes 1048608 | tf_op jit(solution)/shard_map/all_to_all | solution.py:310
  81.3 0.0 copy-done.2
  81.3 0.0 copy-done
  81.3 11.1 %temporal_phase.1 = (bf16[16,32,1024]{2,1,0:T(8,128)(2,1)}, bf16[32,32,512]{2,1,0:T(8,128)(2,1)S(1)}, bf16[32,32,512]{2,1,0:T(8,128)(2,1)}) custom-call(s32[1]{0:T(128)} %bitcast.core_ref, bf16[16,32,1024]{2,1,0:T(8,128)(2,1)S(1)} %bitcast.25, s32[128,1]{1,0:T(8,128)S(1)} %reshape_reshape.8.order_q_ref, s32[1,128]{1,0:T(1,128)S(1)} %reshape_reshape.7.order_k_ref, ...), custom_call_target="tpu_custom_call" | custom-call | tf_op jit(solution)/shard_map/temporal_phase/pallas_call | solution.py:280
  92.5 0.0 copy-start.3
  92.5 4.0 %collective-permute-start.2 = (bf16[32,32,512]{2,1,0:T(8,128)(2,1)S(1)}, bf16[32,32,512]{2,1,0:T(8,128)(2,1)}, u32[]{:S(2)}, u32[]{:S(2)}) collective-permute-start(bf16[32,32,512]{2,1,0:T(8,128)(2,1)S(1)} %get-tuple-element.17), channel_id=1, source_target_pairs={{0,32},{32,0},{64,96},{96,64},{1,33},{33,1},{65,97},{97,65},{2,34}... | collective-permute-start | bytes 3145736 | tf_op jit(solution)/shard_map/ppermute | solution.py:333
  96.4 3.6 %all-to-all-start.3 = ((bf16[8,2,32,1024]{3,2,1,0:T(8,128)(2,1)}), bf16[8,2,32,1024]{3,2,1,0:T(8,128)(2,1)S(1)}, u32[]{:S(2)}, u32[]{:S(2)}) async-start(bf16[8,2,32,1024]{3,2,1,0:T(8,128)(2,1)} %bitcast.33), calls=%async_computation.3 | async-start | bytes 2097152 | tf_op jit(solution)/shard_map/all_to_all | solution.py:310
  100.0 0.0 collective-permute-done.2
  100.0 0.0 copy-done.3
  100.0 2.6 %add_convert_fusion = bf16[32,32,512]{2,1,0:T(8,128)(2,1)} fusion(bf16[32,32,512]{2,1,0:T(8,128)(2,1)} %collective-permute-done.2, bf16[32,32,512]{2,1,0:T(8,128)(2,1)S(1)} %copy-done.3), kind=kLoop, calls=%fused_computation | loop fusion | flops 2097152 | bytes 3145728 | tf_op jit(solution)/shard_map/convert_element_type | solution.py:334
  102.6 14.1 %all-to-all-done.3 = bf16[8,2,32,1024]{3,2,1,0:T(8,128)(2,1)S(1)} async-done(((bf16[8,2,32,1024]{3,2,1,0:T(8,128)(2,1)}), bf16[8,2,32,1024]{3,2,1,0:T(8,128)(2,1)S(1)}, u32[]{:S(2)}, u32[]{:S(2)}) %all-to-all-start.3) | async-done | bytes 1048608 | tf_op jit(solution)/shard_map/all_to_all | solution.py:310
  116.8 5.1 %all-to-all-start.4 = ((bf16[32,32,512]{2,1,0:T(8,128)(2,1)}), bf16[32,32,512]{2,1,0:T(8,128)(2,1)S(1)}, u32[]{:S(2)}, u32[]{:S(2)}) async-start(bf16[32,32,512]{2,1,0:T(8,128)(2,1)} %add_convert_fusion), calls=%async_computation.4 | async-start | bytes 2097152 | tf_op jit(solution)/shard_map/all_to_all | solution.py:310
  121.9 1.1 copy.27
  122.9 13.1 %all-to-all-done.4 = bf16[32,32,512]{2,1,0:T(8,128)(2,1)S(1)} async-done(((bf16[32,32,512]{2,1,0:T(8,128)(2,1)}), bf16[32,32,512]{2,1,0:T(8,128)(2,1)S(1)}, u32[]{:S(2)}, u32[]{:S(2)}) %all-to-all-start.4) | async-done | bytes 1048608 | tf_op jit(solution)/shard_map/all_to_all | solution.py:310
  136.1 0.2 reduce_sum.21
  136.2 10.1 %all-gather = bf16[128,512]{1,0:T(8,128)(2,1)S(1)} all-gather(bf16[32,512]{1,0:T(8,128)(2,1)S(1)} %reduce_sum.21), channel_id=2, replica_groups=mesh['batch'=4,'tm'=8,'space'=4] {'batch'}, dimensions={0}, use_global_device_ids=true | all-gather | bytes 163840 | tf_op jit(solution)/shard_map/all_gather | solution.py:339
  146.3 0.7 copy.28
  (1 shorter events, 0.0 us)
Async XLA Ops:
  0.6 6.0 %copy-start.4 = (bf16[1,2,8,32,1024]{4,3,2,1,0:T(8,128)(2,1)S(1)}, bf16[1,2,8,32,1024]{4,3,2,1,0:T(8,128)(2,1)}, u32[]{:S(2)}) copy-start(bf16[1,2,8,32,1024]{4,3,2,1,0:T(8,128)(2,1)} %param.19) | copy-start | bytes 3145732
  0.6 21.3 %copy-start.1 = (f32[1024]{0:T(1024)S(1)}, f32[1024]{0:T(1024)}, u32[]{:S(2)}) copy-start(f32[1024]{0:T(1024)} %param.13) | copy-start | bytes 12292
  0.6 21.3 %all-to-all-start = ((bf16[8,2,8,4,1024]{4,3,2,1,0:T(4,128)(2,1)}), bf16[8,2,8,4,1024]{4,3,2,1,0:T(4,128)(2,1)S(1)}, u32[]{:S(2)}, u32[]{:S(2)}) async-start(bf16[8,2,8,4,1024]{4,3,2,1,0:T(4,128)(2,1)} %bitcast.32), calls=%async_computation | async-start | bytes 2097152 | tf_op jit(solution)/shard_map/all_to_all | solution.py:310
  31.1 8.5 %copy-start.6 = (s32[1,2]{1,0:T(1,128)S(1)}, s32[1,2]{1,0:T(1,128)}, u32[]{:S(2)}) copy-start(s32[1,2]{1,0:T(1,128)} %param.12) | copy-start | bytes 28
  31.1 32.6 %all-to-all-start.2 = ((bf16[8,2,32,1024]{3,2,1,0:T(8,128)(2,1)}), bf16[8,2,32,1024]{3,2,1,0:T(8,128)(2,1)S(1)}, u32[]{:S(2)}, u32[]{:S(2)}) async-start(bf16[8,2,32,1024]{3,2,1,0:T(8,128)(2,1)} %bitcast.24), calls=%async_computation.2 | async-start | bytes 2097152 | tf_op jit(solution)/shard_map/all_to_all | solution.py:310
  34.7 13.2 %collective-permute-start = (bf16[2,4,32,1024]{3,2,1,0:T(8,128)(2,1)S(1)}, bf16[2,4,32,1024]{3,2,1,0:T(8,128)(2,1)S(1)}, u32[]{:S(2)}, u32[]{:S(2)}) collective-permute-start(bf16[2,4,32,1024]{3,2,1,0:T(8,128)(2,1)S(1)} %get-tuple-element.10), channel_id=1, source_target_pairs={{0,1},{1,2},{2,3},{4,5},{5,6},{6,7},{8,9},{9,10},{10,11},{12,13},{... | collective-permute-start | bytes 1572872 | tf_op jit(solution)/shard_map/ppermute | solution.py:318
  38.3 13.8 %collective-permute-start.1 = (bf16[2,4,32,1024]{3,2,1,0:T(8,128)(2,1)S(1)}, bf16[2,4,32,1024]{3,2,1,0:T(8,128)(2,1)S(1)}, u32[]{:S(2)}, u32[]{:S(2)}) collective-permute-start(bf16[2,4,32,1024]{3,2,1,0:T(8,128)(2,1)S(1)} %get-tuple-element.11), channel_id=1, source_target_pairs={{1,0},{2,1},{3,2},{5,4},{6,5},{7,6},{9,8},{10,9},{11,10},{13,12},{... | collective-permute-start | bytes 1572872 | tf_op jit(solution)/shard_map/ppermute | solution.py:319
  63.7 4.8 %copy-start.5 = (s32[1,16]{1,0:T(1,128)S(1)}, s32[1,16]{1,0:T(1,128)}, u32[]{:S(2)}) copy-start(s32[1,16]{1,0:T(1,128)} %param.11) | copy-start | bytes 196
  63.7 17.6 %copy-start = (f32[1024]{0:T(1024)S(1)}, f32[1024]{0:T(1024)}, u32[]{:S(2)}) copy-start(f32[1024]{0:T(1024)} %param.16) | copy-start | bytes 12292
  63.8 17.6 %copy-start.2 = (bf16[8,2,32,1024]{3,2,1,0:T(8,128)(2,1)}, bf16[8,2,32,1024]{3,2,1,0:T(8,128)(2,1)S(1)}, u32[]{:S(2)}) copy-start(bf16[8,2,32,1024]{3,2,1,0:T(8,128)(2,1)S(1)} %all-to-all-done.2) | copy-start | bytes 3145732
  63.8 17.5 %all-to-all-start.1 = ((bf16[8,2,32,1024]{3,2,1,0:T(8,128)(2,1)}), bf16[8,2,32,1024]{3,2,1,0:T(8,128)(2,1)S(1)}, u32[]{:S(2)}, u32[]{:S(2)}) async-start(bf16[8,2,32,1024]{3,2,1,0:T(8,128)(2,1)} %spatial_phase.1), calls=%async_computation.1 | async-start | bytes 2097152 | tf_op jit(solution)/shard_map/all_to_all | solution.py:310
  92.5 7.6 %copy-start.3 = (bf16[32,32,512]{2,1,0:T(8,128)(2,1)S(1)}, bf16[32,32,512]{2,1,0:T(8,128)(2,1)}, u32[]{:S(2)}) copy-start(bf16[32,32,512]{2,1,0:T(8,128)(2,1)} %get-tuple-element.16) | copy-start | bytes 3145732
  92.5 7.5 %collective-permute-start.2 = (bf16[32,32,512]{2,1,0:T(8,128)(2,1)S(1)}, bf16[32,32,512]{2,1,0:T(8,128)(2,1)}, u32[]{:S(2)}, u32[]{:S(2)}) collective-permute-start(bf16[32,32,512]{2,1,0:T(8,128)(2,1)S(1)} %get-tuple-element.17), channel_id=1, source_target_pairs={{0,32},{32,0},{64,96},{96,64},{1,33},{33,1},{65,97},{97,65},{2,34}... | collective-permute-start | bytes 3145736 | tf_op jit(solution)/shard_map/ppermute | solution.py:333
  96.4 20.3 %all-to-all-start.3 = ((bf16[8,2,32,1024]{3,2,1,0:T(8,128)(2,1)}), bf16[8,2,32,1024]{3,2,1,0:T(8,128)(2,1)S(1)}, u32[]{:S(2)}, u32[]{:S(2)}) async-start(bf16[8,2,32,1024]{3,2,1,0:T(8,128)(2,1)} %bitcast.33), calls=%async_computation.3 | async-start | bytes 2097152 | tf_op jit(solution)/shard_map/all_to_all | solution.py:310
  116.8 19.3 %all-to-all-start.4 = ((bf16[32,32,512]{2,1,0:T(8,128)(2,1)}), bf16[32,32,512]{2,1,0:T(8,128)(2,1)S(1)}, u32[]{:S(2)}, u32[]{:S(2)}) async-start(bf16[32,32,512]{2,1,0:T(8,128)(2,1)} %add_convert_fusion), calls=%async_computation.4 | async-start | bytes 2097152 | tf_op jit(solution)/shard_map/all_to_all | solution.py:310

commit v6 on v3

--- a/solution.py
+++ b/solution.py
@@ -1,5 +1,3 @@
-import functools
-
 import jax
 import jax.numpy as jnp
 from jax import lax
@@ -38,54 +36,51 @@
 HBM = pl.BlockSpec(memory_space=pltpu.HBM)
 
 
-def norm_kernel(x_ref, gain_ref, tok_out, low_ref, high_ref, tok_ref, sems):
-    sources, frames, rows, cols, _ = x_ref.shape
-    half = rows // 2
+def norm_kernel(info_ref, x_ref, gain_ref, tok_out, normed_ref, edge_ref, tok_ref, sem):
+    times, parities, rows, cols, _ = x_ref.shape
+    half = info_ref[1]
     gain = gain_ref[...]
-    for f in range(frames):
-        for h, part_ref in enumerate((low_ref, high_ref)):
-
-            def one_row(r, carry):
-                for s in range(sources):
-                    x = x_ref[s, f, h * half + r]
-                    y = normalized(x.astype(F32), gain).astype(BF)
-                    tok_ref[f, h * half + r, s * cols:(s + 1) * cols, :] = x
-                    part_ref[f, r, s * cols:(s + 1) * cols, :] = y
-                return carry
-
-            lax.fori_loop(0, half, one_row, 0)
-        pltpu.make_async_copy(tok_ref.at[f], tok_out.at[f], sems.at[f]).start()
-    for f in range(frames):
-        pltpu.make_async_copy(tok_ref.at[f], tok_out.at[f], sems.at[f]).wait()
-
-
-def norm_reorder(arrived, gain):
-    sources, frames, rows, cols, _ = arrived.shape
-    wide = sources * cols
+    for o in range(parities):
+        first = jnp.where(half == 0, 1 - o, o) * rows
+
+        def one_row(r, carry):
+            for t in range(times):
+                x = x_ref[t, o, r]
+                y = normalized(x.astype(F32), gain).astype(BF)
+                tok_ref[first + r, t * cols:(t + 1) * cols, :] = x
+                normed_ref[first + r, t * cols:(t + 1) * cols, :] = y
+            return carry
+
+        lax.fori_loop(0, rows, one_row, 0)
+    out = pltpu.make_async_copy(tok_ref, tok_out, sem)
+    out.start()
+    start = jnp.where(half == 0, parities * rows - HALO, 0)
+    edge_ref[...] = normed_ref[pl.ds(start, HALO)]
+    out.wait()
+
+
+def norm_reorder(info, arrived, gain):
+    times, parities, rows, cols, _ = arrived.shape
+    shape = (parities * rows, times * cols, D)
     return pl.pallas_call(
         norm_kernel,
-        in_specs=[VMEM, VMEM],
+        in_specs=[SMEM, VMEM, VMEM],
         out_specs=[HBM, VMEM, VMEM],
-        scratch_shapes=[pltpu.VMEM((frames, rows, wide, D), BF), pltpu.SemaphoreType.DMA((frames,))],
-        out_shape=[pltpu.HBM((frames, rows, wide, D), BF)] + [pltpu.VMEM((frames, rows // 2, wide, D), BF)] * 2,
+        out_shape=[pltpu.HBM(shape, BF), pltpu.VMEM(shape, BF), pltpu.VMEM((HALO,) + shape[1:], BF)],
+        scratch_shapes=[pltpu.VMEM(shape, BF), pltpu.SemaphoreType.DMA],
         compiler_params=pltpu.CompilerParams(vmem_limit_bytes=8 * 2**20),
         name="norm_reorder",
-    )(in_vmem(arrived), gain.reshape(1, D))
+    )(info, in_vmem(arrived), gain.reshape(1, D))
 
 
 def column_copies(w_ref, buf, sems, columns):
     return [pltpu.make_async_copy(w_ref.at[:, c * D:(c + 1) * D], buf.at[i], sems.at[i]) for i, c in enumerate(columns)]
 
 
-def qkv_kernel(low_ref, high_ref, w_ref, out_ref, x_ref, buf, y_ref, sems):
+def qkv_kernel(x_ref, w_ref, out_ref, buf, y_ref, sems):
     copies = column_copies(w_ref, buf, sems, range(3))
     for c in copies:
         c.start()
-    frames, edge, _ = low_ref.shape
-    for f in range(frames):
-        for h, part in enumerate((low_ref, high_ref)):
-            at = (2 * f + h) * edge
-            x_ref[at:at + edge] = part[f]
     for i, c in enumerate(copies):
         c.wait()
         y_ref[i] = jnp.dot(x_ref[...], buf[i], preferred_element_type=F32).astype(BF)
@@ -94,19 +89,17 @@
         pltpu.make_async_copy(y_ref.at[i], out_ref.at[i], sems.at[3 + i]).wait()
 
 
-def qkv_own(low, high, heads):
-    frames, edge, _ = low.shape
-    tokens = 2 * frames * edge
+def qkv_own(x, heads):
+    tokens = x.shape[0]
     return pl.pallas_call(
         qkv_kernel,
-        in_specs=[VMEM, VMEM, HBM],
+        in_specs=[VMEM, HBM],
         out_specs=HBM,
         out_shape=pltpu.HBM((3, tokens, D), BF),
-        scratch_shapes=[pltpu.VMEM((tokens, D), BF), pltpu.VMEM((3, D, D), BF), pltpu.VMEM((3, tokens, D), BF),
-                        pltpu.SemaphoreType.DMA((6,))],
+        scratch_shapes=[pltpu.VMEM((3, D, D), BF), pltpu.VMEM((3, tokens, D), BF), pltpu.SemaphoreType.DMA((6,))],
         compiler_params=pltpu.CompilerParams(vmem_limit_bytes=24 * 2**20),
         name="qkv_own",
-    )(in_vmem(low), in_vmem(high), in_hbm(heads))
+    )(in_vmem(x), in_hbm(heads))
 
 
 def staged_attention(items):
@@ -137,81 +130,80 @@
 TEMPORAL_STAGE = 8
 
 
-def spatial_kernel(info_ref, up_ref, down_ref, qkv_ref, tok_ref, w_ref, wm_ref, mid_out,
-                   q_ref, tok_buf, mid_buf, wkv_buf, wm_buf, k_ref, v_ref, ctx_ref, bias_ref, sems, *, rows, all_rows):
-    frames, extent, _ = k_ref.shape
-    tokens = ctx_ref.shape[0] // frames
-    cols = tokens // rows
+def spatial_kernel(info_ref, halo_ref, qkv_ref, tok_ref, w_ref, wm_ref, mid_out,
+                   q_ref, tok_buf, mid_buf, wkv_buf, wm_buf, k_ref, v_ref, ctx_ref, bias_ref, sems):
+    rows, cols, _ = tok_buf.shape
+    tokens = rows * cols
     edge = HALO * cols
+    reach, half = info_ref[0], info_ref[1]
     weights = column_copies(w_ref, wkv_buf, sems, (1, 2))
     own = [pltpu.make_async_copy(qkv_ref.at[0], q_ref, sems.at[2])]
-    for f in range(frames):
-        mine = pl.ds(f * tokens, tokens)
-        for i, buf in ((1, k_ref), (2, v_ref)):
-            own.append(pltpu.make_async_copy(qkv_ref.at[i, mine], buf.at[f, edge:edge + tokens], sems.at[2 + 2 * f + i]))
-    last = [pltpu.make_async_copy(wm_ref, wm_buf, sems.at[7]), pltpu.make_async_copy(tok_ref, tok_buf, sems.at[8])]
+    for i, buf in ((1, k_ref), (2, v_ref)):
+        own.append(pltpu.make_async_copy(qkv_ref.at[i], buf.at[edge:edge + tokens], sems.at[2 + i]))
+    last = [pltpu.make_async_copy(wm_ref, wm_buf, sems.at[5]), pltpu.make_async_copy(tok_ref, tok_buf, sems.at[6])]
     for c in weights + own + last:
         c.start()
-    first_row = info_ref[frames] * rows
-    qrow = lax.broadcasted_iota(jnp.int32, (tokens, extent), 0) // cols
-    krow = lax.broadcasted_iota(jnp.int32, (tokens, extent), 1) // cols - HALO
-    inside = (krow + first_row >= 0) & (krow + first_row < all_rows)
-    distance = jnp.where(inside, jnp.abs(krow - qrow), all_rows)
-    for f in range(frames):
-        bias_ref[f] = jnp.where(distance <= info_ref[f], 0.0, MASKED)
-    halo = jnp.concatenate([up_ref[...].reshape(frames * edge, D), down_ref[...].reshape(frames * edge, D)], axis=0)
+    blocks, n, extent = bias_ref.shape
+    qrow = lax.broadcasted_iota(jnp.int32, (n, extent), 0) // cols
+    krow = lax.broadcasted_iota(jnp.int32, (n, extent), 1) // cols - HALO
+    near = jnp.abs(krow - qrow) <= reach
+    for j in range(blocks):
+        at = krow + (j * HALO + half * rows)
+        bias_ref[j] = jnp.where(near & (at >= 0) & (at < 2 * rows), 0.0, MASKED)
+    there = jnp.where(half == 0, edge + tokens, 0)
+    empty = jnp.where(half == 0, 0, edge + tokens)
+    halo = halo_ref[...].reshape(edge, D)
     for c, w, buf in zip(weights, range(2), (k_ref, v_ref)):
         c.wait()
         side = jnp.dot(halo, wkv_buf[w], preferred_element_type=F32).astype(BF)
-        for f in range(frames):
-            buf[f, 0:edge] = side[f * edge:(f + 1) * edge]
-            buf[f, edge + tokens:] = side[(frames + f) * edge:(frames + f + 1) * edge]
+        buf[pl.ds(pl.multiple_of(there, edge), edge)] = side
+        buf[pl.ds(pl.multiple_of(empty, edge), edge)] = jnp.zeros_like(side)
     for c in own:
         c.wait()
-    half = tokens // 2
     items = []
-    for f in range(frames):
-        for pair in range(PAIRS):
-            at = slice(pair * WIDE, (pair + 1) * WIDE)
-            for side in range(2):
-                keys = slice(side * edge, side * edge + half + 2 * edge)
-                rows_in = slice(side * half, (side + 1) * half)
-                mine = slice(f * tokens + side * half, f * tokens + (side + 1) * half)
-                items.append((reader(q_ref, mine, at), reader(k_ref, f, keys, at), reader(v_ref, f, keys, at),
-                              reader(bias_ref, f, rows_in, keys), ctx_ref, (mine, at)))
+    for pair in range(PAIRS):
+        at = slice(pair * WIDE, (pair + 1) * WIDE)
+        for j in range(blocks):
+            keys = slice(j * edge, j * edge + extent)
+            mine = slice(j * n, (j + 1) * n)
+            items.append((reader(q_ref, mine, at), reader(k_ref, keys, at), reader(v_ref, keys, at),
+                          reader(bias_ref, j), ctx_ref, (mine, at)))
     for i in range(0, len(items), SPATIAL_STAGE):
         staged_attention(items[i:i + SPATIAL_STAGE])
     for c in last:
         c.wait()
     sent = []
-    for f in range(frames):
-        mid = jnp.dot(ctx_ref[f * tokens:(f + 1) * tokens], wm_buf[...], preferred_element_type=F32)
-        mid = mid + tok_buf[f].reshape(tokens, D).astype(F32)
-        mid_buf[:, f] = mid.astype(BF).reshape(rows, cols, D)
-        sent.append(pltpu.make_async_copy(mid_buf.at[:, f], mid_out.at[:, f], sems.at[9 + f]))
-        sent[f].start()
+    part, strip = rows // 2, tokens // 2
+    for i in range(2):
+        mid = jnp.dot(ctx_ref[i * strip:(i + 1) * strip], wm_buf[...], preferred_element_type=F32)
+        mid = mid + tok_buf[i * part:(i + 1) * part].reshape(strip, D).astype(F32)
+        mid_buf[i] = mid.astype(BF).reshape(part, cols, D)
+        parity = jnp.where(half == 0, 1 - i, i)
+        sent.append(pltpu.make_async_copy(mid_buf.at[i], mid_out.at[:, parity], sems.at[7 + i]))
+        sent[i].start()
     for c in sent:
         c.wait()
 
 
-def spatial_phase(info, up, down, qkv, tok, heads, merge, all_rows):
-    frames, rows, cols, _ = tok.shape
+def spatial_phase(info, halo, qkv, tok, heads, merge):
+    rows, cols, _ = tok.shape
     tokens = rows * cols
-    extent = tokens + 2 * HALO * cols
+    edge = HALO * cols
+    extent = tokens + 2 * edge
     return pl.pallas_call(
-        functools.partial(spatial_kernel, rows=rows, all_rows=all_rows),
-        in_specs=[SMEM, VMEM, VMEM, HBM, HBM, HBM, HBM],
+        spatial_kernel,
+        in_specs=[SMEM, VMEM, HBM, HBM, HBM, HBM],
         out_specs=HBM,
-        out_shape=pltpu.HBM((rows, frames, cols, D), BF),
-        scratch_shapes=[pltpu.VMEM((frames * tokens, D), BF), pltpu.VMEM((frames, rows, cols, D), BF),
-                        pltpu.VMEM((rows, frames, cols, D), BF),
+        out_shape=pltpu.HBM((rows // 2, 2, cols, D), BF),
+        scratch_shapes=[pltpu.VMEM((tokens, D), BF), pltpu.VMEM((rows, cols, D), BF),
+                        pltpu.VMEM((2, rows // 2, cols, D), BF),
                         pltpu.VMEM((2, D, D), BF), pltpu.VMEM((D, D), BF),
-                        pltpu.VMEM((frames, extent, D), BF), pltpu.VMEM((frames, extent, D), BF),
-                        pltpu.VMEM((frames * tokens, D), BF), pltpu.VMEM((frames, tokens, extent), F32),
-                        pltpu.SemaphoreType.DMA((9 + frames,))],
+                        pltpu.VMEM((extent, D), BF), pltpu.VMEM((extent, D), BF),
+                        pltpu.VMEM((tokens, D), BF), pltpu.VMEM((tokens // edge, edge, 3 * edge), F32),
+                        pltpu.SemaphoreType.DMA((9,))],
         compiler_params=pltpu.CompilerParams(vmem_limit_bytes=40 * 2**20),
         name="spatial_phase",
-    )(info, in_vmem(up), in_vmem(down), *[in_hbm(v) for v in (qkv, tok, heads, merge)])
+    )(info, in_vmem(halo), *[in_hbm(v) for v in (qkv, tok, heads, merge)])
 
 
 GROUP = 8
@@ -313,23 +305,25 @@
     _, frame_count, rows, cols, _ = clip_tokens.shape
     frames = frame_count // tm
     wide = tm * cols
+    tokens = rows * wide
     exchange = lambda v, axis: lax.all_to_all(v, axis, split_axis=0, concat_axis=0, tiled=True)
 
-    arrived = exchange(clip_tokens.reshape(tm, frames, rows, cols, D), "tm")
+    here = lax.axis_index("space").astype(jnp.int32)
+    half = here >> 1
+    parity = (here & 1) ^ (1 - half)
+    reach = jnp.where(parity == 0, row_reach[0, 0], row_reach[0, 1])
+    info = jnp.stack([reach, half]).astype(jnp.int32)
+    halves = [[t * space + s for t in range(tm) for s in pair] for pair in ((1, 0), (2, 3))]
+    swap = lambda v: lax.all_to_all(v, ("tm", "space"), split_axis=0, concat_axis=0, axis_index_groups=halves, tiled=True)
+    arrived = swap(clip_tokens.reshape(frame_count, rows, cols, D))
     cot = cotangent.reshape(frames, rows, wide, D).swapaxes(0, 1)
-    tok, low, high = norm_reorder(arrived, spatial_gain)
-    up = [(i, i + 1) for i in range(space - 1)]
-    down = [(j, i) for i, j in up]
-    edge = HALO * wide
-    above = lax.ppermute(high, "space", up)
-    below = lax.ppermute(low, "space", down)
-    qkv = qkv_own(low.reshape(frames, edge, D), high.reshape(frames, edge, D), spatial_heads)
+    tok, normed, edge_rows = norm_reorder(info, arrived.reshape(tm, frames, rows, cols, D), spatial_gain)
+    halo = lax.ppermute(edge_rows, "space", [(i, space - 1 - i) for i in range(space)])
+    qkv = qkv_own(normed.reshape(frames * tokens, D), spatial_heads)
     cot, qkv = lax.optimization_barrier((cot, qkv))
     cot = exchange(cot, "tm")
-    here = lax.axis_index("space").astype(jnp.int32)
-    info = jnp.concatenate([row_reach.reshape(frames), here.reshape(1)])
-    middle = spatial_phase(info, above, below, qkv, tok, spatial_heads, spatial_merge, rows * space)
-    mid = exchange(middle, "tm").reshape(frame_count, wide, D)
+    middle = spatial_phase(info, halo, qkv, tok, spatial_heads, spatial_merge)
+    mid = swap(middle.reshape(frame_count, wide, D))
     core = jnp.stack([lax.axis_index("batch") & 1, here]).astype(jnp.int32)
     out, send, keep = temporal_phase(
         core, mid, frame_order.reshape(frame_count), temporal_gain, cot.reshape(frame_count, wide, D),

time: 141 us -> 137 us (0.972)
  waiting for transfers between devices: 55.4 us -> 43.5 us
  starting transfers between devices: 35.5 us -> 40.9 us
    all_to_all x5 -> x3, waiting for transfers between devices: 30.3 us -> 4.88 us  [per_device(): lax.all_to_all(v, axis, split_axis=0, concat_axis=0, tiled=True)]
    all_to_all x0 -> x2, waiting for transfers between devices: none -> 20.7 us  [per_device(): lax.all_to_all(v, ('tm', 'space'), split_axis=0, concat_axis=0, axis_inde...]
    all_to_all x0 -> x2, starting transfers between devices: none -> 13.7 us  [per_device(): lax.all_to_all(v, ('tm', 'space'), split_axis=0, concat_axis=0, axis_inde...]
    all_to_all x5 -> x3, starting transfers between devices: 22.8 us -> 14.7 us  [per_device(): lax.all_to_all(v, axis, split_axis=0, concat_axis=0, tiled=True)]
    ppermute x2 -> x1, waiting for transfers between devices: 12.4 us -> 4.6 us  [per_device(): lax.ppermute(edge_rows, 'space', [(i, space - 1 - i) for i in range(space)])]
    ppermute x2 -> x1, starting transfers between devices: 4.87 us -> 3.3 us  [per_device(): lax.ppermute(edge_rows, 'space', [(i, space - 1 - i) for i in range(space)])]
  transfers between devices with their start and end apart: 11 -> 10, of which waited for: 8 -> 7; matrix products, arithmetic and copies ran while one was open for 5% -> 6% of each run, Pallas kernels for 8% -> 8%
where the time goes in v6:
time: 137 us; the launch traced here: 136 us
  waiting for transfers between devices  43.5 us (32%)
  starting transfers between devices  40.9 us (30%)
  Pallas kernels  32.2 us (24%)
  blocking collectives  8.87 us (6%)
  local copies, waits for them, and re-layouts  4.97 us (4%)
  other arithmetic  3.41 us (2%)
  between operations  2.13 us (2%)
    all_to_all x2, waiting for transfers between devices, per_device(): lax.all_to_all(v, ('tm', 'space'), split_axis=0, concat_axis=0, axis_inde...  20.7 us
    all_to_all x3, starting transfers between devices, per_device(): lax.all_to_all(v, axis, split_axis=0, concat_axis=0, tiled=True)  14.7 us
    all_to_all x2, starting transfers between devices, per_device(): lax.all_to_all(v, ('tm', 'space'), split_axis=0, concat_axis=0, axis_inde...  13.7 us
    ppermute x3, waiting for transfers between devices, per_device(): lax.ppermute(chip[k].astype(BF), 'space', [(i, (i + k) % space) for i in...  13.3 us
    pallas_call x1, Pallas kernels, temporal_phase(): pl.pallas_call(temporal_kernel, in_specs=[SMEM] + [VMEM] * 4 + [HBM] * 3,...  11.7 us
    pallas_call x1, Pallas kernels, spatial_phase(): pl.pallas_call(spatial_kernel, in_specs=[SMEM, VMEM, HBM, HBM, HBM, HBM],...  10.7 us
    all_gather x1, blocking collectives, per_device(): lax.all_gather(over_tm, 'batch').astype(F32)  8.87 us
    pallas_call x1, Pallas kernels, qkv_own(): pl.pallas_call(qkv_kernel, in_specs=[VMEM, HBM], out_specs=HBM, out_shape...  6.38 us
  transfers between devices with their start and end apart: 10, of which 7 were waited for; matrix products, arithmetic and copies ran while one was open for 6% of the time, Pallas kernels for 8%

profile of v6, /device:TPU:1, one launch (start us, length us, event | category | flops | bytes accessed | tf_op | source)
XLA Modules:
  0.0 136.0 jit_solution(1650279757278744359)
XLA Ops:
  0.6 0.0 copy-start.3
  0.6 0.0 copy-start.1
  0.6 7.6 %all-to-all-start = ((bf16[16,8,4,1024]{3,2,1,0:T(4,128)(2,1)}), bf16[16,8,4,1024]{3,2,1,0:T(4,128)(2,1)S(1)}, u32[]{:S(2)}, u32[]{:S(2)}) async-start(bf16[16,8,4,1024]{3,2,1,0:T(4,128)(2,1)} %bitcast.49), calls=%async_computation | async-start | bytes 2097152 | tf_op jit(solution)/shard_map/all_to_all | solution.py:317
  8.3 2.3 %copy.30 = bf16[1,2,8,32,1024]{4,3,1,2,0:T(8,128)(2,1)} copy(bf16[1,2,8,32,1024]{4,3,2,1,0:T(8,128)(2,1)} %param.19) | data formatting | bytes 2097152 | tf_op args[9]
  10.6 0.0 copy-done.3
  10.6 0.7 fusion.6
  12.7 0.1 pad_add_fusion.1.info_ref
  12.7 9.4 %all-to-all-done = bf16[16,8,4,1024]{3,2,1,0:T(4,128)(2,1)S(1)} async-done(((bf16[16,8,4,1024]{3,2,1,0:T(4,128)(2,1)}), bf16[16,8,4,1024]{3,2,1,0:T(4,128)(2,1)S(1)}, u32[]{:S(2)}, u32[]{:S(2)}) %all-to-all-start) | async-done | bytes 1048608 | tf_op jit(solution)/shard_map/all_to_all | solution.py:317
  22.1 0.0 copy-done.1
  22.1 3.5 %norm_reorder.1 = (bf16[16,32,1024]{2,1,0:T(8,128)(2,1)}, bf16[16,32,1024]{2,1,0:T(8,128)(2,1)S(1)}, bf16[4,32,1024]{2,1,0:T(8,128)(2,1)S(1)}) custom-call(s32[2]{0:T(128)S(1)} %pad_add_fusion.1.info_ref, bf16[8,2,8,4,1024]{4,3,2,1,0:T(4,128)(2,1)S(1)} %bitcast.42, f32[1,1024]{1,0:T(1,128)S(1)} %bitcast.45), custom_call_target="tpu_custom_call" | custom-call | tf_op jit(solution)/shard_map/norm_reorder/pallas_call | solution.py:65
  25.6 6.4 %qkv_own.1.qkv_ref = bf16[3,512,1024]{2,1,0:T(8,128)(2,1)} custom-call(bf16[512,1024]{1,0:T(8,128)(2,1)S(1)} %bitcast.43, bf16[1024,3072]{1,0:T(8,128)(2,1)} %w_ref.4), custom_call_target="tpu_custom_call" | custom-call | tf_op jit(solution)/shard_map/qkv_own/pallas_call | solution.py:94
  32.0 5.8 %all-to-all-start.2 = ((bf16[8,2,32,1024]{3,2,1,0:T(8,128)(2,1)}), bf16[8,2,32,1024]{3,2,1,0:T(8,128)(2,1)S(1)}, u32[]{:S(2)}, u32[]{:S(2)}) async-start(bf16[8,2,32,1024]{3,2,1,0:T(8,128)(2,1)} %bitcast.41), calls=%async_computation.2 | async-start | bytes 2097152 | tf_op jit(solution)/shard_map/all_to_all | solution.py:309
  37.8 3.3 %collective-permute-start = (bf16[4,32,1024]{2,1,0:T(8,128)(2,1)S(1)}, bf16[4,32,1024]{2,1,0:T(8,128)(2,1)S(1)}, u32[]{:S(2)}, u32[]{:S(2)}) collective-permute-start(bf16[4,32,1024]{2,1,0:T(8,128)(2,1)S(1)} %get-tuple-element.10), channel_id=1, source_target_pairs={{0,3},{1,2},{2,1},{3,0},{4,7},{5,6},{6,5},{7,4},{8,11},{9,10},{10,... | collective-permute-start | bytes 786440 | tf_op jit(solution)/shard_map/ppermute | solution.py:321
  41.1 4.6 %collective-permute-done.halo_ref = bf16[4,32,1024]{2,1,0:T(8,128)(2,1)S(1)} collective-permute-done((bf16[4,32,1024]{2,1,0:T(8,128)(2,1)S(1)}, bf16[4,32,1024]{2,1,0:T(8,128)(2,1)S(1)}, u32[]{:S(2)}, u32[]{:S(2)}) %collective-permute-start) | collective-permute-done | bytes 262176 | tf_op jit(solution)/shard_map/ppermute | solution.py:321
  45.7 0.0 copy-start.4
  45.7 0.0 copy-start
  45.7 10.7 %spatial_phase.1 = bf16[8,2,32,1024]{3,2,1,0:T(8,128)(2,1)} custom-call(s32[2]{0:T(128)S(1)} %pad_add_fusion.1.info_ref, bf16[4,32,1024]{2,1,0:T(8,128)(2,1)S(1)} %collective-permute-done.halo_ref, bf16[3,512,1024]{2,1,0:T(8,128)(2,1)} %qkv_own.1.qkv_ref, bf16[16,32,1024]{2,1,0:T(8,128)(2,1)} %get-tuple-element.13.tok_ref, bf16[1024,3072]{1,0:T(8,128)(2,1)} %w_ref.4, ...), custom_call_target="tpu_custom_call" | custom-call | tf_op jit(solution)/shard_map/spatial_phase/pallas_call | solution.py:193
  56.4 0.0 all-to-all-done.2
  56.4 0.0 copy-start.2
  56.4 6.1 %all-to-all-start.1 = ((bf16[16,32,1024]{2,1,0:T(8,128)(2,1)}), bf16[16,32,1024]{2,1,0:T(8,128)(2,1)S(1)}, u32[]{:S(2)}, u32[]{:S(2)}) async-start(bf16[16,32,1024]{2,1,0:T(8,128)(2,1)} %bitcast.48), calls=%async_computation.1 | async-start | bytes 2097152 | tf_op jit(solution)/shard_map/all_to_all | solution.py:317
  62.5 0.0 copy-done.4
  62.5 0.1 broadcast_in_dim.3
  62.6 0.1 reshape_reshape.8.order_q_ref
  62.7 0.1 reshape_reshape.7.order_k_ref
  62.8 0.1 pad_add_fusion.core_ref
  62.8 11.3 %all-to-all-done.1.mid_ref = bf16[16,32,1024]{2,1,0:T(8,128)(2,1)S(1)} async-done(((bf16[16,32,1024]{2,1,0:T(8,128)(2,1)}), bf16[16,32,1024]{2,1,0:T(8,128)(2,1)S(1)}, u32[]{:S(2)}, u32[]{:S(2)}) %all-to-all-start.1) | async-done | bytes 1048608 | tf_op jit(solution)/shard_map/all_to_all | solution.py:317
  74.2 0.0 copy-done.2
  74.2 0.0 copy-done
  74.2 11.7 %temporal_phase.1 = (bf16[16,32,1024]{2,1,0:T(8,128)(2,1)}, bf16[4,8,32,512]{3,2,1,0:T(8,128)(2,1)S(1)}, bf16[4,8,32,512]{3,2,1,0:T(8,128)(2,1)}) custom-call(s32[2]{0:T(128)S(1)} %pad_add_fusion.core_ref, bf16[16,32,1024]{2,1,0:T(8,128)(2,1)S(1)} %all-to-all-done.1.mid_ref, s32[128,1]{1,0:T(8,128)S(1)} %reshape_reshape.8.order_q_ref, ...), custom_call_target="tpu_custom_call" | custom-call | tf_op jit(solution)/shard_map/temporal_phase/pallas_call | solution.py:278
  85.8 4.9 %collective-permute-start.1 = (bf16[4,8,32,512]{3,2,1,0:T(8,128)(2,1)S(1)}, bf16[4,8,32,512]{3,2,1,0:T(8,128)(2,1)S(1)}, u32[]{:S(2)}, u32[]{:S(2)}) collective-permute-start(bf16[4,8,32,512]{3,2,1,0:T(8,128)(2,1)S(1)} %get-tuple-element.17), channel_id=1, source_target_pairs={{0,32},{32,0},{64,96},{96,64},{1,33},{33,1},{65,97},{97,65},{2,34}... | collective-permute-start | bytes 3145736 | tf_op jit(solution)/shard_map/ppermute | solution.py:333
  90.7 3.8 %all-to-all-start.3 = ((bf16[8,2,32,1024]{3,2,1,0:T(8,128)(2,1)}), bf16[8,2,32,1024]{3,2,1,0:T(8,128)(2,1)S(1)}, u32[]{:S(2)}, u32[]{:S(2)}) async-start(bf16[8,2,32,1024]{3,2,1,0:T(8,128)(2,1)} %bitcast.50), calls=%async_computation.3 | async-start | bytes 2097152 | tf_op jit(solution)/shard_map/all_to_all | solution.py:309
  94.5 0.0 collective-permute-done.1
  94.5 1.4 %fusion.3 = (bf16[8,32,512]{2,1,0:T(8,128)(2,1)S(1)}, bf16[8,32,512]{2,1,0:T(8,128)(2,1)S(1)}, bf16[8,32,512]{2,1,0:T(8,128)(2,1)S(1)}) fusion(bf16[4,8,32,512]{3,2,1,0:T(8,128)(2,1)S(1)} %collective-permute-done.1, bf16[4,8,32,512]{3,2,1,0:T(8,128)(2,1)} %get-tuple-element.16), kind=kLoop, calls=%fused_computation.8 | loop fusion | flops 1572864 | bytes 2359296 | tf_op jit(solution)/shard_map/convert_element_type | solution.py:337
  95.9 2.3 %collective-permute-start.4 = (bf16[8,32,512]{2,1,0:T(8,128)(2,1)S(1)}, bf16[8,32,512]{2,1,0:T(8,128)(2,1)S(1)}, u32[]{:S(2)}, u32[]{:S(2)}) collective-permute-start(bf16[8,32,512]{2,1,0:T(8,128)(2,1)S(1)} %get-tuple-element.25), channel_id=1, source_target_pairs={{0,3},{1,0},{2,1},{3,2},{4,7},{5,4},{6,5},{7,6},{8,11},{9,8},{10,9... | collective-permute-start | bytes 786440 | tf_op jit(solution)/shard_map/ppermute | solution.py:337
  98.1 1.3 collective-permute-start.3
  99.4 0.8 collective-permute-start.2
  100.2 3.7 %collective-permute-done.4 = bf16[8,32,512]{2,1,0:T(8,128)(2,1)S(1)} collective-permute-done((bf16[8,32,512]{2,1,0:T(8,128)(2,1)S(1)}, bf16[8,32,512]{2,1,0:T(8,128)(2,1)S(1)}, u32[]{:S(2)}, u32[]{:S(2)}) %collective-permute-start.4) | collective-permute-done | bytes 262176 | tf_op jit(solution)/shard_map/ppermute | solution.py:337
  103.9 3.1 %collective-permute-done.3 = bf16[8,32,512]{2,1,0:T(8,128)(2,1)S(1)} collective-permute-done((bf16[8,32,512]{2,1,0:T(8,128)(2,1)S(1)}, bf16[8,32,512]{2,1,0:T(8,128)(2,1)S(1)}, u32[]{:S(2)}, u32[]{:S(2)}) %collective-permute-start.3) | collective-permute-done | bytes 262176 | tf_op jit(solution)/shard_map/ppermute | solution.py:337
  107.0 6.5 %collective-permute-done.2 = bf16[8,32,512]{2,1,0:T(8,128)(2,1)S(1)} collective-permute-done((bf16[8,32,512]{2,1,0:T(8,128)(2,1)S(1)}, bf16[8,32,512]{2,1,0:T(8,128)(2,1)S(1)}, u32[]{:S(2)}, u32[]{:S(2)}) %collective-permute-start.2) | collective-permute-done | bytes 262176 | tf_op jit(solution)/shard_map/ppermute | solution.py:337
  113.5 1.8 %fusion.2 = bf16[8,32,512]{2,1,0:T(8,128)(2,1)} fusion(bf16[8,32,512]{2,1,0:T(8,128)(2,1)S(1)} %collective-permute-done.4, bf16[8,32,512]{2,1,0:T(8,128)(2,1)S(1)} %collective-permute-done.3, bf16[8,32,512]{2,1,0:T(8,128)(2,1)S(1)} %collective-permute-done.2, bf16[4,8,32,512]{3,2,1,0:T(8,128)(2,1)S(1)} %collective-permute-done.1, ...), kind=kLoop, calls=%fused_computation.4 | loop fusion | flops 1310720 | bytes 1572864 | tf_op jit(solution)/shard_map/convert_element_type | solution.py:341
  115.3 0.0 all-to-all-done.3
  115.3 5.1 %all-to-all-start.4 = ((bf16[8,32,512]{2,1,0:T(8,128)(2,1)}), bf16[8,32,512]{2,1,0:T(8,128)(2,1)S(1)}, u32[]{:S(2)}, u32[]{:S(2)}) async-start(bf16[8,32,512]{2,1,0:T(8,128)(2,1)} %fusion.2), calls=%async_computation.4 | async-start | bytes 524288 | tf_op jit(solution)/shard_map/all_to_all | solution.py:309
  120.5 1.1 copy.27
  121.5 4.9 %all-to-all-done.4 = bf16[8,32,512]{2,1,0:T(8,128)(2,1)S(1)} async-done(((bf16[8,32,512]{2,1,0:T(8,128)(2,1)}), bf16[8,32,512]{2,1,0:T(8,128)(2,1)S(1)}, u32[]{:S(2)}, u32[]{:S(2)}) %all-to-all-start.4) | async-done | bytes 262176 | tf_op jit(solution)/shard_map/all_to_all | solution.py:309
  126.5 8.9 %all-gather = bf16[128,512]{1,0:T(8,128)(2,1)S(1)} all-gather(bf16[32,512]{1,0:T(8,128)(2,1)S(1)} %reduce_sum.21), channel_id=2, replica_groups=mesh['batch'=4,'tm'=8,'space'=4] {'batch'}, dimensions={0}, use_global_device_ids=true | all-gather | bytes 163840 | tf_op jit(solution)/shard_map/all_gather | solution.py:345
  135.3 0.7 copy.28
  (2 shorter events, 0.1 us)
Async XLA Ops:
  0.6 10.0 %copy-start.3 = (s32[1,2]{1,0:T(1,128)S(1)}, s32[1,2]{1,0:T(1,128)}, u32[]{:S(2)}) copy-start(s32[1,2]{1,0:T(1,128)} %param.12) | copy-start | bytes 28
  0.6 21.5 %copy-start.1 = (f32[1024]{0:T(1024)S(1)}, f32[1024]{0:T(1024)}, u32[]{:S(2)}) copy-start(f32[1024]{0:T(1024)} %param.13) | copy-start | bytes 12292
  0.6 21.5 %all-to-all-start = ((bf16[16,8,4,1024]{3,2,1,0:T(4,128)(2,1)}), bf16[16,8,4,1024]{3,2,1,0:T(4,128)(2,1)S(1)}, u32[]{:S(2)}, u32[]{:S(2)}) async-start(bf16[16,8,4,1024]{3,2,1,0:T(4,128)(2,1)} %bitcast.49), calls=%async_computation | async-start | bytes 2097152 | tf_op jit(solution)/shard_map/all_to_all | solution.py:317
  32.0 24.4 %all-to-all-start.2 = ((bf16[8,2,32,1024]{3,2,1,0:T(8,128)(2,1)}), bf16[8,2,32,1024]{3,2,1,0:T(8,128)(2,1)S(1)}, u32[]{:S(2)}, u32[]{:S(2)}) async-start(bf16[8,2,32,1024]{3,2,1,0:T(8,128)(2,1)} %bitcast.41), calls=%async_computation.2 | async-start | bytes 2097152 | tf_op jit(solution)/shard_map/all_to_all | solution.py:309
  37.8 7.9 %collective-permute-start = (bf16[4,32,1024]{2,1,0:T(8,128)(2,1)S(1)}, bf16[4,32,1024]{2,1,0:T(8,128)(2,1)S(1)}, u32[]{:S(2)}, u32[]{:S(2)}) collective-permute-start(bf16[4,32,1024]{2,1,0:T(8,128)(2,1)S(1)} %get-tuple-element.10), channel_id=1, source_target_pairs={{0,3},{1,2},{2,1},{3,0},{4,7},{5,6},{6,5},{7,4},{8,11},{9,10},{10,... | collective-permute-start | bytes 786440 | tf_op jit(solution)/shard_map/ppermute | solution.py:321
  45.7 16.8 %copy-start.4 = (s32[1,16]{1,0:T(1,128)S(1)}, s32[1,16]{1,0:T(1,128)}, u32[]{:S(2)}) copy-start(s32[1,16]{1,0:T(1,128)} %param.11) | copy-start | bytes 196
  45.7 28.4 %copy-start = (f32[1024]{0:T(1024)S(1)}, f32[1024]{0:T(1024)}, u32[]{:S(2)}) copy-start(f32[1024]{0:T(1024)} %param.16) | copy-start | bytes 12292
  56.4 17.7 %copy-start.2 = (bf16[8,2,32,1024]{3,2,1,0:T(8,128)(2,1)}, bf16[8,2,32,1024]{3,2,1,0:T(8,128)(2,1)S(1)}, u32[]{:S(2)}) copy-start(bf16[8,2,32,1024]{3,2,1,0:T(8,128)(2,1)S(1)} %all-to-all-done.2) | copy-start | bytes 3145732
  56.4 17.7 %all-to-all-start.1 = ((bf16[16,32,1024]{2,1,0:T(8,128)(2,1)}), bf16[16,32,1024]{2,1,0:T(8,128)(2,1)S(1)}, u32[]{:S(2)}, u32[]{:S(2)}) async-start(bf16[16,32,1024]{2,1,0:T(8,128)(2,1)} %bitcast.48), calls=%async_computation.1 | async-start | bytes 2097152 | tf_op jit(solution)/shard_map/all_to_all | solution.py:317
  85.8 8.6 %collective-permute-start.1 = (bf16[4,8,32,512]{3,2,1,0:T(8,128)(2,1)S(1)}, bf16[4,8,32,512]{3,2,1,0:T(8,128)(2,1)S(1)}, u32[]{:S(2)}, u32[]{:S(2)}) collective-permute-start(bf16[4,8,32,512]{3,2,1,0:T(8,128)(2,1)S(1)} %get-tuple-element.17), channel_id=1, source_target_pairs={{0,32},{32,0},{64,96},{96,64},{1,33},{33,1},{65,97},{97,65},{2,34}... | collective-permute-start | bytes 3145736 | tf_op jit(solution)/shard_map/ppermute | solution.py:333
  90.7 24.6 %all-to-all-start.3 = ((bf16[8,2,32,1024]{3,2,1,0:T(8,128)(2,1)}), bf16[8,2,32,1024]{3,2,1,0:T(8,128)(2,1)S(1)}, u32[]{:S(2)}, u32[]{:S(2)}) async-start(bf16[8,2,32,1024]{3,2,1,0:T(8,128)(2,1)} %bitcast.50), calls=%async_computation.3 | async-start | bytes 2097152 | tf_op jit(solution)/shard_map/all_to_all | solution.py:309
  95.9 8.0 %collective-permute-start.4 = (bf16[8,32,512]{2,1,0:T(8,128)(2,1)S(1)}, bf16[8,32,512]{2,1,0:T(8,128)(2,1)S(1)}, u32[]{:S(2)}, u32[]{:S(2)}) collective-permute-start(bf16[8,32,512]{2,1,0:T(8,128)(2,1)S(1)} %get-tuple-element.25), channel_id=1, source_target_pairs={{0,3},{1,0},{2,1},{3,2},{4,7},{5,4},{6,5},{7,6},{8,11},{9,8},{10,9... | collective-permute-start | bytes 786440 | tf_op jit(solution)/shard_map/ppermute | solution.py:337
  98.1 8.8 %collective-permute-start.3 = (bf16[8,32,512]{2,1,0:T(8,128)(2,1)S(1)}, bf16[8,32,512]{2,1,0:T(8,128)(2,1)S(1)}, u32[]{:S(2)}, u32[]{:S(2)}) collective-permute-start(bf16[8,32,512]{2,1,0:T(8,128)(2,1)S(1)} %get-tuple-element.26), channel_id=1, source_target_pairs={{0,2},{1,3},{2,0},{3,1},{4,6},{5,7},{6,4},{7,5},{8,10},{9,11},{10,... | collective-permute-start | bytes 786440 | tf_op jit(solution)/shard_map/ppermute | solution.py:337
  99.4 14.1 %collective-permute-start.2 = (bf16[8,32,512]{2,1,0:T(8,128)(2,1)S(1)}, bf16[8,32,512]{2,1,0:T(8,128)(2,1)S(1)}, u32[]{:S(2)}, u32[]{:S(2)}) collective-permute-start(bf16[8,32,512]{2,1,0:T(8,128)(2,1)S(1)} %get-tuple-element.24), channel_id=1, source_target_pairs={{0,1},{1,2},{2,3},{3,0},{4,5},{5,6},{6,7},{7,4},{8,9},{9,10},{10,1... | collective-permute-start | bytes 786440 | tf_op jit(solution)/shard_map/ppermute | solution.py:337
  115.3 11.1 %all-to-all-start.4 = ((bf16[8,32,512]{2,1,0:T(8,128)(2,1)}), bf16[8,32,512]{2,1,0:T(8,128)(2,1)S(1)}, u32[]{:S(2)}, u32[]{:S(2)}) async-start(bf16[8,32,512]{2,1,0:T(8,128)(2,1)} %fusion.2), calls=%async_computation.4 | async-start | bytes 524288 | tf_op jit(solution)/shard_map/all_to_all | solution.py:309

commit v7 on v6

--- a/solution.py
+++ b/solution.py
@@ -52,11 +52,13 @@
             return carry
 
         lax.fori_loop(0, rows, one_row, 0)
-    out = pltpu.make_async_copy(tok_ref, tok_out, sem)
-    out.start()
+        done = pl.ds(first, rows)
+        pltpu.make_async_copy(tok_ref.at[done], tok_out.at[done], sem.at[o]).start()
     start = jnp.where(half == 0, parities * rows - HALO, 0)
     edge_ref[...] = normed_ref[pl.ds(start, HALO)]
-    out.wait()
+    for o in range(parities):
+        done = pl.ds(jnp.where(half == 0, 1 - o, o) * rows, rows)
+        pltpu.make_async_copy(tok_ref.at[done], tok_out.at[done], sem.at[o]).wait()
 
 
 def norm_reorder(info, arrived, gain):
@@ -67,7 +69,7 @@
         in_specs=[SMEM, VMEM, VMEM],
         out_specs=[HBM, VMEM, VMEM],
         out_shape=[pltpu.HBM(shape, BF), pltpu.VMEM(shape, BF), pltpu.VMEM((HALO,) + shape[1:], BF)],
-        scratch_shapes=[pltpu.VMEM(shape, BF), pltpu.SemaphoreType.DMA],
+        scratch_shapes=[pltpu.VMEM(shape, BF), pltpu.SemaphoreType.DMA((2,))],
         compiler_params=pltpu.CompilerParams(vmem_limit_bytes=8 * 2**20),
         name="norm_reorder",
     )(info, in_vmem(arrived), gain.reshape(1, D))
@@ -77,26 +79,36 @@
     return [pltpu.make_async_copy(w_ref.at[:, c * D:(c + 1) * D], buf.at[i], sems.at[i]) for i, c in enumerate(columns)]
 
 
-def qkv_kernel(x_ref, w_ref, out_ref, buf, y_ref, sems):
-    copies = column_copies(w_ref, buf, sems, range(3))
+QKV_PIECE = 512
+
+
+def qkv_kernel(x_ref, w_ref, out_ref, buf, y_ref, sems, out_sems):
+    pieces = buf.shape[0]
+    copies = [pltpu.make_async_copy(w_ref.at[:, i * QKV_PIECE:(i + 1) * QKV_PIECE], buf.at[i], sems.at[i])
+              for i in range(pieces)]
     for c in copies:
         c.start()
+    sent = []
     for i, c in enumerate(copies):
         c.wait()
         y_ref[i] = jnp.dot(x_ref[...], buf[i], preferred_element_type=F32).astype(BF)
-        pltpu.make_async_copy(y_ref.at[i], out_ref.at[i], sems.at[3 + i]).start()
-    for i in range(3):
-        pltpu.make_async_copy(y_ref.at[i], out_ref.at[i], sems.at[3 + i]).wait()
+        third, at = divmod(i * QKV_PIECE, D)
+        sent.append(pltpu.make_async_copy(y_ref.at[i], out_ref.at[third, :, at:at + QKV_PIECE], out_sems.at[i]))
+        sent[i].start()
+    for c in sent:
+        c.wait()
 
 
 def qkv_own(x, heads):
     tokens = x.shape[0]
+    pieces = 3 * D // QKV_PIECE
     return pl.pallas_call(
         qkv_kernel,
         in_specs=[VMEM, HBM],
         out_specs=HBM,
         out_shape=pltpu.HBM((3, tokens, D), BF),
-        scratch_shapes=[pltpu.VMEM((3, D, D), BF), pltpu.VMEM((3, tokens, D), BF), pltpu.SemaphoreType.DMA((6,))],
+        scratch_shapes=[pltpu.VMEM((pieces, D, QKV_PIECE), BF), pltpu.VMEM((pieces, tokens, QKV_PIECE), BF),
+                        pltpu.SemaphoreType.DMA((pieces,)), pltpu.SemaphoreType.DMA((pieces,))],
         compiler_params=pltpu.CompilerParams(vmem_limit_bytes=24 * 2**20),
         name="qkv_own",
     )(in_vmem(x), in_hbm(heads))
@@ -289,6 +301,32 @@
       in_hbm(cot), in_hbm(heads), in_hbm(merge))
 
 
+def sum_kernel(keep_ref, got_ref, *refs):
+    parts, (out_ref, own_ref, sems) = refs[:-3], refs[-3:]
+    copies = [pltpu.make_async_copy(r.at[0], own_ref.at[i], sems.at[i]) for i, r in enumerate((keep_ref, got_ref))]
+    for c in copies:
+        c.start()
+    total = parts[0][...].astype(F32)
+    for p in parts[1:]:
+        total = total + p[...].astype(F32)
+    for c in copies:
+        c.wait()
+    out_ref[...] = (total + own_ref[0].astype(F32) + own_ref[1].astype(F32)).astype(BF)
+
+
+def space_sum(keep, got, moved):
+    shape = moved[0].shape
+    return pl.pallas_call(
+        sum_kernel,
+        in_specs=[HBM, HBM] + [VMEM] * len(moved),
+        out_specs=VMEM,
+        out_shape=pltpu.VMEM(shape, BF),
+        scratch_shapes=[pltpu.VMEM((2,) + shape, BF), pltpu.SemaphoreType.DMA((2,))],
+        compiler_params=pltpu.CompilerParams(vmem_limit_bytes=8 * 2**20),
+        name="space_sum",
+    )(in_hbm(keep), in_hbm(got), *[in_vmem(p) for p in moved])
+
+
 def per_device(
     clip_tokens,
     frame_order,
@@ -319,9 +357,9 @@
     cot = cotangent.reshape(frames, rows, wide, D).swapaxes(0, 1)
     tok, normed, edge_rows = norm_reorder(info, arrived.reshape(tm, frames, rows, cols, D), spatial_gain)
     halo = lax.ppermute(edge_rows, "space", [(i, space - 1 - i) for i in range(space)])
+    cot, normed = lax.optimization_barrier((cot, normed))
+    cot = exchange(cot, "tm")
     qkv = qkv_own(normed.reshape(frames * tokens, D), spatial_heads)
-    cot, qkv = lax.optimization_barrier((cot, qkv))
-    cot = exchange(cot, "tm")
     middle = spatial_phase(info, halo, qkv, tok, spatial_heads, spatial_merge)
     mid = swap(middle.reshape(frame_count, wide, D))
     core = jnp.stack([lax.axis_index("batch") & 1, here]).astype(jnp.int32)
@@ -332,13 +370,10 @@
     batch = lax.axis_size("batch")
     got = lax.ppermute(send, "batch", [(i, i ^ 1) for i in range(batch)])
     output = exchange(out.reshape(tm, frames, wide, D), "tm").swapaxes(0, 1)
-    chip = [keep[k].astype(F32) + got[k].astype(F32) for k in range(space)]
-    total = chip[0]
-    moved = [lax.ppermute(chip[k].astype(BF), "space", [(i, (i + k) % space) for i in range(space)])
+    chip = [keep[k].astype(F32) + got[k].astype(F32) for k in range(1, space)]
+    moved = [lax.ppermute(chip[k - 1].astype(BF), "space", [(i, (i + k) % space) for i in range(space)])
              for k in range(1, space)]
-    for part in moved:
-        total = total + part.astype(F32)
-    over_space = total.astype(BF)
+    over_space = space_sum(keep, got, moved)
     over_tm = exchange(over_space, "tm")
     over_tm = over_tm.astype(F32).sum(0).astype(BF)
     block = over_tm.shape[0]

time: 137 us -> 131 us (0.956)
  waiting for transfers between devices: 43.5 us -> 37.4 us
  Pallas kernels: 32.2 us -> 33.9 us
  other arithmetic: 3.41 us -> 1.96 us
    ppermute x1, waiting for transfers between devices: 4.6 us -> 0.01 us  [per_device(): lax.ppermute(edge_rows, 'space', [(i, space - 1 - i) for i in range(space)])]
    ppermute x3, waiting for transfers between devices: 13.3 us -> 10.9 us  [per_device(): lax.ppermute(chip[k - 1].astype(BF), 'space', [(i, (i + k) % space) for i...]
    pallas_call x0 -> x1, Pallas kernels: none -> 1.82 us  [space_sum(): pl.pallas_call(sum_kernel, in_specs=[HBM, HBM] + [VMEM] * len(moved), out...]
    convert_element_type x2 -> x1, other arithmetic: 3.2 us -> 1.74 us  [per_device(): chip[k - 1].astype(BF)]
    unnamed x12 -> x14, local copies, waits for them, and re-layouts: 3.41 us -> 3.41 us
  transfers between devices with their start and end apart: 10 -> 10, of which waited for: 7 -> 5; matrix products, arithmetic and copies ran while one was open for 6% -> 5% of each run, Pallas kernels for 8% -> 15%
where the time goes in v7:
time: 131 us; the launch traced here: 130 us
  starting transfers between devices  40 us (31%)
  waiting for transfers between devices  37.4 us (29%)
  Pallas kernels  33.9 us (26%)
  blocking collectives  9.7 us (7%)
  local copies, waits for them, and re-layouts  4.97 us (4%)
  between operations  2.05 us (2%)
  other arithmetic  1.96 us (1%)
    all_to_all x2, waiting for transfers between devices, per_device(): lax.all_to_all(v, ('tm', 'space'), split_axis=0, concat_axis=0, axis_inde...  21.7 us
    all_to_all x3, starting transfers between devices, per_device(): lax.all_to_all(v, axis, split_axis=0, concat_axis=0, tiled=True)  14.7 us
    all_to_all x2, starting transfers between devices, per_device(): lax.all_to_all(v, ('tm', 'space'), split_axis=0, concat_axis=0, axis_inde...  14 us
    pallas_call x1, Pallas kernels, temporal_phase(): pl.pallas_call(temporal_kernel, in_specs=[SMEM] + [VMEM] * 4 + [HBM] * 3,...  11.7 us
    ppermute x3, waiting for transfers between devices, per_device(): lax.ppermute(chip[k - 1].astype(BF), 'space', [(i, (i + k) % space) for i...  10.9 us
    pallas_call x1, Pallas kernels, spatial_phase(): pl.pallas_call(spatial_kernel, in_specs=[SMEM, VMEM, HBM, HBM, HBM, HBM],...  10.6 us
    all_gather x1, blocking collectives, per_device(): lax.all_gather(over_tm, 'batch').astype(F32)  9.7 us
    pallas_call x1, Pallas kernels, qkv_own(): pl.pallas_call(qkv_kernel, in_specs=[VMEM, HBM], out_specs=HBM, out_shape...  6.43 us
  transfers between devices with their start and end apart: 10, of which 5 were waited for; matrix products, arithmetic and copies ran while one was open for 5% of the time, Pallas kernels for 15%

profile of v7, /device:TPU:1, one launch (start us, length us, event | category | flops | bytes accessed | tf_op | source)
XLA Modules:
  0.0 129.9 jit_solution(14479572371404949749)
XLA Ops:
  0.6 0.0 copy-start.4
  0.6 0.0 copy-start.1
  0.6 7.6 %all-to-all-start = ((bf16[16,8,4,1024]{3,2,1,0:T(4,128)(2,1)}), bf16[16,8,4,1024]{3,2,1,0:T(4,128)(2,1)S(1)}, u32[]{:S(2)}, u32[]{:S(2)}) async-start(bf16[16,8,4,1024]{3,2,1,0:T(4,128)(2,1)} %bitcast.41), calls=%async_computation | async-start | bytes 2097152 | tf_op jit(solution)/shard_map/all_to_all | solution.py:355
  8.3 2.3 %copy.30 = bf16[1,2,8,32,1024]{4,3,1,2,0:T(8,128)(2,1)} copy(bf16[1,2,8,32,1024]{4,3,2,1,0:T(8,128)(2,1)} %param.19) | data formatting | bytes 2097152 | tf_op args[9]
  10.6 0.0 copy-done.4
  10.6 0.7 fusion.3
  12.5 0.1 pad_add_fusion.1.info_ref
  12.6 9.5 %all-to-all-done = bf16[16,8,4,1024]{3,2,1,0:T(4,128)(2,1)S(1)} async-done(((bf16[16,8,4,1024]{3,2,1,0:T(4,128)(2,1)}), bf16[16,8,4,1024]{3,2,1,0:T(4,128)(2,1)S(1)}, u32[]{:S(2)}, u32[]{:S(2)}) %all-to-all-start) | async-done | bytes 1048608 | tf_op jit(solution)/shard_map/all_to_all | solution.py:355
  22.1 0.0 copy-done.1
  22.1 3.3 %norm_reorder.1 = (bf16[16,32,1024]{2,1,0:T(8,128)(2,1)}, bf16[16,32,1024]{2,1,0:T(8,128)(2,1)S(1)}, bf16[4,32,1024]{2,1,0:T(8,128)(2,1)S(1)}) custom-call(s32[2]{0:T(128)S(1)} %pad_add_fusion.1.info_ref, bf16[8,2,8,4,1024]{4,3,2,1,0:T(4,128)(2,1)S(1)} %bitcast.34, f32[1,1024]{1,0:T(1,128)S(1)} %bitcast.37), custom_call_target="tpu_custom_call" | custom-call | tf_op jit(solution)/shard_map/norm_reorder/pallas_call | solution.py:67
  25.4 5.8 %all-to-all-start.2 = ((bf16[8,2,32,1024]{3,2,1,0:T(8,128)(2,1)}), bf16[8,2,32,1024]{3,2,1,0:T(8,128)(2,1)S(1)}, u32[]{:S(2)}, u32[]{:S(2)}) async-start(bf16[8,2,32,1024]{3,2,1,0:T(8,128)(2,1)} %bitcast.33), calls=%async_computation.2 | async-start | bytes 2097152 | tf_op jit(solution)/shard_map/all_to_all | solution.py:347
  31.3 3.3 %collective-permute-start = (bf16[4,32,1024]{2,1,0:T(8,128)(2,1)S(1)}, bf16[4,32,1024]{2,1,0:T(8,128)(2,1)S(1)}, u32[]{:S(2)}, u32[]{:S(2)}) collective-permute-start(bf16[4,32,1024]{2,1,0:T(8,128)(2,1)S(1)} %get-tuple-element.10), channel_id=1, source_target_pairs={{0,3},{1,2},{2,1},{3,0},{4,7},{5,6},{6,5},{7,4},{8,11},{9,10},{10,... | collective-permute-start | bytes 786440 | tf_op jit(solution)/shard_map/ppermute | solution.py:359
  34.6 6.4 %qkv_own.1.qkv_ref = bf16[3,512,1024]{2,1,0:T(8,128)(2,1)} custom-call(bf16[512,1024]{1,0:T(8,128)(2,1)S(1)} %bitcast.35, bf16[1024,3072]{1,0:T(8,128)(2,1)} %w_ref.4), custom_call_target="tpu_custom_call" | custom-call | tf_op jit(solution)/shard_map/qkv_own/pallas_call | solution.py:105
  41.0 0.0 collective-permute-done.halo_ref
  41.0 0.0 copy-start.5
  41.0 0.0 copy-start
  41.0 10.6 %spatial_phase.1 = bf16[8,2,32,1024]{3,2,1,0:T(8,128)(2,1)} custom-call(s32[2]{0:T(128)S(1)} %pad_add_fusion.1.info_ref, bf16[4,32,1024]{2,1,0:T(8,128)(2,1)S(1)} %collective-permute-done.halo_ref, bf16[3,512,1024]{2,1,0:T(8,128)(2,1)} %qkv_own.1.qkv_ref, bf16[16,32,1024]{2,1,0:T(8,128)(2,1)} %get-tuple-element.13.tok_ref, bf16[1024,3072]{1,0:T(8,128)(2,1)} %w_ref.4, ...), custom_call_target="tpu_custom_call" | custom-call | tf_op jit(solution)/shard_map/spatial_phase/pallas_call | solution.py:205
  51.7 0.0 all-to-all-done.2
  51.7 0.0 copy-start.2
  51.7 6.3 %all-to-all-start.1 = ((bf16[16,32,1024]{2,1,0:T(8,128)(2,1)}), bf16[16,32,1024]{2,1,0:T(8,128)(2,1)S(1)}, u32[]{:S(2)}, u32[]{:S(2)}) async-start(bf16[16,32,1024]{2,1,0:T(8,128)(2,1)} %bitcast.40), calls=%async_computation.1 | async-start | bytes 2097152 | tf_op jit(solution)/shard_map/all_to_all | solution.py:355
  58.1 0.0 copy-done.5
  58.1 0.1 broadcast_in_dim.3
  58.1 0.1 reshape_reshape.8.order_q_ref
  58.2 0.1 reshape_reshape.7.order_k_ref
  58.3 0.1 pad_add_fusion.core_ref
  58.4 12.2 %all-to-all-done.1.mid_ref = bf16[16,32,1024]{2,1,0:T(8,128)(2,1)S(1)} async-done(((bf16[16,32,1024]{2,1,0:T(8,128)(2,1)}), bf16[16,32,1024]{2,1,0:T(8,128)(2,1)S(1)}, u32[]{:S(2)}, u32[]{:S(2)}) %all-to-all-start.1) | async-done | bytes 1048608 | tf_op jit(solution)/shard_map/all_to_all | solution.py:355
  70.6 0.0 copy-done.2
  70.6 0.0 copy-done
  70.6 11.7 %temporal_phase.1 = (bf16[16,32,1024]{2,1,0:T(8,128)(2,1)}, bf16[4,8,32,512]{3,2,1,0:T(8,128)(2,1)S(1)}, bf16[4,8,32,512]{3,2,1,0:T(8,128)(2,1)}) custom-call(s32[2]{0:T(128)S(1)} %pad_add_fusion.core_ref, bf16[16,32,1024]{2,1,0:T(8,128)(2,1)S(1)} %all-to-all-done.1.mid_ref, s32[128,1]{1,0:T(8,128)S(1)} %reshape_reshape.8.order_q_ref, ...), custom_call_target="tpu_custom_call" | custom-call | tf_op jit(solution)/shard_map/temporal_phase/pallas_call | solution.py:290
  82.3 4.2 %collective-permute-start.1 = (bf16[4,8,32,512]{3,2,1,0:T(8,128)(2,1)S(1)}, bf16[4,8,32,512]{3,2,1,0:T(8,128)(2,1)S(1)}, u32[]{:S(2)}, u32[]{:S(2)}) collective-permute-start(bf16[4,8,32,512]{3,2,1,0:T(8,128)(2,1)S(1)} %get-tuple-element.17), channel_id=1, source_target_pairs={{0,32},{32,0},{64,96},{96,64},{1,33},{33,1},{65,97},{97,65},{2,34}... | collective-permute-start | bytes 3145736 | tf_op jit(solution)/shard_map/ppermute | solution.py:371
  86.4 3.8 %all-to-all-start.3 = ((bf16[8,2,32,1024]{3,2,1,0:T(8,128)(2,1)}), bf16[8,2,32,1024]{3,2,1,0:T(8,128)(2,1)S(1)}, u32[]{:S(2)}, u32[]{:S(2)}) async-start(bf16[8,2,32,1024]{3,2,1,0:T(8,128)(2,1)} %bitcast.42), calls=%async_computation.3 | async-start | bytes 2097152 | tf_op jit(solution)/shard_map/all_to_all | solution.py:347
  90.2 0.0 collective-permute-done.1.got_ref
  90.2 0.0 copy-start.3
  90.3 1.7 %fusion.2 = (bf16[8,32,512]{2,1,0:T(8,128)(2,1)S(1)}, bf16[8,32,512]{2,1,0:T(8,128)(2,1)S(1)}, bf16[8,32,512]{2,1,0:T(8,128)(2,1)S(1)}) fusion(bf16[4,8,32,512]{3,2,1,0:T(8,128)(2,1)S(1)} %collective-permute-done.1.got_ref, bf16[4,8,32,512]{3,2,1,0:T(8,128)(2,1)} %get-tuple-element.16.keep_ref), kind=kLoop, calls=%fused_computation.6 | loop fusion | flops 1572864 | bytes 2359296 | tf_op jit(solution)/shard_map/convert_element_type | solution.py:374
  92.0 1.4 %collective-permute-start.2 = (bf16[8,32,512]{2,1,0:T(8,128)(2,1)S(1)}, bf16[8,32,512]{2,1,0:T(8,128)(2,1)S(1)}, u32[]{:S(2)}, u32[]{:S(2)}) collective-permute-start(bf16[8,32,512]{2,1,0:T(8,128)(2,1)S(1)} %get-tuple-element.26), channel_id=1, source_target_pairs={{0,1},{1,2},{2,3},{3,0},{4,5},{5,6},{6,7},{7,4},{8,9},{9,10},{10,1... | collective-permute-start | bytes 786440 | tf_op jit(solution)/shard_map/ppermute | solution.py:374
  93.4 0.0 collective-permute-start.3
  93.4 2.5 %collective-permute-start.4 = (bf16[8,32,512]{2,1,0:T(8,128)(2,1)S(1)}, bf16[8,32,512]{2,1,0:T(8,128)(2,1)S(1)}, u32[]{:S(2)}, u32[]{:S(2)}) collective-permute-start(bf16[8,32,512]{2,1,0:T(8,128)(2,1)S(1)} %get-tuple-element.24), channel_id=1, source_target_pairs={{0,3},{1,0},{2,1},{3,2},{4,7},{5,4},{6,5},{7,6},{8,11},{9,8},{10,9... | collective-permute-start | bytes 786440 | tf_op jit(solution)/shard_map/ppermute | solution.py:374
  95.9 10.6 %collective-permute-done.2.refs_0_ = bf16[8,32,512]{2,1,0:T(8,128)(2,1)S(1)} collective-permute-done((bf16[8,32,512]{2,1,0:T(8,128)(2,1)S(1)}, bf16[8,32,512]{2,1,0:T(8,128)(2,1)S(1)}, u32[]{:S(2)}, u32[]{:S(2)}) %collective-permute-start.2) | collective-permute-done | bytes 262176 | tf_op jit(solution)/shard_map/ppermute | solution.py:374
  106.5 0.0 collective-permute-done.3.refs_1_
  106.5 0.3 collective-permute-done.4.refs_2_
  106.8 0.0 copy-done.3
  106.8 1.8 %space_sum.1 = bf16[8,32,512]{2,1,0:T(8,128)(2,1)} custom-call(bf16[4,8,32,512]{3,2,1,0:T(8,128)(2,1)} %get-tuple-element.16.keep_ref, bf16[4,8,32,512]{3,2,1,0:T(8,128)(2,1)} %copy-done.3, bf16[8,32,512]{2,1,0:T(8,128)(2,1)S(1)} %collective-permute-done.2.refs_0_, bf16[8,32,512]{2,1,0:T(8,128)(2,1)S(1)} %collective-permute-done.3.refs_1_, ...), custom_call_target="tpu_custom_call" | custom-call | tf_op jit(solution)/shard_map/space_sum/pallas_call | solution.py:319
  108.6 0.0 all-to-all-done.3
  108.6 5.0 %all-to-all-start.4 = ((bf16[8,32,512]{2,1,0:T(8,128)(2,1)}), bf16[8,32,512]{2,1,0:T(8,128)(2,1)S(1)}, u32[]{:S(2)}, u32[]{:S(2)}) async-start(bf16[8,32,512]{2,1,0:T(8,128)(2,1)} %space_sum.1), calls=%async_computation.4 | async-start | bytes 524288 | tf_op jit(solution)/shard_map/all_to_all | solution.py:347
  113.7 1.1 copy.27
  114.7 4.8 %all-to-all-done.4 = bf16[8,32,512]{2,1,0:T(8,128)(2,1)S(1)} async-done(((bf16[8,32,512]{2,1,0:T(8,128)(2,1)}), bf16[8,32,512]{2,1,0:T(8,128)(2,1)S(1)}, u32[]{:S(2)}, u32[]{:S(2)}) %all-to-all-start.4) | async-done | bytes 262176 | tf_op jit(solution)/shard_map/all_to_all | solution.py:347
  119.5 9.7 %all-gather = bf16[128,512]{1,0:T(8,128)(2,1)S(1)} all-gather(bf16[32,512]{1,0:T(8,128)(2,1)S(1)} %reduce_sum.21), channel_id=2, replica_groups=mesh['batch'=4,'tm'=8,'space'=4] {'batch'}, dimensions={0}, use_global_device_ids=true | all-gather | bytes 163840 | tf_op jit(solution)/shard_map/all_gather | solution.py:380
  129.3 0.7 copy.28
  (2 shorter events, 0.1 us)
Async XLA Ops:
  0.6 10.0 %copy-start.4 = (s32[1,2]{1,0:T(1,128)S(1)}, s32[1,2]{1,0:T(1,128)}, u32[]{:S(2)}) copy-start(s32[1,2]{1,0:T(1,128)} %param.12) | copy-start | bytes 28
  0.6 21.5 %copy-start.1 = (f32[1024]{0:T(1024)S(1)}, f32[1024]{0:T(1024)}, u32[]{:S(2)}) copy-start(f32[1024]{0:T(1024)} %param.13) | copy-start | bytes 12292
  0.6 21.5 %all-to-all-start = ((bf16[16,8,4,1024]{3,2,1,0:T(4,128)(2,1)}), bf16[16,8,4,1024]{3,2,1,0:T(4,128)(2,1)S(1)}, u32[]{:S(2)}, u32[]{:S(2)}) async-start(bf16[16,8,4,1024]{3,2,1,0:T(4,128)(2,1)} %bitcast.41), calls=%async_computation | async-start | bytes 2097152 | tf_op jit(solution)/shard_map/all_to_all | solution.py:355
  25.4 26.3 %all-to-all-start.2 = ((bf16[8,2,32,1024]{3,2,1,0:T(8,128)(2,1)}), bf16[8,2,32,1024]{3,2,1,0:T(8,128)(2,1)S(1)}, u32[]{:S(2)}, u32[]{:S(2)}) async-start(bf16[8,2,32,1024]{3,2,1,0:T(8,128)(2,1)} %bitcast.33), calls=%async_computation.2 | async-start | bytes 2097152 | tf_op jit(solution)/shard_map/all_to_all | solution.py:347
  31.3 9.7 %collective-permute-start = (bf16[4,32,1024]{2,1,0:T(8,128)(2,1)S(1)}, bf16[4,32,1024]{2,1,0:T(8,128)(2,1)S(1)}, u32[]{:S(2)}, u32[]{:S(2)}) collective-permute-start(bf16[4,32,1024]{2,1,0:T(8,128)(2,1)S(1)} %get-tuple-element.10), channel_id=1, source_target_pairs={{0,3},{1,2},{2,1},{3,0},{4,7},{5,6},{6,5},{7,4},{8,11},{9,10},{10,... | collective-permute-start | bytes 786440 | tf_op jit(solution)/shard_map/ppermute | solution.py:359
  41.0 17.0 %copy-start.5 = (s32[1,16]{1,0:T(1,128)S(1)}, s32[1,16]{1,0:T(1,128)}, u32[]{:S(2)}) copy-start(s32[1,16]{1,0:T(1,128)} %param.11) | copy-start | bytes 196
  41.0 29.5 %copy-start = (f32[1024]{0:T(1024)S(1)}, f32[1024]{0:T(1024)}, u32[]{:S(2)}) copy-start(f32[1024]{0:T(1024)} %param.16) | copy-start | bytes 12292
  51.7 18.9 %copy-start.2 = (bf16[8,2,32,1024]{3,2,1,0:T(8,128)(2,1)}, bf16[8,2,32,1024]{3,2,1,0:T(8,128)(2,1)S(1)}, u32[]{:S(2)}) copy-start(bf16[8,2,32,1024]{3,2,1,0:T(8,128)(2,1)S(1)} %all-to-all-done.2) | copy-start | bytes 3145732
  51.7 18.9 %all-to-all-start.1 = ((bf16[16,32,1024]{2,1,0:T(8,128)(2,1)}), bf16[16,32,1024]{2,1,0:T(8,128)(2,1)S(1)}, u32[]{:S(2)}, u32[]{:S(2)}) async-start(bf16[16,32,1024]{2,1,0:T(8,128)(2,1)} %bitcast.40), calls=%async_computation.1 | async-start | bytes 2097152 | tf_op jit(solution)/shard_map/all_to_all | solution.py:355
  82.3 8.0 %collective-permute-start.1 = (bf16[4,8,32,512]{3,2,1,0:T(8,128)(2,1)S(1)}, bf16[4,8,32,512]{3,2,1,0:T(8,128)(2,1)S(1)}, u32[]{:S(2)}, u32[]{:S(2)}) collective-permute-start(bf16[4,8,32,512]{3,2,1,0:T(8,128)(2,1)S(1)} %get-tuple-element.17), channel_id=1, source_target_pairs={{0,32},{32,0},{64,96},{96,64},{1,33},{33,1},{65,97},{97,65},{2,34}... | collective-permute-start | bytes 3145736 | tf_op jit(solution)/shard_map/ppermute | solution.py:371
  86.4 22.2 %all-to-all-start.3 = ((bf16[8,2,32,1024]{3,2,1,0:T(8,128)(2,1)}), bf16[8,2,32,1024]{3,2,1,0:T(8,128)(2,1)S(1)}, u32[]{:S(2)}, u32[]{:S(2)}) async-start(bf16[8,2,32,1024]{3,2,1,0:T(8,128)(2,1)} %bitcast.42), calls=%async_computation.3 | async-start | bytes 2097152 | tf_op jit(solution)/shard_map/all_to_all | solution.py:347
  90.2 16.6 %copy-start.3 = (bf16[4,8,32,512]{3,2,1,0:T(8,128)(2,1)}, bf16[4,8,32,512]{3,2,1,0:T(8,128)(2,1)S(1)}, u32[]{:S(2)}) copy-start(bf16[4,8,32,512]{3,2,1,0:T(8,128)(2,1)S(1)} %collective-permute-done.1.got_ref) | copy-start | bytes 3145732
  92.0 14.5 %collective-permute-start.2 = (bf16[8,32,512]{2,1,0:T(8,128)(2,1)S(1)}, bf16[8,32,512]{2,1,0:T(8,128)(2,1)S(1)}, u32[]{:S(2)}, u32[]{:S(2)}) collective-permute-start(bf16[8,32,512]{2,1,0:T(8,128)(2,1)S(1)} %get-tuple-element.26), channel_id=1, source_target_pairs={{0,1},{1,2},{2,3},{3,0},{4,5},{5,6},{6,7},{7,4},{8,9},{9,10},{10,1... | collective-permute-start | bytes 786440 | tf_op jit(solution)/shard_map/ppermute | solution.py:374
  93.4 13.1 %collective-permute-start.3 = (bf16[8,32,512]{2,1,0:T(8,128)(2,1)S(1)}, bf16[8,32,512]{2,1,0:T(8,128)(2,1)S(1)}, u32[]{:S(2)}, u32[]{:S(2)}) collective-permute-start(bf16[8,32,512]{2,1,0:T(8,128)(2,1)S(1)} %get-tuple-element.25), channel_id=1, source_target_pairs={{0,2},{1,3},{2,0},{3,1},{4,6},{5,7},{6,4},{7,5},{8,10},{9,11},{10,... | collective-permute-start | bytes 786440 | tf_op jit(solution)/shard_map/ppermute | solution.py:374
  93.4 13.4 %collective-permute-start.4 = (bf16[8,32,512]{2,1,0:T(8,128)(2,1)S(1)}, bf16[8,32,512]{2,1,0:T(8,128)(2,1)S(1)}, u32[]{:S(2)}, u32[]{:S(2)}) collective-permute-start(bf16[8,32,512]{2,1,0:T(8,128)(2,1)S(1)} %get-tuple-element.24), channel_id=1, source_target_pairs={{0,3},{1,0},{2,1},{3,2},{4,7},{5,4},{6,5},{7,6},{8,11},{9,8},{10,9... | collective-permute-start | bytes 786440 | tf_op jit(solution)/shard_map/ppermute | solution.py:374
  108.6 10.9 %all-to-all-start.4 = ((bf16[8,32,512]{2,1,0:T(8,128)(2,1)}), bf16[8,32,512]{2,1,0:T(8,128)(2,1)S(1)}, u32[]{:S(2)}, u32[]{:S(2)}) async-start(bf16[8,32,512]{2,1,0:T(8,128)(2,1)} %space_sum.1), calls=%async_computation.4 | async-start | bytes 524288 | tf_op jit(solution)/shard_map/all_to_all | solution.py:347

commit v8 on v7

--- a/solution.py
+++ b/solution.py
@@ -36,42 +36,25 @@
 HBM = pl.BlockSpec(memory_space=pltpu.HBM)
 
 
-def norm_kernel(info_ref, x_ref, gain_ref, tok_out, normed_ref, edge_ref, tok_ref, sem):
-    times, parities, rows, cols, _ = x_ref.shape
-    half = info_ref[1]
+def edge_kernel(info_ref, x_ref, gain_ref, edge_ref):
+    times, _, rows, cols, _ = x_ref.shape
+    start = jnp.where(info_ref[1] == 0, rows - HALO, 0)
     gain = gain_ref[...]
-    for o in range(parities):
-        first = jnp.where(half == 0, 1 - o, o) * rows
-
-        def one_row(r, carry):
-            for t in range(times):
-                x = x_ref[t, o, r]
-                y = normalized(x.astype(F32), gain).astype(BF)
-                tok_ref[first + r, t * cols:(t + 1) * cols, :] = x
-                normed_ref[first + r, t * cols:(t + 1) * cols, :] = y
-            return carry
-
-        lax.fori_loop(0, rows, one_row, 0)
-        done = pl.ds(first, rows)
-        pltpu.make_async_copy(tok_ref.at[done], tok_out.at[done], sem.at[o]).start()
-    start = jnp.where(half == 0, parities * rows - HALO, 0)
-    edge_ref[...] = normed_ref[pl.ds(start, HALO)]
-    for o in range(parities):
-        done = pl.ds(jnp.where(half == 0, 1 - o, o) * rows, rows)
-        pltpu.make_async_copy(tok_ref.at[done], tok_out.at[done], sem.at[o]).wait()
-
-
-def norm_reorder(info, arrived, gain):
-    times, parities, rows, cols, _ = arrived.shape
-    shape = (parities * rows, times * cols, D)
+    for r in range(HALO):
+        for t in range(times):
+            y = normalized(x_ref[t, 0, start + r].astype(F32), gain)
+            edge_ref[r, t * cols:(t + 1) * cols, :] = y.astype(BF)
+
+
+def edge_norm(info, arrived, gain):
+    times, _, _, cols, _ = arrived.shape
     return pl.pallas_call(
-        norm_kernel,
+        edge_kernel,
         in_specs=[SMEM, VMEM, VMEM],
-        out_specs=[HBM, VMEM, VMEM],
-        out_shape=[pltpu.HBM(shape, BF), pltpu.VMEM(shape, BF), pltpu.VMEM((HALO,) + shape[1:], BF)],
-        scratch_shapes=[pltpu.VMEM(shape, BF), pltpu.SemaphoreType.DMA((2,))],
-        compiler_params=pltpu.CompilerParams(vmem_limit_bytes=8 * 2**20),
-        name="norm_reorder",
+        out_specs=VMEM,
+        out_shape=pltpu.VMEM((HALO, times * cols, D), BF),
+        compiler_params=pltpu.CompilerParams(vmem_limit_bytes=4 * 2**20),
+        name="edge_norm",
     )(info, in_vmem(arrived), gain.reshape(1, D))
 
 
@@ -79,39 +62,64 @@
     return [pltpu.make_async_copy(w_ref.at[:, c * D:(c + 1) * D], buf.at[i], sems.at[i]) for i, c in enumerate(columns)]
 
 
-QKV_PIECE = 512
-
-
-def qkv_kernel(x_ref, w_ref, out_ref, buf, y_ref, sems, out_sems):
+QKV_PIECE = 1024
+
+
+def qkv_kernel(info_ref, arrived_ref, gain_ref, w_ref, out_ref, tok_out, x_ref, tok_ref, buf, y_ref, sems, out_sems, tok_sems):
     pieces = buf.shape[0]
     copies = [pltpu.make_async_copy(w_ref.at[:, i * QKV_PIECE:(i + 1) * QKV_PIECE], buf.at[i], sems.at[i])
               for i in range(pieces)]
     for c in copies:
         c.start()
+    times, parities, rows, cols, _ = arrived_ref.shape
+    wide = times * cols
+    half = info_ref[1]
+    gain = gain_ref[...]
+    kept = []
+    for o in range(parities):
+        first = jnp.where(half == 0, 1 - o, o) * rows
+
+        def one_row(r, carry):
+            for t in range(times):
+                x = arrived_ref[t, o, r]
+                y = normalized(x.astype(F32), gain).astype(BF)
+                tok_ref[first + r, t * cols:(t + 1) * cols, :] = x
+                x_ref[first + r, t * cols:(t + 1) * cols, :] = y
+            return carry
+
+        lax.fori_loop(0, rows, one_row, 0)
+        done = pl.ds(first, rows)
+        kept.append(pltpu.make_async_copy(tok_ref.at[done], tok_out.at[done], tok_sems.at[o]))
+        kept[o].start()
     sent = []
+    x = x_ref[...].reshape(parities * rows * wide, D)
     for i, c in enumerate(copies):
         c.wait()
-        y_ref[i] = jnp.dot(x_ref[...], buf[i], preferred_element_type=F32).astype(BF)
+        y_ref[i] = jnp.dot(x, buf[i], preferred_element_type=F32).astype(BF)
         third, at = divmod(i * QKV_PIECE, D)
         sent.append(pltpu.make_async_copy(y_ref.at[i], out_ref.at[third, :, at:at + QKV_PIECE], out_sems.at[i]))
         sent[i].start()
-    for c in sent:
-        c.wait()
-
-
-def qkv_own(x, heads):
-    tokens = x.shape[0]
+    for c in sent + kept:
+        c.wait()
+
+
+def qkv_own(info, arrived, gain, heads):
+    times, parities, rows, cols, _ = arrived.shape
+    shape = (parities * rows, times * cols, D)
+    tokens = shape[0] * shape[1]
     pieces = 3 * D // QKV_PIECE
     return pl.pallas_call(
         qkv_kernel,
-        in_specs=[VMEM, HBM],
-        out_specs=HBM,
-        out_shape=pltpu.HBM((3, tokens, D), BF),
-        scratch_shapes=[pltpu.VMEM((pieces, D, QKV_PIECE), BF), pltpu.VMEM((pieces, tokens, QKV_PIECE), BF),
-                        pltpu.SemaphoreType.DMA((pieces,)), pltpu.SemaphoreType.DMA((pieces,))],
-        compiler_params=pltpu.CompilerParams(vmem_limit_bytes=24 * 2**20),
+        in_specs=[SMEM, VMEM, VMEM, HBM],
+        out_specs=[HBM, HBM],
+        out_shape=[pltpu.HBM((3, tokens, D), BF), pltpu.HBM(shape, BF)],
+        scratch_shapes=[pltpu.VMEM(shape, BF), pltpu.VMEM(shape, BF),
+                        pltpu.VMEM((pieces, D, QKV_PIECE), BF), pltpu.VMEM((pieces, tokens, QKV_PIECE), BF),
+                        pltpu.SemaphoreType.DMA((pieces,)), pltpu.SemaphoreType.DMA((pieces,)),
+                        pltpu.SemaphoreType.DMA((2,))],
+        compiler_params=pltpu.CompilerParams(vmem_limit_bytes=28 * 2**20),
         name="qkv_own",
-    )(in_vmem(x), in_hbm(heads))
+    )(info, in_vmem(arrived), gain.reshape(1, D), in_hbm(heads))
 
 
 def staged_attention(items):
@@ -139,7 +147,7 @@
 
 
 SPATIAL_STAGE = 4
-TEMPORAL_STAGE = 8
+TEMPORAL_STAGE = 16
 
 
 def spatial_kernel(info_ref, halo_ref, qkv_ref, tok_ref, w_ref, wm_ref, mid_out,
@@ -153,7 +161,7 @@
     for i, buf in ((1, k_ref), (2, v_ref)):
         own.append(pltpu.make_async_copy(qkv_ref.at[i], buf.at[edge:edge + tokens], sems.at[2 + i]))
     last = [pltpu.make_async_copy(wm_ref, wm_buf, sems.at[5]), pltpu.make_async_copy(tok_ref, tok_buf, sems.at[6])]
-    for c in weights + own + last:
+    for c in own + weights + last:
         c.start()
     blocks, n, extent = bias_ref.shape
     qrow = lax.broadcasted_iota(jnp.int32, (n, extent), 0) // cols
@@ -162,6 +170,23 @@
     for j in range(blocks):
         at = krow + (j * HALO + half * rows)
         bias_ref[j] = jnp.where(near & (at >= 0) & (at < 2 * rows), 0.0, MASKED)
+    for c in own:
+        c.wait()
+
+    def attend(chosen):
+        items = []
+        for pair in range(PAIRS):
+            at = slice(pair * WIDE, (pair + 1) * WIDE)
+            for j in chosen:
+                keys = slice(j * edge, j * edge + extent)
+                mine = slice(j * n, (j + 1) * n)
+                items.append((reader(q_ref, mine, at), reader(k_ref, keys, at), reader(v_ref, keys, at),
+                              reader(bias_ref, j), ctx_ref, (mine, at)))
+        for i in range(0, len(items), SPATIAL_STAGE):
+            staged_attention(items[i:i + SPATIAL_STAGE])
+
+    inner = [j for j in range(blocks) if j * edge >= edge and j * edge + extent <= edge + tokens]
+    attend(inner)
     there = jnp.where(half == 0, edge + tokens, 0)
     empty = jnp.where(half == 0, 0, edge + tokens)
     halo = halo_ref[...].reshape(edge, D)
@@ -170,18 +195,7 @@
         side = jnp.dot(halo, wkv_buf[w], preferred_element_type=F32).astype(BF)
         buf[pl.ds(pl.multiple_of(there, edge), edge)] = side
         buf[pl.ds(pl.multiple_of(empty, edge), edge)] = jnp.zeros_like(side)
-    for c in own:
-        c.wait()
-    items = []
-    for pair in range(PAIRS):
-        at = slice(pair * WIDE, (pair + 1) * WIDE)
-        for j in range(blocks):
-            keys = slice(j * edge, j * edge + extent)
-            mine = slice(j * n, (j + 1) * n)
-            items.append((reader(q_ref, mine, at), reader(k_ref, keys, at), reader(v_ref, keys, at),
-                          reader(bias_ref, j), ctx_ref, (mine, at)))
-    for i in range(0, len(items), SPATIAL_STAGE):
-        staged_attention(items[i:i + SPATIAL_STAGE])
+    attend([j for j in range(blocks) if j not in inner])
     for c in last:
         c.wait()
     sent = []
@@ -222,8 +236,8 @@
 
 
 def temporal_kernel(core_ref, mid_ref, order_q_ref, order_k_ref, gain_ref, cot_ref, w_ref, wm_ref,
-                    out_hbm, send_ref, keep_hbm,
-                    out_ref, keep_ref, wqkv_buf, wm_buf, cot_buf, normed_ref, q_ref, k_ref, v_ref, ctx_ref, cotb_ref, sems):
+                    out_hbm, send_ref, keep_ref,
+                    out_ref, wqkv_buf, wm_buf, cot_buf, normed_ref, q_ref, k_ref, v_ref, ctx_ref, cotb_ref, sems):
     frames, cols, _ = mid_ref.shape
     groups = cols // GROUP
     n = frames * GROUP
@@ -267,8 +281,6 @@
             for t in range(times):
                 row = (t * spaces + s) * block
                 ref[slot, t] = grad[row:row + block]
-    kept = pltpu.make_async_copy(keep_ref, keep_hbm, sems.at[5])
-    kept.start()
     copies[4].wait()
     y = jnp.dot(ctx_ref[...], wm_buf[...], preferred_element_type=F32)
     for g in range(groups):
@@ -277,7 +289,6 @@
     done = pltpu.make_async_copy(out_ref, out_hbm, sems.at[6])
     done.start()
     done.wait()
-    kept.wait()
 
 
 def temporal_phase(core, mid, order, gain, cot, heads, merge, spaces, times):
@@ -290,9 +301,9 @@
     return pl.pallas_call(
         temporal_kernel,
         in_specs=[SMEM] + [VMEM] * 4 + [HBM] * 3,
-        out_specs=[HBM, VMEM, HBM],
-        out_shape=[pltpu.HBM((frames, cols, D), BF), pltpu.VMEM(part, BF), pltpu.HBM(part, BF)],
-        scratch_shapes=[pltpu.VMEM((frames, cols, D), BF), pltpu.VMEM(part, BF), pltpu.VMEM((3, D, D), BF), pltpu.VMEM((D, D), BF), pltpu.VMEM((frames, cols, D), BF)]
+        out_specs=[HBM, VMEM, VMEM],
+        out_shape=[pltpu.HBM((frames, cols, D), BF), pltpu.VMEM(part, BF), pltpu.VMEM(part, BF)],
+        scratch_shapes=[pltpu.VMEM((frames, cols, D), BF), pltpu.VMEM((3, D, D), BF), pltpu.VMEM((D, D), BF), pltpu.VMEM((frames, cols, D), BF)]
         + [pltpu.VMEM((tokens, D), BF)] * 6
         + [pltpu.SemaphoreType.DMA((7,))],
         compiler_params=pltpu.CompilerParams(vmem_limit_bytes=40 * 2**20),
@@ -343,7 +354,6 @@
     _, frame_count, rows, cols, _ = clip_tokens.shape
     frames = frame_count // tm
     wide = tm * cols
-    tokens = rows * wide
     exchange = lambda v, axis: lax.all_to_all(v, axis, split_axis=0, concat_axis=0, tiled=True)
 
     here = lax.axis_index("space").astype(jnp.int32)
@@ -355,11 +365,12 @@
     swap = lambda v: lax.all_to_all(v, ("tm", "space"), split_axis=0, concat_axis=0, axis_index_groups=halves, tiled=True)
     arrived = swap(clip_tokens.reshape(frame_count, rows, cols, D))
     cot = cotangent.reshape(frames, rows, wide, D).swapaxes(0, 1)
-    tok, normed, edge_rows = norm_reorder(info, arrived.reshape(tm, frames, rows, cols, D), spatial_gain)
+    arrived = arrived.reshape(tm, frames, rows, cols, D)
+    edge_rows = edge_norm(info, arrived, spatial_gain)
     halo = lax.ppermute(edge_rows, "space", [(i, space - 1 - i) for i in range(space)])
-    cot, normed = lax.optimization_barrier((cot, normed))
+    cot, arrived = lax.optimization_barrier((cot, arrived))
     cot = exchange(cot, "tm")
-    qkv = qkv_own(normed.reshape(frames * tokens, D), spatial_heads)
+    qkv, tok = qkv_own(info, arrived, spatial_gain, spatial_heads)
     middle = spatial_phase(info, halo, qkv, tok, spatial_heads, spatial_merge)
     mid = swap(middle.reshape(frame_count, wide, D))
     core = jnp.stack([lax.axis_index("batch") & 1, here]).astype(jnp.int32)

time: 131 us -> 130 us (level)
  Pallas kernels: 33.9 us -> 31.8 us
  waiting for transfers between devices: 37.4 us -> 39.3 us
    all_to_all x2, waiting for transfers between devices: 21.7 us -> 23.7 us  [per_device(): lax.all_to_all(v, ('tm', 'space'), split_axis=0, concat_axis=0, axis_inde...]
    pallas_call x2, Pallas kernels: 9.76 us -> 8.25 us  [the longest x1 7.49 us: qkv_own(): pl.pallas_call(qkv_kernel, in_specs=[SMEM, VMEM, VMEM, HBM], out_specs=[H...]
  transfers between devices with their start and end apart: 10 -> 10, of which waited for: 5 -> 5; matrix products, arithmetic and copies ran while one was open for 5% -> 4% of each run, Pallas kernels for 15% -> 16%
where the time goes in v8:
time: 130 us
  starting transfers between devices  40.1 us (31%)
  waiting for transfers between devices  39.3 us (30%)
  Pallas kernels  31.8 us (24%)
  blocking collectives  9.7 us (7%)
  local copies, waits for them, and re-layouts  4.97 us (4%)
  between operations  2.05 us (2%)
  other arithmetic  1.58 us (1%)
    all_to_all x2, waiting for transfers between devices, per_device(): lax.all_to_all(v, ('tm', 'space'), split_axis=0, concat_axis=0, axis_inde...  23.7 us
    all_to_all x3, starting transfers between devices, per_device(): lax.all_to_all(v, axis, split_axis=0, concat_axis=0, tiled=True)  14.7 us
    all_to_all x2, starting transfers between devices, per_device(): lax.all_to_all(v, ('tm', 'space'), split_axis=0, concat_axis=0, axis_inde...  14 us
    pallas_call x1, Pallas kernels, temporal_phase(): pl.pallas_call(temporal_kernel, in_specs=[SMEM] + [VMEM] * 4 + [HBM] * 3,...  11.4 us
    ppermute x3, waiting for transfers between devices, per_device(): lax.ppermute(chip[k - 1].astype(BF), 'space', [(i, (i + k) % space) for i...  10.9 us
    pallas_call x1, Pallas kernels, spatial_phase(): pl.pallas_call(spatial_kernel, in_specs=[SMEM, VMEM, HBM, HBM, HBM, HBM],...  10.3 us
    all_gather x1, blocking collectives, per_device(): lax.all_gather(over_tm, 'batch').astype(F32)  9.7 us
    pallas_call x1, Pallas kernels, qkv_own(): pl.pallas_call(qkv_kernel, in_specs=[SMEM, VMEM, VMEM, HBM], out_specs=[H...  7.49 us
  transfers between devices with their start and end apart: 10, of which 5 were waited for; matrix products, arithmetic and copies ran while one was open for 4% of the time, Pallas kernels for 16%

profile of v8, /device:TPU:1, one launch (start us, length us, event | category | flops | bytes accessed | tf_op | source)
XLA Modules:
  0.0 129.6 jit_solution(5096414167101579925)
XLA Ops:
  0.6 0.0 copy-start.4
  0.6 0.0 copy-start.1
  0.6 7.6 %all-to-all-start = ((bf16[16,8,4,1024]{3,2,1,0:T(4,128)(2,1)}), bf16[16,8,4,1024]{3,2,1,0:T(4,128)(2,1)S(1)}, u32[]{:S(2)}, u32[]{:S(2)}) async-start(bf16[16,8,4,1024]{3,2,1,0:T(4,128)(2,1)} %bitcast.41), calls=%async_computation | async-start | bytes 2097152 | tf_op jit(solution)/shard_map/all_to_all | solution.py:365
  8.3 2.3 %copy.30 = bf16[1,2,8,32,1024]{4,3,1,2,0:T(8,128)(2,1)} copy(bf16[1,2,8,32,1024]{4,3,2,1,0:T(8,128)(2,1)} %param.19) | data formatting | bytes 2097152 | tf_op args[9]
  10.6 11.5 %all-to-all-done = bf16[16,8,4,1024]{3,2,1,0:T(4,128)(2,1)S(1)} async-done(((bf16[16,8,4,1024]{3,2,1,0:T(4,128)(2,1)}), bf16[16,8,4,1024]{3,2,1,0:T(4,128)(2,1)S(1)}, u32[]{:S(2)}, u32[]{:S(2)}) %all-to-all-start) | async-done | bytes 1048608 | tf_op jit(solution)/shard_map/all_to_all | solution.py:365
  22.1 5.8 %all-to-all-start.2 = ((bf16[8,2,32,1024]{3,2,1,0:T(8,128)(2,1)}), bf16[8,2,32,1024]{3,2,1,0:T(8,128)(2,1)S(1)}, u32[]{:S(2)}, u32[]{:S(2)}) async-start(bf16[8,2,32,1024]{3,2,1,0:T(8,128)(2,1)} %bitcast.32), calls=%async_computation.2 | async-start | bytes 2097152 | tf_op jit(solution)/shard_map/all_to_all | solution.py:357
  27.9 0.0 copy-done.4
  27.9 0.7 fusion.3
  29.8 0.1 pad_add_fusion.1.info_ref
  29.9 0.0 copy-done.1
  29.9 0.8 edge_norm.1
  30.7 3.4 %collective-permute-start = (bf16[4,32,1024]{2,1,0:T(8,128)(2,1)S(1)}, bf16[4,32,1024]{2,1,0:T(8,128)(2,1)S(1)}, u32[]{:S(2)}, u32[]{:S(2)}) collective-permute-start(bf16[4,32,1024]{2,1,0:T(8,128)(2,1)S(1)} %edge_norm.1), channel_id=1, source_target_pairs={{0,3},{1,2},{2,1},{3,0},{4,7},{5,6},{6,5},{7,4},{8,11},{9,10},{10,... | collective-permute-start | bytes 786440 | tf_op jit(solution)/shard_map/ppermute | solution.py:370
  34.1 7.5 %qkv_own.1 = (bf16[3,512,1024]{2,1,0:T(8,128)(2,1)}, bf16[16,32,1024]{2,1,0:T(8,128)(2,1)}) custom-call(s32[2]{0:T(128)S(1)} %pad_add_fusion.1.info_ref, bf16[8,2,8,4,1024]{4,3,2,1,0:T(4,128)(2,1)S(1)} %bitcast.34, f32[1,1024]{1,0:T(1,128)S(1)} %bitcast.36, bf16[1024,3072]{1,0:T(8,128)(2,1)} %w_ref.4), custom_call_target="tpu_custom_call" | custom-call | tf_op jit(solution)/shard_map/qkv_own/pallas_call | solution.py:111
  41.6 0.0 collective-permute-done.halo_ref
  41.6 0.0 copy-start.5
  41.6 0.0 copy-start.2
  41.6 10.3 %spatial_phase.1 = bf16[8,2,32,1024]{3,2,1,0:T(8,128)(2,1)} custom-call(s32[2]{0:T(128)S(1)} %pad_add_fusion.1.info_ref, bf16[4,32,1024]{2,1,0:T(8,128)(2,1)S(1)} %collective-permute-done.halo_ref, bf16[3,512,1024]{2,1,0:T(8,128)(2,1)} %get-tuple-element.10.qkv_ref, bf16[16,32,1024]{2,1,0:T(8,128)(2,1)} %get-tuple-element.11.tok_ref, ...), custom_call_target="tpu_custom_call" | custom-call | tf_op jit(solution)/shard_map/spatial_phase/pallas_call | solution.py:219
  52.0 0.0 all-to-all-done.2
  52.0 0.0 copy-start.3
  52.0 6.3 %all-to-all-start.1 = ((bf16[16,32,1024]{2,1,0:T(8,128)(2,1)}), bf16[16,32,1024]{2,1,0:T(8,128)(2,1)S(1)}, u32[]{:S(2)}, u32[]{:S(2)}) async-start(bf16[16,32,1024]{2,1,0:T(8,128)(2,1)} %bitcast.40), calls=%async_computation.1 | async-start | bytes 2097152 | tf_op jit(solution)/shard_map/all_to_all | solution.py:365
  58.3 0.0 copy-done.5
  58.3 0.1 broadcast_in_dim.3
  58.4 0.1 reshape_reshape.8.order_q_ref
  58.5 0.1 reshape_reshape.7.order_k_ref
  58.6 0.1 pad_add_fusion.core_ref
  58.7 12.2 %all-to-all-done.1.mid_ref = bf16[16,32,1024]{2,1,0:T(8,128)(2,1)S(1)} async-done(((bf16[16,32,1024]{2,1,0:T(8,128)(2,1)}), bf16[16,32,1024]{2,1,0:T(8,128)(2,1)S(1)}, u32[]{:S(2)}, u32[]{:S(2)}) %all-to-all-start.1) | async-done | bytes 1048608 | tf_op jit(solution)/shard_map/all_to_all | solution.py:365
  70.8 0.0 copy-done.3
  70.8 0.0 copy-done.2
  70.8 11.4 %temporal_phase.1 = (bf16[16,32,1024]{2,1,0:T(8,128)(2,1)}, bf16[4,8,32,512]{3,2,1,0:T(8,128)(2,1)S(1)}, bf16[4,8,32,512]{3,2,1,0:T(8,128)(2,1)S(1)}) custom-call(s32[2]{0:T(128)S(1)} %pad_add_fusion.core_ref, bf16[16,32,1024]{2,1,0:T(8,128)(2,1)S(1)} %all-to-all-done.1.mid_ref, s32[128,1]{1,0:T(8,128)S(1)} %reshape_reshape.8.order_q_ref, ...), custom_call_target="tpu_custom_call" | custom-call | tf_op jit(solution)/shard_map/temporal_phase/pallas_call | solution.py:301
  82.2 0.0 copy-start
  82.3 4.2 %collective-permute-start.1 = (bf16[4,8,32,512]{3,2,1,0:T(8,128)(2,1)S(1)}, bf16[4,8,32,512]{3,2,1,0:T(8,128)(2,1)}, u32[]{:S(2)}, u32[]{:S(2)}) collective-permute-start(bf16[4,8,32,512]{3,2,1,0:T(8,128)(2,1)S(1)} %get-tuple-element.15), channel_id=1, source_target_pairs={{0,32},{32,0},{64,96},{96,64},{1,33},{33,1},{65,97},{97,65},{2,34}... | collective-permute-start | bytes 3145736 | tf_op jit(solution)/shard_map/ppermute | solution.py:382
  86.4 3.8 %all-to-all-start.3 = ((bf16[8,2,32,1024]{3,2,1,0:T(8,128)(2,1)}), bf16[8,2,32,1024]{3,2,1,0:T(8,128)(2,1)S(1)}, u32[]{:S(2)}, u32[]{:S(2)}) async-start(bf16[8,2,32,1024]{3,2,1,0:T(8,128)(2,1)} %bitcast.42), calls=%async_computation.3 | async-start | bytes 2097152 | tf_op jit(solution)/shard_map/all_to_all | solution.py:357
  90.3 0.0 collective-permute-done.1.got_ref
  90.3 1.4 %fusion.2 = (bf16[8,32,512]{2,1,0:T(8,128)(2,1)S(1)}, bf16[8,32,512]{2,1,0:T(8,128)(2,1)S(1)}, bf16[8,32,512]{2,1,0:T(8,128)(2,1)S(1)}) fusion(bf16[4,8,32,512]{3,2,1,0:T(8,128)(2,1)} %collective-permute-done.1.got_ref, bf16[4,8,32,512]{3,2,1,0:T(8,128)(2,1)S(1)} %get-tuple-element.14.keep_ref), kind=kLoop, calls=%fused_computation.6 | loop fusion | flops 1572864 | bytes 2359296 | tf_op jit(solution)/shard_map/convert_element_type | solution.py:385
  91.6 1.4 %collective-permute-start.2 = (bf16[8,32,512]{2,1,0:T(8,128)(2,1)S(1)}, bf16[8,32,512]{2,1,0:T(8,128)(2,1)S(1)}, u32[]{:S(2)}, u32[]{:S(2)}) collective-permute-start(bf16[8,32,512]{2,1,0:T(8,128)(2,1)S(1)} %get-tuple-element.24), channel_id=1, source_target_pairs={{0,1},{1,2},{2,3},{3,0},{4,5},{5,6},{6,7},{7,4},{8,9},{9,10},{10,1... | collective-permute-start | bytes 786440 | tf_op jit(solution)/shard_map/ppermute | solution.py:385
  93.1 0.0 collective-permute-start.3
  93.1 2.5 %collective-permute-start.4 = (bf16[8,32,512]{2,1,0:T(8,128)(2,1)S(1)}, bf16[8,32,512]{2,1,0:T(8,128)(2,1)S(1)}, u32[]{:S(2)}, u32[]{:S(2)}) collective-permute-start(bf16[8,32,512]{2,1,0:T(8,128)(2,1)S(1)} %get-tuple-element.22), channel_id=1, source_target_pairs={{0,3},{1,0},{2,1},{3,2},{4,7},{5,4},{6,5},{7,6},{8,11},{9,8},{10,9... | collective-permute-start | bytes 786440 | tf_op jit(solution)/shard_map/ppermute | solution.py:385
  95.5 10.6 %collective-permute-done.2.refs_0_ = bf16[8,32,512]{2,1,0:T(8,128)(2,1)S(1)} collective-permute-done((bf16[8,32,512]{2,1,0:T(8,128)(2,1)S(1)}, bf16[8,32,512]{2,1,0:T(8,128)(2,1)S(1)}, u32[]{:S(2)}, u32[]{:S(2)}) %collective-permute-start.2) | collective-permute-done | bytes 262176 | tf_op jit(solution)/shard_map/ppermute | solution.py:385
  106.1 0.0 collective-permute-done.3.refs_1_
  106.1 0.3 collective-permute-done.4.refs_2_
  106.4 0.0 copy-done
  106.4 1.8 %space_sum.1 = bf16[8,32,512]{2,1,0:T(8,128)(2,1)} custom-call(bf16[4,8,32,512]{3,2,1,0:T(8,128)(2,1)} %copy-done, bf16[4,8,32,512]{3,2,1,0:T(8,128)(2,1)} %collective-permute-done.1.got_ref, bf16[8,32,512]{2,1,0:T(8,128)(2,1)S(1)} %collective-permute-done.2.refs_0_, bf16[8,32,512]{2,1,0:T(8,128)(2,1)S(1)} %collective-permute-done.3.refs_1_, ...), custom_call_target="tpu_custom_call" | custom-call | tf_op jit(solution)/shard_map/space_sum/pallas_call | solution.py:330
  108.3 0.0 all-to-all-done.3
  108.3 5.0 %all-to-all-start.4 = ((bf16[8,32,512]{2,1,0:T(8,128)(2,1)}), bf16[8,32,512]{2,1,0:T(8,128)(2,1)S(1)}, u32[]{:S(2)}, u32[]{:S(2)}) async-start(bf16[8,32,512]{2,1,0:T(8,128)(2,1)} %space_sum.1), calls=%async_computation.4 | async-start | bytes 524288 | tf_op jit(solution)/shard_map/all_to_all | solution.py:357
  113.3 1.1 copy.27
  114.4 4.8 %all-to-all-done.4 = bf16[8,32,512]{2,1,0:T(8,128)(2,1)S(1)} async-done(((bf16[8,32,512]{2,1,0:T(8,128)(2,1)}), bf16[8,32,512]{2,1,0:T(8,128)(2,1)S(1)}, u32[]{:S(2)}, u32[]{:S(2)}) %all-to-all-start.4) | async-done | bytes 262176 | tf_op jit(solution)/shard_map/all_to_all | solution.py:357
  119.2 9.7 %all-gather = bf16[128,512]{1,0:T(8,128)(2,1)S(1)} all-gather(bf16[32,512]{1,0:T(8,128)(2,1)S(1)} %reduce_sum.21), channel_id=2, replica_groups=mesh['batch'=4,'tm'=8,'space'=4] {'batch'}, dimensions={0}, use_global_device_ids=true | all-gather | bytes 163840 | tf_op jit(solution)/shard_map/all_gather | solution.py:391
  128.9 0.7 copy.28
  (2 shorter events, 0.1 us)
Async XLA Ops:
  0.6 27.3 %copy-start.4 = (s32[1,2]{1,0:T(1,128)S(1)}, s32[1,2]{1,0:T(1,128)}, u32[]{:S(2)}) copy-start(s32[1,2]{1,0:T(1,128)} %param.12) | copy-start | bytes 28
  0.6 29.3 %copy-start.1 = (f32[1024]{0:T(1024)S(1)}, f32[1024]{0:T(1024)}, u32[]{:S(2)}) copy-start(f32[1024]{0:T(1024)} %param.13) | copy-start | bytes 12292
  0.6 21.5 %all-to-all-start = ((bf16[16,8,4,1024]{3,2,1,0:T(4,128)(2,1)}), bf16[16,8,4,1024]{3,2,1,0:T(4,128)(2,1)S(1)}, u32[]{:S(2)}, u32[]{:S(2)}) async-start(bf16[16,8,4,1024]{3,2,1,0:T(4,128)(2,1)} %bitcast.41), calls=%async_computation | async-start | bytes 2097152 | tf_op jit(solution)/shard_map/all_to_all | solution.py:365
  22.1 29.9 %all-to-all-start.2 = ((bf16[8,2,32,1024]{3,2,1,0:T(8,128)(2,1)}), bf16[8,2,32,1024]{3,2,1,0:T(8,128)(2,1)S(1)}, u32[]{:S(2)}, u32[]{:S(2)}) async-start(bf16[8,2,32,1024]{3,2,1,0:T(8,128)(2,1)} %bitcast.32), calls=%async_computation.2 | async-start | bytes 2097152 | tf_op jit(solution)/shard_map/all_to_all | solution.py:357
  30.7 10.9 %collective-permute-start = (bf16[4,32,1024]{2,1,0:T(8,128)(2,1)S(1)}, bf16[4,32,1024]{2,1,0:T(8,128)(2,1)S(1)}, u32[]{:S(2)}, u32[]{:S(2)}) collective-permute-start(bf16[4,32,1024]{2,1,0:T(8,128)(2,1)S(1)} %edge_norm.1), channel_id=1, source_target_pairs={{0,3},{1,2},{2,1},{3,0},{4,7},{5,6},{6,5},{7,4},{8,11},{9,10},{10,... | collective-permute-start | bytes 786440 | tf_op jit(solution)/shard_map/ppermute | solution.py:370
  41.6 16.7 %copy-start.5 = (s32[1,16]{1,0:T(1,128)S(1)}, s32[1,16]{1,0:T(1,128)}, u32[]{:S(2)}) copy-start(s32[1,16]{1,0:T(1,128)} %param.11) | copy-start | bytes 196
  41.6 29.2 %copy-start.2 = (f32[1024]{0:T(1024)S(1)}, f32[1024]{0:T(1024)}, u32[]{:S(2)}) copy-start(f32[1024]{0:T(1024)} %param.16) | copy-start | bytes 12292
  52.0 18.9 %copy-start.3 = (bf16[8,2,32,1024]{3,2,1,0:T(8,128)(2,1)}, bf16[8,2,32,1024]{3,2,1,0:T(8,128)(2,1)S(1)}, u32[]{:S(2)}) copy-start(bf16[8,2,32,1024]{3,2,1,0:T(8,128)(2,1)S(1)} %all-to-all-done.2) | copy-start | bytes 3145732
  52.0 18.8 %all-to-all-start.1 = ((bf16[16,32,1024]{2,1,0:T(8,128)(2,1)}), bf16[16,32,1024]{2,1,0:T(8,128)(2,1)S(1)}, u32[]{:S(2)}, u32[]{:S(2)}) async-start(bf16[16,32,1024]{2,1,0:T(8,128)(2,1)} %bitcast.40), calls=%async_computation.1 | async-start | bytes 2097152 | tf_op jit(solution)/shard_map/all_to_all | solution.py:365
  82.2 24.2 %copy-start = (bf16[4,8,32,512]{3,2,1,0:T(8,128)(2,1)}, bf16[4,8,32,512]{3,2,1,0:T(8,128)(2,1)S(1)}, u32[]{:S(2)}) copy-start(bf16[4,8,32,512]{3,2,1,0:T(8,128)(2,1)S(1)} %get-tuple-element.14.keep_ref) | copy-start | bytes 3145732
  82.3 8.0 %collective-permute-start.1 = (bf16[4,8,32,512]{3,2,1,0:T(8,128)(2,1)S(1)}, bf16[4,8,32,512]{3,2,1,0:T(8,128)(2,1)}, u32[]{:S(2)}, u32[]{:S(2)}) collective-permute-start(bf16[4,8,32,512]{3,2,1,0:T(8,128)(2,1)S(1)} %get-tuple-element.15), channel_id=1, source_target_pairs={{0,32},{32,0},{64,96},{96,64},{1,33},{33,1},{65,97},{97,65},{2,34}... | collective-permute-start | bytes 3145736 | tf_op jit(solution)/shard_map/ppermute | solution.py:382
  86.4 21.8 %all-to-all-start.3 = ((bf16[8,2,32,1024]{3,2,1,0:T(8,128)(2,1)}), bf16[8,2,32,1024]{3,2,1,0:T(8,128)(2,1)S(1)}, u32[]{:S(2)}, u32[]{:S(2)}) async-start(bf16[8,2,32,1024]{3,2,1,0:T(8,128)(2,1)} %bitcast.42), calls=%async_computation.3 | async-start | bytes 2097152 | tf_op jit(solution)/shard_map/all_to_all | solution.py:357
  91.6 14.5 %collective-permute-start.2 = (bf16[8,32,512]{2,1,0:T(8,128)(2,1)S(1)}, bf16[8,32,512]{2,1,0:T(8,128)(2,1)S(1)}, u32[]{:S(2)}, u32[]{:S(2)}) collective-permute-start(bf16[8,32,512]{2,1,0:T(8,128)(2,1)S(1)} %get-tuple-element.24), channel_id=1, source_target_pairs={{0,1},{1,2},{2,3},{3,0},{4,5},{5,6},{6,7},{7,4},{8,9},{9,10},{10,1... | collective-permute-start | bytes 786440 | tf_op jit(solution)/shard_map/ppermute | solution.py:385
  93.1 13.0 %collective-permute-start.3 = (bf16[8,32,512]{2,1,0:T(8,128)(2,1)S(1)}, bf16[8,32,512]{2,1,0:T(8,128)(2,1)S(1)}, u32[]{:S(2)}, u32[]{:S(2)}) collective-permute-start(bf16[8,32,512]{2,1,0:T(8,128)(2,1)S(1)} %get-tuple-element.23), channel_id=1, source_target_pairs={{0,2},{1,3},{2,0},{3,1},{4,6},{5,7},{6,4},{7,5},{8,10},{9,11},{10,... | collective-permute-start | bytes 786440 | tf_op jit(solution)/shard_map/ppermute | solution.py:385
  93.1 13.4 %collective-permute-start.4 = (bf16[8,32,512]{2,1,0:T(8,128)(2,1)S(1)}, bf16[8,32,512]{2,1,0:T(8,128)(2,1)S(1)}, u32[]{:S(2)}, u32[]{:S(2)}) collective-permute-start(bf16[8,32,512]{2,1,0:T(8,128)(2,1)S(1)} %get-tuple-element.22), channel_id=1, source_target_pairs={{0,3},{1,0},{2,1},{3,2},{4,7},{5,4},{6,5},{7,6},{8,11},{9,8},{10,9... | collective-permute-start | bytes 786440 | tf_op jit(solution)/shard_map/ppermute | solution.py:385
  108.3 10.9 %all-to-all-start.4 = ((bf16[8,32,512]{2,1,0:T(8,128)(2,1)}), bf16[8,32,512]{2,1,0:T(8,128)(2,1)S(1)}, u32[]{:S(2)}, u32[]{:S(2)}) async-start(bf16[8,32,512]{2,1,0:T(8,128)(2,1)} %space_sum.1), calls=%async_computation.4 | async-start | bytes 524288 | tf_op jit(solution)/shard_map/all_to_all | solution.py:357

commit v9 on v8

--- a/solution.py
+++ b/solution.py
@@ -235,13 +235,13 @@
 GROUP = 8
 
 
-def temporal_kernel(core_ref, mid_ref, order_q_ref, order_k_ref, gain_ref, cot_ref, w_ref, wm_ref,
-                    out_hbm, send_ref, keep_ref,
-                    out_ref, wqkv_buf, wm_buf, cot_buf, normed_ref, q_ref, k_ref, v_ref, ctx_ref, cotb_ref, sems):
+def temporal_kernel(core_ref, mid_ref, order_q_ref, order_k_ref, gain_ref, wq_ref, cot_ref, w_ref, wm_ref,
+                    out_hbm, send_ref, keep_hbm,
+                    out_ref, keep_ref, wqkv_buf, wm_buf, cot_buf, normed_ref, q_ref, k_ref, v_ref, ctx_ref, cotb_ref, sems):
     frames, cols, _ = mid_ref.shape
     groups = cols // GROUP
     n = frames * GROUP
-    copies = column_copies(w_ref, wqkv_buf, sems, range(3))
+    copies = column_copies(w_ref, wqkv_buf, sems, (1, 2))
     copies.append(pltpu.make_async_copy(cot_ref, cot_buf, sems.at[3]))
     copies.append(pltpu.make_async_copy(wm_ref, wm_buf, sems.at[4]))
     for c in copies:
@@ -250,10 +250,11 @@
     for g in range(groups):
         x = mid_ref[:, g * GROUP:(g + 1) * GROUP, :].astype(F32).reshape(n, D)
         normed_ref[g * n:(g + 1) * n] = normalized(x, gain).astype(BF)
-    for i, buf in enumerate((q_ref, k_ref, v_ref)):
+    q_ref[...] = jnp.dot(normed_ref[...], wq_ref[...], preferred_element_type=F32).astype(BF)
+    for i, buf in enumerate((k_ref, v_ref)):
         copies[i].wait()
         buf[...] = jnp.dot(normed_ref[...], wqkv_buf[i], preferred_element_type=F32).astype(BF)
-    copies[3].wait()
+    copies[2].wait()
     for g in range(groups):
         cotb_ref[g * n:(g + 1) * n] = cot_buf[:, g * GROUP:(g + 1) * GROUP, :].astype(F32).reshape(n, D).astype(BF)
     place_q = lax.broadcasted_iota(jnp.int32, (n, n), 0) % GROUP
@@ -281,7 +282,9 @@
             for t in range(times):
                 row = (t * spaces + s) * block
                 ref[slot, t] = grad[row:row + block]
-    copies[4].wait()
+    kept = pltpu.make_async_copy(keep_ref, keep_hbm, sems.at[5])
+    kept.start()
+    copies[3].wait()
     y = jnp.dot(ctx_ref[...], wm_buf[...], preferred_element_type=F32)
     for g in range(groups):
         x = mid_ref[:, g * GROUP:(g + 1) * GROUP, :].astype(F32) + y[g * n:(g + 1) * n].reshape(frames, GROUP, D)
@@ -289,6 +292,7 @@
     done = pltpu.make_async_copy(out_ref, out_hbm, sems.at[6])
     done.start()
     done.wait()
+    kept.wait()
 
 
 def temporal_phase(core, mid, order, gain, cot, heads, merge, spaces, times):
@@ -298,44 +302,55 @@
     spread = jnp.repeat(order, GROUP)
     block = D // (spaces * times)
     part = (spaces, times, block, D // 2)
+    first_third = heads[:, :D]
     return pl.pallas_call(
         temporal_kernel,
-        in_specs=[SMEM] + [VMEM] * 4 + [HBM] * 3,
-        out_specs=[HBM, VMEM, VMEM],
-        out_shape=[pltpu.HBM((frames, cols, D), BF), pltpu.VMEM(part, BF), pltpu.VMEM(part, BF)],
-        scratch_shapes=[pltpu.VMEM((frames, cols, D), BF), pltpu.VMEM((3, D, D), BF), pltpu.VMEM((D, D), BF), pltpu.VMEM((frames, cols, D), BF)]
+        in_specs=[SMEM] + [VMEM] * 5 + [HBM] * 3,
+        out_specs=[HBM, VMEM, HBM],
+        out_shape=[pltpu.HBM((frames, cols, D), BF), pltpu.VMEM(part, BF), pltpu.HBM(part, BF)],
+        scratch_shapes=[pltpu.VMEM((frames, cols, D), BF), pltpu.VMEM(part, BF), pltpu.VMEM((2, D, D), BF), pltpu.VMEM((D, D), BF), pltpu.VMEM((frames, cols, D), BF)]
         + [pltpu.VMEM((tokens, D), BF)] * 6
         + [pltpu.SemaphoreType.DMA((7,))],
         compiler_params=pltpu.CompilerParams(vmem_limit_bytes=40 * 2**20),
         name="temporal_phase",
     )(core, in_vmem(mid), spread.reshape(n, 1), spread.reshape(1, n), gain.reshape(1, D),
-      in_hbm(cot), in_hbm(heads), in_hbm(merge))
-
-
-def sum_kernel(keep_ref, got_ref, *refs):
-    parts, (out_ref, own_ref, sems) = refs[:-3], refs[-3:]
-    copies = [pltpu.make_async_copy(r.at[0], own_ref.at[i], sems.at[i]) for i, r in enumerate((keep_ref, got_ref))]
-    for c in copies:
-        c.start()
-    total = parts[0][...].astype(F32)
-    for p in parts[1:]:
+      in_vmem(first_third), in_hbm(cot), in_hbm(heads), in_hbm(merge))
+
+
+def own_kernel(keep_ref, got_ref, out_ref):
+    out_ref[...] = keep_ref[...].astype(F32) + got_ref[...].astype(F32)
+
+
+def own_slot(keep, got):
+    shape = keep.shape[1:]
+    first = pl.BlockSpec((None,) + shape, lambda i: (0, 0, 0, 0))
+    return pl.pallas_call(
+        own_kernel,
+        grid=(1,),
+        in_specs=[first, first],
+        out_specs=pl.BlockSpec(shape, lambda i: (0, 0, 0)),
+        out_shape=jax.ShapeDtypeStruct(shape, F32),
+        compiler_params=pltpu.CompilerParams(vmem_limit_bytes=8 * 2**20),
+        name="own_slot",
+    )(in_hbm(keep), got)
+
+
+def sum_kernel(own_ref, *refs):
+    total = own_ref[...]
+    for p in refs[:-1]:
         total = total + p[...].astype(F32)
-    for c in copies:
-        c.wait()
-    out_ref[...] = (total + own_ref[0].astype(F32) + own_ref[1].astype(F32)).astype(BF)
-
-
-def space_sum(keep, got, moved):
-    shape = moved[0].shape
+    refs[-1][...] = total.astype(BF)
+
+
+def space_sum(own, moved):
     return pl.pallas_call(
         sum_kernel,
-        in_specs=[HBM, HBM] + [VMEM] * len(moved),
+        in_specs=[VMEM] * (1 + len(moved)),
         out_specs=VMEM,
-        out_shape=pltpu.VMEM(shape, BF),
-        scratch_shapes=[pltpu.VMEM((2,) + shape, BF), pltpu.SemaphoreType.DMA((2,))],
+        out_shape=pltpu.VMEM(own.shape, BF),
         compiler_params=pltpu.CompilerParams(vmem_limit_bytes=8 * 2**20),
         name="space_sum",
-    )(in_hbm(keep), in_hbm(got), *[in_vmem(p) for p in moved])
+    )(in_vmem(own), *[in_vmem(p) for p in moved])
 
 
 def per_device(
@@ -384,7 +399,8 @@
     chip = [keep[k].astype(F32) + got[k].astype(F32) for k in range(1, space)]
     moved = [lax.ppermute(chip[k - 1].astype(BF), "space", [(i, (i + k) % space) for i in range(space)])
              for k in range(1, space)]
-    over_space = space_sum(keep, got, moved)
+    own = own_slot(keep, got)
+    over_space = space_sum(own, moved)
     over_tm = exchange(over_space, "tm")
     over_tm = over_tm.astype(F32).sum(0).astype(BF)
     block = over_tm.shape[0]

time: 130 us -> 130 us (level)
  waiting for transfers between devices: 39.3 us -> 36.6 us
  local copies, waits for them, and re-layouts: 4.97 us -> 6.74 us
    all_to_all x2, waiting for transfers between devices: 23.7 us -> 21.9 us  [per_device(): lax.all_to_all(v, ('tm', 'space'), split_axis=0, concat_axis=0, axis_inde...]
    slice x0 -> x1, local copies, waits for them, and re-layouts: none -> 1.76 us  [temporal_phase(): first_third = heads[:, :D]]
    pallas_call x2 -> x3, Pallas kernels: 13.2 us -> 13.7 us  [the longest x1 11.9 us: temporal_phase(): pl.pallas_call(temporal_kernel, in_specs=[SMEM] + [VMEM] * 5 + [HBM] * 3,...]
    unnamed x14 -> x12, local copies, waits for them, and re-layouts: 3.41 us -> 3.41 us
  transfers between devices with their start and end apart: 10 -> 10, of which waited for: 5 -> 5; matrix products, arithmetic and copies ran while one was open for 4% -> 6% of each run, Pallas kernels for 16% -> 16%
where the time goes in v9:
time: 130 us; the launch traced here: 129 us
  starting transfers between devices  40.2 us (31%)
  waiting for transfers between devices  36.6 us (28%)
  Pallas kernels  32.4 us (25%)
  blocking collectives  9.7 us (7%)
  local copies, waits for them, and re-layouts  6.74 us (5%)
  between operations  2.17 us (2%)
  other arithmetic  1.58 us (1%)
    all_to_all x2, waiting for transfers between devices, per_device(): lax.all_to_all(v, ('tm', 'space'), split_axis=0, concat_axis=0, axis_inde...  21.9 us
    all_to_all x3, starting transfers between devices, per_device(): lax.all_to_all(v, axis, split_axis=0, concat_axis=0, tiled=True)  14.7 us
    all_to_all x2, starting transfers between devices, per_device(): lax.all_to_all(v, ('tm', 'space'), split_axis=0, concat_axis=0, axis_inde...  14.1 us
    pallas_call x1, Pallas kernels, temporal_phase(): pl.pallas_call(temporal_kernel, in_specs=[SMEM] + [VMEM] * 5 + [HBM] * 3,...  11.9 us
    pallas_call x1, Pallas kernels, spatial_phase(): pl.pallas_call(spatial_kernel, in_specs=[SMEM, VMEM, HBM, HBM, HBM, HBM],...  10.4 us
    ppermute x3, waiting for transfers between devices, per_device(): lax.ppermute(chip[k - 1].astype(BF), 'space', [(i, (i + k) % space) for i...  9.89 us
    all_gather x1, blocking collectives, per_device(): lax.all_gather(over_tm, 'batch').astype(F32)  9.7 us
    pallas_call x1, Pallas kernels, qkv_own(): pl.pallas_call(qkv_kernel, in_specs=[SMEM, VMEM, VMEM, HBM], out_specs=[H...  7.49 us
  transfers between devices with their start and end apart: 10, of which 5 were waited for; matrix products, arithmetic and copies ran while one was open for 6% of the time, Pallas kernels for 16%

profile of v9, /device:TPU:1, one launch (start us, length us, event | category | flops | bytes accessed | tf_op | source)
XLA Modules:
  0.0 129.3 jit_solution(14734466458824126031)
XLA Ops:
  0.6 0.0 copy-start.3
  0.6 0.0 copy-start
  0.6 7.6 %all-to-all-start = ((bf16[16,8,4,1024]{3,2,1,0:T(4,128)(2,1)}), bf16[16,8,4,1024]{3,2,1,0:T(4,128)(2,1)S(1)}, u32[]{:S(2)}, u32[]{:S(2)}) async-start(bf16[16,8,4,1024]{3,2,1,0:T(4,128)(2,1)} %bitcast.41), calls=%async_computation | async-start | bytes 2097152 | tf_op jit(solution)/shard_map/all_to_all | solution.py:380
  8.3 2.3 %copy.30 = bf16[1,2,8,32,1024]{4,3,1,2,0:T(8,128)(2,1)} copy(bf16[1,2,8,32,1024]{4,3,2,1,0:T(8,128)(2,1)} %param.19) | data formatting | bytes 2097152 | tf_op args[9]
  10.6 11.5 %all-to-all-done = bf16[16,8,4,1024]{3,2,1,0:T(4,128)(2,1)S(1)} async-done(((bf16[16,8,4,1024]{3,2,1,0:T(4,128)(2,1)}), bf16[16,8,4,1024]{3,2,1,0:T(4,128)(2,1)S(1)}, u32[]{:S(2)}, u32[]{:S(2)}) %all-to-all-start) | async-done | bytes 1048608 | tf_op jit(solution)/shard_map/all_to_all | solution.py:380
  22.1 5.8 %all-to-all-start.2 = ((bf16[8,2,32,1024]{3,2,1,0:T(8,128)(2,1)}), bf16[8,2,32,1024]{3,2,1,0:T(8,128)(2,1)S(1)}, u32[]{:S(2)}, u32[]{:S(2)}) async-start(bf16[8,2,32,1024]{3,2,1,0:T(8,128)(2,1)} %bitcast.32), calls=%async_computation.2 | async-start | bytes 2097152 | tf_op jit(solution)/shard_map/all_to_all | solution.py:372
  27.9 0.0 copy-done.3
  27.9 0.7 fusion.3
  30.0 0.1 pad_add_fusion.1.info_ref
  30.1 0.0 copy-done
  30.1 0.8 edge_norm.1
  30.8 3.4 %collective-permute-start = (bf16[4,32,1024]{2,1,0:T(8,128)(2,1)S(1)}, bf16[4,32,1024]{2,1,0:T(8,128)(2,1)S(1)}, u32[]{:S(2)}, u32[]{:S(2)}) collective-permute-start(bf16[4,32,1024]{2,1,0:T(8,128)(2,1)S(1)} %edge_norm.1), channel_id=1, source_target_pairs={{0,3},{1,2},{2,1},{3,0},{4,7},{5,6},{6,5},{7,4},{8,11},{9,10},{10,... | collective-permute-start | bytes 786440 | tf_op jit(solution)/shard_map/ppermute | solution.py:385
  34.2 7.5 %qkv_own.1 = (bf16[3,512,1024]{2,1,0:T(8,128)(2,1)}, bf16[16,32,1024]{2,1,0:T(8,128)(2,1)}) custom-call(s32[2]{0:T(128)S(1)} %pad_add_fusion.1.info_ref, bf16[8,2,8,4,1024]{4,3,2,1,0:T(4,128)(2,1)S(1)} %bitcast.34, f32[1,1024]{1,0:T(1,128)S(1)} %bitcast.36, bf16[1024,3072]{1,0:T(8,128)(2,1)} %w_ref.4), custom_call_target="tpu_custom_call" | custom-call | tf_op jit(solution)/shard_map/qkv_own/pallas_call | solution.py:111
  41.7 0.0 collective-permute-done.halo_ref
  41.7 0.0 copy-start.4
  41.7 10.4 %spatial_phase.1 = bf16[8,2,32,1024]{3,2,1,0:T(8,128)(2,1)} custom-call(s32[2]{0:T(128)S(1)} %pad_add_fusion.1.info_ref, bf16[4,32,1024]{2,1,0:T(8,128)(2,1)S(1)} %collective-permute-done.halo_ref, bf16[3,512,1024]{2,1,0:T(8,128)(2,1)} %get-tuple-element.10.qkv_ref, bf16[16,32,1024]{2,1,0:T(8,128)(2,1)} %get-tuple-element.11.tok_ref, ...), custom_call_target="tpu_custom_call" | custom-call | tf_op jit(solution)/shard_map/spatial_phase/pallas_call | solution.py:219
  52.1 0.0 all-to-all-done.2
  52.1 0.0 copy-start.2
  52.2 0.0 copy-start.1
  52.2 6.5 %all-to-all-start.1 = ((bf16[16,32,1024]{2,1,0:T(8,128)(2,1)}), bf16[16,32,1024]{2,1,0:T(8,128)(2,1)S(1)}, u32[]{:S(2)}, u32[]{:S(2)}) async-start(bf16[16,32,1024]{2,1,0:T(8,128)(2,1)} %bitcast.40), calls=%async_computation.1 | async-start | bytes 2097152 | tf_op jit(solution)/shard_map/all_to_all | solution.py:380
  58.6 0.0 copy-done.2
  58.7 0.0 copy-done.4
  58.7 0.1 broadcast_in_dim.3
  58.7 0.1 reshape_reshape.8.order_q_ref
  58.8 0.1 reshape_reshape.7.order_k_ref
  58.9 1.8 %slice.29.wq_ref = bf16[1024,1024]{1,0:T(8,128)(2,1)S(1)} slice(bf16[1024,3072]{1,0:T(8,128)(2,1)} %w_ref.5), slice={[0:1024], [0:1024]} | slice | bytes 4194304 | tf_op jit(solution)/shard_map/slice | solution.py:305
  60.7 0.1 pad_add_fusion.core_ref
  60.8 10.4 %all-to-all-done.1.mid_ref = bf16[16,32,1024]{2,1,0:T(8,128)(2,1)S(1)} async-done(((bf16[16,32,1024]{2,1,0:T(8,128)(2,1)}), bf16[16,32,1024]{2,1,0:T(8,128)(2,1)S(1)}, u32[]{:S(2)}, u32[]{:S(2)}) %all-to-all-start.1) | async-done | bytes 1048608 | tf_op jit(solution)/shard_map/all_to_all | solution.py:380
  71.2 0.0 copy-done.1
  71.2 11.9 %temporal_phase.1 = (bf16[16,32,1024]{2,1,0:T(8,128)(2,1)}, bf16[4,8,32,512]{3,2,1,0:T(8,128)(2,1)}, bf16[4,8,32,512]{3,2,1,0:T(8,128)(2,1)}) custom-call(s32[2]{0:T(128)S(1)} %pad_add_fusion.core_ref, bf16[16,32,1024]{2,1,0:T(8,128)(2,1)S(1)} %all-to-all-done.1.mid_ref, s32[128,1]{1,0:T(8,128)S(1)} %reshape_reshape.8.order_q_ref, ...), custom_call_target="tpu_custom_call" | custom-call | tf_op jit(solution)/shard_map/temporal_phase/pallas_call | solution.py:306
  83.1 4.2 %collective-permute-start.1 = (bf16[4,8,32,512]{3,2,1,0:T(8,128)(2,1)}, bf16[4,8,32,512]{3,2,1,0:T(8,128)(2,1)S(1)}, u32[]{:S(2)}, u32[]{:S(2)}) collective-permute-start(bf16[4,8,32,512]{3,2,1,0:T(8,128)(2,1)} %get-tuple-element.15), channel_id=1, source_target_pairs={{0,32},{32,0},{64,96},{96,64},{1,33},{33,1},{65,97},{97,65},{2,34}... | collective-permute-start | bytes 3145736 | tf_op jit(solution)/shard_map/ppermute | solution.py:397
  87.2 3.8 %all-to-all-start.3 = ((bf16[8,2,32,1024]{3,2,1,0:T(8,128)(2,1)}), bf16[8,2,32,1024]{3,2,1,0:T(8,128)(2,1)S(1)}, u32[]{:S(2)}, u32[]{:S(2)}) async-start(bf16[8,2,32,1024]{3,2,1,0:T(8,128)(2,1)} %bitcast.42), calls=%async_computation.3 | async-start | bytes 2097152 | tf_op jit(solution)/shard_map/all_to_all | solution.py:372
  91.1 0.0 collective-permute-done.1.got_ref
  91.1 1.4 %fusion.2 = (bf16[8,32,512]{2,1,0:T(8,128)(2,1)S(1)}, bf16[8,32,512]{2,1,0:T(8,128)(2,1)S(1)}, bf16[8,32,512]{2,1,0:T(8,128)(2,1)S(1)}) fusion(bf16[4,8,32,512]{3,2,1,0:T(8,128)(2,1)S(1)} %collective-permute-done.1.got_ref, bf16[4,8,32,512]{3,2,1,0:T(8,128)(2,1)} %get-tuple-element.14.keep_ref), kind=kLoop, calls=%fused_computation.6 | loop fusion | flops 1572864 | bytes 2359296 | tf_op jit(solution)/shard_map/convert_element_type | solution.py:400
  92.4 1.4 %collective-permute-start.2 = (bf16[8,32,512]{2,1,0:T(8,128)(2,1)S(1)}, bf16[8,32,512]{2,1,0:T(8,128)(2,1)S(1)}, u32[]{:S(2)}, u32[]{:S(2)}) collective-permute-start(bf16[8,32,512]{2,1,0:T(8,128)(2,1)S(1)} %get-tuple-element.24), channel_id=1, source_target_pairs={{0,1},{1,2},{2,3},{3,0},{4,5},{5,6},{6,7},{7,4},{8,9},{9,10},{10,1... | collective-permute-start | bytes 786440 | tf_op jit(solution)/shard_map/ppermute | solution.py:400
  93.8 0.0 collective-permute-start.3
  93.8 2.5 %collective-permute-start.4 = (bf16[8,32,512]{2,1,0:T(8,128)(2,1)S(1)}, bf16[8,32,512]{2,1,0:T(8,128)(2,1)S(1)}, u32[]{:S(2)}, u32[]{:S(2)}) collective-permute-start(bf16[8,32,512]{2,1,0:T(8,128)(2,1)S(1)} %get-tuple-element.22), channel_id=1, source_target_pairs={{0,3},{1,0},{2,1},{3,2},{4,7},{5,4},{6,5},{7,6},{8,11},{9,8},{10,9... | collective-permute-start | bytes 786440 | tf_op jit(solution)/shard_map/ppermute | solution.py:400
  96.3 1.0 own_slot.1.own_ref
  97.3 9.6 %collective-permute-done.2.refs_0_ = bf16[8,32,512]{2,1,0:T(8,128)(2,1)S(1)} collective-permute-done((bf16[8,32,512]{2,1,0:T(8,128)(2,1)S(1)}, bf16[8,32,512]{2,1,0:T(8,128)(2,1)S(1)}, u32[]{:S(2)}, u32[]{:S(2)}) %collective-permute-start.2) | collective-permute-done | bytes 262176 | tf_op jit(solution)/shard_map/ppermute | solution.py:400
  106.9 0.0 collective-permute-done.3.refs_1_
  106.9 0.3 collective-permute-done.4.refs_2_
  107.2 0.8 space_sum.1
  108.1 0.0 all-to-all-done.3
  108.1 5.0 %all-to-all-start.4 = ((bf16[8,32,512]{2,1,0:T(8,128)(2,1)}), bf16[8,32,512]{2,1,0:T(8,128)(2,1)S(1)}, u32[]{:S(2)}, u32[]{:S(2)}) async-start(bf16[8,32,512]{2,1,0:T(8,128)(2,1)} %space_sum.1), calls=%async_computation.4 | async-start | bytes 524288 | tf_op jit(solution)/shard_map/all_to_all | solution.py:372
  113.1 1.1 copy.27
  114.2 4.8 %all-to-all-done.4 = bf16[8,32,512]{2,1,0:T(8,128)(2,1)S(1)} async-done(((bf16[8,32,512]{2,1,0:T(8,128)(2,1)}), bf16[8,32,512]{2,1,0:T(8,128)(2,1)S(1)}, u32[]{:S(2)}, u32[]{:S(2)}) %all-to-all-start.4) | async-done | bytes 262176 | tf_op jit(solution)/shard_map/all_to_all | solution.py:372
  119.0 9.7 %all-gather = bf16[128,512]{1,0:T(8,128)(2,1)S(1)} all-gather(bf16[32,512]{1,0:T(8,128)(2,1)S(1)} %reduce_sum.21), channel_id=2, replica_groups=mesh['batch'=4,'tm'=8,'space'=4] {'batch'}, dimensions={0}, use_global_device_ids=true | all-gather | bytes 163840 | tf_op jit(solution)/shard_map/all_gather | solution.py:407
  128.7 0.7 copy.28
  (2 shorter events, 0.1 us)
Async XLA Ops:
  0.6 27.3 %copy-start.3 = (s32[1,2]{1,0:T(1,128)S(1)}, s32[1,2]{1,0:T(1,128)}, u32[]{:S(2)}) copy-start(s32[1,2]{1,0:T(1,128)} %param.12) | copy-start | bytes 28
  0.6 29.4 %copy-start = (f32[1024]{0:T(1024)S(1)}, f32[1024]{0:T(1024)}, u32[]{:S(2)}) copy-start(f32[1024]{0:T(1024)} %param.13) | copy-start | bytes 12292
  0.6 21.5 %all-to-all-start = ((bf16[16,8,4,1024]{3,2,1,0:T(4,128)(2,1)}), bf16[16,8,4,1024]{3,2,1,0:T(4,128)(2,1)S(1)}, u32[]{:S(2)}, u32[]{:S(2)}) async-start(bf16[16,8,4,1024]{3,2,1,0:T(4,128)(2,1)} %bitcast.41), calls=%async_computation | async-start | bytes 2097152 | tf_op jit(solution)/shard_map/all_to_all | solution.py:380
  22.1 30.0 %all-to-all-start.2 = ((bf16[8,2,32,1024]{3,2,1,0:T(8,128)(2,1)}), bf16[8,2,32,1024]{3,2,1,0:T(8,128)(2,1)S(1)}, u32[]{:S(2)}, u32[]{:S(2)}) async-start(bf16[8,2,32,1024]{3,2,1,0:T(8,128)(2,1)} %bitcast.32), calls=%async_computation.2 | async-start | bytes 2097152 | tf_op jit(solution)/shard_map/all_to_all | solution.py:372
  30.8 10.9 %collective-permute-start = (bf16[4,32,1024]{2,1,0:T(8,128)(2,1)S(1)}, bf16[4,32,1024]{2,1,0:T(8,128)(2,1)S(1)}, u32[]{:S(2)}, u32[]{:S(2)}) collective-permute-start(bf16[4,32,1024]{2,1,0:T(8,128)(2,1)S(1)} %edge_norm.1), channel_id=1, source_target_pairs={{0,3},{1,2},{2,1},{3,0},{4,7},{5,6},{6,5},{7,4},{8,11},{9,10},{10,... | collective-permute-start | bytes 786440 | tf_op jit(solution)/shard_map/ppermute | solution.py:385
  41.7 16.9 %copy-start.4 = (s32[1,16]{1,0:T(1,128)S(1)}, s32[1,16]{1,0:T(1,128)}, u32[]{:S(2)}) copy-start(s32[1,16]{1,0:T(1,128)} %param.11) | copy-start | bytes 196
  52.1 6.5 %copy-start.2 = (bf16[8,2,32,1024]{3,2,1,0:T(8,128)(2,1)}, bf16[8,2,32,1024]{3,2,1,0:T(8,128)(2,1)S(1)}, u32[]{:S(2)}) copy-start(bf16[8,2,32,1024]{3,2,1,0:T(8,128)(2,1)S(1)} %all-to-all-done.2) | copy-start | bytes 3145732
  52.2 19.0 %copy-start.1 = (f32[1024]{0:T(1024)S(1)}, f32[1024]{0:T(1024)}, u32[]{:S(2)}) copy-start(f32[1024]{0:T(1024)} %param.16) | copy-start | bytes 12292
  52.2 19.0 %all-to-all-start.1 = ((bf16[16,32,1024]{2,1,0:T(8,128)(2,1)}), bf16[16,32,1024]{2,1,0:T(8,128)(2,1)S(1)}, u32[]{:S(2)}, u32[]{:S(2)}) async-start(bf16[16,32,1024]{2,1,0:T(8,128)(2,1)} %bitcast.40), calls=%async_computation.1 | async-start | bytes 2097152 | tf_op jit(solution)/shard_map/all_to_all | solution.py:380
  83.1 8.0 %collective-permute-start.1 = (bf16[4,8,32,512]{3,2,1,0:T(8,128)(2,1)}, bf16[4,8,32,512]{3,2,1,0:T(8,128)(2,1)S(1)}, u32[]{:S(2)}, u32[]{:S(2)}) collective-permute-start(bf16[4,8,32,512]{3,2,1,0:T(8,128)(2,1)} %get-tuple-element.15), channel_id=1, source_target_pairs={{0,32},{32,0},{64,96},{96,64},{1,33},{33,1},{65,97},{97,65},{2,34}... | collective-permute-start | bytes 3145736 | tf_op jit(solution)/shard_map/ppermute | solution.py:397
  87.2 20.8 %all-to-all-start.3 = ((bf16[8,2,32,1024]{3,2,1,0:T(8,128)(2,1)}), bf16[8,2,32,1024]{3,2,1,0:T(8,128)(2,1)S(1)}, u32[]{:S(2)}, u32[]{:S(2)}) async-start(bf16[8,2,32,1024]{3,2,1,0:T(8,128)(2,1)} %bitcast.42), calls=%async_computation.3 | async-start | bytes 2097152 | tf_op jit(solution)/shard_map/all_to_all | solution.py:372
  92.4 14.5 %collective-permute-start.2 = (bf16[8,32,512]{2,1,0:T(8,128)(2,1)S(1)}, bf16[8,32,512]{2,1,0:T(8,128)(2,1)S(1)}, u32[]{:S(2)}, u32[]{:S(2)}) collective-permute-start(bf16[8,32,512]{2,1,0:T(8,128)(2,1)S(1)} %get-tuple-element.24), channel_id=1, source_target_pairs={{0,1},{1,2},{2,3},{3,0},{4,5},{5,6},{6,7},{7,4},{8,9},{9,10},{10,1... | collective-permute-start | bytes 786440 | tf_op jit(solution)/shard_map/ppermute | solution.py:400
  93.8 13.0 %collective-permute-start.3 = (bf16[8,32,512]{2,1,0:T(8,128)(2,1)S(1)}, bf16[8,32,512]{2,1,0:T(8,128)(2,1)S(1)}, u32[]{:S(2)}, u32[]{:S(2)}) collective-permute-start(bf16[8,32,512]{2,1,0:T(8,128)(2,1)S(1)} %get-tuple-element.23), channel_id=1, source_target_pairs={{0,2},{1,3},{2,0},{3,1},{4,6},{5,7},{6,4},{7,5},{8,10},{9,11},{10,... | collective-permute-start | bytes 786440 | tf_op jit(solution)/shard_map/ppermute | solution.py:400
  93.8 13.4 %collective-permute-start.4 = (bf16[8,32,512]{2,1,0:T(8,128)(2,1)S(1)}, bf16[8,32,512]{2,1,0:T(8,128)(2,1)S(1)}, u32[]{:S(2)}, u32[]{:S(2)}) collective-permute-start(bf16[8,32,512]{2,1,0:T(8,128)(2,1)S(1)} %get-tuple-element.22), channel_id=1, source_target_pairs={{0,3},{1,0},{2,1},{3,2},{4,7},{5,4},{6,5},{7,6},{8,11},{9,8},{10,9... | collective-permute-start | bytes 786440 | tf_op jit(solution)/shard_map/ppermute | solution.py:400
  108.1 10.9 %all-to-all-start.4 = ((bf16[8,32,512]{2,1,0:T(8,128)(2,1)}), bf16[8,32,512]{2,1,0:T(8,128)(2,1)S(1)}, u32[]{:S(2)}, u32[]{:S(2)}) async-start(bf16[8,32,512]{2,1,0:T(8,128)(2,1)} %space_sum.1), calls=%async_computation.4 | async-start | bytes 524288 | tf_op jit(solution)/shard_map/all_to_all | solution.py:372

commit v10 on v9

--- a/solution.py
+++ b/solution.py
@@ -235,26 +235,31 @@
 GROUP = 8
 
 
-def temporal_kernel(core_ref, mid_ref, order_q_ref, order_k_ref, gain_ref, wq_ref, cot_ref, w_ref, wm_ref,
-                    out_hbm, send_ref, keep_hbm,
-                    out_ref, keep_ref, wqkv_buf, wm_buf, cot_buf, normed_ref, q_ref, k_ref, v_ref, ctx_ref, cotb_ref, sems):
+def temporal_kernel(core_ref, mid_ref, order_q_ref, order_k_ref, gain_ref, w_ref, wm_ref, *refs):
+    cot_refs, refs = refs[:-15], refs[-15:]
+    (out_hbm, send_ref, keep_hbm, out_ref, keep_ref, wqkv_buf, wm_buf, cot_buf, normed_ref,
+     q_ref, k_ref, v_ref, ctx_ref, cotb_ref, sems) = refs
     frames, cols, _ = mid_ref.shape
     groups = cols // GROUP
     n = frames * GROUP
-    copies = column_copies(w_ref, wqkv_buf, sems, (1, 2))
-    copies.append(pltpu.make_async_copy(cot_ref, cot_buf, sems.at[3]))
+    copies = column_copies(w_ref, wqkv_buf, sems, range(3))
     copies.append(pltpu.make_async_copy(wm_ref, wm_buf, sems.at[4]))
+    times = len(cot_refs)
+    pair = frames // times
+    for i, ref in enumerate(cot_refs):
+        source = lax.rem(core_ref[2] + times - i, times)
+        copies.append(pltpu.make_async_copy(ref, cot_buf.at[pl.ds(source * pair, pair)], sems.at[7 + i]))
     for c in copies:
         c.start()
     gain = gain_ref[...]
     for g in range(groups):
         x = mid_ref[:, g * GROUP:(g + 1) * GROUP, :].astype(F32).reshape(n, D)
         normed_ref[g * n:(g + 1) * n] = normalized(x, gain).astype(BF)
-    q_ref[...] = jnp.dot(normed_ref[...], wq_ref[...], preferred_element_type=F32).astype(BF)
-    for i, buf in enumerate((k_ref, v_ref)):
+    for i, buf in enumerate((q_ref, k_ref, v_ref)):
         copies[i].wait()
         buf[...] = jnp.dot(normed_ref[...], wqkv_buf[i], preferred_element_type=F32).astype(BF)
-    copies[2].wait()
+    for c in copies[4:]:
+        c.wait()
     for g in range(groups):
         cotb_ref[g * n:(g + 1) * n] = cot_buf[:, g * GROUP:(g + 1) * GROUP, :].astype(F32).reshape(n, D).astype(BF)
     place_q = lax.broadcasted_iota(jnp.int32, (n, n), 0) % GROUP
@@ -302,19 +307,18 @@
     spread = jnp.repeat(order, GROUP)
     block = D // (spaces * times)
     part = (spaces, times, block, D // 2)
-    first_third = heads[:, :D]
     return pl.pallas_call(
         temporal_kernel,
-        in_specs=[SMEM] + [VMEM] * 5 + [HBM] * 3,
+        in_specs=[SMEM] + [VMEM] * 4 + [HBM] * (2 + len(cot)),
         out_specs=[HBM, VMEM, HBM],
         out_shape=[pltpu.HBM((frames, cols, D), BF), pltpu.VMEM(part, BF), pltpu.HBM(part, BF)],
-        scratch_shapes=[pltpu.VMEM((frames, cols, D), BF), pltpu.VMEM(part, BF), pltpu.VMEM((2, D, D), BF), pltpu.VMEM((D, D), BF), pltpu.VMEM((frames, cols, D), BF)]
+        scratch_shapes=[pltpu.VMEM((frames, cols, D), BF), pltpu.VMEM(part, BF), pltpu.VMEM((3, D, D), BF), pltpu.VMEM((D, D), BF), pltpu.VMEM((frames, cols, D), BF)]
         + [pltpu.VMEM((tokens, D), BF)] * 6
-        + [pltpu.SemaphoreType.DMA((7,))],
+        + [pltpu.SemaphoreType.DMA((7 + len(cot),))],
         compiler_params=pltpu.CompilerParams(vmem_limit_bytes=40 * 2**20),
         name="temporal_phase",
     )(core, in_vmem(mid), spread.reshape(n, 1), spread.reshape(1, n), gain.reshape(1, D),
-      in_vmem(first_third), in_hbm(cot), in_hbm(heads), in_hbm(merge))
+      in_hbm(heads), in_hbm(merge), *[in_hbm(c) for c in cot])
 
 
 def own_kernel(keep_ref, got_ref, out_ref):
@@ -339,7 +343,8 @@
     total = own_ref[...]
     for p in refs[:-1]:
         total = total + p[...].astype(F32)
-    refs[-1][...] = total.astype(BF)
+    refs[-1][0] = total.astype(BF)
+    refs[-1][1] = refs[-1][0]
 
 
 def space_sum(own, moved):
@@ -347,7 +352,7 @@
         sum_kernel,
         in_specs=[VMEM] * (1 + len(moved)),
         out_specs=VMEM,
-        out_shape=pltpu.VMEM(own.shape, BF),
+        out_shape=pltpu.VMEM((2,) + own.shape, BF),
         compiler_params=pltpu.CompilerParams(vmem_limit_bytes=8 * 2**20),
         name="space_sum",
     )(in_vmem(own), *[in_vmem(p) for p in moved])
@@ -379,18 +384,19 @@
     halves = [[t * space + s for t in range(tm) for s in pair] for pair in ((1, 0), (2, 3))]
     swap = lambda v: lax.all_to_all(v, ("tm", "space"), split_axis=0, concat_axis=0, axis_index_groups=halves, tiled=True)
     arrived = swap(clip_tokens.reshape(frame_count, rows, cols, D))
-    cot = cotangent.reshape(frames, rows, wide, D).swapaxes(0, 1)
+    time = lax.axis_index("tm").astype(jnp.int32)
+    rows_of = cotangent.reshape(frames, rows, wide, D)
+    cot = [lax.dynamic_index_in_dim(rows_of, (time + k) % tm, 1, keepdims=False) for k in range(tm)]
+    cot[1:] = [lax.ppermute(cot[k], "tm", [(i, (i + k) % tm) for i in range(tm)]) for k in range(1, tm)]
     arrived = arrived.reshape(tm, frames, rows, cols, D)
     edge_rows = edge_norm(info, arrived, spatial_gain)
     halo = lax.ppermute(edge_rows, "space", [(i, space - 1 - i) for i in range(space)])
-    cot, arrived = lax.optimization_barrier((cot, arrived))
-    cot = exchange(cot, "tm")
     qkv, tok = qkv_own(info, arrived, spatial_gain, spatial_heads)
     middle = spatial_phase(info, halo, qkv, tok, spatial_heads, spatial_merge)
     mid = swap(middle.reshape(frame_count, wide, D))
-    core = jnp.stack([lax.axis_index("batch") & 1, here]).astype(jnp.int32)
+    core = jnp.stack([lax.axis_index("batch") & 1, here, time]).astype(jnp.int32)
     out, send, keep = temporal_phase(
-        core, mid, frame_order.reshape(frame_count), temporal_gain, cot.reshape(frame_count, wide, D),
+        core, mid, frame_order.reshape(frame_count), temporal_gain, cot,
         temporal_heads, temporal_merge, space, tm,
     )
     batch = lax.axis_size("batch")
@@ -401,11 +407,16 @@
              for k in range(1, space)]
     own = own_slot(keep, got)
     over_space = space_sum(own, moved)
-    over_tm = exchange(over_space, "tm")
-    over_tm = over_tm.astype(F32).sum(0).astype(BF)
-    block = over_tm.shape[0]
-    parts = lax.all_gather(over_tm, "batch").astype(F32).reshape(batch // 2, 2, block, D // 2).sum(0)
-    weight_grad = parts.swapaxes(0, 1).reshape(block, D)
+    planes = [[(2 * y + c) * tm + t for y in range(batch // 2) for t in range(tm)] for c in range(2)]
+    pieces = lax.all_to_all(
+        over_space.reshape(2 * tm, *over_space.shape[2:]), ("batch", "tm"), split_axis=0, concat_axis=0,
+        axis_index_groups=planes, tiled=True,
+    )
+    mine = pieces.astype(F32).sum(0).astype(BF)
+    other = lax.ppermute(mine, "batch", [(i, i ^ 1) for i in range(batch)])
+    weight_grad = jnp.where(
+        core[0] == 0, jnp.concatenate([mine, other], axis=1), jnp.concatenate([other, mine], axis=1)
+    ).astype(F32)
     return (output.reshape(1, frames, rows, wide, D), weight_grad)
 
 

time: 130 us -> 149 us (1.15)
  waiting for transfers between devices: 36.6 us -> 45.7 us
  blocking collectives: 9.7 us -> 16.2 us
  starting transfers between devices: 40.2 us -> 44.7 us
  local copies, waits for them, and re-layouts: 6.74 us -> 4.72 us
    all_to_all x0 -> x1, blocking collectives: none -> 16.2 us  [per_device(): lax.all_to_all(over_space.reshape(2 * tm, *over_space.shape[2:]), ('batch...]
    ppermute x0 -> x8, starting transfers between devices: none -> 15.3 us  [the longest x7 12.9 us: per_device(): lax.ppermute(cot[k], 'tm', [(i, (i + k) % tm) for i in range(tm)])]
    all_to_all x3 -> x1, starting transfers between devices: 14.7 us -> 3.56 us  [per_device(): lax.all_to_all(v, axis, split_axis=0, concat_axis=0, tiled=True)]
    all_to_all x2, waiting for transfers between devices: 21.9 us -> 11.1 us  [per_device(): lax.all_to_all(v, ('tm', 'space'), split_axis=0, concat_axis=0, axis_inde...]
    ppermute x0 -> x8, waiting for transfers between devices: none -> 9.93 us  [the longest x7 9.93 us: per_device(): lax.ppermute(cot[k], 'tm', [(i, (i + k) % tm) for i in range(tm)])]
    all_gather x1 -> x0, blocking collectives: 9.7 us -> none  [per_device(): lax.all_gather(over_tm, 'batch').astype(F32)]
    all_to_all x3 -> x1, waiting for transfers between devices: 4.76 us -> 11.3 us  [per_device(): lax.all_to_all(v, axis, split_axis=0, concat_axis=0, tiled=True)]
    ppermute x1, waiting for transfers between devices: 0.01 us -> 2.29 us  [per_device(): got = lax.ppermute(send, 'batch', [(i, i ^ 1) for i in range(batch)])]
  transfers between devices with their start and end apart: 10 -> 16, of which waited for: 5 -> 8; matrix products, arithmetic and copies ran while one was open for 6% -> 2% of each run, Pallas kernels for 16% -> 6%
where the time goes in v10:
time: 149 us; the launch traced here: 147 us
  waiting for transfers between devices  45.7 us (31%)
  starting transfers between devices  44.7 us (30%)
  Pallas kernels  31.3 us (21%)
  blocking collectives  16.2 us (11%)
  local copies, waits for them, and re-layouts  4.72 us (3%)
  other arithmetic  2.22 us (1%)
  between operations  2.13 us (1%)
    all_to_all x1, blocking collectives, per_device(): lax.all_to_all(over_space.reshape(2 * tm, *over_space.shape[2:]), ('batch...  16.2 us
    all_to_all x2, starting transfers between devices, per_device(): lax.all_to_all(v, ('tm', 'space'), split_axis=0, concat_axis=0, axis_inde...  14.5 us
    ppermute x7, starting transfers between devices, per_device(): lax.ppermute(cot[k], 'tm', [(i, (i + k) % tm) for i in range(tm)])  12.9 us
    pallas_call x1, Pallas kernels, temporal_phase(): pl.pallas_call(temporal_kernel, in_specs=[SMEM] + [VMEM] * 4 + [HBM] * (2...  11.5 us
    all_to_all x1, waiting for transfers between devices, per_device(): lax.all_to_all(v, axis, split_axis=0, concat_axis=0, tiled=True)  11.3 us
    all_to_all x2, waiting for transfers between devices, per_device(): lax.all_to_all(v, ('tm', 'space'), split_axis=0, concat_axis=0, axis_inde...  11.1 us
    ppermute x3, waiting for transfers between devices, per_device(): lax.ppermute(chip[k - 1].astype(BF), 'space', [(i, (i + k) % space) for i...  11 us
    pallas_call x1, Pallas kernels, spatial_phase(): pl.pallas_call(spatial_kernel, in_specs=[SMEM, VMEM, HBM, HBM, HBM, HBM],...  10.4 us
  transfers between devices with their start and end apart: 16, of which 8 were waited for; matrix products, arithmetic and copies ran while one was open for 2% of the time, Pallas kernels for 6%

profile of v10, /device:TPU:1, one launch (start us, length us, event | category | flops | bytes accessed | tf_op | source)
XLA Modules:
  0.0 147.0 jit_solution(16318937563892443628)
XLA Ops:
  0.6 0.0 copy-start.1
  0.6 7.5 %all-to-all-start = ((bf16[16,8,4,1024]{3,2,1,0:T(4,128)(2,1)}), bf16[16,8,4,1024]{3,2,1,0:T(4,128)(2,1)S(1)}, u32[]{:S(2)}, u32[]{:S(2)}) async-start(bf16[16,8,4,1024]{3,2,1,0:T(4,128)(2,1)} %bitcast.48), calls=%async_computation | async-start | bytes 2097152 | tf_op jit(solution)/shard_map/all_to_all | solution.py:385
  8.2 1.3 fusion.4
  10.8 0.1 pad_add_fusion.1.info_ref
  10.8 11.1 %all-to-all-done = bf16[16,8,4,1024]{3,2,1,0:T(4,128)(2,1)S(1)} async-done(((bf16[16,8,4,1024]{3,2,1,0:T(4,128)(2,1)}), bf16[16,8,4,1024]{3,2,1,0:T(4,128)(2,1)S(1)}, u32[]{:S(2)}, u32[]{:S(2)}) %all-to-all-start) | async-done | bytes 1048608 | tf_op jit(solution)/shard_map/all_to_all | solution.py:385
  22.0 0.7 copy-done
  22.7 0.8 edge_norm.1
  23.4 3.4 %collective-permute-start = (bf16[4,32,1024]{2,1,0:T(8,128)(2,1)S(1)}, bf16[4,32,1024]{2,1,0:T(8,128)(2,1)S(1)}, u32[]{:S(2)}, u32[]{:S(2)}) collective-permute-start(bf16[4,32,1024]{2,1,0:T(8,128)(2,1)S(1)} %edge_norm.1), channel_id=1, source_target_pairs={{0,3},{1,2},{2,1},{3,0},{4,7},{5,6},{6,5},{7,4},{8,11},{9,10},{10,... | collective-permute-start | bytes 786440 | tf_op jit(solution)/shard_map/ppermute | solution.py:393
  26.8 7.5 %qkv_own.1 = (bf16[3,512,1024]{2,1,0:T(8,128)(2,1)}, bf16[16,32,1024]{2,1,0:T(8,128)(2,1)}) custom-call(s32[2]{0:T(128)S(1)} %pad_add_fusion.1.info_ref, bf16[8,2,8,4,1024]{4,3,2,1,0:T(4,128)(2,1)S(1)} %bitcast.41, f32[1,1024]{1,0:T(1,128)S(1)} %bitcast.44, bf16[1024,3072]{1,0:T(8,128)(2,1)} %w_ref.4), custom_call_target="tpu_custom_call" | custom-call | tf_op jit(solution)/shard_map/qkv_own/pallas_call | solution.py:111
  34.3 0.0 copy-start.3
  34.3 10.4 %spatial_phase.1 = bf16[8,2,32,1024]{3,2,1,0:T(8,128)(2,1)} custom-call(s32[2]{0:T(128)S(1)} %pad_add_fusion.1.info_ref, bf16[4,32,1024]{2,1,0:T(8,128)(2,1)S(1)} %collective-permute-done.halo_ref, bf16[3,512,1024]{2,1,0:T(8,128)(2,1)} %get-tuple-element.7.qkv_ref, bf16[16,32,1024]{2,1,0:T(8,128)(2,1)} %get-tuple-element.8.tok_ref, ...), custom_call_target="tpu_custom_call" | custom-call | tf_op jit(solution)/shard_map/spatial_phase/pallas_call | solution.py:219
  44.7 0.0 copy-start.11
  44.7 0.0 copy-start.2
  44.7 7.0 %all-to-all-start.1 = ((bf16[16,32,1024]{2,1,0:T(8,128)(2,1)}), bf16[16,32,1024]{2,1,0:T(8,128)(2,1)S(1)}, u32[]{:S(2)}, u32[]{:S(2)}) async-start(bf16[16,32,1024]{2,1,0:T(8,128)(2,1)} %bitcast.47), calls=%async_computation.1 | async-start | bytes 2097152 | tf_op jit(solution)/shard_map/all_to_all | solution.py:385
  51.7 0.8 dynamic-slice_bitcast_fusion
  52.5 1.2 collective-permute-start.1
  53.8 1.1 collective-permute-start.2
  54.9 1.8 %collective-permute-start.3 = (bf16[2,32,1024]{2,1,0:T(8,128)(2,1)S(1)}, bf16[2,32,1024]{2,1,0:T(8,128)(2,1)S(1)}, u32[]{:S(2)}, u32[]{:S(2)}) collective-permute-start(bf16[2,32,1024]{2,1,0:T(8,128)(2,1)S(1)} %get-tuple-element.20), channel_id=1, source_target_pairs={{0,12},{4,16},{8,20},{12,24},{16,28},{20,0},{24,4},{28,8},{1,13},{... | collective-permute-start | bytes 393224 | tf_op jit(solution)/shard_map/ppermute | solution.py:390
  56.7 1.8 %collective-permute-start.4 = (bf16[2,32,1024]{2,1,0:T(8,128)(2,1)S(1)}, bf16[2,32,1024]{2,1,0:T(8,128)(2,1)S(1)}, u32[]{:S(2)}, u32[]{:S(2)}) collective-permute-start(bf16[2,32,1024]{2,1,0:T(8,128)(2,1)S(1)} %get-tuple-element.19), channel_id=1, source_target_pairs={{0,16},{4,20},{8,24},{12,28},{16,0},{20,4},{24,8},{28,12},{1,17},{... | collective-permute-start | bytes 393224 | tf_op jit(solution)/shard_map/ppermute | solution.py:390
  58.5 2.7 %collective-permute-start.5 = (bf16[2,32,1024]{2,1,0:T(8,128)(2,1)S(1)}, bf16[2,32,1024]{2,1,0:T(8,128)(2,1)S(1)}, u32[]{:S(2)}, u32[]{:S(2)}) collective-permute-start(bf16[2,32,1024]{2,1,0:T(8,128)(2,1)S(1)} %get-tuple-element.18), channel_id=1, source_target_pairs={{0,20},{4,24},{8,28},{12,0},{16,4},{20,8},{24,12},{28,16},{1,21},{... | collective-permute-start | bytes 393224 | tf_op jit(solution)/shard_map/ppermute | solution.py:390
  61.2 7.4 %collective-permute-done.1.refs_1_ = bf16[2,32,1024]{2,1,0:T(8,128)(2,1)S(1)} collective-permute-done((bf16[2,32,1024]{2,1,0:T(8,128)(2,1)S(1)}, bf16[2,32,1024]{2,1,0:T(8,128)(2,1)S(1)}, u32[]{:S(2)}, u32[]{:S(2)}) %collective-permute-start.1) | collective-permute-done | bytes 131104 | tf_op jit(solution)/shard_map/ppermute | solution.py:390
  68.6 2.2 %collective-permute-start.6 = (bf16[2,32,1024]{2,1,0:T(8,128)(2,1)S(1)}, bf16[2,32,1024]{2,1,0:T(8,128)(2,1)S(1)}, u32[]{:S(2)}, u32[]{:S(2)}) collective-permute-start(bf16[2,32,1024]{2,1,0:T(8,128)(2,1)S(1)} %get-tuple-element.24), channel_id=1, source_target_pairs={{0,24},{4,28},{8,0},{12,4},{16,8},{20,12},{24,16},{28,20},{1,25},{... | collective-permute-start | bytes 393224 | tf_op jit(solution)/shard_map/ppermute | solution.py:390
  70.8 2.1 %collective-permute-start.7 = (bf16[2,32,1024]{2,1,0:T(8,128)(2,1)S(1)}, bf16[2,32,1024]{2,1,0:T(8,128)(2,1)S(1)}, u32[]{:S(2)}, u32[]{:S(2)}) collective-permute-start(bf16[2,32,1024]{2,1,0:T(8,128)(2,1)S(1)} %get-tuple-element.17), channel_id=1, source_target_pairs={{0,28},{4,0},{8,4},{12,8},{16,12},{20,16},{24,20},{28,24},{1,29},{... | collective-permute-start | bytes 393224 | tf_op jit(solution)/shard_map/ppermute | solution.py:390
  72.9 0.1 broadcast_in_dim.3
  73.0 0.1 reshape_reshape.8.order_q_ref
  73.1 0.1 reshape_reshape.7.order_k_ref
  73.2 0.1 pad_add_fusion.core_ref
  73.2 0.6 collective-permute-done.3.refs_3_
  73.9 1.9 %collective-permute-done.7.refs_7_ = bf16[2,32,1024]{2,1,0:T(8,128)(2,1)S(1)} collective-permute-done((bf16[2,32,1024]{2,1,0:T(8,128)(2,1)S(1)}, bf16[2,32,1024]{2,1,0:T(8,128)(2,1)S(1)}, u32[]{:S(2)}, u32[]{:S(2)}) %collective-permute-start.7) | collective-permute-done | bytes 131104 | tf_op jit(solution)/shard_map/ppermute | solution.py:390
  75.8 0.6 copy-done.10
  76.4 11.5 %temporal_phase.1 = (bf16[16,32,1024]{2,1,0:T(8,128)(2,1)}, bf16[4,8,32,512]{3,2,1,0:T(8,128)(2,1)S(1)}, bf16[4,8,32,512]{3,2,1,0:T(8,128)(2,1)}) custom-call(s32[3]{0:T(128)S(1)} %pad_add_fusion.core_ref, bf16[16,32,1024]{2,1,0:T(8,128)(2,1)S(1)} %all-to-all-done.1.mid_ref, s32[128,1]{1,0:T(8,128)S(1)} %reshape_reshape.8.order_q_ref, ...), custom_call_target="tpu_custom_call" | custom-call | tf_op jit(solution)/shard_map/temporal_phase/pallas_call | solution.py:310
  87.9 5.2 %collective-permute-start.8 = (bf16[4,8,32,512]{3,2,1,0:T(8,128)(2,1)S(1)}, bf16[4,8,32,512]{3,2,1,0:T(8,128)(2,1)S(1)}, u32[]{:S(2)}, u32[]{:S(2)}) collective-permute-start(bf16[4,8,32,512]{3,2,1,0:T(8,128)(2,1)S(1)} %get-tuple-element.11), channel_id=1, source_target_pairs={{0,32},{32,0},{64,96},{96,64},{1,33},{33,1},{65,97},{97,65},{2,34}... | collective-permute-start | bytes 3145736 | tf_op jit(solution)/shard_map/ppermute | solution.py:403
  93.1 2.3 %collective-permute-done.8.got_ref = bf16[4,8,32,512]{3,2,1,0:T(8,128)(2,1)S(1)} collective-permute-done((bf16[4,8,32,512]{3,2,1,0:T(8,128)(2,1)S(1)}, bf16[4,8,32,512]{3,2,1,0:T(8,128)(2,1)S(1)}, u32[]{:S(2)}, u32[]{:S(2)}) %collective-permute-start.8) | collective-permute-done | bytes 1048608 | tf_op jit(solution)/shard_map/ppermute | solution.py:403
  95.4 1.3 fusion.2
  96.7 0.1 collective-permute-start.9
  96.8 1.2 collective-permute-start.10
  98.0 1.4 collective-permute-start.11
  99.4 1.0 own_slot.1.own_ref
  100.4 10.6 %collective-permute-done.9.refs_0_ = bf16[8,32,512]{2,1,0:T(8,128)(2,1)S(1)} collective-permute-done((bf16[8,32,512]{2,1,0:T(8,128)(2,1)S(1)}, bf16[8,32,512]{2,1,0:T(8,128)(2,1)S(1)}, u32[]{:S(2)}, u32[]{:S(2)}) %collective-permute-start.9) | collective-permute-done | bytes 262176 | tf_op jit(solution)/shard_map/ppermute | solution.py:406
  111.1 0.4 collective-permute-done.11.refs_2_
  111.5 0.2 space_sum.1
  111.7 16.2 %all_to_all.20 = bf16[16,32,512]{2,1,0:T(8,128)(2,1)S(1)} all-to-all(bf16[16,32,512]{2,1,0:T(8,128)(2,1)S(1)} %bitcast.42), channel_id=1, replica_groups={{0,4,8,12,16,20,24,28,64,68,72,76,80,84,88,92},{32,36,40,44,48,52,56,60..., dimensions={0} | all-to-all | bytes 1048576 | tf_op jit(solution)/shard_map/all_to_all | solution.py:411
  127.9 3.6 %all-to-all-start.2 = ((bf16[8,2,32,1024]{3,2,1,0:T(8,128)(2,1)}), bf16[8,2,32,1024]{3,2,1,0:T(8,128)(2,1)S(1)}, u32[]{:S(2)}, u32[]{:S(2)}) async-start(bf16[8,2,32,1024]{3,2,1,0:T(8,128)(2,1)} %bitcast.21), calls=%async_computation.2 | async-start | bytes 2097152 | tf_op jit(solution)/shard_map/all_to_all | solution.py:377
  131.5 0.1 reduce_sum.12
  131.6 2.4 %collective-permute-start.12 = (bf16[32,512]{1,0:T(8,128)(2,1)S(1)}, bf16[32,512]{1,0:T(8,128)(2,1)S(1)}, u32[]{:S(2)}, u32[]{:S(2)}) collective-permute-start(bf16[32,512]{1,0:T(8,128)(2,1)S(1)} %reduce_sum.12), channel_id=1, source_target_pairs={{0,32},{32,0},{64,96},{96,64},{1,33},{33,1},{65,97},{97,65},{2,34}... | collective-permute-start | bytes 98312 | tf_op jit(solution)/shard_map/ppermute | solution.py:416
  133.9 11.3 %all-to-all-done.2 = bf16[8,2,32,1024]{3,2,1,0:T(8,128)(2,1)S(1)} async-done(((bf16[8,2,32,1024]{3,2,1,0:T(8,128)(2,1)}), bf16[8,2,32,1024]{3,2,1,0:T(8,128)(2,1)S(1)}, u32[]{:S(2)}, u32[]{:S(2)}) %all-to-all-start.2) | async-done | bytes 1048608 | tf_op jit(solution)/shard_map/all_to_all | solution.py:377
  145.3 1.1 copy.17
  146.3 0.7 fusion.3
  (26 shorter events, 0.1 us)
Async XLA Ops:
  0.6 26.2 %copy-start.1 = (f32[1024]{0:T(1024)S(1)}, f32[1024]{0:T(1024)}, u32[]{:S(2)}) copy-start(f32[1024]{0:T(1024)} %param.13) | copy-start | bytes 12292
  0.6 21.3 %all-to-all-start = ((bf16[16,8,4,1024]{3,2,1,0:T(4,128)(2,1)}), bf16[16,8,4,1024]{3,2,1,0:T(4,128)(2,1)S(1)}, u32[]{:S(2)}, u32[]{:S(2)}) async-start(bf16[16,8,4,1024]{3,2,1,0:T(4,128)(2,1)} %bitcast.48), calls=%async_computation | async-start | bytes 2097152 | tf_op jit(solution)/shard_map/all_to_all | solution.py:385
  22.0 0.7 copy-start
  23.4 10.9 %collective-permute-start = (bf16[4,32,1024]{2,1,0:T(8,128)(2,1)S(1)}, bf16[4,32,1024]{2,1,0:T(8,128)(2,1)S(1)}, u32[]{:S(2)}, u32[]{:S(2)}) collective-permute-start(bf16[4,32,1024]{2,1,0:T(8,128)(2,1)S(1)} %edge_norm.1), channel_id=1, source_target_pairs={{0,3},{1,2},{2,1},{3,0},{4,7},{5,6},{6,5},{7,4},{8,11},{9,10},{10,... | collective-permute-start | bytes 786440 | tf_op jit(solution)/shard_map/ppermute | solution.py:393
  34.3 17.4 %copy-start.3 = (bf16[1,2,8,32,1024]{4,3,2,1,0:T(8,128)(2,1)S(1)}, bf16[1,2,8,32,1024]{4,3,2,1,0:T(8,128)(2,1)}, u32[]{:S(2)}) copy-start(bf16[1,2,8,32,1024]{4,3,2,1,0:T(8,128)(2,1)} %param.19) | copy-start | bytes 3145732
  44.7 28.2 %copy-start.11 = (s32[1,16]{1,0:T(1,128)S(1)}, s32[1,16]{1,0:T(1,128)}, u32[]{:S(2)}) copy-start(s32[1,16]{1,0:T(1,128)} %param.11) | copy-start | bytes 196
  44.7 31.7 %copy-start.2 = (f32[1024]{0:T(1024)S(1)}, f32[1024]{0:T(1024)}, u32[]{:S(2)}) copy-start(f32[1024]{0:T(1024)} %param.16) | copy-start | bytes 12292
  44.7 31.0 %all-to-all-start.1 = ((bf16[16,32,1024]{2,1,0:T(8,128)(2,1)}), bf16[16,32,1024]{2,1,0:T(8,128)(2,1)S(1)}, u32[]{:S(2)}, u32[]{:S(2)}) async-start(bf16[16,32,1024]{2,1,0:T(8,128)(2,1)} %bitcast.47), calls=%async_computation.1 | async-start | bytes 2097152 | tf_op jit(solution)/shard_map/all_to_all | solution.py:385
  52.5 16.1 %collective-permute-start.1 = (bf16[2,32,1024]{2,1,0:T(8,128)(2,1)S(1)}, bf16[2,32,1024]{2,1,0:T(8,128)(2,1)S(1)}, u32[]{:S(2)}, u32[]{:S(2)}) collective-permute-start(bf16[2,32,1024]{2,1,0:T(8,128)(2,1)S(1)} %get-tuple-element.22), channel_id=1, source_target_pairs={{0,4},{4,8},{8,12},{12,16},{16,20},{20,24},{24,28},{28,0},{1,5},{5... | collective-permute-start | bytes 393224 | tf_op jit(solution)/shard_map/ppermute | solution.py:390
  53.8 17.0 %collective-permute-start.2 = (bf16[2,32,1024]{2,1,0:T(8,128)(2,1)S(1)}, bf16[2,32,1024]{2,1,0:T(8,128)(2,1)S(1)}, u32[]{:S(2)}, u32[]{:S(2)}) collective-permute-start(bf16[2,32,1024]{2,1,0:T(8,128)(2,1)S(1)} %get-tuple-element.21), channel_id=1, source_target_pairs={{0,8},{4,12},{8,16},{12,20},{16,24},{20,28},{24,0},{28,4},{1,9},{5... | collective-permute-start | bytes 393224 | tf_op jit(solution)/shard_map/ppermute | solution.py:390
  54.9 18.9 %collective-permute-start.3 = (bf16[2,32,1024]{2,1,0:T(8,128)(2,1)S(1)}, bf16[2,32,1024]{2,1,0:T(8,128)(2,1)S(1)}, u32[]{:S(2)}, u32[]{:S(2)}) collective-permute-start(bf16[2,32,1024]{2,1,0:T(8,128)(2,1)S(1)} %get-tuple-element.20), channel_id=1, source_target_pairs={{0,12},{4,16},{8,20},{12,24},{16,28},{20,0},{24,4},{28,8},{1,13},{... | collective-permute-start | bytes 393224 | tf_op jit(solution)/shard_map/ppermute | solution.py:390
  56.7 17.1 %collective-permute-start.4 = (bf16[2,32,1024]{2,1,0:T(8,128)(2,1)S(1)}, bf16[2,32,1024]{2,1,0:T(8,128)(2,1)S(1)}, u32[]{:S(2)}, u32[]{:S(2)}) collective-permute-start(bf16[2,32,1024]{2,1,0:T(8,128)(2,1)S(1)} %get-tuple-element.19), channel_id=1, source_target_pairs={{0,16},{4,20},{8,24},{12,28},{16,0},{20,4},{24,8},{28,12},{1,17},{... | collective-permute-start | bytes 393224 | tf_op jit(solution)/shard_map/ppermute | solution.py:390
  58.5 15.4 %collective-permute-start.5 = (bf16[2,32,1024]{2,1,0:T(8,128)(2,1)S(1)}, bf16[2,32,1024]{2,1,0:T(8,128)(2,1)S(1)}, u32[]{:S(2)}, u32[]{:S(2)}) collective-permute-start(bf16[2,32,1024]{2,1,0:T(8,128)(2,1)S(1)} %get-tuple-element.18), channel_id=1, source_target_pairs={{0,20},{4,24},{8,28},{12,0},{16,4},{20,8},{24,12},{28,16},{1,21},{... | collective-permute-start | bytes 393224 | tf_op jit(solution)/shard_map/ppermute | solution.py:390
  68.6 7.2 %copy-start.4 = (bf16[2,32,1024]{2,1,0:T(8,128)(2,1)}, bf16[2,32,1024]{2,1,0:T(8,128)(2,1)S(1)}, u32[]{:S(2)}) copy-start(bf16[2,32,1024]{2,1,0:T(8,128)(2,1)S(1)} %collective-permute-done.1.refs_1_) | copy-start | bytes 393220
  68.6 5.2 %collective-permute-start.6 = (bf16[2,32,1024]{2,1,0:T(8,128)(2,1)S(1)}, bf16[2,32,1024]{2,1,0:T(8,128)(2,1)S(1)}, u32[]{:S(2)}, u32[]{:S(2)}) collective-permute-start(bf16[2,32,1024]{2,1,0:T(8,128)(2,1)S(1)} %get-tuple-element.24), channel_id=1, source_target_pairs={{0,24},{4,28},{8,0},{12,4},{16,8},{20,12},{24,16},{28,20},{1,25},{... | collective-permute-start | bytes 393224 | tf_op jit(solution)/shard_map/ppermute | solution.py:390
  70.8 5.0 %copy-start.5 = (bf16[2,32,1024]{2,1,0:T(8,128)(2,1)}, bf16[2,32,1024]{2,1,0:T(8,128)(2,1)S(1)}, u32[]{:S(2)}) copy-start(bf16[2,32,1024]{2,1,0:T(8,128)(2,1)S(1)} %collective-permute-done.2.refs_2_) | copy-start | bytes 393220
  70.8 5.0 %collective-permute-start.7 = (bf16[2,32,1024]{2,1,0:T(8,128)(2,1)S(1)}, bf16[2,32,1024]{2,1,0:T(8,128)(2,1)S(1)}, u32[]{:S(2)}, u32[]{:S(2)}) collective-permute-start(bf16[2,32,1024]{2,1,0:T(8,128)(2,1)S(1)} %get-tuple-element.17), channel_id=1, source_target_pairs={{0,28},{4,0},{8,4},{12,8},{16,12},{20,16},{24,20},{28,24},{1,29},{... | collective-permute-start | bytes 393224 | tf_op jit(solution)/shard_map/ppermute | solution.py:390
  73.8 2.0 %copy-start.6 = (bf16[2,32,1024]{2,1,0:T(8,128)(2,1)}, bf16[2,32,1024]{2,1,0:T(8,128)(2,1)S(1)}, u32[]{:S(2)}) copy-start(bf16[2,32,1024]{2,1,0:T(8,128)(2,1)S(1)} %collective-permute-done.3.refs_3_) | copy-start | bytes 393220
  73.8 2.0 %copy-start.7 = (bf16[2,32,1024]{2,1,0:T(8,128)(2,1)}, bf16[2,32,1024]{2,1,0:T(8,128)(2,1)S(1)}, u32[]{:S(2)}) copy-start(bf16[2,32,1024]{2,1,0:T(8,128)(2,1)S(1)} %collective-permute-done.4.refs_4_) | copy-start | bytes 393220
  73.8 2.0 %copy-start.8 = (bf16[2,32,1024]{2,1,0:T(8,128)(2,1)}, bf16[2,32,1024]{2,1,0:T(8,128)(2,1)S(1)}, u32[]{:S(2)}) copy-start(bf16[2,32,1024]{2,1,0:T(8,128)(2,1)S(1)} %collective-permute-done.5.refs_5_) | copy-start | bytes 393220
  73.8 2.0 %copy-start.9 = (bf16[2,32,1024]{2,1,0:T(8,128)(2,1)}, bf16[2,32,1024]{2,1,0:T(8,128)(2,1)S(1)}, u32[]{:S(2)}) copy-start(bf16[2,32,1024]{2,1,0:T(8,128)(2,1)S(1)} %collective-permute-done.6.refs_6_) | copy-start | bytes 393220
  75.8 0.6 copy-start.10
  87.9 7.5 %collective-permute-start.8 = (bf16[4,8,32,512]{3,2,1,0:T(8,128)(2,1)S(1)}, bf16[4,8,32,512]{3,2,1,0:T(8,128)(2,1)S(1)}, u32[]{:S(2)}, u32[]{:S(2)}) collective-permute-start(bf16[4,8,32,512]{3,2,1,0:T(8,128)(2,1)S(1)} %get-tuple-element.11), channel_id=1, source_target_pairs={{0,32},{32,0},{64,96},{96,64},{1,33},{33,1},{65,97},{97,65},{2,34}... | collective-permute-start | bytes 3145736 | tf_op jit(solution)/shard_map/ppermute | solution.py:403
  96.7 14.4 %collective-permute-start.9 = (bf16[8,32,512]{2,1,0:T(8,128)(2,1)S(1)}, bf16[8,32,512]{2,1,0:T(8,128)(2,1)S(1)}, u32[]{:S(2)}, u32[]{:S(2)}) collective-permute-start(bf16[8,32,512]{2,1,0:T(8,128)(2,1)S(1)} %get-tuple-element.16), channel_id=1, source_target_pairs={{0,1},{1,2},{2,3},{3,0},{4,5},{5,6},{6,7},{7,4},{8,9},{9,10},{10,1... | collective-permute-start | bytes 786440 | tf_op jit(solution)/shard_map/ppermute | solution.py:406
  96.8 14.3 %collective-permute-start.10 = (bf16[8,32,512]{2,1,0:T(8,128)(2,1)S(1)}, bf16[8,32,512]{2,1,0:T(8,128)(2,1)S(1)}, u32[]{:S(2)}, u32[]{:S(2)}) collective-permute-start(bf16[8,32,512]{2,1,0:T(8,128)(2,1)S(1)} %get-tuple-element.15), channel_id=1, source_target_pairs={{0,2},{1,3},{2,0},{3,1},{4,6},{5,7},{6,4},{7,5},{8,10},{9,11},{10,... | collective-permute-start | bytes 786440 | tf_op jit(solution)/shard_map/ppermute | solution.py:406
  98.0 13.5 %collective-permute-start.11 = (bf16[8,32,512]{2,1,0:T(8,128)(2,1)S(1)}, bf16[8,32,512]{2,1,0:T(8,128)(2,1)S(1)}, u32[]{:S(2)}, u32[]{:S(2)}) collective-permute-start(bf16[8,32,512]{2,1,0:T(8,128)(2,1)S(1)} %get-tuple-element.14), channel_id=1, source_target_pairs={{0,3},{1,0},{2,1},{3,2},{4,7},{5,4},{6,5},{7,6},{8,11},{9,8},{10,9... | collective-permute-start | bytes 786440 | tf_op jit(solution)/shard_map/ppermute | solution.py:406
  127.9 17.4 %all-to-all-start.2 = ((bf16[8,2,32,1024]{3,2,1,0:T(8,128)(2,1)}), bf16[8,2,32,1024]{3,2,1,0:T(8,128)(2,1)S(1)}, u32[]{:S(2)}, u32[]{:S(2)}) async-start(bf16[8,2,32,1024]{3,2,1,0:T(8,128)(2,1)} %bitcast.21), calls=%async_computation.2 | async-start | bytes 2097152 | tf_op jit(solution)/shard_map/all_to_all | solution.py:377
  131.6 14.8 %collective-permute-start.12 = (bf16[32,512]{1,0:T(8,128)(2,1)S(1)}, bf16[32,512]{1,0:T(8,128)(2,1)S(1)}, u32[]{:S(2)}, u32[]{:S(2)}) collective-permute-start(bf16[32,512]{1,0:T(8,128)(2,1)S(1)} %reduce_sum.12), channel_id=1, source_target_pairs={{0,32},{32,0},{64,96},{96,64},{1,33},{33,1},{65,97},{97,65},{2,34}... | collective-permute-start | bytes 98312 | tf_op jit(solution)/shard_map/ppermute | solution.py:416

commit v11 on v9

--- a/solution.py
+++ b/solution.py
@@ -235,13 +235,13 @@
 GROUP = 8
 
 
-def temporal_kernel(core_ref, mid_ref, order_q_ref, order_k_ref, gain_ref, wq_ref, cot_ref, w_ref, wm_ref,
+def temporal_kernel(core_ref, mid_ref, order_q_ref, order_k_ref, gain_ref, cot_ref, w_ref, wm_ref,
                     out_hbm, send_ref, keep_hbm,
                     out_ref, keep_ref, wqkv_buf, wm_buf, cot_buf, normed_ref, q_ref, k_ref, v_ref, ctx_ref, cotb_ref, sems):
     frames, cols, _ = mid_ref.shape
     groups = cols // GROUP
     n = frames * GROUP
-    copies = column_copies(w_ref, wqkv_buf, sems, (1, 2))
+    copies = column_copies(w_ref, wqkv_buf, sems, range(3))
     copies.append(pltpu.make_async_copy(cot_ref, cot_buf, sems.at[3]))
     copies.append(pltpu.make_async_copy(wm_ref, wm_buf, sems.at[4]))
     for c in copies:
@@ -250,11 +250,10 @@
     for g in range(groups):
         x = mid_ref[:, g * GROUP:(g + 1) * GROUP, :].astype(F32).reshape(n, D)
         normed_ref[g * n:(g + 1) * n] = normalized(x, gain).astype(BF)
-    q_ref[...] = jnp.dot(normed_ref[...], wq_ref[...], preferred_element_type=F32).astype(BF)
-    for i, buf in enumerate((k_ref, v_ref)):
+    for i, buf in enumerate((q_ref, k_ref, v_ref)):
         copies[i].wait()
         buf[...] = jnp.dot(normed_ref[...], wqkv_buf[i], preferred_element_type=F32).astype(BF)
-    copies[2].wait()
+    copies[3].wait()
     for g in range(groups):
         cotb_ref[g * n:(g + 1) * n] = cot_buf[:, g * GROUP:(g + 1) * GROUP, :].astype(F32).reshape(n, D).astype(BF)
     place_q = lax.broadcasted_iota(jnp.int32, (n, n), 0) % GROUP
@@ -284,7 +283,7 @@
                 ref[slot, t] = grad[row:row + block]
     kept = pltpu.make_async_copy(keep_ref, keep_hbm, sems.at[5])
     kept.start()
-    copies[3].wait()
+    copies[4].wait()
     y = jnp.dot(ctx_ref[...], wm_buf[...], preferred_element_type=F32)
     for g in range(groups):
         x = mid_ref[:, g * GROUP:(g + 1) * GROUP, :].astype(F32) + y[g * n:(g + 1) * n].reshape(frames, GROUP, D)
@@ -302,19 +301,18 @@
     spread = jnp.repeat(order, GROUP)
     block = D // (spaces * times)
     part = (spaces, times, block, D // 2)
-    first_third = heads[:, :D]
     return pl.pallas_call(
         temporal_kernel,
-        in_specs=[SMEM] + [VMEM] * 5 + [HBM] * 3,
+        in_specs=[SMEM] + [VMEM] * 4 + [HBM] * 3,
         out_specs=[HBM, VMEM, HBM],
         out_shape=[pltpu.HBM((frames, cols, D), BF), pltpu.VMEM(part, BF), pltpu.HBM(part, BF)],
-        scratch_shapes=[pltpu.VMEM((frames, cols, D), BF), pltpu.VMEM(part, BF), pltpu.VMEM((2, D, D), BF), pltpu.VMEM((D, D), BF), pltpu.VMEM((frames, cols, D), BF)]
+        scratch_shapes=[pltpu.VMEM((frames, cols, D), BF), pltpu.VMEM(part, BF), pltpu.VMEM((3, D, D), BF), pltpu.VMEM((D, D), BF), pltpu.VMEM((frames, cols, D), BF)]
         + [pltpu.VMEM((tokens, D), BF)] * 6
         + [pltpu.SemaphoreType.DMA((7,))],
         compiler_params=pltpu.CompilerParams(vmem_limit_bytes=40 * 2**20),
         name="temporal_phase",
     )(core, in_vmem(mid), spread.reshape(n, 1), spread.reshape(1, n), gain.reshape(1, D),
-      in_vmem(first_third), in_hbm(cot), in_hbm(heads), in_hbm(merge))
+      in_hbm(cot), in_hbm(heads), in_hbm(merge))
 
 
 def own_kernel(keep_ref, got_ref, out_ref):
@@ -401,11 +399,16 @@
              for k in range(1, space)]
     own = own_slot(keep, got)
     over_space = space_sum(own, moved)
-    over_tm = exchange(over_space, "tm")
-    over_tm = over_tm.astype(F32).sum(0).astype(BF)
-    block = over_tm.shape[0]
-    parts = lax.all_gather(over_tm, "batch").astype(F32).reshape(batch // 2, 2, block, D // 2).sum(0)
-    weight_grad = parts.swapaxes(0, 1).reshape(block, D)
+    pieces = exchange(over_space, "tm")
+    mine = pieces.astype(F32).sum(0).astype(BF)
+    swapped = [lax.ppermute(mine, "batch", [(i, i ^ m) for i in range(batch)]).astype(F32) for m in (2, 3, 1)]
+    own_half = mine.astype(F32) + swapped[0]
+    other_half = swapped[1] + swapped[2]
+    weight_grad = jnp.where(
+        core[0] == 0,
+        jnp.concatenate([own_half, other_half], axis=1),
+        jnp.concatenate([other_half, own_half], axis=1),
+    )
     return (output.reshape(1, frames, rows, wide, D), weight_grad)
 
 

time: 130 us -> 141 us (1.085)
  waiting for transfers between devices: 36.6 us -> 48.3 us
  starting transfers between devices: 40.2 us -> 43.5 us
  local copies, waits for them, and re-layouts: 6.74 us -> 4.24 us
    all_gather x1 -> x0, blocking collectives: 9.7 us -> none  [per_device(): lax.all_gather(over_tm, 'batch').astype(F32)]
    all_to_all x0 -> x1, blocking collectives: none -> 9.44 us  [per_device(): lax.all_to_all(v, axis, split_axis=0, concat_axis=0, tiled=True)]
    ppermute x0 -> x3, starting transfers between devices: none -> 8.84 us  [per_device(): lax.ppermute(mine, 'batch', [(i, i ^ m) for i in range(batch)]).astype(F32)]
    all_to_all x3 -> x2, waiting for transfers between devices: 4.76 us -> 10.2 us  [per_device(): lax.all_to_all(v, axis, split_axis=0, concat_axis=0, tiled=True)]
    all_to_all x3 -> x2, starting transfers between devices: 14.7 us -> 9.37 us  [per_device(): lax.all_to_all(v, axis, split_axis=0, concat_axis=0, tiled=True)]
    ppermute x1, waiting for transfers between devices: 0.01 us -> 2.29 us  [per_device(): got = lax.ppermute(send, 'batch', [(i, i ^ 1) for i in range(batch)])]
    ppermute x0 -> x3, waiting for transfers between devices: none -> 2.17 us  [per_device(): lax.ppermute(mine, 'batch', [(i, i ^ m) for i in range(batch)]).astype(F32)]
    all_to_all x2, waiting for transfers between devices: 21.9 us -> 23.7 us  [per_device(): lax.all_to_all(v, ('tm', 'space'), split_axis=0, concat_axis=0, axis_inde...]
  transfers between devices with their start and end apart: 10 -> 12, of which waited for: 5 -> 7; matrix products, arithmetic and copies ran while one was open for 6% -> 3% of each run, Pallas kernels for 16% -> 14%
where the time goes in v11:
time: 141 us
  waiting for transfers between devices  48.3 us (34%)
  starting transfers between devices  43.5 us (31%)
  Pallas kernels  31.2 us (22%)
  blocking collectives  9.44 us (7%)
  local copies, waits for them, and re-layouts  4.24 us (3%)
  other arithmetic  2.25 us (2%)
  between operations  2.05 us (1%)
    all_to_all x2, waiting for transfers between devices, per_device(): lax.all_to_all(v, ('tm', 'space'), split_axis=0, concat_axis=0, axis_inde...  23.7 us
    all_to_all x2, starting transfers between devices, per_device(): lax.all_to_all(v, ('tm', 'space'), split_axis=0, concat_axis=0, axis_inde...  14 us
    pallas_call x1, Pallas kernels, temporal_phase(): pl.pallas_call(temporal_kernel, in_specs=[SMEM] + [VMEM] * 4 + [HBM] * 3,...  11.4 us
    pallas_call x1, Pallas kernels, spatial_phase(): pl.pallas_call(spatial_kernel, in_specs=[SMEM, VMEM, HBM, HBM, HBM, HBM],...  10.3 us
    all_to_all x2, waiting for transfers between devices, per_device(): lax.all_to_all(v, axis, split_axis=0, concat_axis=0, tiled=True)  10.2 us
    ppermute x3, waiting for transfers between devices, per_device(): lax.ppermute(chip[k - 1].astype(BF), 'space', [(i, (i + k) % space) for i...  9.98 us
    all_to_all x1, blocking collectives, per_device(): lax.all_to_all(v, axis, split_axis=0, concat_axis=0, tiled=True)  9.44 us
    all_to_all x2, starting transfers between devices, per_device(): lax.all_to_all(v, axis, split_axis=0, concat_axis=0, tiled=True)  9.37 us
  transfers between devices with their start and end apart: 12, of which 7 were waited for; matrix products, arithmetic and copies ran while one was open for 3% of the time, Pallas kernels for 14%

profile of v11, /device:TPU:1, one launch (start us, length us, event | category | flops | bytes accessed | tf_op | source)
XLA Modules:
  0.0 140.9 jit_solution(16711954350252595825)
XLA Ops:
  0.6 0.0 copy-start.3
  0.6 0.0 copy-start
  0.6 7.6 %all-to-all-start = ((bf16[16,8,4,1024]{3,2,1,0:T(4,128)(2,1)}), bf16[16,8,4,1024]{3,2,1,0:T(4,128)(2,1)S(1)}, u32[]{:S(2)}, u32[]{:S(2)}) async-start(bf16[16,8,4,1024]{3,2,1,0:T(4,128)(2,1)} %bitcast.36), calls=%async_computation | async-start | bytes 2097152 | tf_op jit(solution)/shard_map/all_to_all | solution.py:378
  8.3 2.3 %copy.22 = bf16[1,2,8,32,1024]{4,3,1,2,0:T(8,128)(2,1)} copy(bf16[1,2,8,32,1024]{4,3,2,1,0:T(8,128)(2,1)} %param.19) | data formatting | bytes 2097152 | tf_op args[9]
  10.6 11.5 %all-to-all-done = bf16[16,8,4,1024]{3,2,1,0:T(4,128)(2,1)S(1)} async-done(((bf16[16,8,4,1024]{3,2,1,0:T(4,128)(2,1)}), bf16[16,8,4,1024]{3,2,1,0:T(4,128)(2,1)S(1)}, u32[]{:S(2)}, u32[]{:S(2)}) %all-to-all-start) | async-done | bytes 1048608 | tf_op jit(solution)/shard_map/all_to_all | solution.py:378
  22.1 5.8 %all-to-all-start.2 = ((bf16[8,2,32,1024]{3,2,1,0:T(8,128)(2,1)}), bf16[8,2,32,1024]{3,2,1,0:T(8,128)(2,1)S(1)}, u32[]{:S(2)}, u32[]{:S(2)}) async-start(bf16[8,2,32,1024]{3,2,1,0:T(8,128)(2,1)} %bitcast.27), calls=%async_computation.2 | async-start | bytes 2097152 | tf_op jit(solution)/shard_map/all_to_all | solution.py:370
  27.9 0.6 fusion.3
  29.8 0.1 pad_add_fusion.1.info_ref
  29.9 0.8 edge_norm.1
  30.7 3.4 %collective-permute-start = (bf16[4,32,1024]{2,1,0:T(8,128)(2,1)S(1)}, bf16[4,32,1024]{2,1,0:T(8,128)(2,1)S(1)}, u32[]{:S(2)}, u32[]{:S(2)}) collective-permute-start(bf16[4,32,1024]{2,1,0:T(8,128)(2,1)S(1)} %edge_norm.1), channel_id=1, source_target_pairs={{0,3},{1,2},{2,1},{3,0},{4,7},{5,6},{6,5},{7,4},{8,11},{9,10},{10,... | collective-permute-start | bytes 786440 | tf_op jit(solution)/shard_map/ppermute | solution.py:383
  34.0 7.5 %qkv_own.1 = (bf16[3,512,1024]{2,1,0:T(8,128)(2,1)}, bf16[16,32,1024]{2,1,0:T(8,128)(2,1)}) custom-call(s32[2]{0:T(128)S(1)} %pad_add_fusion.1.info_ref, bf16[8,2,8,4,1024]{4,3,2,1,0:T(4,128)(2,1)S(1)} %bitcast.29, f32[1,1024]{1,0:T(1,128)S(1)} %bitcast.31, bf16[1024,3072]{1,0:T(8,128)(2,1)} %w_ref.4), custom_call_target="tpu_custom_call" | custom-call | tf_op jit(solution)/shard_map/qkv_own/pallas_call | solution.py:111
  41.5 0.0 collective-permute-done.halo_ref
  41.6 0.0 copy-start.4
  41.6 0.0 copy-start.1
  41.6 10.3 %spatial_phase.1 = bf16[8,2,32,1024]{3,2,1,0:T(8,128)(2,1)} custom-call(s32[2]{0:T(128)S(1)} %pad_add_fusion.1.info_ref, bf16[4,32,1024]{2,1,0:T(8,128)(2,1)S(1)} %collective-permute-done.halo_ref, bf16[3,512,1024]{2,1,0:T(8,128)(2,1)} %get-tuple-element.10.qkv_ref, bf16[16,32,1024]{2,1,0:T(8,128)(2,1)} %get-tuple-element.11.tok_ref, ...), custom_call_target="tpu_custom_call" | custom-call | tf_op jit(solution)/shard_map/spatial_phase/pallas_call | solution.py:219
  51.9 0.0 all-to-all-done.2
  51.9 0.0 copy-start.2
  52.0 6.3 %all-to-all-start.1 = ((bf16[16,32,1024]{2,1,0:T(8,128)(2,1)}), bf16[16,32,1024]{2,1,0:T(8,128)(2,1)S(1)}, u32[]{:S(2)}, u32[]{:S(2)}) async-start(bf16[16,32,1024]{2,1,0:T(8,128)(2,1)} %bitcast.35), calls=%async_computation.1 | async-start | bytes 2097152 | tf_op jit(solution)/shard_map/all_to_all | solution.py:378
  58.3 0.0 copy-done.4
  58.3 0.1 broadcast_in_dim.3
  58.4 0.1 reshape_reshape.8.order_q_ref
  58.5 0.1 reshape_reshape.7.order_k_ref
  58.6 0.1 pad_add_fusion.core_ref
  58.6 12.2 %all-to-all-done.1.mid_ref = bf16[16,32,1024]{2,1,0:T(8,128)(2,1)S(1)} async-done(((bf16[16,32,1024]{2,1,0:T(8,128)(2,1)}), bf16[16,32,1024]{2,1,0:T(8,128)(2,1)S(1)}, u32[]{:S(2)}, u32[]{:S(2)}) %all-to-all-start.1) | async-done | bytes 1048608 | tf_op jit(solution)/shard_map/all_to_all | solution.py:378
  70.8 0.0 copy-done.2
  70.8 11.4 %temporal_phase.1 = (bf16[16,32,1024]{2,1,0:T(8,128)(2,1)}, bf16[4,8,32,512]{3,2,1,0:T(8,128)(2,1)S(1)}, bf16[4,8,32,512]{3,2,1,0:T(8,128)(2,1)}) custom-call(s32[2]{0:T(128)S(1)} %pad_add_fusion.core_ref, bf16[16,32,1024]{2,1,0:T(8,128)(2,1)S(1)} %all-to-all-done.1.mid_ref, s32[128,1]{1,0:T(8,128)S(1)} %reshape_reshape.8.order_q_ref, ...), custom_call_target="tpu_custom_call" | custom-call | tf_op jit(solution)/shard_map/temporal_phase/pallas_call | solution.py:304
  82.3 4.2 %collective-permute-start.1 = (bf16[4,8,32,512]{3,2,1,0:T(8,128)(2,1)S(1)}, bf16[4,8,32,512]{3,2,1,0:T(8,128)(2,1)S(1)}, u32[]{:S(2)}, u32[]{:S(2)}) collective-permute-start(bf16[4,8,32,512]{3,2,1,0:T(8,128)(2,1)S(1)} %get-tuple-element.15), channel_id=1, source_target_pairs={{0,32},{32,0},{64,96},{96,64},{1,33},{33,1},{65,97},{97,65},{2,34}... | collective-permute-start | bytes 3145736 | tf_op jit(solution)/shard_map/ppermute | solution.py:395
  86.4 2.3 %collective-permute-done.1.got_ref = bf16[4,8,32,512]{3,2,1,0:T(8,128)(2,1)S(1)} collective-permute-done((bf16[4,8,32,512]{3,2,1,0:T(8,128)(2,1)S(1)}, bf16[4,8,32,512]{3,2,1,0:T(8,128)(2,1)S(1)}, u32[]{:S(2)}, u32[]{:S(2)}) %collective-permute-start.1) | collective-permute-done | bytes 1048608 | tf_op jit(solution)/shard_map/ppermute | solution.py:395
  88.7 1.4 fusion.2
  90.1 1.3 collective-permute-start.2
  91.4 0.1 collective-permute-start.3
  91.4 2.4 %collective-permute-start.4 = (bf16[8,32,512]{2,1,0:T(8,128)(2,1)S(1)}, bf16[8,32,512]{2,1,0:T(8,128)(2,1)S(1)}, u32[]{:S(2)}, u32[]{:S(2)}) collective-permute-start(bf16[8,32,512]{2,1,0:T(8,128)(2,1)S(1)} %get-tuple-element.18), channel_id=1, source_target_pairs={{0,3},{1,0},{2,1},{3,2},{4,7},{5,4},{6,5},{7,6},{8,11},{9,8},{10,9... | collective-permute-start | bytes 786440 | tf_op jit(solution)/shard_map/ppermute | solution.py:398
  93.8 1.0 own_slot.1.own_ref
  94.8 9.6 %collective-permute-done.2.refs_0_ = bf16[8,32,512]{2,1,0:T(8,128)(2,1)S(1)} collective-permute-done((bf16[8,32,512]{2,1,0:T(8,128)(2,1)S(1)}, bf16[8,32,512]{2,1,0:T(8,128)(2,1)S(1)}, u32[]{:S(2)}, u32[]{:S(2)}) %collective-permute-start.2) | collective-permute-done | bytes 262176 | tf_op jit(solution)/shard_map/ppermute | solution.py:398
  104.5 0.0 collective-permute-done.3.refs_1_
  104.5 0.3 collective-permute-done.4.refs_2_
  104.8 0.1 space_sum.1
  104.9 9.4 %all_to_all.25 = bf16[8,32,512]{2,1,0:T(8,128)(2,1)S(1)} all-to-all(bf16[8,32,512]{2,1,0:T(8,128)(2,1)S(1)} %space_sum.1), channel_id=1, replica_groups=mesh['batch'=4,'tm'=8,'space'=4] {'tm'}, dimensions={0} | all-to-all | bytes 524288 | tf_op jit(solution)/shard_map/all_to_all | solution.py:370
  114.4 3.6 %all-to-all-start.3 = ((bf16[8,2,32,1024]{3,2,1,0:T(8,128)(2,1)}), bf16[8,2,32,1024]{3,2,1,0:T(8,128)(2,1)S(1)}, u32[]{:S(2)}, u32[]{:S(2)}) async-start(bf16[8,2,32,1024]{3,2,1,0:T(8,128)(2,1)} %bitcast.15), calls=%async_computation.3 | async-start | bytes 2097152 | tf_op jit(solution)/shard_map/all_to_all | solution.py:370
  118.0 2.7 %collective-permute-start.5 = (bf16[32,512]{1,0:T(8,128)(2,1)S(1)}, bf16[32,512]{1,0:T(8,128)(2,1)S(1)}, u32[]{:S(2)}, u32[]{:S(2)}) collective-permute-start(bf16[32,512]{1,0:T(8,128)(2,1)S(1)} %reduce_sum.12), channel_id=1, source_target_pairs={{0,64},{32,96},{64,0},{96,32},{1,65},{33,97},{65,1},{97,33},{2,66}... | collective-permute-start | bytes 98312 | tf_op jit(solution)/shard_map/ppermute | solution.py:404
  120.7 10.1 %all-to-all-done.3 = bf16[8,2,32,1024]{3,2,1,0:T(8,128)(2,1)S(1)} async-done(((bf16[8,2,32,1024]{3,2,1,0:T(8,128)(2,1)}), bf16[8,2,32,1024]{3,2,1,0:T(8,128)(2,1)S(1)}, u32[]{:S(2)}, u32[]{:S(2)}) %all-to-all-start.3) | async-done | bytes 1048608 | tf_op jit(solution)/shard_map/all_to_all | solution.py:370
  130.8 1.1 copy.20
  131.9 6.1 %collective-permute-start.6 = (bf16[32,512]{1,0:T(8,128)(2,1)S(1)}, bf16[32,512]{1,0:T(8,128)(2,1)S(1)}, u32[]{:S(2)}, u32[]{:S(2)}) collective-permute-start(bf16[32,512]{1,0:T(8,128)(2,1)S(1)} %reduce_sum.12), channel_id=1, source_target_pairs={{0,96},{32,64},{64,32},{96,0},{1,97},{33,65},{65,33},{97,1},{2,98}... | collective-permute-start | bytes 98312 | tf_op jit(solution)/shard_map/ppermute | solution.py:404
  138.1 0.0 collective-permute-start.7
  138.1 0.0 collective-permute-done.5
  138.1 2.2 %collective-permute-done.6 = bf16[32,512]{1,0:T(8,128)(2,1)S(1)} collective-permute-done((bf16[32,512]{1,0:T(8,128)(2,1)S(1)}, bf16[32,512]{1,0:T(8,128)(2,1)S(1)}, u32[]{:S(2)}, u32[]{:S(2)}) %collective-permute-start.6) | collective-permute-done | bytes 32800 | tf_op jit(solution)/shard_map/ppermute | solution.py:404
  140.2 0.0 collective-permute-done.7
  140.3 0.7 maximum_select_fusion
  (6 shorter events, 0.1 us)
Async XLA Ops:
  0.6 27.3 %copy-start.3 = (s32[1,2]{1,0:T(1,128)S(1)}, s32[1,2]{1,0:T(1,128)}, u32[]{:S(2)}) copy-start(s32[1,2]{1,0:T(1,128)} %param.12) | copy-start | bytes 28
  0.6 29.2 %copy-start = (f32[1024]{0:T(1024)S(1)}, f32[1024]{0:T(1024)}, u32[]{:S(2)}) copy-start(f32[1024]{0:T(1024)} %param.13) | copy-start | bytes 12292
  0.6 21.5 %all-to-all-start = ((bf16[16,8,4,1024]{3,2,1,0:T(4,128)(2,1)}), bf16[16,8,4,1024]{3,2,1,0:T(4,128)(2,1)S(1)}, u32[]{:S(2)}, u32[]{:S(2)}) async-start(bf16[16,8,4,1024]{3,2,1,0:T(4,128)(2,1)} %bitcast.36), calls=%async_computation | async-start | bytes 2097152 | tf_op jit(solution)/shard_map/all_to_all | solution.py:378
  22.1 29.8 %all-to-all-start.2 = ((bf16[8,2,32,1024]{3,2,1,0:T(8,128)(2,1)}), bf16[8,2,32,1024]{3,2,1,0:T(8,128)(2,1)S(1)}, u32[]{:S(2)}, u32[]{:S(2)}) async-start(bf16[8,2,32,1024]{3,2,1,0:T(8,128)(2,1)} %bitcast.27), calls=%async_computation.2 | async-start | bytes 2097152 | tf_op jit(solution)/shard_map/all_to_all | solution.py:370
  30.7 10.9 %collective-permute-start = (bf16[4,32,1024]{2,1,0:T(8,128)(2,1)S(1)}, bf16[4,32,1024]{2,1,0:T(8,128)(2,1)S(1)}, u32[]{:S(2)}, u32[]{:S(2)}) collective-permute-start(bf16[4,32,1024]{2,1,0:T(8,128)(2,1)S(1)} %edge_norm.1), channel_id=1, source_target_pairs={{0,3},{1,2},{2,1},{3,0},{4,7},{5,6},{6,5},{7,4},{8,11},{9,10},{10,... | collective-permute-start | bytes 786440 | tf_op jit(solution)/shard_map/ppermute | solution.py:383
  41.6 16.7 %copy-start.4 = (s32[1,16]{1,0:T(1,128)S(1)}, s32[1,16]{1,0:T(1,128)}, u32[]{:S(2)}) copy-start(s32[1,16]{1,0:T(1,128)} %param.11) | copy-start | bytes 196
  41.6 29.2 %copy-start.1 = (f32[1024]{0:T(1024)S(1)}, f32[1024]{0:T(1024)}, u32[]{:S(2)}) copy-start(f32[1024]{0:T(1024)} %param.16) | copy-start | bytes 12292
  51.9 18.9 %copy-start.2 = (bf16[8,2,32,1024]{3,2,1,0:T(8,128)(2,1)}, bf16[8,2,32,1024]{3,2,1,0:T(8,128)(2,1)S(1)}, u32[]{:S(2)}) copy-start(bf16[8,2,32,1024]{3,2,1,0:T(8,128)(2,1)S(1)} %all-to-all-done.2) | copy-start | bytes 3145732
  52.0 18.9 %all-to-all-start.1 = ((bf16[16,32,1024]{2,1,0:T(8,128)(2,1)}), bf16[16,32,1024]{2,1,0:T(8,128)(2,1)S(1)}, u32[]{:S(2)}, u32[]{:S(2)}) async-start(bf16[16,32,1024]{2,1,0:T(8,128)(2,1)} %bitcast.35), calls=%async_computation.1 | async-start | bytes 2097152 | tf_op jit(solution)/shard_map/all_to_all | solution.py:378
  82.3 6.5 %collective-permute-start.1 = (bf16[4,8,32,512]{3,2,1,0:T(8,128)(2,1)S(1)}, bf16[4,8,32,512]{3,2,1,0:T(8,128)(2,1)S(1)}, u32[]{:S(2)}, u32[]{:S(2)}) collective-permute-start(bf16[4,8,32,512]{3,2,1,0:T(8,128)(2,1)S(1)} %get-tuple-element.15), channel_id=1, source_target_pairs={{0,32},{32,0},{64,96},{96,64},{1,33},{33,1},{65,97},{97,65},{2,34}... | collective-permute-start | bytes 3145736 | tf_op jit(solution)/shard_map/ppermute | solution.py:395
  90.1 14.4 %collective-permute-start.2 = (bf16[8,32,512]{2,1,0:T(8,128)(2,1)S(1)}, bf16[8,32,512]{2,1,0:T(8,128)(2,1)S(1)}, u32[]{:S(2)}, u32[]{:S(2)}) collective-permute-start(bf16[8,32,512]{2,1,0:T(8,128)(2,1)S(1)} %get-tuple-element.20), channel_id=1, source_target_pairs={{0,1},{1,2},{2,3},{3,0},{4,5},{5,6},{6,7},{7,4},{8,9},{9,10},{10,1... | collective-permute-start | bytes 786440 | tf_op jit(solution)/shard_map/ppermute | solution.py:398
  91.4 13.1 %collective-permute-start.3 = (bf16[8,32,512]{2,1,0:T(8,128)(2,1)S(1)}, bf16[8,32,512]{2,1,0:T(8,128)(2,1)S(1)}, u32[]{:S(2)}, u32[]{:S(2)}) collective-permute-start(bf16[8,32,512]{2,1,0:T(8,128)(2,1)S(1)} %get-tuple-element.19), channel_id=1, source_target_pairs={{0,2},{1,3},{2,0},{3,1},{4,6},{5,7},{6,4},{7,5},{8,10},{9,11},{10,... | collective-permute-start | bytes 786440 | tf_op jit(solution)/shard_map/ppermute | solution.py:398
  91.4 13.4 %collective-permute-start.4 = (bf16[8,32,512]{2,1,0:T(8,128)(2,1)S(1)}, bf16[8,32,512]{2,1,0:T(8,128)(2,1)S(1)}, u32[]{:S(2)}, u32[]{:S(2)}) collective-permute-start(bf16[8,32,512]{2,1,0:T(8,128)(2,1)S(1)} %get-tuple-element.18), channel_id=1, source_target_pairs={{0,3},{1,0},{2,1},{3,2},{4,7},{5,4},{6,5},{7,6},{8,11},{9,8},{10,9... | collective-permute-start | bytes 786440 | tf_op jit(solution)/shard_map/ppermute | solution.py:398
  114.4 16.5 %all-to-all-start.3 = ((bf16[8,2,32,1024]{3,2,1,0:T(8,128)(2,1)}), bf16[8,2,32,1024]{3,2,1,0:T(8,128)(2,1)S(1)}, u32[]{:S(2)}, u32[]{:S(2)}) async-start(bf16[8,2,32,1024]{3,2,1,0:T(8,128)(2,1)} %bitcast.15), calls=%async_computation.3 | async-start | bytes 2097152 | tf_op jit(solution)/shard_map/all_to_all | solution.py:370
  118.0 20.1 %collective-permute-start.5 = (bf16[32,512]{1,0:T(8,128)(2,1)S(1)}, bf16[32,512]{1,0:T(8,128)(2,1)S(1)}, u32[]{:S(2)}, u32[]{:S(2)}) collective-permute-start(bf16[32,512]{1,0:T(8,128)(2,1)S(1)} %reduce_sum.12), channel_id=1, source_target_pairs={{0,64},{32,96},{64,0},{96,32},{1,65},{33,97},{65,1},{97,33},{2,66}... | collective-permute-start | bytes 98312 | tf_op jit(solution)/shard_map/ppermute | solution.py:404
  131.9 8.3 %collective-permute-start.6 = (bf16[32,512]{1,0:T(8,128)(2,1)S(1)}, bf16[32,512]{1,0:T(8,128)(2,1)S(1)}, u32[]{:S(2)}, u32[]{:S(2)}) collective-permute-start(bf16[32,512]{1,0:T(8,128)(2,1)S(1)} %reduce_sum.12), channel_id=1, source_target_pairs={{0,96},{32,64},{64,32},{96,0},{1,97},{33,65},{65,33},{97,1},{2,98}... | collective-permute-start | bytes 98312 | tf_op jit(solution)/shard_map/ppermute | solution.py:404
  138.1 2.2 %collective-permute-start.7 = (bf16[32,512]{1,0:T(8,128)(2,1)S(1)}, bf16[32,512]{1,0:T(8,128)(2,1)S(1)}, u32[]{:S(2)}, u32[]{:S(2)}) collective-permute-start(bf16[32,512]{1,0:T(8,128)(2,1)S(1)} %reduce_sum.12), channel_id=1, source_target_pairs={{0,32},{32,0},{64,96},{96,64},{1,33},{33,1},{65,97},{97,65},{2,34}... | collective-permute-start | bytes 98312 | tf_op jit(solution)/shard_map/ppermute | solution.py:404

commit v12 on v11

--- a/solution.py
+++ b/solution.py
@@ -337,7 +337,8 @@
     total = own_ref[...]
     for p in refs[:-1]:
         total = total + p[...].astype(F32)
-    refs[-1][...] = total.astype(BF)
+    refs[-1][0] = total.astype(BF)
+    refs[-1][1] = refs[-1][0]
 
 
 def space_sum(own, moved):
@@ -345,7 +346,7 @@
         sum_kernel,
         in_specs=[VMEM] * (1 + len(moved)),
         out_specs=VMEM,
-        out_shape=pltpu.VMEM(own.shape, BF),
+        out_shape=pltpu.VMEM((2,) + own.shape, BF),
         compiler_params=pltpu.CompilerParams(vmem_limit_bytes=8 * 2**20),
         name="space_sum",
     )(in_vmem(own), *[in_vmem(p) for p in moved])
@@ -396,19 +397,19 @@
     output = exchange(out.reshape(tm, frames, wide, D), "tm").swapaxes(0, 1)
     chip = [keep[k].astype(F32) + got[k].astype(F32) for k in range(1, space)]
     moved = [lax.ppermute(chip[k - 1].astype(BF), "space", [(i, (i + k) % space) for i in range(space)])
-             for k in range(1, space)]
+             for k in sorted(range(1, space), key=lambda k: -min(k, space - k))]
     own = own_slot(keep, got)
     over_space = space_sum(own, moved)
-    pieces = exchange(over_space, "tm")
+    planes = [[(2 * y + c) * tm + t for y in range(batch // 2) for t in range(tm)] for c in range(2)]
+    pieces = lax.all_to_all(
+        over_space.reshape(2 * tm, *over_space.shape[2:]), ("batch", "tm"), split_axis=0, concat_axis=0,
+        axis_index_groups=planes, tiled=True,
+    )
     mine = pieces.astype(F32).sum(0).astype(BF)
-    swapped = [lax.ppermute(mine, "batch", [(i, i ^ m) for i in range(batch)]).astype(F32) for m in (2, 3, 1)]
-    own_half = mine.astype(F32) + swapped[0]
-    other_half = swapped[1] + swapped[2]
+    other = lax.ppermute(mine, "batch", [(i, i ^ 1) for i in range(batch)])
     weight_grad = jnp.where(
-        core[0] == 0,
-        jnp.concatenate([own_half, other_half], axis=1),
-        jnp.concatenate([other_half, own_half], axis=1),
-    )
+        core[0] == 0, jnp.concatenate([mine, other], axis=1), jnp.concatenate([other, mine], axis=1)
+    ).astype(F32)
     return (output.reshape(1, frames, rows, wide, D), weight_grad)
 
 

time: 141 us -> 143 us (1.014)
  blocking collectives: 9.44 us -> 16.7 us
  starting transfers between devices: 43.5 us -> 36.4 us
    all_to_all x1, blocking collectives: 9.44 us -> 16.7 us  [per_device(): lax.all_to_all(over_space.reshape(2 * tm, *over_space.shape[2:]), ('batch...]
    ppermute x3 -> x1, starting transfers between devices: 8.84 us -> 1.82 us  [per_device(): other = lax.ppermute(mine, 'batch', [(i, i ^ 1) for i in range(batch)])]
    all_to_all x2, waiting for transfers between devices: 10.2 us -> 12.4 us  [per_device(): lax.all_to_all(v, axis, split_axis=0, concat_axis=0, tiled=True)]
    ppermute x3 -> x1, waiting for transfers between devices: 2.17 us -> 0.01 us  [per_device(): other = lax.ppermute(mine, 'batch', [(i, i ^ 1) for i in range(batch)])]
  transfers between devices with their start and end apart: 12 -> 10, of which waited for: 7 -> 6; matrix products, arithmetic and copies ran while one was open for 3% -> 3% of each run, Pallas kernels for 14% -> 14%
where the time goes in v12:
time: 143 us; the launch traced here: 142 us
  waiting for transfers between devices  49.2 us (34%)
  starting transfers between devices  36.4 us (25%)
  Pallas kernels  31.3 us (22%)
  blocking collectives  16.7 us (12%)
  local copies, waits for them, and re-layouts  4.22 us (3%)
  other arithmetic  2.27 us (2%)
  between operations  1.97 us (1%)
    all_to_all x2, waiting for transfers between devices, per_device(): lax.all_to_all(v, ('tm', 'space'), split_axis=0, concat_axis=0, axis_inde...  23.7 us
    all_to_all x1, blocking collectives, per_device(): lax.all_to_all(over_space.reshape(2 * tm, *over_space.shape[2:]), ('batch...  16.7 us
    all_to_all x2, starting transfers between devices, per_device(): lax.all_to_all(v, ('tm', 'space'), split_axis=0, concat_axis=0, axis_inde...  14 us
    all_to_all x2, waiting for transfers between devices, per_device(): lax.all_to_all(v, axis, split_axis=0, concat_axis=0, tiled=True)  12.4 us
    pallas_call x1, Pallas kernels, temporal_phase(): pl.pallas_call(temporal_kernel, in_specs=[SMEM] + [VMEM] * 4 + [HBM] * 3,...  11.4 us
    ppermute x3, waiting for transfers between devices, per_device(): lax.ppermute(chip[k - 1].astype(BF), 'space', [(i, (i + k) % space) for i...  10.8 us
    pallas_call x1, Pallas kernels, spatial_phase(): pl.pallas_call(spatial_kernel, in_specs=[SMEM, VMEM, HBM, HBM, HBM, HBM],...  10.4 us
    all_to_all x2, starting transfers between devices, per_device(): lax.all_to_all(v, axis, split_axis=0, concat_axis=0, tiled=True)  9.37 us
  transfers between devices with their start and end apart: 10, of which 6 were waited for; matrix products, arithmetic and copies ran while one was open for 3% of the time, Pallas kernels for 14%

profile of v12, /device:TPU:1, one launch (start us, length us, event | category | flops | bytes accessed | tf_op | source)
XLA Modules:
  0.0 142.1 jit_solution(18022650045737333148)
XLA Ops:
  0.6 0.0 copy-start.3
  0.6 0.0 copy-start
  0.6 7.6 %all-to-all-start = ((bf16[16,8,4,1024]{3,2,1,0:T(4,128)(2,1)}), bf16[16,8,4,1024]{3,2,1,0:T(4,128)(2,1)S(1)}, u32[]{:S(2)}, u32[]{:S(2)}) async-start(bf16[16,8,4,1024]{3,2,1,0:T(4,128)(2,1)} %bitcast.38), calls=%async_computation | async-start | bytes 2097152 | tf_op jit(solution)/shard_map/all_to_all | solution.py:379
  8.3 2.3 %copy.22 = bf16[1,2,8,32,1024]{4,3,1,2,0:T(8,128)(2,1)} copy(bf16[1,2,8,32,1024]{4,3,2,1,0:T(8,128)(2,1)} %param.19) | data formatting | bytes 2097152 | tf_op args[9]
  10.6 11.5 %all-to-all-done = bf16[16,8,4,1024]{3,2,1,0:T(4,128)(2,1)S(1)} async-done(((bf16[16,8,4,1024]{3,2,1,0:T(4,128)(2,1)}), bf16[16,8,4,1024]{3,2,1,0:T(4,128)(2,1)S(1)}, u32[]{:S(2)}, u32[]{:S(2)}) %all-to-all-start) | async-done | bytes 1048608 | tf_op jit(solution)/shard_map/all_to_all | solution.py:379
  22.1 5.8 %all-to-all-start.2 = ((bf16[8,2,32,1024]{3,2,1,0:T(8,128)(2,1)}), bf16[8,2,32,1024]{3,2,1,0:T(8,128)(2,1)S(1)}, u32[]{:S(2)}, u32[]{:S(2)}) async-start(bf16[8,2,32,1024]{3,2,1,0:T(8,128)(2,1)} %bitcast.28), calls=%async_computation.2 | async-start | bytes 2097152 | tf_op jit(solution)/shard_map/all_to_all | solution.py:371
  27.9 0.0 copy-done.3
  27.9 0.6 fusion.4
  29.7 0.1 pad_add_fusion.1.info_ref
  29.8 0.0 copy-done
  29.8 0.8 edge_norm.1
  30.6 3.4 %collective-permute-start = (bf16[4,32,1024]{2,1,0:T(8,128)(2,1)S(1)}, bf16[4,32,1024]{2,1,0:T(8,128)(2,1)S(1)}, u32[]{:S(2)}, u32[]{:S(2)}) collective-permute-start(bf16[4,32,1024]{2,1,0:T(8,128)(2,1)S(1)} %edge_norm.1), channel_id=1, source_target_pairs={{0,3},{1,2},{2,1},{3,0},{4,7},{5,6},{6,5},{7,4},{8,11},{9,10},{10,... | collective-permute-start | bytes 786440 | tf_op jit(solution)/shard_map/ppermute | solution.py:384
  33.9 7.5 %qkv_own.1 = (bf16[3,512,1024]{2,1,0:T(8,128)(2,1)}, bf16[16,32,1024]{2,1,0:T(8,128)(2,1)}) custom-call(s32[2]{0:T(128)S(1)} %pad_add_fusion.1.info_ref, bf16[8,2,8,4,1024]{4,3,2,1,0:T(4,128)(2,1)S(1)} %bitcast.30, f32[1,1024]{1,0:T(1,128)S(1)} %bitcast.33, bf16[1024,3072]{1,0:T(8,128)(2,1)} %w_ref.4), custom_call_target="tpu_custom_call" | custom-call | tf_op jit(solution)/shard_map/qkv_own/pallas_call | solution.py:111
  41.4 0.0 collective-permute-done.halo_ref
  41.5 0.0 copy-start.4
  41.5 0.0 copy-start.1
  41.5 10.4 %spatial_phase.1 = bf16[8,2,32,1024]{3,2,1,0:T(8,128)(2,1)} custom-call(s32[2]{0:T(128)S(1)} %pad_add_fusion.1.info_ref, bf16[4,32,1024]{2,1,0:T(8,128)(2,1)S(1)} %collective-permute-done.halo_ref, bf16[3,512,1024]{2,1,0:T(8,128)(2,1)} %get-tuple-element.10.qkv_ref, bf16[16,32,1024]{2,1,0:T(8,128)(2,1)} %get-tuple-element.11.tok_ref, ...), custom_call_target="tpu_custom_call" | custom-call | tf_op jit(solution)/shard_map/spatial_phase/pallas_call | solution.py:219
  51.9 0.0 all-to-all-done.2
  51.9 0.0 copy-start.2
  51.9 6.3 %all-to-all-start.1 = ((bf16[16,32,1024]{2,1,0:T(8,128)(2,1)}), bf16[16,32,1024]{2,1,0:T(8,128)(2,1)S(1)}, u32[]{:S(2)}, u32[]{:S(2)}) async-start(bf16[16,32,1024]{2,1,0:T(8,128)(2,1)} %bitcast.37), calls=%async_computation.1 | async-start | bytes 2097152 | tf_op jit(solution)/shard_map/all_to_all | solution.py:379
  58.2 0.0 copy-done.4
  58.2 0.1 broadcast_in_dim.3
  58.3 0.1 reshape_reshape.8.order_q_ref
  58.4 0.1 reshape_reshape.7.order_k_ref
  58.5 0.1 pad_add_fusion.core_ref
  58.6 12.2 %all-to-all-done.1.mid_ref = bf16[16,32,1024]{2,1,0:T(8,128)(2,1)S(1)} async-done(((bf16[16,32,1024]{2,1,0:T(8,128)(2,1)}), bf16[16,32,1024]{2,1,0:T(8,128)(2,1)S(1)}, u32[]{:S(2)}, u32[]{:S(2)}) %all-to-all-start.1) | async-done | bytes 1048608 | tf_op jit(solution)/shard_map/all_to_all | solution.py:379
  70.8 0.0 copy-done.2
  70.8 0.0 copy-done.1
  70.8 11.4 %temporal_phase.1 = (bf16[16,32,1024]{2,1,0:T(8,128)(2,1)}, bf16[4,8,32,512]{3,2,1,0:T(8,128)(2,1)S(1)}, bf16[4,8,32,512]{3,2,1,0:T(8,128)(2,1)}) custom-call(s32[2]{0:T(128)S(1)} %pad_add_fusion.core_ref, bf16[16,32,1024]{2,1,0:T(8,128)(2,1)S(1)} %all-to-all-done.1.mid_ref, s32[128,1]{1,0:T(8,128)S(1)} %reshape_reshape.8.order_q_ref, ...), custom_call_target="tpu_custom_call" | custom-call | tf_op jit(solution)/shard_map/temporal_phase/pallas_call | solution.py:304
  82.2 4.1 %collective-permute-start.1 = (bf16[4,8,32,512]{3,2,1,0:T(8,128)(2,1)S(1)}, bf16[4,8,32,512]{3,2,1,0:T(8,128)(2,1)S(1)}, u32[]{:S(2)}, u32[]{:S(2)}) collective-permute-start(bf16[4,8,32,512]{3,2,1,0:T(8,128)(2,1)S(1)} %get-tuple-element.15), channel_id=1, source_target_pairs={{0,32},{32,0},{64,96},{96,64},{1,33},{33,1},{65,97},{97,65},{2,34}... | collective-permute-start | bytes 3145736 | tf_op jit(solution)/shard_map/ppermute | solution.py:396
  86.4 2.3 %collective-permute-done.1.got_ref = bf16[4,8,32,512]{3,2,1,0:T(8,128)(2,1)S(1)} collective-permute-done((bf16[4,8,32,512]{3,2,1,0:T(8,128)(2,1)S(1)}, bf16[4,8,32,512]{3,2,1,0:T(8,128)(2,1)S(1)}, u32[]{:S(2)}, u32[]{:S(2)}) %collective-permute-start.1) | collective-permute-done | bytes 1048608 | tf_op jit(solution)/shard_map/ppermute | solution.py:396
  88.7 1.4 fusion.2
  90.0 1.0 collective-permute-start.2
  91.0 0.4 collective-permute-start.3
  91.4 2.3 %collective-permute-start.4 = (bf16[8,32,512]{2,1,0:T(8,128)(2,1)S(1)}, bf16[8,32,512]{2,1,0:T(8,128)(2,1)S(1)}, u32[]{:S(2)}, u32[]{:S(2)}) collective-permute-start(bf16[8,32,512]{2,1,0:T(8,128)(2,1)S(1)} %get-tuple-element.18), channel_id=1, source_target_pairs={{0,3},{1,0},{2,1},{3,2},{4,7},{5,4},{6,5},{7,6},{8,11},{9,8},{10,9... | collective-permute-start | bytes 786440 | tf_op jit(solution)/shard_map/ppermute | solution.py:399
  93.7 1.0 own_slot.1.own_ref
  94.7 4.4 %collective-permute-done.2.refs_0_ = bf16[8,32,512]{2,1,0:T(8,128)(2,1)S(1)} collective-permute-done((bf16[8,32,512]{2,1,0:T(8,128)(2,1)S(1)}, bf16[8,32,512]{2,1,0:T(8,128)(2,1)S(1)}, u32[]{:S(2)}, u32[]{:S(2)}) %collective-permute-start.2) | collective-permute-done | bytes 262176 | tf_op jit(solution)/shard_map/ppermute | solution.py:399
  99.1 6.3 %collective-permute-done.3.refs_1_ = bf16[8,32,512]{2,1,0:T(8,128)(2,1)S(1)} collective-permute-done((bf16[8,32,512]{2,1,0:T(8,128)(2,1)S(1)}, bf16[8,32,512]{2,1,0:T(8,128)(2,1)S(1)}, u32[]{:S(2)}, u32[]{:S(2)}) %collective-permute-start.3) | collective-permute-done | bytes 262176 | tf_op jit(solution)/shard_map/ppermute | solution.py:399
  105.5 0.0 collective-permute-done.4.refs_2_
  105.5 0.2 space_sum.1
  105.7 16.7 %all_to_all.25 = bf16[16,32,512]{2,1,0:T(8,128)(2,1)S(1)} all-to-all(bf16[16,32,512]{2,1,0:T(8,128)(2,1)S(1)} %bitcast.31), channel_id=1, replica_groups={{0,4,8,12,16,20,24,28,64,68,72,76,80,84,88,92},{32,36,40,44,48,52,56,60..., dimensions={0} | all-to-all | bytes 1048576 | tf_op jit(solution)/shard_map/all_to_all | solution.py:404
  122.4 3.6 %all-to-all-start.3 = ((bf16[8,2,32,1024]{3,2,1,0:T(8,128)(2,1)}), bf16[8,2,32,1024]{3,2,1,0:T(8,128)(2,1)S(1)}, u32[]{:S(2)}, u32[]{:S(2)}) async-start(bf16[8,2,32,1024]{3,2,1,0:T(8,128)(2,1)} %bitcast.15), calls=%async_computation.3 | async-start | bytes 2097152 | tf_op jit(solution)/shard_map/all_to_all | solution.py:371
  126.0 0.1 reduce_sum.12
  126.1 1.8 %collective-permute-start.5 = (bf16[32,512]{1,0:T(8,128)(2,1)S(1)}, bf16[32,512]{1,0:T(8,128)(2,1)S(1)}, u32[]{:S(2)}, u32[]{:S(2)}) collective-permute-start(bf16[32,512]{1,0:T(8,128)(2,1)S(1)} %reduce_sum.12), channel_id=1, source_target_pairs={{0,32},{32,0},{64,96},{96,64},{1,33},{33,1},{65,97},{97,65},{2,34}... | collective-permute-start | bytes 98312 | tf_op jit(solution)/shard_map/ppermute | solution.py:409
  127.9 12.4 %all-to-all-done.3 = bf16[8,2,32,1024]{3,2,1,0:T(8,128)(2,1)S(1)} async-done(((bf16[8,2,32,1024]{3,2,1,0:T(8,128)(2,1)}), bf16[8,2,32,1024]{3,2,1,0:T(8,128)(2,1)S(1)}, u32[]{:S(2)}, u32[]{:S(2)}) %all-to-all-start.3) | async-done | bytes 1048608 | tf_op jit(solution)/shard_map/all_to_all | solution.py:371
  140.3 1.1 copy.20
  141.4 0.0 collective-permute-done.5
  141.4 0.7 fusion.3
Async XLA Ops:
  0.6 27.3 %copy-start.3 = (s32[1,2]{1,0:T(1,128)S(1)}, s32[1,2]{1,0:T(1,128)}, u32[]{:S(2)}) copy-start(s32[1,2]{1,0:T(1,128)} %param.12) | copy-start | bytes 28
  0.6 29.1 %copy-start = (f32[1024]{0:T(1024)S(1)}, f32[1024]{0:T(1024)}, u32[]{:S(2)}) copy-start(f32[1024]{0:T(1024)} %param.13) | copy-start | bytes 12292
  0.6 21.5 %all-to-all-start = ((bf16[16,8,4,1024]{3,2,1,0:T(4,128)(2,1)}), bf16[16,8,4,1024]{3,2,1,0:T(4,128)(2,1)S(1)}, u32[]{:S(2)}, u32[]{:S(2)}) async-start(bf16[16,8,4,1024]{3,2,1,0:T(4,128)(2,1)} %bitcast.38), calls=%async_computation | async-start | bytes 2097152 | tf_op jit(solution)/shard_map/all_to_all | solution.py:379
  22.1 29.8 %all-to-all-start.2 = ((bf16[8,2,32,1024]{3,2,1,0:T(8,128)(2,1)}), bf16[8,2,32,1024]{3,2,1,0:T(8,128)(2,1)S(1)}, u32[]{:S(2)}, u32[]{:S(2)}) async-start(bf16[8,2,32,1024]{3,2,1,0:T(8,128)(2,1)} %bitcast.28), calls=%async_computation.2 | async-start | bytes 2097152 | tf_op jit(solution)/shard_map/all_to_all | solution.py:371
  30.6 10.9 %collective-permute-start = (bf16[4,32,1024]{2,1,0:T(8,128)(2,1)S(1)}, bf16[4,32,1024]{2,1,0:T(8,128)(2,1)S(1)}, u32[]{:S(2)}, u32[]{:S(2)}) collective-permute-start(bf16[4,32,1024]{2,1,0:T(8,128)(2,1)S(1)} %edge_norm.1), channel_id=1, source_target_pairs={{0,3},{1,2},{2,1},{3,0},{4,7},{5,6},{6,5},{7,4},{8,11},{9,10},{10,... | collective-permute-start | bytes 786440 | tf_op jit(solution)/shard_map/ppermute | solution.py:384
  41.5 16.8 %copy-start.4 = (s32[1,16]{1,0:T(1,128)S(1)}, s32[1,16]{1,0:T(1,128)}, u32[]{:S(2)}) copy-start(s32[1,16]{1,0:T(1,128)} %param.11) | copy-start | bytes 196
  41.5 29.3 %copy-start.1 = (f32[1024]{0:T(1024)S(1)}, f32[1024]{0:T(1024)}, u32[]{:S(2)}) copy-start(f32[1024]{0:T(1024)} %param.16) | copy-start | bytes 12292
  51.9 18.9 %copy-start.2 = (bf16[8,2,32,1024]{3,2,1,0:T(8,128)(2,1)}, bf16[8,2,32,1024]{3,2,1,0:T(8,128)(2,1)S(1)}, u32[]{:S(2)}) copy-start(bf16[8,2,32,1024]{3,2,1,0:T(8,128)(2,1)S(1)} %all-to-all-done.2) | copy-start | bytes 3145732
  51.9 18.9 %all-to-all-start.1 = ((bf16[16,32,1024]{2,1,0:T(8,128)(2,1)}), bf16[16,32,1024]{2,1,0:T(8,128)(2,1)S(1)}, u32[]{:S(2)}, u32[]{:S(2)}) async-start(bf16[16,32,1024]{2,1,0:T(8,128)(2,1)} %bitcast.37), calls=%async_computation.1 | async-start | bytes 2097152 | tf_op jit(solution)/shard_map/all_to_all | solution.py:379
  82.2 6.4 %collective-permute-start.1 = (bf16[4,8,32,512]{3,2,1,0:T(8,128)(2,1)S(1)}, bf16[4,8,32,512]{3,2,1,0:T(8,128)(2,1)S(1)}, u32[]{:S(2)}, u32[]{:S(2)}) collective-permute-start(bf16[4,8,32,512]{3,2,1,0:T(8,128)(2,1)S(1)} %get-tuple-element.15), channel_id=1, source_target_pairs={{0,32},{32,0},{64,96},{96,64},{1,33},{33,1},{65,97},{97,65},{2,34}... | collective-permute-start | bytes 3145736 | tf_op jit(solution)/shard_map/ppermute | solution.py:396
  90.0 9.1 %collective-permute-start.2 = (bf16[8,32,512]{2,1,0:T(8,128)(2,1)S(1)}, bf16[8,32,512]{2,1,0:T(8,128)(2,1)S(1)}, u32[]{:S(2)}, u32[]{:S(2)}) collective-permute-start(bf16[8,32,512]{2,1,0:T(8,128)(2,1)S(1)} %get-tuple-element.20), channel_id=1, source_target_pairs={{0,2},{1,3},{2,0},{3,1},{4,6},{5,7},{6,4},{7,5},{8,10},{9,11},{10,... | collective-permute-start | bytes 786440 | tf_op jit(solution)/shard_map/ppermute | solution.py:399
  91.0 14.4 %collective-permute-start.3 = (bf16[8,32,512]{2,1,0:T(8,128)(2,1)S(1)}, bf16[8,32,512]{2,1,0:T(8,128)(2,1)S(1)}, u32[]{:S(2)}, u32[]{:S(2)}) collective-permute-start(bf16[8,32,512]{2,1,0:T(8,128)(2,1)S(1)} %get-tuple-element.19), channel_id=1, source_target_pairs={{0,1},{1,2},{2,3},{3,0},{4,5},{5,6},{6,7},{7,4},{8,9},{9,10},{10,1... | collective-permute-start | bytes 786440 | tf_op jit(solution)/shard_map/ppermute | solution.py:399
  91.4 14.1 %collective-permute-start.4 = (bf16[8,32,512]{2,1,0:T(8,128)(2,1)S(1)}, bf16[8,32,512]{2,1,0:T(8,128)(2,1)S(1)}, u32[]{:S(2)}, u32[]{:S(2)}) collective-permute-start(bf16[8,32,512]{2,1,0:T(8,128)(2,1)S(1)} %get-tuple-element.18), channel_id=1, source_target_pairs={{0,3},{1,0},{2,1},{3,2},{4,7},{5,4},{6,5},{7,6},{8,11},{9,8},{10,9... | collective-permute-start | bytes 786440 | tf_op jit(solution)/shard_map/ppermute | solution.py:399
  122.4 17.9 %all-to-all-start.3 = ((bf16[8,2,32,1024]{3,2,1,0:T(8,128)(2,1)}), bf16[8,2,32,1024]{3,2,1,0:T(8,128)(2,1)S(1)}, u32[]{:S(2)}, u32[]{:S(2)}) async-start(bf16[8,2,32,1024]{3,2,1,0:T(8,128)(2,1)} %bitcast.15), calls=%async_computation.3 | async-start | bytes 2097152 | tf_op jit(solution)/shard_map/all_to_all | solution.py:371
  126.1 15.3 %collective-permute-start.5 = (bf16[32,512]{1,0:T(8,128)(2,1)S(1)}, bf16[32,512]{1,0:T(8,128)(2,1)S(1)}, u32[]{:S(2)}, u32[]{:S(2)}) collective-permute-start(bf16[32,512]{1,0:T(8,128)(2,1)S(1)} %reduce_sum.12), channel_id=1, source_target_pairs={{0,32},{32,0},{64,96},{96,64},{1,33},{33,1},{65,97},{97,65},{2,34}... | collective-permute-start | bytes 98312 | tf_op jit(solution)/shard_map/ppermute | solution.py:409

commit v13 on v12

--- a/solution.py
+++ b/solution.py
@@ -80,11 +80,11 @@
         first = jnp.where(half == 0, 1 - o, o) * rows
 
         def one_row(r, carry):
-            for t in range(times):
-                x = arrived_ref[t, o, r]
-                y = normalized(x.astype(F32), gain).astype(BF)
-                tok_ref[first + r, t * cols:(t + 1) * cols, :] = x
-                x_ref[first + r, t * cols:(t + 1) * cols, :] = y
+            for t in range(0, times, 2):
+                at = slice(t * cols, (t + 2) * cols)
+                x = jnp.concatenate([arrived_ref[t + i, o, r].astype(F32) for i in range(2)], axis=0)
+                tok_ref[first + r, at, :] = x.astype(BF)
+                x_ref[first + r, at, :] = normalized(x, gain).astype(BF)
             return carry
 
         lax.fori_loop(0, rows, one_row, 0)
@@ -397,7 +397,7 @@
     output = exchange(out.reshape(tm, frames, wide, D), "tm").swapaxes(0, 1)
     chip = [keep[k].astype(F32) + got[k].astype(F32) for k in range(1, space)]
     moved = [lax.ppermute(chip[k - 1].astype(BF), "space", [(i, (i + k) % space) for i in range(space)])
-             for k in sorted(range(1, space), key=lambda k: -min(k, space - k))]
+             for k in range(1, space)]
     own = own_slot(keep, got)
     over_space = space_sum(own, moved)
     planes = [[(2 * y + c) * tm + t for y in range(batch // 2) for t in range(tm)] for c in range(2)]

time: 143 us -> 143 us (level); the launches traced: 142 us -> 140 us
  waiting for transfers between devices: 49.2 us -> 47.3 us
where the time goes in v13:
time: 143 us; the launch traced here: 140 us
  waiting for transfers between devices  47.3 us (33%)
  starting transfers between devices  37 us (26%)
  Pallas kernels  31.1 us (22%)
  blocking collectives  16.2 us (11%)
  local copies, waits for them, and re-layouts  4.22 us (3%)
  other arithmetic  2.27 us (2%)
  between operations  1.97 us (1%)
    all_to_all x2, waiting for transfers between devices, per_device(): lax.all_to_all(v, ('tm', 'space'), split_axis=0, concat_axis=0, axis_inde...  23.7 us
    all_to_all x1, blocking collectives, per_device(): lax.all_to_all(over_space.reshape(2 * tm, *over_space.shape[2:]), ('batch...  16.2 us
    all_to_all x2, starting transfers between devices, per_device(): lax.all_to_all(v, ('tm', 'space'), split_axis=0, concat_axis=0, axis_inde...  14 us
    pallas_call x1, Pallas kernels, temporal_phase(): pl.pallas_call(temporal_kernel, in_specs=[SMEM] + [VMEM] * 4 + [HBM] * 3,...  11.4 us
    all_to_all x2, waiting for transfers between devices, per_device(): lax.all_to_all(v, axis, split_axis=0, concat_axis=0, tiled=True)  11.3 us
    pallas_call x1, Pallas kernels, spatial_phase(): pl.pallas_call(spatial_kernel, in_specs=[SMEM, VMEM, HBM, HBM, HBM, HBM],...  10.4 us
    ppermute x3, waiting for transfers between devices, per_device(): lax.ppermute(chip[k - 1].astype(BF), 'space', [(i, (i + k) % space) for i...  9.98 us
    all_to_all x2, starting transfers between devices, per_device(): lax.all_to_all(v, axis, split_axis=0, concat_axis=0, tiled=True)  9.37 us
  transfers between devices with their start and end apart: 10, of which 6 were waited for; matrix products, arithmetic and copies ran while one was open for 3% of the time, Pallas kernels for 14%

profile of v13, /device:TPU:1, one launch (start us, length us, event | category | flops | bytes accessed | tf_op | source)
XLA Modules:
  0.0 140.0 jit_solution(10496094681203826110)
XLA Ops:
  0.6 0.0 copy-start.3
  0.6 0.0 copy-start
  0.6 7.6 %all-to-all-start = ((bf16[16,8,4,1024]{3,2,1,0:T(4,128)(2,1)}), bf16[16,8,4,1024]{3,2,1,0:T(4,128)(2,1)S(1)}, u32[]{:S(2)}, u32[]{:S(2)}) async-start(bf16[16,8,4,1024]{3,2,1,0:T(4,128)(2,1)} %bitcast.38), calls=%async_computation | async-start | bytes 2097152 | tf_op jit(solution)/shard_map/all_to_all | solution.py:379
  8.3 2.3 %copy.22 = bf16[1,2,8,32,1024]{4,3,1,2,0:T(8,128)(2,1)} copy(bf16[1,2,8,32,1024]{4,3,2,1,0:T(8,128)(2,1)} %param.19) | data formatting | bytes 2097152 | tf_op args[9]
  10.6 11.5 %all-to-all-done = bf16[16,8,4,1024]{3,2,1,0:T(4,128)(2,1)S(1)} async-done(((bf16[16,8,4,1024]{3,2,1,0:T(4,128)(2,1)}), bf16[16,8,4,1024]{3,2,1,0:T(4,128)(2,1)S(1)}, u32[]{:S(2)}, u32[]{:S(2)}) %all-to-all-start) | async-done | bytes 1048608 | tf_op jit(solution)/shard_map/all_to_all | solution.py:379
  22.1 5.8 %all-to-all-start.2 = ((bf16[8,2,32,1024]{3,2,1,0:T(8,128)(2,1)}), bf16[8,2,32,1024]{3,2,1,0:T(8,128)(2,1)S(1)}, u32[]{:S(2)}, u32[]{:S(2)}) async-start(bf16[8,2,32,1024]{3,2,1,0:T(8,128)(2,1)} %bitcast.28), calls=%async_computation.2 | async-start | bytes 2097152 | tf_op jit(solution)/shard_map/all_to_all | solution.py:371
  27.9 0.0 copy-done.3
  27.9 0.6 fusion.4
  29.7 0.1 pad_add_fusion.1.info_ref
  29.8 0.0 copy-done
  29.8 0.8 edge_norm.1
  30.6 3.4 %collective-permute-start = (bf16[4,32,1024]{2,1,0:T(8,128)(2,1)S(1)}, bf16[4,32,1024]{2,1,0:T(8,128)(2,1)S(1)}, u32[]{:S(2)}, u32[]{:S(2)}) collective-permute-start(bf16[4,32,1024]{2,1,0:T(8,128)(2,1)S(1)} %edge_norm.1), channel_id=1, source_target_pairs={{0,3},{1,2},{2,1},{3,0},{4,7},{5,6},{6,5},{7,4},{8,11},{9,10},{10,... | collective-permute-start | bytes 786440 | tf_op jit(solution)/shard_map/ppermute | solution.py:384
  33.9 7.3 %qkv_own.1 = (bf16[3,512,1024]{2,1,0:T(8,128)(2,1)}, bf16[16,32,1024]{2,1,0:T(8,128)(2,1)}) custom-call(s32[2]{0:T(128)S(1)} %pad_add_fusion.1.info_ref, bf16[8,2,8,4,1024]{4,3,2,1,0:T(4,128)(2,1)S(1)} %bitcast.30, f32[1,1024]{1,0:T(1,128)S(1)} %bitcast.33, bf16[1024,3072]{1,0:T(8,128)(2,1)} %w_ref.4), custom_call_target="tpu_custom_call" | custom-call | tf_op jit(solution)/shard_map/qkv_own/pallas_call | solution.py:111
  41.3 0.0 collective-permute-done.halo_ref
  41.3 0.0 copy-start.4
  41.3 0.0 copy-start.1
  41.3 10.4 %spatial_phase.1 = bf16[8,2,32,1024]{3,2,1,0:T(8,128)(2,1)} custom-call(s32[2]{0:T(128)S(1)} %pad_add_fusion.1.info_ref, bf16[4,32,1024]{2,1,0:T(8,128)(2,1)S(1)} %collective-permute-done.halo_ref, bf16[3,512,1024]{2,1,0:T(8,128)(2,1)} %get-tuple-element.10.qkv_ref, bf16[16,32,1024]{2,1,0:T(8,128)(2,1)} %get-tuple-element.11.tok_ref, ...), custom_call_target="tpu_custom_call" | custom-call | tf_op jit(solution)/shard_map/spatial_phase/pallas_call | solution.py:219
  51.7 0.0 all-to-all-done.2
  51.7 0.0 copy-start.2
  51.7 6.3 %all-to-all-start.1 = ((bf16[16,32,1024]{2,1,0:T(8,128)(2,1)}), bf16[16,32,1024]{2,1,0:T(8,128)(2,1)S(1)}, u32[]{:S(2)}, u32[]{:S(2)}) async-start(bf16[16,32,1024]{2,1,0:T(8,128)(2,1)} %bitcast.37), calls=%async_computation.1 | async-start | bytes 2097152 | tf_op jit(solution)/shard_map/all_to_all | solution.py:379
  58.0 0.0 copy-done.4
  58.0 0.1 broadcast_in_dim.3
  58.1 0.1 reshape_reshape.8.order_q_ref
  58.2 0.1 reshape_reshape.7.order_k_ref
  58.3 0.1 pad_add_fusion.core_ref
  58.4 12.2 %all-to-all-done.1.mid_ref = bf16[16,32,1024]{2,1,0:T(8,128)(2,1)S(1)} async-done(((bf16[16,32,1024]{2,1,0:T(8,128)(2,1)}), bf16[16,32,1024]{2,1,0:T(8,128)(2,1)S(1)}, u32[]{:S(2)}, u32[]{:S(2)}) %all-to-all-start.1) | async-done | bytes 1048608 | tf_op jit(solution)/shard_map/all_to_all | solution.py:379
  70.6 0.0 copy-done.2
  70.6 0.0 copy-done.1
  70.6 11.4 %temporal_phase.1 = (bf16[16,32,1024]{2,1,0:T(8,128)(2,1)}, bf16[4,8,32,512]{3,2,1,0:T(8,128)(2,1)S(1)}, bf16[4,8,32,512]{3,2,1,0:T(8,128)(2,1)}) custom-call(s32[2]{0:T(128)S(1)} %pad_add_fusion.core_ref, bf16[16,32,1024]{2,1,0:T(8,128)(2,1)S(1)} %all-to-all-done.1.mid_ref, s32[128,1]{1,0:T(8,128)S(1)} %reshape_reshape.8.order_q_ref, ...), custom_call_target="tpu_custom_call" | custom-call | tf_op jit(solution)/shard_map/temporal_phase/pallas_call | solution.py:304
  82.0 4.1 %collective-permute-start.1 = (bf16[4,8,32,512]{3,2,1,0:T(8,128)(2,1)S(1)}, bf16[4,8,32,512]{3,2,1,0:T(8,128)(2,1)S(1)}, u32[]{:S(2)}, u32[]{:S(2)}) collective-permute-start(bf16[4,8,32,512]{3,2,1,0:T(8,128)(2,1)S(1)} %get-tuple-element.15), channel_id=1, source_target_pairs={{0,32},{32,0},{64,96},{96,64},{1,33},{33,1},{65,97},{97,65},{2,34}... | collective-permute-start | bytes 3145736 | tf_op jit(solution)/shard_map/ppermute | solution.py:396
  86.2 2.3 %collective-permute-done.1.got_ref = bf16[4,8,32,512]{3,2,1,0:T(8,128)(2,1)S(1)} collective-permute-done((bf16[4,8,32,512]{3,2,1,0:T(8,128)(2,1)S(1)}, bf16[4,8,32,512]{3,2,1,0:T(8,128)(2,1)S(1)}, u32[]{:S(2)}, u32[]{:S(2)}) %collective-permute-start.1) | collective-permute-done | bytes 1048608 | tf_op jit(solution)/shard_map/ppermute | solution.py:396
  88.5 1.4 fusion.2
  89.8 1.3 collective-permute-start.2
  91.1 0.1 collective-permute-start.3
  91.1 2.4 %collective-permute-start.4 = (bf16[8,32,512]{2,1,0:T(8,128)(2,1)S(1)}, bf16[8,32,512]{2,1,0:T(8,128)(2,1)S(1)}, u32[]{:S(2)}, u32[]{:S(2)}) collective-permute-start(bf16[8,32,512]{2,1,0:T(8,128)(2,1)S(1)} %get-tuple-element.18), channel_id=1, source_target_pairs={{0,3},{1,0},{2,1},{3,2},{4,7},{5,4},{6,5},{7,6},{8,11},{9,8},{10,9... | collective-permute-start | bytes 786440 | tf_op jit(solution)/shard_map/ppermute | solution.py:399
  93.6 1.0 own_slot.1.own_ref
  94.6 9.6 %collective-permute-done.2.refs_0_ = bf16[8,32,512]{2,1,0:T(8,128)(2,1)S(1)} collective-permute-done((bf16[8,32,512]{2,1,0:T(8,128)(2,1)S(1)}, bf16[8,32,512]{2,1,0:T(8,128)(2,1)S(1)}, u32[]{:S(2)}, u32[]{:S(2)}) %collective-permute-start.2) | collective-permute-done | bytes 262176 | tf_op jit(solution)/shard_map/ppermute | solution.py:399
  104.2 0.0 collective-permute-done.3.refs_1_
  104.2 0.3 collective-permute-done.4.refs_2_
  104.6 0.2 space_sum.1
  104.8 16.2 %all_to_all.25 = bf16[16,32,512]{2,1,0:T(8,128)(2,1)S(1)} all-to-all(bf16[16,32,512]{2,1,0:T(8,128)(2,1)S(1)} %bitcast.31), channel_id=1, replica_groups={{0,4,8,12,16,20,24,28,64,68,72,76,80,84,88,92},{32,36,40,44,48,52,56,60..., dimensions={0} | all-to-all | bytes 1048576 | tf_op jit(solution)/shard_map/all_to_all | solution.py:404
  120.9 3.6 %all-to-all-start.3 = ((bf16[8,2,32,1024]{3,2,1,0:T(8,128)(2,1)}), bf16[8,2,32,1024]{3,2,1,0:T(8,128)(2,1)S(1)}, u32[]{:S(2)}, u32[]{:S(2)}) async-start(bf16[8,2,32,1024]{3,2,1,0:T(8,128)(2,1)} %bitcast.15), calls=%async_computation.3 | async-start | bytes 2097152 | tf_op jit(solution)/shard_map/all_to_all | solution.py:371
  124.5 0.1 reduce_sum.12
  124.6 2.4 %collective-permute-start.5 = (bf16[32,512]{1,0:T(8,128)(2,1)S(1)}, bf16[32,512]{1,0:T(8,128)(2,1)S(1)}, u32[]{:S(2)}, u32[]{:S(2)}) collective-permute-start(bf16[32,512]{1,0:T(8,128)(2,1)S(1)} %reduce_sum.12), channel_id=1, source_target_pairs={{0,32},{32,0},{64,96},{96,64},{1,33},{33,1},{65,97},{97,65},{2,34}... | collective-permute-start | bytes 98312 | tf_op jit(solution)/shard_map/ppermute | solution.py:409
  127.0 11.3 %all-to-all-done.3 = bf16[8,2,32,1024]{3,2,1,0:T(8,128)(2,1)S(1)} async-done(((bf16[8,2,32,1024]{3,2,1,0:T(8,128)(2,1)}), bf16[8,2,32,1024]{3,2,1,0:T(8,128)(2,1)S(1)}, u32[]{:S(2)}, u32[]{:S(2)}) %all-to-all-start.3) | async-done | bytes 1048608 | tf_op jit(solution)/shard_map/all_to_all | solution.py:371
  138.3 1.1 copy.20
  139.3 0.0 collective-permute-done.5
  139.3 0.7 fusion.3
Async XLA Ops:
  0.6 27.3 %copy-start.3 = (s32[1,2]{1,0:T(1,128)S(1)}, s32[1,2]{1,0:T(1,128)}, u32[]{:S(2)}) copy-start(s32[1,2]{1,0:T(1,128)} %param.12) | copy-start | bytes 28
  0.6 29.1 %copy-start = (f32[1024]{0:T(1024)S(1)}, f32[1024]{0:T(1024)}, u32[]{:S(2)}) copy-start(f32[1024]{0:T(1024)} %param.13) | copy-start | bytes 12292
  0.6 21.5 %all-to-all-start = ((bf16[16,8,4,1024]{3,2,1,0:T(4,128)(2,1)}), bf16[16,8,4,1024]{3,2,1,0:T(4,128)(2,1)S(1)}, u32[]{:S(2)}, u32[]{:S(2)}) async-start(bf16[16,8,4,1024]{3,2,1,0:T(4,128)(2,1)} %bitcast.38), calls=%async_computation | async-start | bytes 2097152 | tf_op jit(solution)/shard_map/all_to_all | solution.py:379
  22.1 29.6 %all-to-all-start.2 = ((bf16[8,2,32,1024]{3,2,1,0:T(8,128)(2,1)}), bf16[8,2,32,1024]{3,2,1,0:T(8,128)(2,1)S(1)}, u32[]{:S(2)}, u32[]{:S(2)}) async-start(bf16[8,2,32,1024]{3,2,1,0:T(8,128)(2,1)} %bitcast.28), calls=%async_computation.2 | async-start | bytes 2097152 | tf_op jit(solution)/shard_map/all_to_all | solution.py:371
  30.6 10.7 %collective-permute-start = (bf16[4,32,1024]{2,1,0:T(8,128)(2,1)S(1)}, bf16[4,32,1024]{2,1,0:T(8,128)(2,1)S(1)}, u32[]{:S(2)}, u32[]{:S(2)}) collective-permute-start(bf16[4,32,1024]{2,1,0:T(8,128)(2,1)S(1)} %edge_norm.1), channel_id=1, source_target_pairs={{0,3},{1,2},{2,1},{3,0},{4,7},{5,6},{6,5},{7,4},{8,11},{9,10},{10,... | collective-permute-start | bytes 786440 | tf_op jit(solution)/shard_map/ppermute | solution.py:384
  41.3 16.8 %copy-start.4 = (s32[1,16]{1,0:T(1,128)S(1)}, s32[1,16]{1,0:T(1,128)}, u32[]{:S(2)}) copy-start(s32[1,16]{1,0:T(1,128)} %param.11) | copy-start | bytes 196
  41.3 29.3 %copy-start.1 = (f32[1024]{0:T(1024)S(1)}, f32[1024]{0:T(1024)}, u32[]{:S(2)}) copy-start(f32[1024]{0:T(1024)} %param.16) | copy-start | bytes 12292
  51.7 18.9 %copy-start.2 = (bf16[8,2,32,1024]{3,2,1,0:T(8,128)(2,1)}, bf16[8,2,32,1024]{3,2,1,0:T(8,128)(2,1)S(1)}, u32[]{:S(2)}) copy-start(bf16[8,2,32,1024]{3,2,1,0:T(8,128)(2,1)S(1)} %all-to-all-done.2) | copy-start | bytes 3145732
  51.7 18.9 %all-to-all-start.1 = ((bf16[16,32,1024]{2,1,0:T(8,128)(2,1)}), bf16[16,32,1024]{2,1,0:T(8,128)(2,1)S(1)}, u32[]{:S(2)}, u32[]{:S(2)}) async-start(bf16[16,32,1024]{2,1,0:T(8,128)(2,1)} %bitcast.37), calls=%async_computation.1 | async-start | bytes 2097152 | tf_op jit(solution)/shard_map/all_to_all | solution.py:379
  82.0 6.4 %collective-permute-start.1 = (bf16[4,8,32,512]{3,2,1,0:T(8,128)(2,1)S(1)}, bf16[4,8,32,512]{3,2,1,0:T(8,128)(2,1)S(1)}, u32[]{:S(2)}, u32[]{:S(2)}) collective-permute-start(bf16[4,8,32,512]{3,2,1,0:T(8,128)(2,1)S(1)} %get-tuple-element.15), channel_id=1, source_target_pairs={{0,32},{32,0},{64,96},{96,64},{1,33},{33,1},{65,97},{97,65},{2,34}... | collective-permute-start | bytes 3145736 | tf_op jit(solution)/shard_map/ppermute | solution.py:396
  89.8 14.4 %collective-permute-start.2 = (bf16[8,32,512]{2,1,0:T(8,128)(2,1)S(1)}, bf16[8,32,512]{2,1,0:T(8,128)(2,1)S(1)}, u32[]{:S(2)}, u32[]{:S(2)}) collective-permute-start(bf16[8,32,512]{2,1,0:T(8,128)(2,1)S(1)} %get-tuple-element.20), channel_id=1, source_target_pairs={{0,1},{1,2},{2,3},{3,0},{4,5},{5,6},{6,7},{7,4},{8,9},{9,10},{10,1... | collective-permute-start | bytes 786440 | tf_op jit(solution)/shard_map/ppermute | solution.py:399
  91.1 13.1 %collective-permute-start.3 = (bf16[8,32,512]{2,1,0:T(8,128)(2,1)S(1)}, bf16[8,32,512]{2,1,0:T(8,128)(2,1)S(1)}, u32[]{:S(2)}, u32[]{:S(2)}) collective-permute-start(bf16[8,32,512]{2,1,0:T(8,128)(2,1)S(1)} %get-tuple-element.19), channel_id=1, source_target_pairs={{0,2},{1,3},{2,0},{3,1},{4,6},{5,7},{6,4},{7,5},{8,10},{9,11},{10,... | collective-permute-start | bytes 786440 | tf_op jit(solution)/shard_map/ppermute | solution.py:399
  91.1 13.4 %collective-permute-start.4 = (bf16[8,32,512]{2,1,0:T(8,128)(2,1)S(1)}, bf16[8,32,512]{2,1,0:T(8,128)(2,1)S(1)}, u32[]{:S(2)}, u32[]{:S(2)}) collective-permute-start(bf16[8,32,512]{2,1,0:T(8,128)(2,1)S(1)} %get-tuple-element.18), channel_id=1, source_target_pairs={{0,3},{1,0},{2,1},{3,2},{4,7},{5,4},{6,5},{7,6},{8,11},{9,8},{10,9... | collective-permute-start | bytes 786440 | tf_op jit(solution)/shard_map/ppermute | solution.py:399
  120.9 17.3 %all-to-all-start.3 = ((bf16[8,2,32,1024]{3,2,1,0:T(8,128)(2,1)}), bf16[8,2,32,1024]{3,2,1,0:T(8,128)(2,1)S(1)}, u32[]{:S(2)}, u32[]{:S(2)}) async-start(bf16[8,2,32,1024]{3,2,1,0:T(8,128)(2,1)} %bitcast.15), calls=%async_computation.3 | async-start | bytes 2097152 | tf_op jit(solution)/shard_map/all_to_all | solution.py:371
  124.6 14.8 %collective-permute-start.5 = (bf16[32,512]{1,0:T(8,128)(2,1)S(1)}, bf16[32,512]{1,0:T(8,128)(2,1)S(1)}, u32[]{:S(2)}, u32[]{:S(2)}) collective-permute-start(bf16[32,512]{1,0:T(8,128)(2,1)S(1)} %reduce_sum.12), channel_id=1, source_target_pairs={{0,32},{32,0},{64,96},{96,64},{1,33},{33,1},{65,97},{97,65},{2,34}... | collective-permute-start | bytes 98312 | tf_op jit(solution)/shard_map/ppermute | solution.py:409
